TPU v7x, 8 devices: a whole 2x2x1 slice. The times are simulated.
8 devices in a mesh: dp: 2 (over z, y), sp: 4 (over x, core).
Axes of the slice: x: 2, y: 2, z: 1, core: 2. Of those that a mesh axis runs over, the one named last changes fastest.
Arguments:
- hidden: bfloat16 [8192, 2048], P(('dp', 'sp')), parts along dimension 0
- grad_out: bfloat16 [8192, 2048], P(('dp', 'sp')), parts along dimension 0
- positions: int32 [8192], P(('dp', 'sp')), parts along dimension 0
- doc_ids: int32 [8192], P(('dp', 'sp')), parts along dimension 0
- w_q: bfloat16 [2048, 2048], replicated
- w_k: bfloat16 [2048, 256], replicated
- w_v: bfloat16 [2048, 256], replicated
- w_o: bfloat16 [2048, 2048], replicated
Outputs:
- output 1: bfloat16 [8192, 2048], P(('dp', 'sp')), parts along dimension 0
- output 2: bfloat16 [8192, 2048], P(('dp', 'sp')), parts along dimension 0
- output 3: float32 [4096, 2048], P('dp'), parts along dimension 0
- output 4: float32 [4096, 256], P('dp'), parts along dimension 0
- output 5: float32 [4096, 256], P('dp'), parts along dimension 0
- output 6: float32 [4096, 2048], P('dp'), parts along dimension 0
There are 2 independent parts. A program takes and returns all parts, laid end to end along the dimension named above; an argument that names none is the same for every part.
All inputs are finite; a program needn't handle non-finite values.
Results may differ from a plain program's by a relative error of at most 0.0116802.
Values are sent between devices in bfloat16 or wider.
A program may use at most 1 GiB of HBM per device.

v0:
```python
import jax
import jax.numpy as jnp
from jax import lax
from jax.sharding import PartitionSpec as P, NamedSharding

HEAD_DIM = 128
ROPE_THETA = 500000.0
ROPE_FACTOR = 8.0
ROPE_LOW = 1.0
ROPE_HIGH = 4.0
ROPE_OLD_CTX = 8192.0
SCORE_LIMIT = 32 * 1024 * 1024
NEG_BIG = -1.0e30


def rope_freqs():
    half_idx = jnp.arange(HEAD_DIM // 2, dtype=jnp.float32)
    inv_freq = jnp.power(ROPE_THETA, -2.0 * half_idx / HEAD_DIM)
    wavelen = 2.0 * jnp.pi / inv_freq
    smooth = (ROPE_OLD_CTX / wavelen - ROPE_LOW) / (ROPE_HIGH - ROPE_LOW)
    mixed_freq = (1.0 - smooth) * inv_freq / ROPE_FACTOR + smooth * inv_freq
    scaled = jnp.where(wavelen > ROPE_OLD_CTX / ROPE_LOW, inv_freq / ROPE_FACTOR, mixed_freq)
    return jnp.where(wavelen < ROPE_OLD_CTX / ROPE_HIGH, inv_freq, scaled)


def rope_tables(pos_vec):
    angles = pos_vec.astype(jnp.float32)[:, None] * rope_freqs()[None, :]
    return jnp.cos(angles)[:, None, :], jnp.sin(angles)[:, None, :]


def rotate(values, cos_tab, sin_tab):
    half_dim = values.shape[-1] // 2
    first_half = values[..., :half_dim]
    second_half = values[..., half_dim:]
    return jnp.concatenate([first_half * cos_tab - second_half * sin_tab, second_half * cos_tab + first_half * sin_tab], axis=-1)


def block_rows(n_query, head_count, n_keys):
    block_len = n_query
    while block_len % 16 == 0 and head_count * block_len * n_keys > SCORE_LIMIT:
        block_len = block_len // 2
    return block_len


def dot_last(lhs_mat, rhs_mat):
    return lax.dot_general(lhs_mat, rhs_mat, (((1,), (1,)), ((), ())), preferred_element_type=jnp.float32)


def dot_first(lhs_mat, rhs_mat):
    return lax.dot_general(lhs_mat, rhs_mat, (((0,), (0,)), ((), ())), preferred_element_type=jnp.float32)


def block_probs(q_blk, k_all, pos_blk, doc_blk, k_pos, k_doc, score_scale):
    scores = jnp.einsum("qhgd,shd->hgqs", q_blk, k_all, preferred_element_type=jnp.float32) * score_scale
    allowed = (k_pos[None, :] <= pos_blk[:, None]) & (k_doc[None, :] == doc_blk[:, None])
    scores = jnp.where(allowed, scores, NEG_BIG)
    row_peak = jnp.max(scores, axis=-1, keepdims=True)
    exp_vals = jnp.exp(scores - row_peak)
    return exp_vals / jnp.sum(exp_vals, axis=-1, keepdims=True)


def attention_fwd(q_grp, k_all, v_all, q_pos, q_doc, k_pos, k_doc):
    n_query, kv_count, group_size, head_dim = q_grp.shape
    block_len = block_rows(n_query, kv_count * group_size, k_all.shape[0])
    n_blocks = n_query // block_len
    score_scale = head_dim ** -0.5

    def fwd_block(block_in):
        q_blk, pos_blk, doc_blk = block_in
        prob_f32 = block_probs(q_blk, k_all, pos_blk, doc_blk, k_pos, k_doc, score_scale)
        context = jnp.einsum("hgqs,shd->qhgd", prob_f32.astype(jnp.bfloat16), v_all, preferred_element_type=jnp.float32)
        return context.astype(jnp.bfloat16)

    blocks = (q_grp.reshape(n_blocks, block_len, kv_count, group_size, head_dim), q_pos.reshape(n_blocks, block_len), q_doc.reshape(n_blocks, block_len))
    return lax.map(fwd_block, blocks).reshape(n_query, kv_count, group_size, head_dim)


def attention_bwd(q_grp, k_all, v_all, d_ctx, q_pos, q_doc, k_pos, k_doc):
    n_query, kv_count, group_size, head_dim = q_grp.shape
    block_len = block_rows(n_query, kv_count * group_size, k_all.shape[0])
    n_blocks = n_query // block_len
    score_scale = head_dim ** -0.5

    def bwd_block(acc_pair, block_in):
        dk_acc, dv_acc = acc_pair
        q_blk, dctx_blk, pos_blk, doc_blk = block_in
        prob_f32 = block_probs(q_blk, k_all, pos_blk, doc_blk, k_pos, k_doc, score_scale)
        d_prob = jnp.einsum("qhgd,shd->hgqs", dctx_blk, v_all, preferred_element_type=jnp.float32)
        row_dot = jnp.sum(prob_f32 * d_prob, axis=-1, keepdims=True)
        d_score = (prob_f32 * (d_prob - row_dot) * score_scale).astype(jnp.bfloat16)
        dq_blk = jnp.einsum("hgqs,shd->qhgd", d_score, k_all, preferred_element_type=jnp.float32).astype(jnp.bfloat16)
        dk_acc = dk_acc + jnp.einsum("hgqs,qhgd->shd", d_score, q_blk, preferred_element_type=jnp.float32)
        dv_acc = dv_acc + jnp.einsum("hgqs,qhgd->shd", prob_f32.astype(jnp.bfloat16), dctx_blk, preferred_element_type=jnp.float32)
        return (dk_acc, dv_acc), dq_blk

    zero_acc = jnp.zeros(k_all.shape, jnp.float32)
    blocks = (q_grp.reshape(n_blocks, block_len, kv_count, group_size, head_dim), d_ctx.reshape(n_blocks, block_len, kv_count, group_size, head_dim), q_pos.reshape(n_blocks, block_len), q_doc.reshape(n_blocks, block_len))
    (dk_acc, dv_acc), dq_blocks = lax.scan(bwd_block, (zero_acc, zero_acc), blocks)
    return dq_blocks.reshape(n_query, kv_count, group_size, head_dim), dk_acc, dv_acc


def project_qkv(hidden, w_q, w_k, w_v, cos_tab, sin_tab):
    tokens = hidden.shape[0]
    q_pre = jnp.dot(hidden, w_q, preferred_element_type=jnp.float32).reshape(tokens, -1, HEAD_DIM)
    k_pre = jnp.dot(hidden, w_k, preferred_element_type=jnp.float32).reshape(tokens, -1, HEAD_DIM)
    v_pre = jnp.dot(hidden, w_v, preferred_element_type=jnp.float32).reshape(tokens, -1, HEAD_DIM)
    q_rot = rotate(q_pre, cos_tab, sin_tab).astype(jnp.bfloat16)
    k_rot = rotate(k_pre, cos_tab, sin_tab).astype(jnp.bfloat16)
    return q_rot, k_rot, v_pre.astype(jnp.bfloat16)


def input_grads(hidden, dq_rot, dk_rot, dv_val, cos_tab, sin_tab, w_q, w_k, w_v):
    tokens = hidden.shape[0]
    dq_pre = rotate(dq_rot, cos_tab, -sin_tab).astype(jnp.bfloat16).reshape(tokens, -1)
    dk_pre = rotate(dk_rot, cos_tab, -sin_tab).astype(jnp.bfloat16).reshape(tokens, -1)
    dv_pre = dv_val.reshape(tokens, -1)
    grad_hidden = (dot_last(dq_pre, w_q) + dot_last(dk_pre, w_k) + dot_last(dv_pre, w_v)).astype(jnp.bfloat16)
    return grad_hidden, dot_first(hidden, dq_pre), dot_first(hidden, dk_pre), dot_first(hidden, dv_pre)


def solution(mesh):
    sp_size = mesh.shape["sp"]

    def device_step(hidden, grad_out, positions, doc_ids, w_q, w_k, w_v, w_o):
        tokens = hidden.shape[0]
        seq_len = tokens * sp_size
        num_q = w_q.shape[1] // HEAD_DIM
        num_kv = w_k.shape[1] // HEAD_DIM
        local_q = num_q // sp_size
        local_kv = max(1, num_kv // sp_size)
        repeat = max(1, sp_size // num_kv)
        cos_tab, sin_tab = rope_tables(positions)
        q_rot, k_rot, v_val = project_qkv(hidden, w_q, w_k, w_v, cos_tab, sin_tab)
        if repeat > 1:
            k_rot = jnp.repeat(k_rot, repeat, axis=1)
            v_val = jnp.repeat(v_val, repeat, axis=1)
        q_heads = lax.all_to_all(q_rot, "sp", 1, 0, tiled=True).reshape(seq_len, local_kv, local_q // local_kv, HEAD_DIM)
        k_heads = lax.all_to_all(k_rot, "sp", 1, 0, tiled=True)
        v_heads = lax.all_to_all(v_val, "sp", 1, 0, tiled=True)
        pos_all = lax.all_gather(positions, "sp", tiled=True)
        doc_all = lax.all_gather(doc_ids, "sp", tiled=True)
        ctx_heads = attention_fwd(q_heads, k_heads, v_heads, pos_all, doc_all, pos_all, doc_all)
        ctx_flat = lax.all_to_all(ctx_heads.reshape(seq_len, local_q, HEAD_DIM), "sp", 0, 1, tiled=True).reshape(tokens, num_q * HEAD_DIM)
        attn_out = jnp.dot(ctx_flat, w_o, preferred_element_type=jnp.float32).astype(jnp.bfloat16)
        d_ctx = dot_last(grad_out, w_o).astype(jnp.bfloat16).reshape(tokens, num_q, HEAD_DIM)
        grad_wo = dot_first(ctx_flat, grad_out)
        d_ctx_heads = lax.all_to_all(d_ctx, "sp", 1, 0, tiled=True).reshape(seq_len, local_kv, local_q // local_kv, HEAD_DIM)
        dq_heads, dk_heads, dv_heads = attention_bwd(q_heads, k_heads, v_heads, d_ctx_heads, pos_all, doc_all, pos_all, doc_all)
        dq_rot = lax.all_to_all(dq_heads.reshape(seq_len, local_q, HEAD_DIM), "sp", 0, 1, tiled=True)
        dk_back = lax.all_to_all(dk_heads.astype(jnp.bfloat16), "sp", 0, 1, tiled=True)
        dv_back = lax.all_to_all(dv_heads.astype(jnp.bfloat16), "sp", 0, 1, tiled=True)
        if repeat > 1:
            dk_back = jnp.sum(dk_back.reshape(tokens, num_kv, repeat, HEAD_DIM), axis=2, dtype=jnp.float32)
            dv_back = jnp.sum(dv_back.reshape(tokens, num_kv, repeat, HEAD_DIM), axis=2, dtype=jnp.float32).astype(jnp.bfloat16)
        grad_hidden, grad_wq, grad_wk, grad_wv = input_grads(hidden, dq_rot, dk_back, dv_back, cos_tab, sin_tab, w_q, w_k, w_v)
        grad_wq, grad_wk, grad_wv, grad_wo = lax.psum((grad_wq, grad_wk, grad_wv, grad_wo), "sp")
        return attn_out, grad_hidden, grad_wq, grad_wk, grad_wv, grad_wo

    tok_spec = P(("dp", "sp"), None)
    vec_spec = P(("dp", "sp"))
    rep_spec = P(None, None)
    part_spec = P("dp", None)
    return jax.shard_map(device_step, mesh=mesh, in_specs=(tok_spec, tok_spec, vec_spec, vec_spec, rep_spec, rep_spec, rep_spec, rep_spec), out_specs=(tok_spec, tok_spec, part_spec, part_spec, part_spec, part_spec), check_vma=False)
```

profile of v0, /device:TPU:0, one launch (start us, length us, event | category | flops | bytes accessed | tf_op | source)
XLA Modules:
  0.0 2153.0 jit_solution(16933371222043034608)
XLA Ops:
  22.6 12.5 convolution_bitcast_fusion.2
  58.2 12.6 convert_bitcast_fusion
  73.9 32.8 %all-to-all-done = bf16[1024,16,128]{2,0,1:T(8,128)(2,1)} async-done(((bf16[1024,16,128]{2,0,1:T(8,128)(2,1)}), bf16[1024,16,128]{2,0,1:T(8,128)(2,1)}, u32[]{:S(2)}, u32[]{:S(2)}) %all-to-all-start) | async-done | bytes 4194336 | tf_op jit(solution)/shard_map/all_to_all | solution.py:137
  115.5 44.1 %all-to-all-done.4 = bf16[1024,16,128]{2,0,1:T(8,128)(2,1)} async-done(((bf16[1024,16,128]{2,0,1:T(8,128)(2,1)}), bf16[1024,16,128]{2,0,1:T(8,128)(2,1)}, u32[]{:S(2)}, u32[]{:S(2)}) %all-to-all-start.4) | async-done | bytes 4194336 | tf_op jit(solution)/shard_map/all_to_all | solution.py:147
  164.2 16.4 all_gather.6
  203.5 824.4 %while.26 = (s32[]{:T(128)}, f32[4096,1,128]{0,2,1:T(8,128)}, f32[4096,1,128]{0,2,1:T(8,128)}, bf16[2,2048,1,4,128]{4,1,0,3,2:T(8,128)(2,1)}, bf16[2,2048,1,4,12...) while((s32[]{:T(128)}, f32[4096,1,128]{0,2,1:T(8,128)}, ...), condition=%wide.region_8.9_spmd.clone, body=%wide.region_4.8_spmd.clone.sunk | while | flops 43850375168 | bytes 1268173440 | solution.py:98
  213.3 47.1 %fusion.131 = (f32[4,2048]{1,0:T(4,128)S(1)}, f32[2048,4,4096]{2,0,1:T(8,128)}) fusion(pred[2048,4096]{1,0:T(8,128)(4,1)S(1)} %compare_and_fusion.5, bf16[4096,1,128]{2,0,1:T(8,128)(2,1)} %get-tuple-element.589, bf16[2,2048,1,4,128]{4,1,3,2,0:T(8,128)(2,1)} %get-tuple-element.584, s32[]{:T(128)} %get-tuple-element.566), kind=kOutput, calls=%fused_computation.31.clone.1 | convolution fusion | flops 8690589696 | bytes 145785344 | tf_op jit(solution)/shard_map/while/body/eval_jaxpr/qhgd,shd->hgqs/dot_general | solution.py:54
  260.5 43.7 %fusion.132 = f32[4,2048]{1,0:T(4,128)S(1)} fusion(f32[2048,4,4096]{2,0,1:T(8,128)} %get-tuple-element.518, f32[4,2048]{1,0:T(4,128)S(1)} %get-tuple-element.519, pred[2048,4096]{1,0:T(8,128)(4,1)} %copy-done.1), kind=kLoop, calls=%fused_computation.30.clone.1 | loop fusion | flops 134209536 | bytes 142671872 | tf_op jit(solution)/shard_map/while/body/eval_jaxpr/reduce_sum | solution.py:59
  304.2 53.0 %fusion.136 = f32[4096,1,128]{0,2,1:T(8,128)} fusion(f32[4,2048]{1,0:T(4,128)S(1)} %fusion.132, f32[4,2048]{1,0:T(4,128)S(1)} %get-tuple-element.519, f32[2048,4,4096]{2,0,1:T(8,128)} %get-tuple-element.518, pred[2048,4096]{1,0:T(8,128)(4,1)} %copy-done.1, f32[4096,1,128]{0,2,1:T(8,128)} %get-tuple-element.568, ...), kind=kOutput, calls=%fused_computation.39.clone.2 | convolution fusion | flops 8758755328 | bytes 148963840 | tf_op jit(solution)/shard_map/while/body/eval_jaxpr/hgqs,qhgd->shd/dot_general | solution.py:93
  357.2 98.9 %fusion.133 = (f32[4,2048]{1,0:T(4,128)S(1)}, f32[2048,4,4096]{2,0,1:T(8,128)}) fusion(f32[4,2048]{1,0:T(4,128)S(1)} %fusion.132, f32[4,2048]{1,0:T(4,128)S(1)} %get-tuple-element.519, f32[2048,4,4096]{2,0,1:T(8,128)} %get-tuple-element.518, pred[2048,4096]{1,0:T(8,128)(4,1)} %copy-done.1, bf16[4096,1,128]{2,0,1:T(8,128)(2,1)S(1)} %copy-done.20, ...), kind=kOutput, calls=%fused_computation.24.clone.2 | convolution fusion | flops 8791252992 | bytes 280068608 | tf_op jit(solution)/shard_map/while/body/eval_jaxpr/qhgd,shd->hgqs/dot_general | solution.py:88
  456.1 105.8 %fusion.134 = bf16[4,2048,4096]{2,1,0:T(8,128)(2,1)} fusion(f32[2048,4,4096]{2,0,1:T(8,128)} %get-tuple-element.520, f32[4,2048]{1,0:T(4,128)S(1)} %get-tuple-element.521, f32[4,2048]{1,0:T(4,128)S(1)} %fusion.132, f32[4,2048]{1,0:T(4,128)S(1)} %get-tuple-element.519, f32[2048,4,4096]{2,0,1:T(8,128)} %get-tuple-element.518, ...), kind=kLoop, calls=%fused_computation.32.clone.1 | loop fusion | flops 268435456 | bytes 344031232 | tf_op jit(solution)/shard_map/reshape.44
  561.9 28.8 %fusion.137 = bf16[2,2048,1,4,128]{4,1,0,3,2:T(8,128)(2,1)} fusion(bf16[2,2048,1,4,128]{4,1,0,3,2:T(8,128)(2,1)} %get-tuple-element.569, s32[]{:T(128)} %get-tuple-element.566, bf16[4,2048,4096]{2,1,0:T(8,128)(2,1)} %fusion.134, bf16[4096,1,128]{2,0,1:T(8,128)(2,1)} %get-tuple-element.589), kind=kOutput, calls=%fused_computation.43.clone.1 | convolution fusion | flops 8590983168 | bytes 70255104 | tf_op jit(solution)/shard_map/while/body/eval_jaxpr/hgqs,shd->qhgd/dot_general | solution.py:91
  590.7 23.5 %fusion.135 = f32[4096,1,128]{0,2,1:T(8,128)S(1)} fusion(bf16[4,2048,4096]{2,1,0:T(8,128)(2,1)} %fusion.134, f32[4096,1,128]{0,2,1:T(8,128)S(1)} %copy-done.3, bf16[2,2048,1,4,128]{4,1,3,2,0:T(8,128)(2,1)} %get-tuple-element.584, s32[]{:T(128)} %get-tuple-element.566, pred[]{:T(512)S(6)} %compare.3), kind=kOutput, calls=%fused_computation.40.clone.1 | convolution fusion | flops 8590983168 | bytes 73400832 | tf_op jit(solution)/shard_map/while/body/eval_jaxpr/hgqs,qhgd->shd/dot_general | solution.py:92
  625.0 47.1 %fusion.131 = (f32[4,2048]{1,0:T(4,128)S(1)}, f32[2048,4,4096]{2,0,1:T(8,128)}) fusion(pred[2048,4096]{1,0:T(8,128)(4,1)S(1)} %compare_and_fusion.5, bf16[4096,1,128]{2,0,1:T(8,128)(2,1)} %get-tuple-element.589, bf16[2,2048,1,4,128]{4,1,3,2,0:T(8,128)(2,1)} %get-tuple-element.584, s32[]{:T(128)} %get-tuple-element.566), kind=kOutput, calls=%fused_computation.31.clone.1 | convolution fusion | flops 8690589696 | bytes 145785344 | tf_op jit(solution)/shard_map/while/body/eval_jaxpr/qhgd,shd->hgqs/dot_general | solution.py:54
  672.1 43.7 %fusion.132 = f32[4,2048]{1,0:T(4,128)S(1)} fusion(f32[2048,4,4096]{2,0,1:T(8,128)} %get-tuple-element.518, f32[4,2048]{1,0:T(4,128)S(1)} %get-tuple-element.519, pred[2048,4096]{1,0:T(8,128)(4,1)} %copy-done.1), kind=kLoop, calls=%fused_computation.30.clone.1 | loop fusion | flops 134209536 | bytes 142671872 | tf_op jit(solution)/shard_map/while/body/eval_jaxpr/reduce_sum | solution.py:59
  715.8 53.7 %fusion.136 = f32[4096,1,128]{0,2,1:T(8,128)} fusion(f32[4,2048]{1,0:T(4,128)S(1)} %fusion.132, f32[4,2048]{1,0:T(4,128)S(1)} %get-tuple-element.519, f32[2048,4,4096]{2,0,1:T(8,128)} %get-tuple-element.518, pred[2048,4096]{1,0:T(8,128)(4,1)} %copy-done.1, f32[4096,1,128]{0,2,1:T(8,128)} %get-tuple-element.568, ...), kind=kOutput, calls=%fused_computation.39.clone.2 | convolution fusion | flops 8758755328 | bytes 148963840 | tf_op jit(solution)/shard_map/while/body/eval_jaxpr/hgqs,qhgd->shd/dot_general | solution.py:93
  769.5 98.9 %fusion.133 = (f32[4,2048]{1,0:T(4,128)S(1)}, f32[2048,4,4096]{2,0,1:T(8,128)}) fusion(f32[4,2048]{1,0:T(4,128)S(1)} %fusion.132, f32[4,2048]{1,0:T(4,128)S(1)} %get-tuple-element.519, f32[2048,4,4096]{2,0,1:T(8,128)} %get-tuple-element.518, pred[2048,4096]{1,0:T(8,128)(4,1)} %copy-done.1, bf16[4096,1,128]{2,0,1:T(8,128)(2,1)S(1)} %copy-done.20, ...), kind=kOutput, calls=%fused_computation.24.clone.2 | convolution fusion | flops 8791252992 | bytes 280068608 | tf_op jit(solution)/shard_map/while/body/eval_jaxpr/qhgd,shd->hgqs/dot_general | solution.py:88
  868.4 105.8 %fusion.134 = bf16[4,2048,4096]{2,1,0:T(8,128)(2,1)} fusion(f32[2048,4,4096]{2,0,1:T(8,128)} %get-tuple-element.520, f32[4,2048]{1,0:T(4,128)S(1)} %get-tuple-element.521, f32[4,2048]{1,0:T(4,128)S(1)} %fusion.132, f32[4,2048]{1,0:T(4,128)S(1)} %get-tuple-element.519, f32[2048,4,4096]{2,0,1:T(8,128)} %get-tuple-element.518, ...), kind=kLoop, calls=%fused_computation.32.clone.1 | loop fusion | flops 268435456 | bytes 344031232 | tf_op jit(solution)/shard_map/reshape.44
  974.2 28.8 %fusion.137 = bf16[2,2048,1,4,128]{4,1,0,3,2:T(8,128)(2,1)} fusion(bf16[2,2048,1,4,128]{4,1,0,3,2:T(8,128)(2,1)} %get-tuple-element.569, s32[]{:T(128)} %get-tuple-element.566, bf16[4,2048,4096]{2,1,0:T(8,128)(2,1)} %fusion.134, bf16[4096,1,128]{2,0,1:T(8,128)(2,1)} %get-tuple-element.589), kind=kOutput, calls=%fused_computation.43.clone.1 | convolution fusion | flops 8590983168 | bytes 70255104 | tf_op jit(solution)/shard_map/while/body/eval_jaxpr/hgqs,shd->qhgd/dot_general | solution.py:91
  1003.1 23.4 %fusion.135 = f32[4096,1,128]{0,2,1:T(8,128)S(1)} fusion(bf16[4,2048,4096]{2,1,0:T(8,128)(2,1)} %fusion.134, f32[4096,1,128]{0,2,1:T(8,128)S(1)} %copy-done.3, bf16[2,2048,1,4,128]{4,1,3,2,0:T(8,128)(2,1)} %get-tuple-element.584, s32[]{:T(128)} %get-tuple-element.566, pred[]{:T(512)S(6)} %compare.3), kind=kOutput, calls=%fused_computation.40.clone.1 | convolution fusion | flops 8590983168 | bytes 73400832 | tf_op jit(solution)/shard_map/while/body/eval_jaxpr/hgqs,qhgd->shd/dot_general | solution.py:92
  1077.0 301.4 %while.25 = (s32[]{:T(128)}, bf16[2,2048,1,4,128]{4,1,0,3,2:T(8,128)(2,1)}, s32[4096]{0:T(1024)}, s32[2,2048]{1,0:T(2,128)}, s32[4096]{0:T(1024)}, /*index=5*/s3...) while((s32[]{:T(128)}, ...), condition=%wide.region_3.4_spmd, body=%wide.region_0.3_spmd.sunk | while | flops 17608720384 | bytes 480494720 | solution.py:75
  1086.4 47.1 %fusion.122 = (f32[4,2048]{1,0:T(4,128)S(1)}, f32[2048,4,4096]{2,0,1:T(8,128)}) fusion(pred[2048,4096]{1,0:T(8,128)(4,1)S(1)} %compare_and_fusion.4, bf16[4096,1,128]{2,0,1:T(8,128)(2,1)} %get-tuple-element.549, bf16[2,2048,1,4,128]{4,1,3,2,0:T(8,128)(2,1)} %get-tuple-element.548, s32[]{:T(128)} %get-tuple-element.532), kind=kOutput, calls=%fused_computation.4.clone.2 | convolution fusion | flops 8690589696 | bytes 145785344 | tf_op jit(solution)/shard_map/while/body/eval_jaxpr/qhgd,shd->hgqs/dot_general | solution.py:54
  1133.5 43.7 %fusion.123 = f32[4,2048]{1,0:T(4,128)S(1)} fusion(f32[2048,4,4096]{2,0,1:T(8,128)} %get-tuple-element.502, f32[4,2048]{1,0:T(4,128)S(1)} %get-tuple-element.503, pred[2048,4096]{1,0:T(8,128)(4,1)} %copy-done.2), kind=kLoop, calls=%fused_computation.3.clone.1 | loop fusion | flops 134209536 | bytes 142671872 | tf_op jit(solution)/shard_map/while/body/eval_jaxpr/reduce_sum | solution.py:59
  1177.2 50.4 %fusion.124 = bf16[2,2048,1,4,128]{4,1,0,3,2:T(8,128)(2,1)} fusion(bf16[2,2048,1,4,128]{4,1,0,3,2:T(8,128)(2,1)} %get-tuple-element.533, s32[]{:T(128)} %get-tuple-element.532, f32[4,2048]{1,0:T(4,128)S(1)} %fusion.123, f32[4,2048]{1,0:T(4,128)S(1)} %get-tuple-element.503, f32[2048,4,4096]{2,0,1:T(8,128)} %get-tuple-element.502, ...), kind=kOutput, calls=%fused_computation.10.clone.1 | convolution fusion | flops 8758755328 | bytes 145818112 | tf_op jit(solution)/shard_map/while/body/eval_jaxpr/hgqs,shd->qhgd/dot_general | solution.py:71
  1237.1 47.1 %fusion.122 = (f32[4,2048]{1,0:T(4,128)S(1)}, f32[2048,4,4096]{2,0,1:T(8,128)}) fusion(pred[2048,4096]{1,0:T(8,128)(4,1)S(1)} %compare_and_fusion.4, bf16[4096,1,128]{2,0,1:T(8,128)(2,1)} %get-tuple-element.549, bf16[2,2048,1,4,128]{4,1,3,2,0:T(8,128)(2,1)} %get-tuple-element.548, s32[]{:T(128)} %get-tuple-element.532), kind=kOutput, calls=%fused_computation.4.clone.2 | convolution fusion | flops 8690589696 | bytes 145785344 | tf_op jit(solution)/shard_map/while/body/eval_jaxpr/qhgd,shd->hgqs/dot_general | solution.py:54
  1284.2 43.7 %fusion.123 = f32[4,2048]{1,0:T(4,128)S(1)} fusion(f32[2048,4,4096]{2,0,1:T(8,128)} %get-tuple-element.502, f32[4,2048]{1,0:T(4,128)S(1)} %get-tuple-element.503, pred[2048,4096]{1,0:T(8,128)(4,1)} %copy-done.2), kind=kLoop, calls=%fused_computation.3.clone.1 | loop fusion | flops 134209536 | bytes 142671872 | tf_op jit(solution)/shard_map/while/body/eval_jaxpr/reduce_sum | solution.py:59
  1327.9 50.4 %fusion.124 = bf16[2,2048,1,4,128]{4,1,0,3,2:T(8,128)(2,1)} fusion(bf16[2,2048,1,4,128]{4,1,0,3,2:T(8,128)(2,1)} %get-tuple-element.533, s32[]{:T(128)} %get-tuple-element.532, f32[4,2048]{1,0:T(4,128)S(1)} %fusion.123, f32[4,2048]{1,0:T(4,128)S(1)} %get-tuple-element.503, f32[2048,4,4096]{2,0,1:T(8,128)} %get-tuple-element.502, ...), kind=kOutput, calls=%fused_computation.10.clone.1 | convolution fusion | flops 8758755328 | bytes 145818112 | tf_op jit(solution)/shard_map/while/body/eval_jaxpr/hgqs,shd->qhgd/dot_general | solution.py:71
  1437.8 15.3 convolution_bitcast_fusion.1
  1474.5 15.5 fusion.72
  1508.1 13.2 convolution_convert_fusion.1
  1521.2 590.4 %all-reduce.3.cloned.1.call-done = (f32[2048,2048]{0,1:T(8,128)}, f32[2048,256]{0,1:T(8,128)}, f32[2048,256]{0,1:T(8,128)}, f32[2048,2048]{1,0:T(8,128)}) async-done(((f32[2048,2048]{0,1:T(8,128)}, f32[2048,256]{0,1:T(8,128)}, f32[2048,256]{0,1:T(8,128)}, f32[2048,2048]{1,0:T(8,128)}), (f32[2048,2048]{0,1:T(8,128)}, f32[2048,256]{0,1:T(8,128)}, f32[2048,256]{0,1:T(8,128)}, ...) | async-done | bytes 37748752 | tf_op jit(solution)/shard_map/psum | solution.py:156
  2111.7 17.7 copy.148
  (153 shorter events, 282.3 us)
Async XLA Ops:
  13.8 21.4 copy-start.11
  17.0 36.1 %all-to-all-start.1 = ((bf16[1024,4,128]{2,0,1:T(8,128)(2,1)}), bf16[1024,4,128]{2,0,1:T(8,128)(2,1)}, u32[]{:S(2)}, u32[]{:S(2)}) async-start(bf16[1024,4,128]{2,0,1:T(8,128)(2,1)} %bitcast.19), calls=%async_computation.1 | async-start | bytes 2097152 | tf_op jit(solution)/shard_map/all_to_all | solution.py:138
  22.4 19.5 copy-start.5
  53.2 53.6 %all-to-all-start = ((bf16[1024,16,128]{2,0,1:T(8,128)(2,1)}), bf16[1024,16,128]{2,0,1:T(8,128)(2,1)}, u32[]{:S(2)}, u32[]{:S(2)}) async-start(bf16[1024,16,128]{2,0,1:T(8,128)(2,1)} %pad_maximum_fusion), calls=%async_computation | async-start | bytes 8388608 | tf_op jit(solution)/shard_map/all_to_all | solution.py:137
  70.8 40.8 %copy-start.17 = (bf16[2048,256]{1,0:T(8,128)(2,1)S(1)}, bf16[2048,256]{1,0:T(8,128)(2,1)}, u32[]{:S(2)}) copy-start(bf16[2048,256]{1,0:T(8,128)(2,1)} %param.18) | copy-start | bytes 3145732
  106.8 52.8 %all-to-all-start.4 = ((bf16[1024,16,128]{2,0,1:T(8,128)(2,1)}), bf16[1024,16,128]{2,0,1:T(8,128)(2,1)}, u32[]{:S(2)}, u32[]{:S(2)}) async-start(bf16[1024,16,128]{2,0,1:T(8,128)(2,1)} %bitcast.333), calls=%async_computation.4 | async-start | bytes 8388608 | tf_op jit(solution)/shard_map/all_to_all | solution.py:147
  111.7 52.5 %copy-start.22 = (s32[1024]{0:T(1024)S(1)}, s32[1024]{0:T(1024)}, u32[]{:S(2)}) copy-start(s32[1024]{0:T(1024)} %param.14) | copy-start | bytes 12292
  111.7 70.3 %copy-start.23 = (s32[1024]{0:T(1024)S(1)}, s32[1024]{0:T(1024)}, u32[]{:S(2)}) copy-start(s32[1024]{0:T(1024)} %param.15) | copy-start | bytes 12292
  160.6 40.3 %all-to-all-start.2 = ((bf16[1024,4,128]{2,0,1:T(8,128)(2,1)}), bf16[1024,4,128]{2,0,1:T(8,128)(2,1)S(1)}, u32[]{:S(2)}, u32[]{:S(2)}) async-start(bf16[1024,4,128]{2,0,1:T(8,128)(2,1)} %bitcast.24), calls=%async_computation.2 | async-start | bytes 2097152 | tf_op jit(solution)/shard_map/all_to_all | solution.py:139
  213.3 47.1 %copy-start.1 = (pred[2048,4096]{1,0:T(8,128)(4,1)}, pred[2048,4096]{1,0:T(8,128)(4,1)S(1)}, u32[]{:S(2)}) copy-start(pred[2048,4096]{1,0:T(8,128)(4,1)S(1)} %compare_and_fusion.5) | copy-start | bytes 25165828 | tf_op jit(solution)/shard_map/while
  304.2 53.0 %copy-start.20 = (bf16[4096,1,128]{2,0,1:T(8,128)(2,1)S(1)}, bf16[4096,1,128]{2,0,1:T(8,128)(2,1)}, u32[]{:S(2)}) copy-start(bf16[4096,1,128]{2,0,1:T(8,128)(2,1)} %get-tuple-element.591) | copy-start | bytes 3145732 | tf_op jit(solution)/shard_map/while
  561.9 28.8 %copy-start.3 = (f32[4096,1,128]{0,2,1:T(8,128)S(1)}, f32[4096,1,128]{0,2,1:T(8,128)}, u32[]{:S(2)}) copy-start(f32[4096,1,128]{0,2,1:T(8,128)} %get-tuple-element.567) | copy-start | bytes 6291460 | tf_op jit(solution)/shard_map/while
  625.0 47.2 %copy-start.1 = (pred[2048,4096]{1,0:T(8,128)(4,1)}, pred[2048,4096]{1,0:T(8,128)(4,1)S(1)}, u32[]{:S(2)}) copy-start(pred[2048,4096]{1,0:T(8,128)(4,1)S(1)} %compare_and_fusion.5) | copy-start | bytes 25165828 | tf_op jit(solution)/shard_map/while
  715.8 53.7 %copy-start.20 = (bf16[4096,1,128]{2,0,1:T(8,128)(2,1)S(1)}, bf16[4096,1,128]{2,0,1:T(8,128)(2,1)}, u32[]{:S(2)}) copy-start(bf16[4096,1,128]{2,0,1:T(8,128)(2,1)} %get-tuple-element.591) | copy-start | bytes 3145732 | tf_op jit(solution)/shard_map/while
  974.2 28.8 %copy-start.3 = (f32[4096,1,128]{0,2,1:T(8,128)S(1)}, f32[4096,1,128]{0,2,1:T(8,128)}, u32[]{:S(2)}) copy-start(f32[4096,1,128]{0,2,1:T(8,128)} %get-tuple-element.567) | copy-start | bytes 6291460 | tf_op jit(solution)/shard_map/while
  1032.2 22.9 %copy-start.14 = (f32[1024,64]{0,1:T(8,128)S(1)}, f32[1024,64]{0,1:T(8,128)}, u32[]{:S(2)}) copy-start(f32[1024,64]{0,1:T(8,128)} %get-tuple-element.371) | copy-start | bytes 786436
  1033.9 17.7 all-to-all-start.6
  1051.6 17.7 copy-start.8
  1051.6 17.7 all-to-all-start.7
  1069.3 7.6 copy-start.7
  1069.3 341.5 %all-to-all-start.5 = ((bf16[4096,4,128]{2,1,0:T(4,128)(2,1)}), bf16[4096,4,128]{2,1,0:T(4,128)(2,1)}, u32[]{:S(2)}, u32[]{:S(2)}) async-start(bf16[4096,4,128]{2,1,0:T(4,128)(2,1)} %copy.137), calls=%async_computation.5 | async-start | bytes 8388608 | tf_op jit(solution)/shard_map/all_to_all | solution.py:149
  1086.4 47.1 %copy-start.2 = (pred[2048,4096]{1,0:T(8,128)(4,1)}, pred[2048,4096]{1,0:T(8,128)(4,1)S(1)}, u32[]{:S(2)}) copy-start(pred[2048,4096]{1,0:T(8,128)(4,1)S(1)} %compare_and_fusion.4) | copy-start | bytes 25165828 | tf_op jit(solution)/shard_map/while
  1133.5 43.7 %copy-start.21 = (bf16[4096,1,128]{2,0,1:T(8,128)(2,1)S(1)}, bf16[4096,1,128]{2,0,1:T(8,128)(2,1)}, u32[]{:S(2)}) copy-start(bf16[4096,1,128]{2,0,1:T(8,128)(2,1)} %get-tuple-element.550) | copy-start | bytes 3145732 | tf_op jit(solution)/shard_map/while
  1237.1 47.1 %copy-start.2 = (pred[2048,4096]{1,0:T(8,128)(4,1)}, pred[2048,4096]{1,0:T(8,128)(4,1)S(1)}, u32[]{:S(2)}) copy-start(pred[2048,4096]{1,0:T(8,128)(4,1)S(1)} %compare_and_fusion.4) | copy-start | bytes 25165828 | tf_op jit(solution)/shard_map/while
  1284.2 43.7 %copy-start.21 = (bf16[4096,1,128]{2,0,1:T(8,128)(2,1)S(1)}, bf16[4096,1,128]{2,0,1:T(8,128)(2,1)}, u32[]{:S(2)}) copy-start(bf16[4096,1,128]{2,0,1:T(8,128)(2,1)} %get-tuple-element.550) | copy-start | bytes 3145732 | tf_op jit(solution)/shard_map/while
  1386.1 11.1 copy-start.12
  1410.8 52.7 %all-to-all-start.3 = ((bf16[4096,4,128]{2,1,0:T(4,128)(2,1)}), bf16[4096,4,128]{2,1,0:T(4,128)(2,1)}, u32[]{:S(2)}, u32[]{:S(2)}) async-start(bf16[4096,4,128]{2,1,0:T(4,128)(2,1)} %copy.129), calls=%async_computation.3 | async-start | bytes 8388608 | tf_op jit(solution)/shard_map/all_to_all | solution.py:143
  1415.7 696.0 %all-reduce.3.cloned.1.call-start = ((), (), s32[]{:S(2)}) async-start(), calls=%async_computation.8 | async-start | bytes 75497472 | tf_op jit(solution)/shard_map/psum | solution.py:156
  1420.5 3.2 copy-start.15
  1493.2 11.5 copy-start.18
  1504.6 3.4 copy-start.10
  2111.7 20.6 copy-start.16
  (7 other events, 12.9 us)
Sparse Core Ops, SparseCore 0:
  1490.1 621.5 all-reduce.2
where the time goes:
time: 2160 us; the launch traced here: 2150 us
  matrix products  800 us (37%)
  waiting for transfers between devices  690 us (32%)
  other arithmetic  460 us (21%)
  local copies, waits for them, and re-layouts  127 us (6%)
  starting transfers between devices  35.6 us (2%)
  blocking collectives  24.7 us (1%)
    psum x1, waiting for transfers between devices, device_step(): lax.psum((grad_wq, grad_wk, grad_wv, grad_wo), 'sp')  590 us
    another operation x6, other arithmetic  226 us
    dot_general x2, matrix products, bwd_block(): jnp.einsum('qhgd,shd->hgqs', dctx_blk, v_all, preferred_element_type=jnp....  198 us
    dot_general x4, matrix products, block_probs(): jnp.einsum('qhgd,shd->hgqs', q_blk, k_all, preferred_element_type=jnp.flo...  189 us
    reduce_sum x4, other arithmetic, block_probs(): return exp_vals / jnp.sum(exp_vals, axis=-1, keepdims=True)  175 us
    dot_general x2, matrix products, bwd_block(): jnp.einsum('hgqs,qhgd->shd', prob_f32.astype(jnp.bfloat16), dctx_blk, pre...  107 us
    dot_general x2, matrix products, fwd_block(): jnp.einsum('hgqs,shd->qhgd', prob_f32.astype(jnp.bfloat16), v_all, prefer...  101 us
    dot_general x2, matrix products, bwd_block(): jnp.einsum('hgqs,shd->qhgd', d_score, k_all, preferred_element_type=jnp.f...  57.7 us
  transfers between devices with their start and end apart: 9, of which 6 were waited for; matrix products, arithmetic and copies ran while one was open for 22% of the time, Pallas kernels for 0%

commit v1 on v0

v1 whole, which is shorter than its diff:
```python
import functools

import jax
import jax.numpy as jnp
from jax import lax
from jax.experimental import pallas as pl
from jax.experimental.pallas import tpu as pltpu
from jax.sharding import PartitionSpec as P

HEAD = 128
ROPE_THETA = 500000.0
ROPE_FACTOR = 8.0
ROPE_LOW = 1.0
ROPE_HIGH = 4.0
ROPE_OLD_CTX = 8192.0
NEG_BIG = -1.0e30
SCALE = HEAD ** -0.5
LOG2E = 1.4426950408889634

PAIR = 2
WIDE = PAIR * HEAD
BQ = 256
BK = 512
ALIGN = 128
BF = jnp.bfloat16
F32 = jnp.float32


def rope_freqs():
    half_idx = jnp.arange(HEAD // 2, dtype=F32)
    inv_freq = jnp.power(ROPE_THETA, -2.0 * half_idx / HEAD)
    wavelen = 2.0 * jnp.pi / inv_freq
    smooth = (ROPE_OLD_CTX / wavelen - ROPE_LOW) / (ROPE_HIGH - ROPE_LOW)
    mixed_freq = (1.0 - smooth) * inv_freq / ROPE_FACTOR + smooth * inv_freq
    scaled = jnp.where(wavelen > ROPE_OLD_CTX / ROPE_LOW, inv_freq / ROPE_FACTOR, mixed_freq)
    return jnp.where(wavelen < ROPE_OLD_CTX / ROPE_HIGH, inv_freq, scaled)


def rope_tables(pos_vec):
    angles = pos_vec.astype(F32)[:, None] * rope_freqs()[None, :]
    cos_half, sin_half = jnp.cos(angles), jnp.sin(angles)
    return jnp.concatenate([cos_half, cos_half], axis=-1), jnp.concatenate([-sin_half, sin_half], axis=-1)


def dot_nn(a, b):
    return lax.dot_general(a, b, (((1,), (0,)), ((), ())), preferred_element_type=F32)


def dot_nt(a, b):
    return lax.dot_general(a, b, (((1,), (1,)), ((), ())), preferred_element_type=F32)


def swap_halves(v):
    return pltpu.roll(v, HEAD // 2, 1)


def cost(flops, nbytes, trans=0):
    return pl.CostEstimate(flops=int(flops), bytes_accessed=int(nbytes), transcendentals=int(trans))


def params(**kw):
    return pltpu.CompilerParams(vmem_limit_bytes=60 * 1024 * 1024, **kw)


def kv_kernel(s_ref, x_ref, wk_ref, wv_ref, cos_ref, sin_ref, *rest):
    out_ref = rest[-1]
    x = x_ref[...]
    k = dot_nn(x, wk_ref[...])
    k = k * cos_ref[...] + swap_halves(k) * sin_ref[...]
    out_ref[:, :HEAD] = k.astype(BF)
    out_ref[:, HEAD:] = dot_nn(x, wv_ref[...]).astype(BF)


def kv_proj(sel, x, w_k, w_v, cos_t, sin_t, prev):
    tokens, width = x.shape
    half = tokens // 2
    extra = [] if prev is None else [prev]
    return pl.pallas_call(
        kv_kernel,
        grid_spec=pltpu.PrefetchScalarGridSpec(
            num_scalar_prefetch=1,
            grid=(2,),
            in_specs=[
                pl.BlockSpec((half, width), lambda m, s: (m, 0)),
                pl.BlockSpec((width, HEAD), lambda m, s: (0, s[0])),
                pl.BlockSpec((width, HEAD), lambda m, s: (0, s[0])),
                pl.BlockSpec((half, HEAD), lambda m, s: (s[1] * 2 + m, 0)),
                pl.BlockSpec((half, HEAD), lambda m, s: (s[1] * 2 + m, 0)),
            ] + [pl.BlockSpec(memory_space=pl.ANY)] * len(extra),
            out_specs=pl.BlockSpec((half, 2 * HEAD), lambda m, s: (s[1] * 2 + m, 0)),
        ),
        out_shape=jax.ShapeDtypeStruct((2 * tokens, 2 * HEAD), BF),
        input_output_aliases={} if prev is None else {6: 0},
        compiler_params=params(),
        cost_estimate=cost(2 * tokens * width * 2 * HEAD, tokens * width * 2),
        name="kv_proj",
    )(sel, x, w_k, w_v, cos_t, sin_t, *extra)


def q_kernel(s_ref, x_ref, wq_ref, cos_ref, sin_ref, *rest):
    out_ref = rest[-1]
    q = dot_nn(x_ref[...], wq_ref[...])
    for h in range(PAIR):
        part = q[:, h * HEAD:(h + 1) * HEAD]
        out_ref[:, h * HEAD:(h + 1) * HEAD] = (part * cos_ref[...] + swap_halves(part) * sin_ref[...]).astype(BF)


def q_proj(sel, x, w_q, cos_t, sin_t, prev):
    tokens, width = x.shape
    cols = w_q.shape[1] // 2
    n = cols // WIDE
    extra = [] if prev is None else [prev]
    return pl.pallas_call(
        q_kernel,
        grid_spec=pltpu.PrefetchScalarGridSpec(
            num_scalar_prefetch=1,
            grid=(n,),
            in_specs=[
                pl.BlockSpec((tokens, width), lambda j, s: (0, 0)),
                pl.BlockSpec((width, WIDE), lambda j, s: (0, s[0] * n + j)),
                pl.BlockSpec((tokens, HEAD), lambda j, s: (s[1], 0)),
                pl.BlockSpec((tokens, HEAD), lambda j, s: (s[1], 0)),
            ] + [pl.BlockSpec(memory_space=pl.ANY)] * len(extra),
            out_specs=pl.BlockSpec((tokens, WIDE), lambda j, s: (s[1], j)),
        ),
        out_shape=jax.ShapeDtypeStruct((2 * tokens, cols), BF),
        input_output_aliases={} if prev is None else {5: 0},
        compiler_params=params(),
        cost_estimate=cost(2 * tokens * width * cols, tokens * width * 2 + cols * width * 2),
        name="q_proj",
    )(sel, x, w_q, cos_t, sin_t, *extra)


def dctx_kernel(s_ref, g_ref, wo_ref, *rest):
    out_ref = rest[-1]
    out_ref[...] = dot_nt(g_ref[...], wo_ref[...]).astype(BF)


def dctx_proj(sel, g, w_o, prev):
    tokens, width = g.shape
    cols = w_o.shape[0] // 2
    n = cols // WIDE
    extra = [] if prev is None else [prev]
    return pl.pallas_call(
        dctx_kernel,
        grid_spec=pltpu.PrefetchScalarGridSpec(
            num_scalar_prefetch=1,
            grid=(n,),
            in_specs=[
                pl.BlockSpec((tokens, width), lambda j, s: (0, 0)),
                pl.BlockSpec((WIDE, width), lambda j, s: (s[0] * n + j, 0)),
            ] + [pl.BlockSpec(memory_space=pl.ANY)] * len(extra),
            out_specs=pl.BlockSpec((tokens, WIDE), lambda j, s: (s[1], j)),
        ),
        out_shape=jax.ShapeDtypeStruct((2 * tokens, cols), BF),
        input_output_aliases={} if prev is None else {3: 0},
        compiler_params=params(),
        cost_estimate=cost(2 * tokens * width * cols, tokens * width * 2 + cols * width * 2),
        name="dctx_proj",
    )(sel, g, w_o, *extra)


def flip_kernel(x_ref, out_ref):
    out_ref[...] = x_ref[...].T


def flip(x):
    rows, cols = x.shape
    step = 512
    return pl.pallas_call(
        flip_kernel,
        grid=(cols // step,),
        in_specs=[pl.BlockSpec((rows, step), lambda n: (0, n))],
        out_specs=pl.BlockSpec((step, rows), lambda n: (n, 0)),
        out_shape=jax.ShapeDtypeStruct((cols, rows), x.dtype),
        compiler_params=params(),
        cost_estimate=cost(rows * cols * 512, rows * cols * 4),
        name="flip",
    )(x)


def attn_kernel(first, lo_ref, nb_ref, q_ref, do_ref, qdoc_ref, kdoc_ref, cos_ref, sin_ref, kvp_ref, kvc_ref, *rest):
    if first:
        act_ref, ctxt_ref, dk_ref, dv_ref = rest[:4]
        scratch = rest[4:]
    else:
        dk_in, dv_in, act_ref, ctxt_ref, dk_ref, dv_ref = rest[:6]
        scratch = rest[6:]
    k_s, v_s, s_s, dp_s, m_s, l_s, d_s, qd_s, ctx_s, dq_s, q_s, do_s, qt_s, dot_s = scratch
    i = pl.program_id(0)
    chip_len = kvc_ref.shape[0]

    @pl.when(i == 0)
    def _():
        k_s[:chip_len, :] = kvp_ref[:, :HEAD]
        v_s[:chip_len, :] = kvp_ref[:, HEAD:]
        k_s[chip_len:2 * chip_len, :] = kvc_ref[:, :HEAD]
        v_s[chip_len:2 * chip_len, :] = kvc_ref[:, HEAD:]
        k_s[2 * chip_len:, :] = jnp.zeros((BK, HEAD), BF)
        v_s[2 * chip_len:, :] = jnp.zeros((BK, HEAD), BF)
        if first:
            dk_ref[...] = jnp.zeros_like(dk_ref)
            dv_ref[...] = jnp.zeros_like(dv_ref)
        else:
            dk_ref[...] = dk_in[...]
            dv_ref[...] = dv_in[...]

    for h in range(PAIR):
        rows = slice(h * BQ, (h + 1) * BQ)
        cols = slice(h * HEAD, (h + 1) * HEAD)
        q_s[rows, :] = q_ref[:, cols]
        do_s[rows, :] = do_ref[:, cols]
        qt_s[:, rows] = q_ref[:, cols].T
        dot_s[:, rows] = do_ref[:, cols].T
    qd_s[...] = jnp.broadcast_to(qdoc_ref[...], (BQ, HEAD))
    m_s[...] = jnp.full(m_s.shape, NEG_BIG, F32)
    l_s[...] = jnp.zeros(l_s.shape, F32)
    d_s[...] = jnp.zeros(d_s.shape, F32)
    ctx_s[...] = jnp.zeros(ctx_s.shape, F32)
    dq_s[...] = jnp.zeros(dq_s.shape, F32)
    lo = lo_ref[i]
    n_blocks = nb_ref[i]
    lanes = BK // HEAD

    def fold(v, op):
        out = v[:, :HEAD]
        for n in range(1, lanes):
            out = op(out, v[:, n * HEAD:(n + 1) * HEAD])
        return out

    def spread(v):
        return jnp.concatenate([v] * lanes, axis=1)

    def offset(b):
        return pl.multiple_of(lo + b * BK, ALIGN)

    def scores(b, carry):
        off = offset(b)
        s = dot_nt(q_s[...], k_s[pl.ds(off, BK), :])
        key = off + lax.broadcasted_iota(jnp.int32, (BQ, BK), 1)
        query = chip_len + i * BQ + lax.broadcasted_iota(jnp.int32, (BQ, BK), 0)
        keep = (key <= query) & (kdoc_ref[:, pl.ds(off, BK)] == spread(qd_s[...]))
        for h in range(PAIR):
            rows = slice(h * BQ, (h + 1) * BQ)
            sh = jnp.where(keep, s[rows, :], NEG_BIG)
            s_s[b, rows, :] = sh
            m_s[rows, :] = jnp.maximum(m_s[rows, :], fold(sh, jnp.maximum))
        return carry

    lax.fori_loop(0, n_blocks, scores, 0)
    m_s[...] = jnp.broadcast_to(jnp.max(m_s[...], axis=1, keepdims=True), m_s.shape)

    def weights(b, carry):
        dp = dot_nt(do_s[...], v_s[pl.ds(offset(b), BK), :])
        e = jnp.exp2((s_s[b] - spread(m_s[...])) * (SCALE * LOG2E))
        s_s[b] = e
        dp_s[b] = dp
        l_s[...] += fold(e, jnp.add)
        d_s[...] += fold(e * dp, jnp.add)
        return carry

    lax.fori_loop(0, n_blocks, weights, 0)
    inv = 1.0 / jnp.sum(l_s[...], axis=1, keepdims=True)
    delta = jnp.sum(d_s[...], axis=1, keepdims=True) * inv
    l_s[...] = jnp.broadcast_to(inv, l_s.shape)
    d_s[...] = jnp.broadcast_to(delta, d_s.shape)

    def grads(b, carry):
        off = offset(b)
        p = s_s[b] * spread(l_s[...])
        pb = p.astype(BF)
        ds = (p * (dp_s[b] - spread(d_s[...])) * SCALE).astype(BF)
        ctx_s[...] += dot_nn(pb, v_s[pl.ds(off, BK), :])
        dq_s[...] += dot_nn(ds, k_s[pl.ds(off, BK), :])
        dv_ref[:, pl.ds(off, BK)] += dot_nn(dot_s[...], pb)
        dk_ref[:, pl.ds(off, BK)] += dot_nn(qt_s[...], ds)
        return carry

    lax.fori_loop(0, n_blocks, grads, 0)
    for h in range(PAIR):
        rows = slice(h * BQ, (h + 1) * BQ)
        cols = slice(h * HEAD, (h + 1) * HEAD)
        ctx = ctx_s[rows, :].astype(BF)
        act_ref[0, :, cols] = ctx
        ctxt_ref[cols, :] = ctx.T
        dq = dq_s[rows, :].astype(BF).astype(F32)
        act_ref[1, :, cols] = (dq * cos_ref[...] - swap_halves(dq) * sin_ref[...]).astype(BF)


def attention(chunk, lo, n_blocks, q, dctx, qdoc, kdoc, cos_t, sin_t, kv_prev, kv_chip, acc):
    chip_len = q.shape[0]
    padded = 2 * chip_len + BK
    max_blocks = 2 * chip_len // BK + 1
    rows = PAIR * BQ
    first = acc is None
    full = lambda shape: pl.BlockSpec(shape, lambda i, *s: (0,) * len(shape))
    acc_shape = jax.ShapeDtypeStruct((HEAD, padded), F32)
    pairs = chip_len * chip_len * PAIR
    return pl.pallas_call(
        functools.partial(attn_kernel, first),
        grid_spec=pltpu.PrefetchScalarGridSpec(
            num_scalar_prefetch=2,
            grid=(chip_len // BQ,),
            in_specs=[
                pl.BlockSpec((BQ, WIDE), lambda i, *s: (i, chunk)),
                pl.BlockSpec((BQ, WIDE), lambda i, *s: (i, chunk)),
                pl.BlockSpec((BQ, 1), lambda i, *s: (i, 0)),
                full((1, padded)),
                pl.BlockSpec((BQ, HEAD), lambda i, *s: (i, 0)),
                pl.BlockSpec((BQ, HEAD), lambda i, *s: (i, 0)),
                full((chip_len, 2 * HEAD)),
                full((chip_len, 2 * HEAD)),
            ] + ([] if first else [full((HEAD, padded))] * 2),
            out_specs=[
                pl.BlockSpec((2, BQ, WIDE), lambda i, *s: (0, i, 0)),
                pl.BlockSpec((WIDE, BQ), lambda i, *s: (0, i)),
                full((HEAD, padded)),
                full((HEAD, padded)),
            ],
            scratch_shapes=[
                pltpu.VMEM((padded, HEAD), BF),
                pltpu.VMEM((padded, HEAD), BF),
                pltpu.VMEM((max_blocks, rows, BK), F32),
                pltpu.VMEM((max_blocks, rows, BK), F32),
                pltpu.VMEM((rows, HEAD), F32),
                pltpu.VMEM((rows, HEAD), F32),
                pltpu.VMEM((rows, HEAD), F32),
                pltpu.VMEM((BQ, HEAD), jnp.int32),
                pltpu.VMEM((rows, HEAD), F32),
                pltpu.VMEM((rows, HEAD), F32),
                pltpu.VMEM((rows, HEAD), BF),
                pltpu.VMEM((rows, HEAD), BF),
                pltpu.VMEM((HEAD, rows), BF),
                pltpu.VMEM((HEAD, rows), BF),
            ],
        ),
        out_shape=[
            jax.ShapeDtypeStruct((2, chip_len, WIDE), BF),
            jax.ShapeDtypeStruct((WIDE, chip_len), BF),
            acc_shape,
            acc_shape,
        ],
        input_output_aliases={} if first else {10: 2, 11: 3},
        compiler_params=params(),
        cost_estimate=cost(pairs * HEAD * 2 * 6, 12 * 1024 * 1024, pairs),
        name="attention",
    )(lo, n_blocks, q, dctx, qdoc, kdoc, cos_t, sin_t, kv_prev, kv_chip, *([] if first else acc))


def kv_finish_kernel(dk_ref, dv_ref, far_ref, cos_ref, sin_ref, out_ref):
    dk = (dk_ref[...] + far_ref[0].astype(F32)).astype(BF).astype(F32).T
    dv = (dv_ref[...] + far_ref[1].astype(F32)).T
    out_ref[:, :HEAD] = (dk * cos_ref[...] - swap_halves(dk) * sin_ref[...]).astype(BF)
    out_ref[:, HEAD:] = dv.astype(BF)


def kv_finish(dk, dv, far, cos_t, sin_t):
    chip_len = cos_t.shape[0]
    step = 512
    skip = chip_len // step
    return pl.pallas_call(
        kv_finish_kernel,
        grid=(chip_len // step,),
        in_specs=[
            pl.BlockSpec((HEAD, step), lambda t: (0, skip + t)),
            pl.BlockSpec((HEAD, step), lambda t: (0, skip + t)),
            pl.BlockSpec((2, HEAD, step), lambda t: (0, 0, t)),
            pl.BlockSpec((step, HEAD), lambda t: (t, 0)),
            pl.BlockSpec((step, HEAD), lambda t: (t, 0)),
        ],
        out_specs=pl.BlockSpec((step, 2 * HEAD), lambda t: (t, 0)),
        out_shape=jax.ShapeDtypeStruct((chip_len, 2 * HEAD), BF),
        compiler_params=params(),
        cost_estimate=cost(chip_len * HEAD * 64, chip_len * HEAD * 16),
        name="kv_finish",
    )(dk, dv, far, cos_t, sin_t)


def wgrad_kernel(s_ref, xt_own, xt_oth, act_ref, g_own, g_oth, ctxt_ref, out_ref):
    tokens = xt_own.shape[1]
    own = pl.ds(pl.multiple_of(s_ref[0] * tokens, tokens), tokens)
    oth = pl.ds(pl.multiple_of((1 - s_ref[0]) * tokens, tokens), tokens)
    out_ref[0] = (dot_nn(xt_own[...], act_ref[0, own, :]) + dot_nn(xt_oth[...], act_ref[0, oth, :])).astype(BF)
    gwo = (dot_nn(ctxt_ref[:, own], g_own[...]) + dot_nn(ctxt_ref[:, oth], g_oth[...])).astype(BF)
    for n in range(gwo.shape[1] // WIDE):
        out_ref[1, n * WIDE:(n + 1) * WIDE, :] = gwo[:, n * WIDE:(n + 1) * WIDE]


def wgrad(core, xt_own, xt_oth, act, g_own, g_oth, ctxt):
    width, tokens = xt_own.shape
    step = 512
    return pl.pallas_call(
        wgrad_kernel,
        grid_spec=pltpu.PrefetchScalarGridSpec(
            num_scalar_prefetch=1,
            grid=(width // step,),
            in_specs=[
                pl.BlockSpec((step, tokens), lambda n, s: (n, 0)),
                pl.BlockSpec((step, tokens), lambda n, s: (n, 0)),
                pl.BlockSpec((1, 2 * tokens, WIDE), lambda n, s: (1, 0, 0)),
                pl.BlockSpec((tokens, step), lambda n, s: (0, n)),
                pl.BlockSpec((tokens, step), lambda n, s: (0, n)),
                pl.BlockSpec((WIDE, 2 * tokens), lambda n, s: (0, 0)),
            ],
            out_specs=pl.BlockSpec((2, step, WIDE), lambda n, s: (0, n, 0)),
        ),
        out_shape=jax.ShapeDtypeStruct((2, width, WIDE), BF),
        compiler_params=params(),
        cost_estimate=cost(8 * tokens * width * WIDE, 8 * tokens * width),
        name="wgrad",
    )(core, xt_own, xt_oth, act, g_own, g_oth, ctxt)


def kvgrad_kernel(s_ref, xt_own, xt_oth, dkv_ref, out_ref):
    tokens = xt_own.shape[1]
    own = pl.ds(pl.multiple_of(s_ref[0] * tokens, tokens), tokens)
    oth = pl.ds(pl.multiple_of((1 - s_ref[0]) * tokens, tokens), tokens)
    out_ref[...] = (dot_nn(xt_own[...], dkv_ref[own, :]) + dot_nn(xt_oth[...], dkv_ref[oth, :])).astype(BF)


def kvgrad(core, xt_own, xt_oth, dkv):
    width, tokens = xt_own.shape
    step = 512
    return pl.pallas_call(
        kvgrad_kernel,
        grid_spec=pltpu.PrefetchScalarGridSpec(
            num_scalar_prefetch=1,
            grid=(width // step,),
            in_specs=[
                pl.BlockSpec((step, tokens), lambda n, s: (n, 0)),
                pl.BlockSpec((step, tokens), lambda n, s: (n, 0)),
                pl.BlockSpec((2 * tokens, 2 * HEAD), lambda n, s: (0, 0)),
            ],
            out_specs=pl.BlockSpec((step, 2 * HEAD), lambda n, s: (n, 0)),
        ),
        out_shape=jax.ShapeDtypeStruct((width, 2 * HEAD), BF),
        compiler_params=params(),
        cost_estimate=cost(4 * tokens * width * 2 * HEAD, 4 * tokens * width),
        name="kvgrad",
    )(core, xt_own, xt_oth, dkv)


def combine_kernel(s_ref, a_ref, b_ref, c_ref, d_ref, *rest):
    gq_ref, go_ref = rest[-2:]

    def put(u_ref, v_ref):
        gq_ref[...] = u_ref[0].astype(F32) + v_ref[0].astype(F32)
        for n in range(u_ref.shape[1] // WIDE):
            rows = slice(n * WIDE, (n + 1) * WIDE)
            go_ref[:, rows] = u_ref[1, rows, :].astype(F32) + v_ref[1, rows, :].astype(F32)

    @pl.when(pl.program_id(0) == 0)
    def _():
        put(a_ref, b_ref)

    @pl.when(pl.program_id(0) == 1)
    def _():
        put(c_ref, d_ref)


def combine(core, chunk, n_chunks, parts, prev):
    width = parts[0].shape[1]
    step = 512
    last = width // step - 1
    near = pl.BlockSpec((2, step, WIDE), lambda w, r, s: (0, r + w * (last - r), 0))
    far = pl.BlockSpec((2, step, WIDE), lambda w, r, s: (0, r * w, 0))

    def place(w, s):
        return (s[0] + w - 2 * s[0] * w) * n_chunks + chunk

    shape = jax.ShapeDtypeStruct((width, 2 * n_chunks * WIDE), F32)
    shape_o = jax.ShapeDtypeStruct((2 * n_chunks * WIDE, width), F32)
    extra = [] if prev is None else list(prev)
    return pl.pallas_call(
        combine_kernel,
        grid_spec=pltpu.PrefetchScalarGridSpec(
            num_scalar_prefetch=1,
            grid=(2, width // step),
            in_specs=[near, near, far, far] + [pl.BlockSpec(memory_space=pl.ANY)] * len(extra),
            out_specs=[
                pl.BlockSpec((step, WIDE), lambda w, r, s: (r, place(w, s))),
                pl.BlockSpec((WIDE, step), lambda w, r, s: (place(w, s), r)),
            ],
        ),
        out_shape=[shape, shape_o],
        input_output_aliases={} if prev is None else {5: 0, 6: 1},
        compiler_params=params(),
        cost_estimate=cost(16 * width * WIDE * 64, 32 * width * WIDE),
        name="combine",
    )(core, *parts, *extra)


def fill_heads(core, own_refs, oth_refs, lhs):
    n = len(own_refs)
    for j in range(n):
        lhs[:, pl.ds(pl.multiple_of((core * n + j) * WIDE, WIDE), WIDE)] = own_refs[j][0]
        lhs[:, pl.ds(pl.multiple_of(((1 - core) * n + j) * WIDE, WIDE), WIDE)] = oth_refs[j][0]


def attn_out_kernel(n, s_ref, *refs):
    own_refs, oth_refs = refs[:n], refs[n:2 * n]
    wo_ref, out_ref, lhs = refs[2 * n:]

    @pl.when(pl.program_id(0) == 0)
    def _():
        fill_heads(s_ref[0], own_refs, oth_refs, lhs)

    out_ref[...] = dot_nn(lhs[...], wo_ref[...]).astype(BF)


def attn_out(core, own, oth, w_o):
    n = len(own)
    tokens = own[0].shape[1] // 2
    heads, width = w_o.shape
    step = 512
    return pl.pallas_call(
        functools.partial(attn_out_kernel, n),
        grid_spec=pltpu.PrefetchScalarGridSpec(
            num_scalar_prefetch=1,
            grid=(width // step,),
            in_specs=[pl.BlockSpec((1, tokens, WIDE), lambda k, s: (0, s[0], 0))] * (2 * n)
            + [pl.BlockSpec((heads, step), lambda k, s: (0, k))],
            out_specs=pl.BlockSpec((tokens, step), lambda k, s: (0, k)),
            scratch_shapes=[pltpu.VMEM((tokens, heads), BF)],
        ),
        out_shape=jax.ShapeDtypeStruct((tokens, width), BF),
        compiler_params=params(),
        cost_estimate=cost(2 * tokens * heads * width, 2 * heads * width + 4 * tokens * width),
        name="attn_out",
    )(core, *own, *oth, w_o)


def hidden_kernel(n, s_ref, *refs):
    own_refs, oth_refs = refs[:n], refs[n:2 * n]
    kv_own, kv_oth, wq_ref, wk_ref, wv_ref, out_ref, lhs, klhs, vlhs = refs[2 * n:]
    core = s_ref[0]

    @pl.when(pl.program_id(0) == 0)
    def _():
        fill_heads(core, own_refs, oth_refs, lhs)
        for place, ref in ((core, kv_own), (1 - core, kv_oth)):
            where = pl.ds(pl.multiple_of(place * HEAD, HEAD), HEAD)
            klhs[:, where] = ref[:, :HEAD]
            vlhs[:, where] = ref[:, HEAD:]

    out_ref[...] = (
        dot_nt(lhs[...], wq_ref[...]) + dot_nt(klhs[...], wk_ref[...]) + dot_nt(vlhs[...], wv_ref[...])
    ).astype(BF)


def grad_hidden(core, own, oth, kv_own, kv_oth, w_q, w_k, w_v):
    n = len(own)
    tokens = own[0].shape[1] // 2
    width, heads = w_q.shape
    kv_cols = w_k.shape[1]
    step = 512
    return pl.pallas_call(
        functools.partial(hidden_kernel, n),
        grid_spec=pltpu.PrefetchScalarGridSpec(
            num_scalar_prefetch=1,
            grid=(width // step,),
            in_specs=[pl.BlockSpec((1, tokens, WIDE), lambda k, s: (1, s[0], 0))] * (2 * n)
            + [pl.BlockSpec((tokens, 2 * HEAD), lambda k, s: (s[0], 0))] * 2
            + [
                pl.BlockSpec((step, heads), lambda k, s: (k, 0)),
                pl.BlockSpec((step, kv_cols), lambda k, s: (k, 0)),
                pl.BlockSpec((step, kv_cols), lambda k, s: (k, 0)),
            ],
            out_specs=pl.BlockSpec((tokens, step), lambda k, s: (0, k)),
            scratch_shapes=[
                pltpu.VMEM((tokens, heads), BF),
                pltpu.VMEM((tokens, kv_cols), BF),
                pltpu.VMEM((tokens, kv_cols), BF),
            ],
        ),
        out_shape=jax.ShapeDtypeStruct((tokens, width), BF),
        compiler_params=params(),
        cost_estimate=cost(2 * tokens * (heads + 2 * kv_cols) * width, 2 * heads * width + 4 * tokens * width),
        name="grad_hidden",
    )(core, *own, *oth, kv_own, kv_oth, w_q, w_k, w_v)


def solution(mesh):
    n_dev = mesh.shape["sp"]
    n_chunks = 4
    near_perm = [(d, d ^ 1) for d in range(n_dev)]
    far_perm = [(d, d ^ 2) for d in range(n_dev)]
    down_perm = [(0, 2), (1, 3)]
    up_perm = [(2, 0), (3, 1)]

    def near(v):
        return lax.ppermute(v, "sp", near_perm)

    def far(v):
        return lax.ppermute(v, "sp", far_perm)

    def device_step(hidden, grad_out, positions, doc_ids, w_q, w_k, w_v, w_o):
        tokens = hidden.shape[0]
        chip_len = 2 * tokens
        assert n_chunks == w_q.shape[1] // (2 * WIDE)
        place = lax.axis_index("sp")
        core_id, chip_id = place % 2, place // 2
        core = core_id.astype(jnp.int32)[None]
        sel_own = jnp.stack([core_id, core_id]).astype(jnp.int32)
        sel_oth = jnp.stack([core_id, 1 - core_id]).astype(jnp.int32)

        pos_doc = jnp.stack([positions, doc_ids])
        pos_doc_oth = near(pos_doc)
        x_oth = near(hidden)
        g_oth = near(grad_out)
        pos_doc = jnp.where(
            core_id == 0,
            jnp.concatenate([pos_doc, pos_doc_oth], axis=1),
            jnp.concatenate([pos_doc_oth, pos_doc], axis=1),
        )
        doc_chip = pos_doc[1]
        doc_far = far(doc_chip)
        cos_t, sin_t = rope_tables(pos_doc[0])

        heads_doc = doc_chip[::BQ]
        lo = jnp.sum(doc_chip[None, :] < heads_doc[:, None], axis=1, dtype=jnp.int32)
        lo_far = jnp.sum(doc_far[None, :] < heads_doc[:, None], axis=1, dtype=jnp.int32)
        lo = lo + jnp.where(chip_id == 0, chip_len, lo_far)
        lo = lo // ALIGN * ALIGN
        end = chip_len + BQ * (1 + jnp.arange(chip_len // BQ, dtype=jnp.int32))
        n_blocks = (end - lo + BK - 1) // BK
        kdoc = jnp.concatenate([doc_far, doc_chip, jnp.zeros((BK,), jnp.int32)])[None, :]
        qdoc = doc_chip[:, None]

        kv = kv_proj(sel_own, hidden, w_k, w_v, cos_t, sin_t, None)
        kv = kv_proj(sel_oth, x_oth, w_k, w_v, cos_t, sin_t, kv)
        kv_prev = lax.ppermute(kv, "sp", down_perm)
        q = q_proj(sel_own, hidden, w_q, cos_t, sin_t, None)
        grad_late, x_late = lax.optimization_barrier((kv, grad_out, x_oth))[1:]
        dctx = dctx_proj(sel_own, grad_late, w_o, None)
        q = q_proj(sel_oth, x_late, w_q, cos_t, sin_t, q)
        dctx = dctx_proj(sel_oth, g_oth, w_o, dctx)
        xt_own, xt_oth = flip(hidden), flip(x_late)

        acc = None
        acts, acts_oth, sums = [], [], None
        for j in range(n_chunks):
            act, ctxt, dk, dv = attention(j, lo, n_blocks, q, dctx, qdoc, kdoc, cos_t, sin_t, kv_prev, kv, acc)
            acc = (dk, dv)
            acts.append(act)
            acts_oth.append(near(act))
            if j == n_chunks - 1:
                dkv_up = jnp.stack([dk[:, :chip_len], dv[:, :chip_len]]).astype(BF)
                dkv_far = lax.ppermute(dkv_up, "sp", up_perm)
            part = wgrad(core, xt_own, xt_oth, act, grad_out, g_oth, ctxt)
            part_far = far(part)
            part_near = near(part)
            acc = lax.optimization_barrier((dk, dv, part))[:2]
            part_far_near = near(part_far)
            sums = combine(core, j, n_chunks, (part, part_far, part_near, part_far_near), sums)
        grad_wq, grad_wo = sums

        dkv = kv_finish(dk, dv, dkv_far, cos_t, sin_t)
        dkv_oth = near(dkv)
        kv_part = kvgrad(core, xt_own, xt_oth, dkv)
        kv_part_far = far(kv_part)
        kv_sum = kv_part.astype(F32) + kv_part_far.astype(F32)
        kv_sum_oth = near(kv_sum)

        def pick(cols):
            a, b = kv_sum[:, cols], kv_sum_oth[:, cols]
            return jnp.where(core_id == 0, jnp.concatenate([a, b], axis=1), jnp.concatenate([b, a], axis=1))

        grad_wk, grad_wv = pick(slice(0, HEAD)), pick(slice(HEAD, 2 * HEAD))
        out = attn_out(core, acts, acts_oth, w_o)
        g_hidden = grad_hidden(core, acts, acts_oth, dkv, dkv_oth, w_q, w_k, w_v)
        return out, g_hidden, grad_wq, grad_wk, grad_wv, grad_wo

    tok_spec = P(("dp", "sp"), None)
    vec_spec = P(("dp", "sp"))
    rep_spec = P(None, None)
    part_spec = P("dp", None)

    return jax.shard_map(
        device_step,
        mesh=mesh,
        in_specs=(tok_spec, tok_spec, vec_spec, vec_spec, rep_spec, rep_spec, rep_spec, rep_spec),
        out_specs=(tok_spec, tok_spec, part_spec, part_spec, part_spec, part_spec),
        check_vma=False,
    )
```

time: 2160 us -> 570 us (0.26)
  matrix products: 800 us -> 0 us
  waiting for transfers between devices: 690 us -> 208 us
  other arithmetic: 460 us -> 14.6 us
  Pallas kernels: 0 us -> 306 us
  local copies, waits for them, and re-layouts: 127 us -> 11.1 us
  blocking collectives: 24.7 us -> 0 us
    dot_general x26 -> x0, matrix products: 800 us -> none  [the longest x2 198 us: bwd_block(): jnp.einsum('qhgd,shd->hgqs', dctx_blk, v_all, preferred_element_type=jnp....]
    psum x1 -> x0, waiting for transfers between devices: 590 us -> none  [device_step(): lax.psum((grad_wq, grad_wk, grad_wv, grad_wo), 'sp')]
    pallas_call x0 -> x24, Pallas kernels: none -> 306 us  [the longest x4 122 us: attention(): pl.pallas_call(functools.partial(attn_kernel, first), grid_spec=pltpu.Pre...]
    another operation x6 -> x5, other arithmetic: 226 us -> 2.04 us  [the longest x1 0.71 us: device_step(): pos_doc = jnp.stack([positions, doc_ids])]
    ppermute x0 -> x25, waiting for transfers between devices: none -> 208 us  [the longest x6 130 us: far(): return lax.ppermute(v, 'sp', far_perm)]
    reduce_sum x6 -> x1, other arithmetic: 178 us -> 0.2 us  [device_step(): jnp.sum(doc_far[None, :] < heads_doc[:, None], axis=1, dtype=jnp.int32)]
    all_to_all x8 -> x0, waiting for transfers between devices: 100 us -> none  [the longest x1 44.1 us: device_step(): lax.all_to_all(d_ctx, 'sp', 1, 0, tiled=True)]
    unnamed x50 -> x20, local copies, waits for them, and re-layouts: 52.6 us -> 2.04 us
  transfers between devices with their start and end apart: 9 -> 25, of which waited for: 6 -> 5; matrix products, arithmetic and copies ran while one was open for 22% -> 4% of each run, Pallas kernels for 0% -> 45%
where the time goes in v1:
time: 570 us; the launch traced here: 568 us
  Pallas kernels  306 us (54%)
  waiting for transfers between devices  208 us (36%)
  starting transfers between devices  28 us (5%)
  other arithmetic  14.6 us (3%)
  local copies, waits for them, and re-layouts  11.1 us (2%)
    ppermute x6, waiting for transfers between devices, far(): return lax.ppermute(v, 'sp', far_perm)  130 us
    pallas_call x4, Pallas kernels, attention(): pl.pallas_call(functools.partial(attn_kernel, first), grid_spec=pltpu.Pre...  122 us
    ppermute x1, waiting for transfers between devices, device_step(): dkv_far = lax.ppermute(dkv_up, 'sp', up_perm)  71.8 us
    pallas_call x4, Pallas kernels, wgrad(): pl.pallas_call(wgrad_kernel, grid_spec=pltpu.PrefetchScalarGridSpec(num_s...  42.9 us
    pallas_call x4, Pallas kernels, combine(): pl.pallas_call(combine_kernel, grid_spec=pltpu.PrefetchScalarGridSpec(num...  38.2 us
    ppermute x6, starting transfers between devices, far(): return lax.ppermute(v, 'sp', far_perm)  20.6 us
    pallas_call x2, Pallas kernels, q_proj(): pl.pallas_call(q_kernel, grid_spec=pltpu.PrefetchScalarGridSpec(num_scala...  19.4 us
    pallas_call x2, Pallas kernels, dctx_proj(): pl.pallas_call(dctx_kernel, grid_spec=pltpu.PrefetchScalarGridSpec(num_sc...  18.6 us
  transfers between devices with their start and end apart: 25, of which 5 were waited for; matrix products, arithmetic and copies ran while one was open for 4% of the time, Pallas kernels for 45%

profile of v1, /device:TPU:0, one launch (start us, length us, event | category | flops | bytes accessed | tf_op | source)
XLA Modules:
  0.0 567.9 jit_solution(13530254953821792343)
XLA Ops:
  4.0 5.3 flip.2.xt_own
  9.2 5.4 collective-permute-done
  14.7 2.9 collective-permute-start.1
  17.5 3.7 fusion.2
  23.9 9.7 %q_proj.2.rest_0_ = bf16[2048,1024]{1,0:T(8,128)(2,1)} custom-call(s32[2]{0:T(128)} %pad_add_fusion.3.s_ref, bf16[1024,2048]{1,0:T(8,128)(2,1)} %x_ref.5, bf16[2048,2048]{1,0:T(8,128)(2,1)} %refs_10_.1, f32[2048,128]{1,0:T(8,128)} %pad_maximum_fusion.cos_ref, f32[2048,128]{1,0:T(8,128)} %pad_maximum_fusion.1.sin_ref), custom_call_target="tpu_custom_call" | custom-call | flops 4294967296 | bytes 8388608 | tf_op jit(solution)/shard_map/q_proj/pallas_call | solution.py:113
  33.6 6.2 %kv_proj.2.rest_0_ = bf16[2048,256]{1,0:T(8,128)(2,1)} custom-call(s32[2]{0:T(128)} %pad_add_fusion.3.s_ref, bf16[1024,2048]{1,0:T(8,128)(2,1)} %x_ref.5, bf16[2048,256]{1,0:T(8,128)(2,1)} %refs_11_.1, bf16[2048,256]{1,0:T(8,128)(2,1)} %refs_12_.1, f32[2048,128]{1,0:T(8,128)} %pad_maximum_fusion.cos_ref, f32[2048,128]{1,0:T(8,128)} %pad_maximum_fusion.1.sin_ref), custom_call_target="tpu_custom_call" | custom-call | flops 1073741824 | bytes 4194304 | tf_op jit(solution)/shard_map/kv_proj/pallas_call | solution.py:78
  42.7 6.2 %kv_proj.3.kvc_ref = bf16[2048,256]{1,0:T(8,128)(2,1)} custom-call(s32[2]{0:T(128)} %pad_add_fusion.2.s_ref, bf16[1024,2048]{1,0:T(8,128)(2,1)} %collective-permute-done.2.x_ref, bf16[2048,256]{1,0:T(8,128)(2,1)} %refs_11_.1, bf16[2048,256]{1,0:T(8,128)(2,1)} %refs_12_.1, f32[2048,128]{1,0:T(8,128)} %pad_maximum_fusion.cos_ref, ...), custom_call_target="tpu_custom_call", output_to_operand_aliasing={{}: (6, {})} | custom-call | flops 1073741824 | bytes 4194304 | tf_op jit(solution)/shard_map/kv_proj/pallas_call | solution.py:78
  51.0 9.7 %q_proj.3.q_ref = bf16[2048,1024]{1,0:T(8,128)(2,1)} custom-call(s32[2]{0:T(128)} %pad_add_fusion.2.s_ref, bf16[1024,2048]{1,0:T(8,128)(2,1)} %collective-permute-done.2.x_ref, bf16[2048,2048]{1,0:T(8,128)(2,1)} %refs_10_.1, f32[2048,128]{1,0:T(8,128)} %pad_maximum_fusion.cos_ref, ...), custom_call_target="tpu_custom_call", output_to_operand_aliasing={{}: (5, {})} | custom-call | flops 4294967296 | bytes 8388608 | tf_op jit(solution)/shard_map/q_proj/pallas_call | solution.py:113
  60.7 5.2 flip.3.xt_oth
  66.0 9.3 %dctx_proj.2.rest_0_ = bf16[2048,1024]{1,0:T(8,128)(2,1)} custom-call(s32[2]{0:T(128)} %pad_add_fusion.3.s_ref, bf16[1024,2048]{1,0:T(8,128)(2,1)} %g_own.7, bf16[2048,2048]{1,0:T(8,128)(2,1)} %refs_8_.1), custom_call_target="tpu_custom_call" | custom-call | flops 4294967296 | bytes 8388608 | tf_op jit(solution)/shard_map/dctx_proj/pallas_call | solution.py:144
  75.3 9.3 %dctx_proj.3.do_ref = bf16[2048,1024]{1,0:T(8,128)(2,1)} custom-call(s32[2]{0:T(128)} %pad_add_fusion.2.s_ref, bf16[1024,2048]{1,0:T(8,128)(2,1)} %collective-permute-done.3.g_ref.g_oth, bf16[2048,2048]{1,0:T(8,128)(2,1)} %refs_8_.1, bf16[2048,1024]{1,0:T(8,128)(2,1)} %dctx_proj.2.rest_0_), custom_call_target="tpu_custom_call", output_to_operand_aliasing={{}: (3, {})} | custom-call | flops 4294967296 | bytes 8388608 | tf_op jit(solution)/shard_map/dctx_proj/pallas_call | solution.py:144
  85.6 29.4 %attention.4 = (bf16[2,2048,256]{2,1,0:T(8,128)(2,1)}, bf16[256,2048]{1,0:T(8,128)(2,1)}, f32[128,4608]{1,0:T(8,128)}, f32[128,4608]{1,0:T(8,128)}) custom-call(s32[8]{0:T(128)} %get-tuple-element.73.lo_ref, s32[8]{0:T(128)} %get-tuple-element.72.nb_ref, bf16[2048,1024]{1,0:T(8,128)(2,1)} %q_proj.3.q_ref, bf16[2048,1024]{1,0:T(8,128)(2,1)} %dctx_proj.3.do_ref, ...), custom_call_target="tpu_custom_call" | custom-call | flops 12884901888 | bytes 12582912 | tf_op jit(solution)/shard_map/attention/pallas_call | solution.py:299
  115.0 10.4 %wgrad.4.a_ref = bf16[2,2048,256]{2,1,0:T(8,128)(2,1)} custom-call(s32[1]{0:T(128)} %bitcast.s_ref, bf16[2048,1024]{1,0:T(8,128)(2,1)} %flip.2.xt_own, bf16[2048,1024]{1,0:T(8,128)(2,1)} %flip.3.xt_oth, bf16[2,2048,256]{2,1,0:T(8,128)(2,1)} %get-tuple-element.40.act_ref.refs_0_, bf16[1024,2048]{1,0:T(8,128)(2,1)} %g_own.7, ...), custom_call_target="tpu_custom_call" | custom-call | flops 4294967296 | bytes 16777216 | tf_op jit(solution)/shard_map/wgrad/pallas_call | solution.py:392
  125.4 15.7 %collective-permute-start.20 = (bf16[2,2048,256]{2,1,0:T(8,128)(2,1)}, bf16[2,2048,256]{2,1,0:T(8,128)(2,1)}, u32[]{:S(2)}, u32[]{:S(2)}) collective-permute-start(bf16[2,2048,256]{2,1,0:T(8,128)(2,1)} %wgrad.4.a_ref), channel_id=1, source_target_pairs={{0,2},{1,3},{2,0},{3,1},{4,6},{5,7},{6,4},{7,5}} | collective-permute-start | bytes 6291464 | tf_op jit(solution)/shard_map/ppermute | solution.py:595
  141.1 30.8 %attention.5 = (bf16[2,2048,256]{2,1,0:T(8,128)(2,1)}, bf16[256,2048]{1,0:T(8,128)(2,1)}, f32[128,4608]{1,0:T(8,128)}, f32[128,4608]{1,0:T(8,128)}) custom-call(s32[8]{0:T(128)} %get-tuple-element.73.lo_ref, s32[8]{0:T(128)} %get-tuple-element.72.nb_ref, bf16[2048,1024]{1,0:T(8,128)(2,1)} %q_proj.3.q_ref, ...), custom_call_target="tpu_custom_call", output_to_operand_aliasing={{2}: (10, {}), {3}: (11, {})} | custom-call | flops 12884901888 | bytes 12582912 | tf_op jit(solution)/shard_map/attention/pallas_call | solution.py:299
  171.9 10.5 %wgrad.5.a_ref = bf16[2,2048,256]{2,1,0:T(8,128)(2,1)} custom-call(s32[1]{0:T(128)} %bitcast.s_ref, bf16[2048,1024]{1,0:T(8,128)(2,1)} %flip.2.xt_own, bf16[2048,1024]{1,0:T(8,128)(2,1)} %flip.3.xt_oth, bf16[2,2048,256]{2,1,0:T(8,128)(2,1)} %get-tuple-element.46.act_ref.refs_1_, bf16[1024,2048]{1,0:T(8,128)(2,1)} %g_own.7, ...), custom_call_target="tpu_custom_call" | custom-call | flops 4294967296 | bytes 16777216 | tf_op jit(solution)/shard_map/wgrad/pallas_call | solution.py:392
  182.4 30.9 %attention.6 = (bf16[2,2048,256]{2,1,0:T(8,128)(2,1)}, bf16[256,2048]{1,0:T(8,128)(2,1)}, f32[128,4608]{1,0:T(8,128)}, f32[128,4608]{1,0:T(8,128)}) custom-call(s32[8]{0:T(128)} %get-tuple-element.73.lo_ref, s32[8]{0:T(128)} %get-tuple-element.72.nb_ref, bf16[2048,1024]{1,0:T(8,128)(2,1)} %q_proj.3.q_ref, ...), custom_call_target="tpu_custom_call", output_to_operand_aliasing={{2}: (10, {}), {3}: (11, {})} | custom-call | flops 12884901888 | bytes 12582912 | tf_op jit(solution)/shard_map/attention/pallas_call | solution.py:299
  213.3 10.5 %wgrad.6.a_ref = bf16[2,2048,256]{2,1,0:T(8,128)(2,1)} custom-call(s32[1]{0:T(128)} %bitcast.s_ref, bf16[2048,1024]{1,0:T(8,128)(2,1)} %flip.2.xt_own, bf16[2048,1024]{1,0:T(8,128)(2,1)} %flip.3.xt_oth, bf16[2,2048,256]{2,1,0:T(8,128)(2,1)} %get-tuple-element.52.act_ref.refs_2_, bf16[1024,2048]{1,0:T(8,128)(2,1)} %g_own.7, ...), custom_call_target="tpu_custom_call" | custom-call | flops 4294967296 | bytes 16777216 | tf_op jit(solution)/shard_map/wgrad/pallas_call | solution.py:392
  223.8 30.8 %attention.7 = (bf16[2,2048,256]{2,1,0:T(8,128)(2,1)}, bf16[256,2048]{1,0:T(8,128)(2,1)}, f32[128,4608]{1,0:T(8,128)}, f32[128,4608]{1,0:T(8,128)}) custom-call(s32[8]{0:T(128)} %get-tuple-element.73.lo_ref, s32[8]{0:T(128)} %get-tuple-element.72.nb_ref, bf16[2048,1024]{1,0:T(8,128)(2,1)} %q_proj.3.q_ref, ...), custom_call_target="tpu_custom_call", output_to_operand_aliasing={{2}: (10, {}), {3}: (11, {})} | custom-call | flops 12884901888 | bytes 12582912 | tf_op jit(solution)/shard_map/attention/pallas_call | solution.py:299
  259.1 71.8 %collective-permute-done.9.far_ref = bf16[2,128,2048]{2,1,0:T(8,128)(2,1)S(1)} collective-permute-done((bf16[2,128,2048]{2,1,0:T(8,128)(2,1)S(1)}, bf16[2,128,2048]{2,1,0:T(8,128)(2,1)S(1)}, u32[]{:S(2)}, u32[]{:S(2)}) %collective-permute-start.9) | collective-permute-done | bytes 1048608 | tf_op jit(solution)/shard_map/ppermute | solution.py:649
  330.9 11.5 %wgrad.7.a_ref = bf16[2,2048,256]{2,1,0:T(8,128)(2,1)} custom-call(s32[1]{0:T(128)} %bitcast.s_ref, bf16[2048,1024]{1,0:T(8,128)(2,1)} %flip.2.xt_own, bf16[2048,1024]{1,0:T(8,128)(2,1)} %flip.3.xt_oth, bf16[2,2048,256]{2,1,0:T(8,128)(2,1)} %get-tuple-element.58.refs_3_.act_ref, bf16[1024,2048]{1,0:T(8,128)(2,1)} %g_own.7, ...), custom_call_target="tpu_custom_call" | custom-call | flops 4294967296 | bytes 16777216 | tf_op jit(solution)/shard_map/wgrad/pallas_call | solution.py:392
  344.1 4.4 kv_finish.1.refs_8_.dkv_ref
  348.5 6.7 %kvgrad.1 = bf16[2048,256]{1,0:T(8,128)(2,1)} custom-call(s32[1]{0:T(128)} %bitcast.s_ref, bf16[2048,1024]{1,0:T(8,128)(2,1)} %flip.2.xt_own, bf16[2048,1024]{1,0:T(8,128)(2,1)} %flip.3.xt_oth, bf16[2048,256]{1,0:T(8,128)(2,1)} %kv_finish.1.refs_8_.dkv_ref), custom_call_target="tpu_custom_call" | custom-call | flops 2147483648 | bytes 8388608 | tf_op jit(solution)/shard_map/kvgrad/pallas_call | solution.py:424
  355.6 24.1 %collective-permute-done.17.b_ref = bf16[2,2048,256]{2,1,0:T(8,128)(2,1)} collective-permute-done((bf16[2,2048,256]{2,1,0:T(8,128)(2,1)}, bf16[2,2048,256]{2,1,0:T(8,128)(2,1)}, u32[]{:S(2)}, u32[]{:S(2)}) %collective-permute-start.17) | collective-permute-done | bytes 2097184 | tf_op jit(solution)/shard_map/ppermute | solution.py:595
  379.7 67.3 %collective-permute-done.23 = bf16[2048,256]{1,0:T(8,128)(2,1)S(1)} collective-permute-done((bf16[2048,256]{1,0:T(8,128)(2,1)}, bf16[2048,256]{1,0:T(8,128)(2,1)S(1)}, u32[]{:S(2)}, u32[]{:S(2)}) %collective-permute-start.23) | collective-permute-done | bytes 1048608 | tf_op jit(solution)/shard_map/ppermute | solution.py:595
  451.8 39.1 %collective-permute-done.14.b_ref = bf16[2,2048,256]{2,1,0:T(8,128)(2,1)} collective-permute-done((bf16[2,2048,256]{2,1,0:T(8,128)(2,1)S(1)}, bf16[2,2048,256]{2,1,0:T(8,128)(2,1)}, u32[]{:S(2)}, u32[]{:S(2)}) %collective-permute-start.14) | collective-permute-done | bytes 2097184 | tf_op jit(solution)/shard_map/ppermute | solution.py:595
  491.3 13.8 %attn_out.1 = bf16[1024,2048]{1,0:T(8,128)(2,1)} custom-call(s32[1]{0:T(128)} %bitcast.s_ref, bf16[2,2048,256]{2,1,0:T(8,128)(2,1)} %get-tuple-element.40.act_ref.refs_0_, bf16[2,2048,256]{2,1,0:T(8,128)(2,1)} %get-tuple-element.46.act_ref.refs_1_, bf16[2,2048,256]{2,1,0:T(8,128)(2,1)} %get-tuple-element.52.act_ref.refs_2_, ...), custom_call_target="tpu_custom_call" | custom-call | flops 8589934592 | bytes 16777216 | tf_op jit(solution)/shard_map/attn_out/pallas_call | solution.py:516
  508.4 17.0 %grad_hidden.1 = bf16[1024,2048]{1,0:T(8,128)(2,1)} custom-call(s32[1]{0:T(128)} %bitcast.s_ref, bf16[2,2048,256]{2,1,0:T(8,128)(2,1)} %get-tuple-element.40.act_ref.refs_0_, bf16[2,2048,256]{2,1,0:T(8,128)(2,1)} %get-tuple-element.46.act_ref.refs_1_, bf16[2,2048,256]{2,1,0:T(8,128)(2,1)} %get-tuple-element.52.act_ref.refs_2_, ...), custom_call_target="tpu_custom_call" | custom-call | flops 10737418240 | bytes 16777216 | tf_op jit(solution)/shard_map/grad_hidden/pallas_call | solution.py:557
  525.3 9.5 %combine.4 = (f32[2048,2048]{1,0:T(8,128)}, f32[2048,2048]{1,0:T(8,128)}) custom-call(s32[1]{0:T(128)} %bitcast.s_ref, bf16[2,2048,256]{2,1,0:T(8,128)(2,1)} %wgrad.4.a_ref, bf16[2,2048,256]{2,1,0:T(8,128)(2,1)} %collective-permute-done.20.b_ref, bf16[2,2048,256]{2,1,0:T(8,128)(2,1)} %copy-done.3, bf16[2,2048,256]{2,1,0:T(8,128)(2,1)} %collective-permute-done.22.d_ref), custom_call_target="tpu_custom_call" | custom-call | flops 536870912 | bytes 16777216 | tf_op jit(solution)/shard_map/combine/pallas_call | solution.py:474
  534.9 9.5 %combine.5 = (f32[2048,2048]{1,0:T(8,128)}, f32[2048,2048]{1,0:T(8,128)}) custom-call(s32[1]{0:T(128)} %bitcast.s_ref, bf16[2,2048,256]{2,1,0:T(8,128)(2,1)} %wgrad.5.a_ref, bf16[2,2048,256]{2,1,0:T(8,128)(2,1)} %collective-permute-done.17.b_ref, bf16[2,2048,256]{2,1,0:T(8,128)(2,1)} %collective-permute-done.18.c_ref, ...), custom_call_target="tpu_custom_call", output_to_operand_aliasing={{0}: (5, {}), {1}: (6, {})} | custom-call | flops 536870912 | bytes 16777216 | tf_op jit(solution)/shard_map/combine/pallas_call | solution.py:474
  544.4 9.6 %combine.6 = (f32[2048,2048]{1,0:T(8,128)}, f32[2048,2048]{1,0:T(8,128)}) custom-call(s32[1]{0:T(128)} %bitcast.s_ref, bf16[2,2048,256]{2,1,0:T(8,128)(2,1)} %wgrad.6.a_ref, bf16[2,2048,256]{2,1,0:T(8,128)(2,1)} %collective-permute-done.14.b_ref, bf16[2,2048,256]{2,1,0:T(8,128)(2,1)} %collective-permute-done.15.c_ref, ...), custom_call_target="tpu_custom_call", output_to_operand_aliasing={{0}: (5, {}), {1}: (6, {})} | custom-call | flops 536870912 | bytes 16777216 | tf_op jit(solution)/shard_map/combine/pallas_call | solution.py:474
  558.4 9.5 %combine.7 = (f32[2048,2048]{1,0:T(8,128)}, f32[2048,2048]{1,0:T(8,128)}) custom-call(s32[1]{0:T(128)} %bitcast.s_ref, bf16[2,2048,256]{2,1,0:T(8,128)(2,1)} %wgrad.7.a_ref, bf16[2,2048,256]{2,1,0:T(8,128)(2,1)} %collective-permute-done.11.b_ref, bf16[2,2048,256]{2,1,0:T(8,128)(2,1)} %collective-permute-done.12.c_ref, ...), custom_call_target="tpu_custom_call", output_to_operand_aliasing={{0}: (5, {}), {1}: (6, {})} | custom-call | flops 536870912 | bytes 16777216 | tf_op jit(solution)/shard_map/combine/pallas_call | solution.py:474
  (85 shorter events, 31.6 us)
Async XLA Ops:
  0.6 42.1 %collective-permute-start.2 = (bf16[1024,2048]{1,0:T(8,128)(2,1)}, bf16[1024,2048]{1,0:T(8,128)(2,1)}, u32[]{:S(2)}, u32[]{:S(2)}) collective-permute-start(bf16[1024,2048]{1,0:T(8,128)(2,1)} %x_ref.5), channel_id=1, source_target_pairs={{0,1},{1,0},{2,3},{3,2},{4,5},{5,4},{6,7},{7,6}} | collective-permute-start | bytes 12582920 | tf_op jit(solution)/shard_map/ppermute | solution.py:592
  1.5 73.8 %collective-permute-start.3 = (bf16[1024,2048]{1,0:T(8,128)(2,1)}, bf16[1024,2048]{1,0:T(8,128)(2,1)}, u32[]{:S(2)}, u32[]{:S(2)}) collective-permute-start(bf16[1024,2048]{1,0:T(8,128)(2,1)} %g_own.7), channel_id=1, source_target_pairs={{0,1},{1,0},{2,3},{3,2},{4,5},{5,4},{6,7},{7,6}} | collective-permute-start | bytes 12582920 | tf_op jit(solution)/shard_map/ppermute | solution.py:592
  2.2 12.4 %collective-permute-start = (s32[2,1024]{1,0:T(2,128)S(1)}, s32[2,1024]{1,0:T(2,128)S(1)}, u32[]{:S(2)}, u32[]{:S(2)}) collective-permute-start(s32[2,1024]{1,0:T(2,128)S(1)} %pad_add_fusion.1), channel_id=1, source_target_pairs={{0,1},{1,0},{2,3},{3,2},{4,5},{5,4},{6,7},{7,6}} | collective-permute-start | bytes 24584 | tf_op jit(solution)/shard_map/ppermute | solution.py:592
  4.0 10.7 %copy-start.5 = (s32[1024]{0:T(1024)S(1)}, s32[1024]{0:T(1024)}, u32[]{:S(2)}) copy-start(s32[1024]{0:T(1024)} %param.11) | copy-start | bytes 12292
  4.0 10.7 %copy-start.6 = (s32[1024]{0:T(1024)S(1)}, s32[1024]{0:T(1024)}, u32[]{:S(2)}) copy-start(s32[1024]{0:T(1024)} %param.10) | copy-start | bytes 12292
  14.7 26.6 %collective-permute-start.1 = (s32[2048]{0:T(1024)S(1)}, s32[2048]{0:T(1024)S(1)}, u32[]{:S(2)}, u32[]{:S(2)}) collective-permute-start(s32[2048]{0:T(1024)S(1)} %bitcast.12), channel_id=1, source_target_pairs={{0,2},{1,3},{2,0},{3,1},{4,6},{5,7},{6,4},{7,5}} | collective-permute-start | bytes 24584 | tf_op jit(solution)/shard_map/ppermute | solution.py:595
  48.9 35.8 %collective-permute-start.4 = (bf16[2048,256]{1,0:T(8,128)(2,1)}, bf16[2048,256]{1,0:T(8,128)(2,1)S(1)}, u32[]{:S(2)}, u32[]{:S(2)}) collective-permute-start(bf16[2048,256]{1,0:T(8,128)(2,1)} %kv_proj.3.kvc_ref), channel_id=1, source_target_pairs={{0,2},{1,3},{4,6},{5,7}} | collective-permute-start | bytes 3145736 | tf_op jit(solution)/shard_map/ppermute | solution.py:632
  125.4 205.4 %collective-permute-start.21 = (bf16[2,2048,256]{2,1,0:T(8,128)(2,1)}, bf16[2,2048,256]{2,1,0:T(8,128)(2,1)S(1)}, u32[]{:S(2)}, u32[]{:S(2)}) collective-permute-start(bf16[2,2048,256]{2,1,0:T(8,128)(2,1)} %wgrad.4.a_ref), channel_id=1, source_target_pairs={{0,1},{1,0},{2,3},{3,2},{4,5},{5,4},{6,7},{7,6}} | collective-permute-start | bytes 6291464 | tf_op jit(solution)/shard_map/ppermute | solution.py:592
  125.4 217.0 %collective-permute-start.20 = (bf16[2,2048,256]{2,1,0:T(8,128)(2,1)}, bf16[2,2048,256]{2,1,0:T(8,128)(2,1)}, u32[]{:S(2)}, u32[]{:S(2)}) collective-permute-start(bf16[2,2048,256]{2,1,0:T(8,128)(2,1)} %wgrad.4.a_ref), channel_id=1, source_target_pairs={{0,2},{1,3},{2,0},{3,1},{4,6},{5,7},{6,4},{7,5}} | collective-permute-start | bytes 6291464 | tf_op jit(solution)/shard_map/ppermute | solution.py:595
  257.2 73.6 %collective-permute-start.9 = (bf16[2,128,2048]{2,1,0:T(8,128)(2,1)S(1)}, bf16[2,128,2048]{2,1,0:T(8,128)(2,1)S(1)}, u32[]{:S(2)}, u32[]{:S(2)}) collective-permute-start(bf16[2,128,2048]{2,1,0:T(8,128)(2,1)S(1)} %pad_maximum_fusion.2), channel_id=1, source_target_pairs={{2,0},{3,1},{6,4},{7,5}} | collective-permute-start | bytes 3145736 | tf_op jit(solution)/shard_map/ppermute | solution.py:649
  258.5 96.7 %collective-permute-start.5 = (bf16[2,2048,256]{2,1,0:T(8,128)(2,1)}, bf16[2,2048,256]{2,1,0:T(8,128)(2,1)}, u32[]{:S(2)}, u32[]{:S(2)}) collective-permute-start(bf16[2,2048,256]{2,1,0:T(8,128)(2,1)} %get-tuple-element.40.act_ref.refs_0_), channel_id=1, source_target_pairs={{0,1},{1,0},{2,3},{3,2},{4,5},{5,4},{6,7},{7,6}} | collective-permute-start | bytes 6291464 | tf_op jit(solution)/shard_map/ppermute | solution.py:592
  258.6 96.9 %collective-permute-start.18 = (bf16[2,2048,256]{2,1,0:T(8,128)(2,1)}, bf16[2,2048,256]{2,1,0:T(8,128)(2,1)}, u32[]{:S(2)}, u32[]{:S(2)}) collective-permute-start(bf16[2,2048,256]{2,1,0:T(8,128)(2,1)} %wgrad.5.a_ref), channel_id=1, source_target_pairs={{0,1},{1,0},{2,3},{3,2},{4,5},{5,4},{6,7},{7,6}} | collective-permute-start | bytes 6291464 | tf_op jit(solution)/shard_map/ppermute | solution.py:592
  330.8 11.5 %copy-start.4 = (bf16[2,128,2048]{2,1,0:T(8,128)(2,1)}, bf16[2,128,2048]{2,1,0:T(8,128)(2,1)S(1)}, u32[]{:S(2)}) copy-start(bf16[2,128,2048]{2,1,0:T(8,128)(2,1)S(1)} %collective-permute-done.9.far_ref) | copy-start | bytes 3145732
  330.8 48.8 %collective-permute-start.17 = (bf16[2,2048,256]{2,1,0:T(8,128)(2,1)}, bf16[2,2048,256]{2,1,0:T(8,128)(2,1)}, u32[]{:S(2)}, u32[]{:S(2)}) collective-permute-start(bf16[2,2048,256]{2,1,0:T(8,128)(2,1)} %wgrad.5.a_ref), channel_id=1, source_target_pairs={{0,2},{1,3},{2,0},{3,1},{4,6},{5,7},{6,4},{7,5}} | collective-permute-start | bytes 6291464 | tf_op jit(solution)/shard_map/ppermute | solution.py:595
  330.8 11.5 %copy-start.3 = (bf16[2,2048,256]{2,1,0:T(8,128)(2,1)}, bf16[2,2048,256]{2,1,0:T(8,128)(2,1)S(1)}, u32[]{:S(2)}) copy-start(bf16[2,2048,256]{2,1,0:T(8,128)(2,1)S(1)} %collective-permute-done.21.c_ref) | copy-start | bytes 6291460
  330.8 48.8 %collective-permute-start.6 = (bf16[2,2048,256]{2,1,0:T(8,128)(2,1)}, bf16[2,2048,256]{2,1,0:T(8,128)(2,1)}, u32[]{:S(2)}, u32[]{:S(2)}) collective-permute-start(bf16[2,2048,256]{2,1,0:T(8,128)(2,1)} %get-tuple-element.46.act_ref.refs_1_), channel_id=1, source_target_pairs={{0,1},{1,0},{2,3},{3,2},{4,5},{5,4},{6,7},{7,6}} | collective-permute-start | bytes 6291464 | tf_op jit(solution)/shard_map/ppermute | solution.py:592
  342.4 106.1 %collective-permute-start.11 = (bf16[2,2048,256]{2,1,0:T(8,128)(2,1)}, bf16[2,2048,256]{2,1,0:T(8,128)(2,1)}, u32[]{:S(2)}, u32[]{:S(2)}) collective-permute-start(bf16[2,2048,256]{2,1,0:T(8,128)(2,1)} %wgrad.7.a_ref), channel_id=1, source_target_pairs={{0,2},{1,3},{2,0},{3,1},{4,6},{5,7},{6,4},{7,5}} | collective-permute-start | bytes 6291464 | tf_op jit(solution)/shard_map/ppermute | solution.py:595
  348.5 7.1 %copy-start.2 = (bf16[2048,256]{1,0:T(8,128)(2,1)S(1)}, bf16[2048,256]{1,0:T(8,128)(2,1)}, u32[]{:S(2)}) copy-start(bf16[2048,256]{1,0:T(8,128)(2,1)} %kv_finish.1.refs_8_.dkv_ref) | copy-start | bytes 3145732
  348.5 31.2 %copy-start = (bf16[2,2048,256]{2,1,0:T(8,128)(2,1)S(1)}, bf16[2,2048,256]{2,1,0:T(8,128)(2,1)}, u32[]{:S(2)}) copy-start(bf16[2,2048,256]{2,1,0:T(8,128)(2,1)} %wgrad.6.a_ref) | copy-start | bytes 6291460
  355.2 91.8 %collective-permute-start.23 = (bf16[2048,256]{1,0:T(8,128)(2,1)}, bf16[2048,256]{1,0:T(8,128)(2,1)S(1)}, u32[]{:S(2)}, u32[]{:S(2)}) collective-permute-start(bf16[2048,256]{1,0:T(8,128)(2,1)} %kvgrad.1), channel_id=1, source_target_pairs={{0,2},{1,3},{2,0},{3,1},{4,6},{5,7},{6,4},{7,5}} | collective-permute-start | bytes 3145736 | tf_op jit(solution)/shard_map/ppermute | solution.py:595
  355.6 91.4 %collective-permute-start.10 = (bf16[2048,256]{1,0:T(8,128)(2,1)S(1)}, bf16[2048,256]{1,0:T(8,128)(2,1)S(1)}, u32[]{:S(2)}, u32[]{:S(2)}) collective-permute-start(bf16[2048,256]{1,0:T(8,128)(2,1)S(1)} %copy-done.2), channel_id=1, source_target_pairs={{0,1},{1,0},{2,3},{3,2},{4,5},{5,4},{6,7},{7,6}} | collective-permute-start | bytes 3145736 | tf_op jit(solution)/shard_map/ppermute | solution.py:592
  379.6 71.6 %collective-permute-start.8 = (bf16[2,2048,256]{2,1,0:T(8,128)(2,1)}, bf16[2,2048,256]{2,1,0:T(8,128)(2,1)S(1)}, u32[]{:S(2)}, u32[]{:S(2)}) collective-permute-start(bf16[2,2048,256]{2,1,0:T(8,128)(2,1)} %get-tuple-element.58.refs_3_.act_ref), channel_id=1, source_target_pairs={{0,1},{1,0},{2,3},{3,2},{4,5},{5,4},{6,7},{7,6}} | collective-permute-start | bytes 6291464 | tf_op jit(solution)/shard_map/ppermute | solution.py:592
  379.7 111.2 %collective-permute-start.14 = (bf16[2,2048,256]{2,1,0:T(8,128)(2,1)S(1)}, bf16[2,2048,256]{2,1,0:T(8,128)(2,1)}, u32[]{:S(2)}, u32[]{:S(2)}) collective-permute-start(bf16[2,2048,256]{2,1,0:T(8,128)(2,1)S(1)} %copy-done), channel_id=1, source_target_pairs={{0,2},{1,3},{2,0},{3,1},{4,6},{5,7},{6,4},{7,5}} | collective-permute-start | bytes 6291464 | tf_op jit(solution)/shard_map/ppermute | solution.py:595
  447.0 43.9 %collective-permute-start.7 = (bf16[2,2048,256]{2,1,0:T(8,128)(2,1)}, bf16[2,2048,256]{2,1,0:T(8,128)(2,1)}, u32[]{:S(2)}, u32[]{:S(2)}) collective-permute-start(bf16[2,2048,256]{2,1,0:T(8,128)(2,1)} %get-tuple-element.52.act_ref.refs_2_), channel_id=1, source_target_pairs={{0,1},{1,0},{2,3},{3,2},{4,5},{5,4},{6,7},{7,6}} | collective-permute-start | bytes 6291464 | tf_op jit(solution)/shard_map/ppermute | solution.py:592
  447.9 57.3 %collective-permute-start.22 = (bf16[2,2048,256]{2,1,0:T(8,128)(2,1)}, bf16[2,2048,256]{2,1,0:T(8,128)(2,1)}, u32[]{:S(2)}, u32[]{:S(2)}) collective-permute-start(bf16[2,2048,256]{2,1,0:T(8,128)(2,1)} %collective-permute-done.20.b_ref), channel_id=1, source_target_pairs={{0,1},{1,0},{2,3},{3,2},{4,5},{5,4},{6,7},{7,6}} | collective-permute-start | bytes 6291464 | tf_op jit(solution)/shard_map/ppermute | solution.py:592
  448.4 56.8 %collective-permute-start.19 = (bf16[2,2048,256]{2,1,0:T(8,128)(2,1)}, bf16[2,2048,256]{2,1,0:T(8,128)(2,1)}, u32[]{:S(2)}, u32[]{:S(2)}) collective-permute-start(bf16[2,2048,256]{2,1,0:T(8,128)(2,1)} %collective-permute-done.17.b_ref), channel_id=1, source_target_pairs={{0,1},{1,0},{2,3},{3,2},{4,5},{5,4},{6,7},{7,6}} | collective-permute-start | bytes 6291464 | tf_op jit(solution)/shard_map/ppermute | solution.py:592
  451.3 39.6 %copy-start.7 = (bf16[2,2048,256]{2,1,0:T(8,128)(2,1)}, bf16[2,2048,256]{2,1,0:T(8,128)(2,1)S(1)}, u32[]{:S(2)}) copy-start(bf16[2,2048,256]{2,1,0:T(8,128)(2,1)S(1)} %collective-permute-done.8.refs_7_) | copy-start | bytes 6291460
  451.3 93.1 %collective-permute-start.15 = (bf16[2,2048,256]{2,1,0:T(8,128)(2,1)S(1)}, bf16[2,2048,256]{2,1,0:T(8,128)(2,1)}, u32[]{:S(2)}, u32[]{:S(2)}) collective-permute-start(bf16[2,2048,256]{2,1,0:T(8,128)(2,1)S(1)} %copy-done), channel_id=1, source_target_pairs={{0,1},{1,0},{2,3},{3,2},{4,5},{5,4},{6,7},{7,6}} | collective-permute-start | bytes 6291464 | tf_op jit(solution)/shard_map/ppermute | solution.py:592
  490.8 63.1 %collective-permute-start.24 = (f32[2048,256]{1,0:T(8,128)}, f32[2048,256]{1,0:T(8,128)}, u32[]{:S(2)}, u32[]{:S(2)}) collective-permute-start(f32[2048,256]{1,0:T(8,128)} %convert_add_fusion), channel_id=1, source_target_pairs={{0,1},{1,0},{2,3},{3,2},{4,5},{5,4},{6,7},{7,6}} | collective-permute-start | bytes 6291464 | tf_op jit(solution)/shard_map/ppermute | solution.py:592
  490.8 53.6 %collective-permute-start.16 = (bf16[2,2048,256]{2,1,0:T(8,128)(2,1)}, bf16[2,2048,256]{2,1,0:T(8,128)(2,1)}, u32[]{:S(2)}, u32[]{:S(2)}) collective-permute-start(bf16[2,2048,256]{2,1,0:T(8,128)(2,1)} %collective-permute-done.14.b_ref), channel_id=1, source_target_pairs={{0,1},{1,0},{2,3},{3,2},{4,5},{5,4},{6,7},{7,6}} | collective-permute-start | bytes 6291464 | tf_op jit(solution)/shard_map/ppermute | solution.py:592
  505.2 53.2 %collective-permute-start.12 = (bf16[2,2048,256]{2,1,0:T(8,128)(2,1)}, bf16[2,2048,256]{2,1,0:T(8,128)(2,1)}, u32[]{:S(2)}, u32[]{:S(2)}) collective-permute-start(bf16[2,2048,256]{2,1,0:T(8,128)(2,1)} %wgrad.7.a_ref), channel_id=1, source_target_pairs={{0,1},{1,0},{2,3},{3,2},{4,5},{5,4},{6,7},{7,6}} | collective-permute-start | bytes 6291464 | tf_op jit(solution)/shard_map/ppermute | solution.py:592
  505.3 53.1 %collective-permute-start.13 = (bf16[2,2048,256]{2,1,0:T(8,128)(2,1)}, bf16[2,2048,256]{2,1,0:T(8,128)(2,1)}, u32[]{:S(2)}, u32[]{:S(2)}) collective-permute-start(bf16[2,2048,256]{2,1,0:T(8,128)(2,1)} %collective-permute-done.11.b_ref), channel_id=1, source_target_pairs={{0,1},{1,0},{2,3},{3,2},{4,5},{5,4},{6,7},{7,6}} | collective-permute-start | bytes 6291464 | tf_op jit(solution)/shard_map/ppermute | solution.py:592
  (3 other events, 3.8 us)

commit v2 on v1

v2 whole, which is shorter than its diff:
```python
import functools

import jax
import jax.numpy as jnp
from jax import lax
from jax.experimental import pallas as pl
from jax.experimental.pallas import tpu as pltpu
from jax.sharding import PartitionSpec as P

HEAD = 128
ROPE_THETA = 500000.0
ROPE_FACTOR = 8.0
ROPE_LOW = 1.0
ROPE_HIGH = 4.0
ROPE_OLD_CTX = 8192.0
NEG_BIG = -1.0e30
SCALE = HEAD ** -0.5
LOG2E = 1.4426950408889634

PAIR = 2
WIDE = PAIR * HEAD
BQ = 512
BK = 512
ALIGN = 128
BF = jnp.bfloat16
F32 = jnp.float32


def rope_freqs():
    half_idx = jnp.arange(HEAD // 2, dtype=F32)
    inv_freq = jnp.power(ROPE_THETA, -2.0 * half_idx / HEAD)
    wavelen = 2.0 * jnp.pi / inv_freq
    smooth = (ROPE_OLD_CTX / wavelen - ROPE_LOW) / (ROPE_HIGH - ROPE_LOW)
    mixed_freq = (1.0 - smooth) * inv_freq / ROPE_FACTOR + smooth * inv_freq
    scaled = jnp.where(wavelen > ROPE_OLD_CTX / ROPE_LOW, inv_freq / ROPE_FACTOR, mixed_freq)
    return jnp.where(wavelen < ROPE_OLD_CTX / ROPE_HIGH, inv_freq, scaled)


def rope_table(pos_vec):
    angles = pos_vec.astype(F32)[:, None] * rope_freqs()[None, :]
    return jnp.concatenate([jnp.cos(angles), jnp.sin(angles)], axis=-1)


def dot_nn(a, b):
    return lax.dot_general(a, b, (((1,), (0,)), ((), ())), preferred_element_type=F32)


def dot_nt(a, b):
    return lax.dot_general(a, b, (((1,), (1,)), ((), ())), preferred_element_type=F32)


def swap_halves(v):
    return pltpu.roll(v, HEAD // 2, 1)


def spread_table(tab):
    low = lax.broadcasted_iota(jnp.int32, tab.shape, 1) < HEAD // 2
    other = swap_halves(tab)
    return jnp.where(low, tab, other), jnp.where(low, -other, tab)


def cost(flops, nbytes, trans=0):
    return pl.CostEstimate(flops=int(flops), bytes_accessed=int(nbytes), transcendentals=int(trans))


def params(**kw):
    return pltpu.CompilerParams(vmem_limit_bytes=62 * 1024 * 1024, **kw)


def span(index, size):
    return pl.ds(pl.multiple_of(index * size, size), size)


def kv_kernel(s_ref, x_ref, wk_ref, wv_ref, tab_ref, out_ref, w_s):
    @pl.when(pl.program_id(0) == 0)
    def _():
        w_s[:, :HEAD] = wk_ref[...]
        w_s[:, HEAD:] = wv_ref[...]

    kv = dot_nn(x_ref[...], w_s[...])
    cos_t, sin_t = spread_table(tab_ref[...])
    k = kv[:, :HEAD]
    out_ref[:, :HEAD] = (k * cos_t + swap_halves(k) * sin_t).astype(BF)
    out_ref[:, HEAD:] = kv[:, HEAD:].astype(BF)


def kv_proj(core, x, w_k, w_v, tab):
    tokens, width = x.shape
    step = tokens // 4
    return pl.pallas_call(
        kv_kernel,
        grid_spec=pltpu.PrefetchScalarGridSpec(
            num_scalar_prefetch=1,
            grid=(tokens // step,),
            in_specs=[
                pl.BlockSpec((step, width), lambda m, s: (m, 0)),
                pl.BlockSpec((width, HEAD), lambda m, s: (0, s[0])),
                pl.BlockSpec((width, HEAD), lambda m, s: (0, s[0])),
                pl.BlockSpec((step, HEAD), lambda m, s: (m, 0)),
            ],
            out_specs=pl.BlockSpec((step, 2 * HEAD), lambda m, s: (m, 0)),
            scratch_shapes=[pltpu.VMEM((width, 2 * HEAD), BF)],
        ),
        out_shape=jax.ShapeDtypeStruct((tokens, 2 * HEAD), BF),
        compiler_params=params(),
        cost_estimate=cost(2 * tokens * width * 2 * HEAD, tokens * width * 2),
        name="kv_proj",
    )(core, x, w_k, w_v, tab)


def q_kernel(s_ref, x_ref, wq_ref, tab_ref, *rest):
    out_ref = rest[-1]
    q = dot_nn(x_ref[...], wq_ref[...])
    cos_t, sin_t = spread_table(tab_ref[...])
    for h in range(wq_ref.shape[1] // HEAD):
        part = q[:, h * HEAD:(h + 1) * HEAD]
        out_ref[:, h * HEAD:(h + 1) * HEAD] = (part * cos_t + swap_halves(part) * sin_t).astype(BF)


def q_proj(sel, x, w_q, tab, prev):
    tokens, width = x.shape
    cols = w_q.shape[1] // 2
    step = 512
    rows = tokens // 2
    n = cols // step
    extra = [] if prev is None else [prev]
    return pl.pallas_call(
        q_kernel,
        grid_spec=pltpu.PrefetchScalarGridSpec(
            num_scalar_prefetch=1,
            grid=(n, 2),
            in_specs=[
                pl.BlockSpec((rows, width), lambda j, m, s: (m, 0)),
                pl.BlockSpec((width, step), lambda j, m, s: (0, s[0] * n + j)),
                pl.BlockSpec((rows, HEAD), lambda j, m, s: (m, 0)),
            ] + [pl.BlockSpec(memory_space=pl.ANY)] * len(extra),
            out_specs=pl.BlockSpec((rows, step), lambda j, m, s: (s[1] * 2 + m, j)),
        ),
        out_shape=jax.ShapeDtypeStruct((2 * tokens, cols), BF),
        input_output_aliases={} if prev is None else {4: 0},
        compiler_params=params(),
        cost_estimate=cost(2 * tokens * width * cols, tokens * width * 2 + cols * width * 2),
        name="q_proj",
    )(sel, x, w_q, tab, *extra)


def dctx_kernel(s_ref, g_ref, wo_ref, *rest):
    out_ref = rest[-1]
    out_ref[...] = dot_nt(g_ref[...], wo_ref[...]).astype(BF)


def dctx_proj(sel, g, w_o, prev):
    tokens, width = g.shape
    cols = w_o.shape[0] // 2
    step = 512
    rows = tokens // 2
    n = cols // step
    extra = [] if prev is None else [prev]
    return pl.pallas_call(
        dctx_kernel,
        grid_spec=pltpu.PrefetchScalarGridSpec(
            num_scalar_prefetch=1,
            grid=(n, 2),
            in_specs=[
                pl.BlockSpec((rows, width), lambda j, m, s: (m, 0)),
                pl.BlockSpec((step, width), lambda j, m, s: (s[0] * n + j, 0)),
            ] + [pl.BlockSpec(memory_space=pl.ANY)] * len(extra),
            out_specs=pl.BlockSpec((rows, step), lambda j, m, s: (s[1] * 2 + m, j)),
        ),
        out_shape=jax.ShapeDtypeStruct((2 * tokens, cols), BF),
        input_output_aliases={} if prev is None else {3: 0},
        compiler_params=params(),
        cost_estimate=cost(2 * tokens * width * cols, tokens * width * 2 + cols * width * 2),
        name="dctx_proj",
    )(sel, g, w_o, *extra)


def attn_kernel(
    core_ref, lo_ref, nb_ref, q_ref, do_ref, kdoc_ref, tab_own, tab_oth, kvp_own, kvp_oth, kvc_own, kvc_oth,
    act_ref, actt_ref, dkv_ref,
    k_s, v_s, s_s, dp_s, m_s, l_s, d_s, qd_s, ctx_s, dq_s, q_s, do_s, qt_s, dot_s, tab_s, dk_s, dv_s,
):
    i = pl.program_id(0)
    tokens = kvc_own.shape[0]
    chip_len = 2 * tokens
    core = core_ref[0]

    @pl.when(i == 0)
    def _():
        for base, place, ref in ((0, core, kvp_own), (0, 1 - core, kvp_oth), (2, core, kvc_own), (2, 1 - core, kvc_oth)):
            where = span(base + place, tokens)
            k_s[where, :] = ref[:, :HEAD]
            v_s[where, :] = ref[:, HEAD:]
        k_s[2 * chip_len:, :] = jnp.zeros((BK, HEAD), BF)
        v_s[2 * chip_len:, :] = jnp.zeros((BK, HEAD), BF)
        tab_s[span(core, tokens), :] = tab_own[...]
        tab_s[span(1 - core, tokens), :] = tab_oth[...]
        dk_s[...] = jnp.zeros_like(dk_s)
        dv_s[...] = jnp.zeros_like(dv_s)

    for h in range(PAIR):
        rows = slice(h * BQ, (h + 1) * BQ)
        cols = slice(h * HEAD, (h + 1) * HEAD)
        q_s[rows, :] = q_ref[:, cols]
        do_s[rows, :] = do_ref[:, cols]
        qt_s[:, rows] = q_ref[:, cols].T
        dot_s[:, rows] = do_ref[:, cols].T
    qdoc = kdoc_ref[:, pl.ds(pl.multiple_of(chip_len + i * BQ, BQ), BQ)]
    qd_s[...] = jnp.broadcast_to(qdoc, (HEAD, BQ)).T
    m_s[...] = jnp.full(m_s.shape, NEG_BIG, F32)
    l_s[...] = jnp.zeros(l_s.shape, F32)
    d_s[...] = jnp.zeros(d_s.shape, F32)
    ctx_s[...] = jnp.zeros(ctx_s.shape, F32)
    dq_s[...] = jnp.zeros(dq_s.shape, F32)
    lo = lo_ref[i]
    n_blocks = nb_ref[i]
    lanes = BK // HEAD

    def fold(v, op):
        out = v[:, :HEAD]
        for n in range(1, lanes):
            out = op(out, v[:, n * HEAD:(n + 1) * HEAD])
        return out

    def spread(v):
        return jnp.concatenate([v] * lanes, axis=1)

    def offset(b):
        return pl.multiple_of(lo + b * BK, ALIGN)

    def scores(b, carry):
        off = offset(b)
        s = dot_nt(q_s[...], k_s[pl.ds(off, BK), :])
        key = off + lax.broadcasted_iota(jnp.int32, (BQ, BK), 1)
        query = chip_len + i * BQ + lax.broadcasted_iota(jnp.int32, (BQ, BK), 0)
        keep = (key <= query) & (kdoc_ref[:, pl.ds(off, BK)] == spread(qd_s[...]))
        for h in range(PAIR):
            rows = slice(h * BQ, (h + 1) * BQ)
            sh = jnp.where(keep, s[rows, :], NEG_BIG)
            s_s[b, rows, :] = sh
            m_s[rows, :] = jnp.maximum(m_s[rows, :], fold(sh, jnp.maximum))
        return carry

    lax.fori_loop(0, n_blocks, scores, 0)
    m_s[...] = jnp.broadcast_to(jnp.max(m_s[...], axis=1, keepdims=True), m_s.shape)

    def weights(b, carry):
        dp = dot_nt(do_s[...], v_s[pl.ds(offset(b), BK), :])
        e = jnp.exp2((s_s[b] - spread(m_s[...])) * (SCALE * LOG2E))
        s_s[b] = e
        dp_s[b] = dp
        l_s[...] += fold(e, jnp.add)
        d_s[...] += fold(e * dp, jnp.add)
        return carry

    lax.fori_loop(0, n_blocks, weights, 0)
    inv = 1.0 / jnp.sum(l_s[...], axis=1, keepdims=True)
    delta = jnp.sum(d_s[...], axis=1, keepdims=True) * inv
    l_s[...] = jnp.broadcast_to(inv, l_s.shape)
    d_s[...] = jnp.broadcast_to(delta, d_s.shape)

    def grads(b, carry):
        off = offset(b)
        p = s_s[b] * spread(l_s[...])
        pb = p.astype(BF)
        ds = (p * (dp_s[b] - spread(d_s[...])) * SCALE).astype(BF)
        ctx_s[...] += dot_nn(pb, v_s[pl.ds(off, BK), :])
        dq_s[...] += dot_nn(ds, k_s[pl.ds(off, BK), :])
        dv_s[:, pl.ds(off, BK)] += dot_nn(dot_s[...], pb)
        dk_s[:, pl.ds(off, BK)] += dot_nn(qt_s[...], ds)
        return carry

    lax.fori_loop(0, n_blocks, grads, 0)
    cos_t, sin_t = spread_table(tab_s[span(i, BQ), :])
    for h in range(PAIR):
        rows = slice(h * BQ, (h + 1) * BQ)
        cols = slice(h * HEAD, (h + 1) * HEAD)
        ctx = ctx_s[rows, :].astype(BF)
        act_ref[0, :, cols] = ctx
        actt_ref[0, cols, :] = ctx.T
        dq = dq_s[rows, :].astype(BF).astype(F32)
        dq = (dq * cos_t - swap_halves(dq) * sin_t).astype(BF)
        act_ref[1, :, cols] = dq
        actt_ref[1, cols, :] = dq.T

    @pl.when(i == pl.num_programs(0) - 1)
    def _():
        dkv_ref[0] = dk_s[:, :2 * chip_len].astype(BF)
        dkv_ref[1] = dv_s[:, :2 * chip_len].astype(BF)


def attention(chunk, core, lo, n_blocks, q, dctx, kdoc, tab_own, tab_oth, kv_prev, kv_chip):
    chip_len = q.shape[0]
    tokens = chip_len // 2
    padded = 2 * chip_len + BK
    max_blocks = 2 * chip_len // BK + 1
    rows = PAIR * BQ
    full = lambda shape: pl.BlockSpec(shape, lambda i, *s: (0,) * len(shape))
    pairs = chip_len * chip_len * PAIR
    return pl.pallas_call(
        attn_kernel,
        grid_spec=pltpu.PrefetchScalarGridSpec(
            num_scalar_prefetch=3,
            grid=(chip_len // BQ,),
            in_specs=[
                pl.BlockSpec((BQ, WIDE), lambda i, *s: (i, chunk)),
                pl.BlockSpec((BQ, WIDE), lambda i, *s: (i, chunk)),
                full((1, padded)),
            ] + [full((tokens, HEAD))] * 2 + [full((tokens, 2 * HEAD))] * 4,
            out_specs=[
                pl.BlockSpec((2, BQ, WIDE), lambda i, *s: (0, i, 0)),
                pl.BlockSpec((2, WIDE, BQ), lambda i, *s: (0, 0, i)),
                full((2, HEAD, 2 * chip_len)),
            ],
            scratch_shapes=[
                pltpu.VMEM((padded, HEAD), BF),
                pltpu.VMEM((padded, HEAD), BF),
                pltpu.VMEM((max_blocks, rows, BK), F32),
                pltpu.VMEM((max_blocks, rows, BK), F32),
                pltpu.VMEM((rows, HEAD), F32),
                pltpu.VMEM((rows, HEAD), F32),
                pltpu.VMEM((rows, HEAD), F32),
                pltpu.VMEM((BQ, HEAD), jnp.int32),
                pltpu.VMEM((rows, HEAD), F32),
                pltpu.VMEM((rows, HEAD), F32),
                pltpu.VMEM((rows, HEAD), BF),
                pltpu.VMEM((rows, HEAD), BF),
                pltpu.VMEM((HEAD, rows), BF),
                pltpu.VMEM((HEAD, rows), BF),
                pltpu.VMEM((chip_len, HEAD), F32),
                pltpu.VMEM((HEAD, padded), F32),
                pltpu.VMEM((HEAD, padded), F32),
            ],
        ),
        out_shape=[
            jax.ShapeDtypeStruct((2, chip_len, WIDE), BF),
            jax.ShapeDtypeStruct((2, WIDE, chip_len), BF),
            jax.ShapeDtypeStruct((2, HEAD, 2 * chip_len), BF),
        ],
        compiler_params=params(),
        cost_estimate=cost(pairs * HEAD * 2 * 8, 12 * 1024 * 1024, pairs),
        name="attention",
    )(core, lo, n_blocks, q, dctx, kdoc, tab_own, tab_oth, *kv_prev, *kv_chip)


def kv_finish_kernel(n, s_ref, *refs):
    far_ref, tab_own, tab_oth, out_ref, outt_ref, tab_s = refs[n:]
    tokens = tab_own.shape[0]
    step = out_ref.shape[0]

    @pl.when(pl.program_id(0) == 0)
    def _():
        tab_s[span(s_ref[0], tokens), :] = tab_own[...]
        tab_s[span(1 - s_ref[0], tokens), :] = tab_oth[...]

    total = far_ref[...].astype(F32)
    for ref in refs[:n]:
        total = total + ref[...].astype(F32)
    cos_t, sin_t = spread_table(tab_s[span(pl.program_id(0), step), :])
    dk = total[0].astype(BF).astype(F32).T
    dk = (dk * cos_t - swap_halves(dk) * sin_t).astype(BF)
    dvt = total[1].astype(BF)
    out_ref[:, :HEAD] = dk
    out_ref[:, HEAD:] = dvt.T
    outt_ref[:HEAD, :] = dk.T
    outt_ref[HEAD:, :] = dvt


def kv_finish(core, parts, far, tab_own, tab_oth):
    tokens = tab_own.shape[0]
    chip_len = 2 * tokens
    step = 512
    skip = chip_len // step
    return pl.pallas_call(
        functools.partial(kv_finish_kernel, len(parts)),
        grid_spec=pltpu.PrefetchScalarGridSpec(
            num_scalar_prefetch=1,
            grid=(chip_len // step,),
            in_specs=[pl.BlockSpec((2, HEAD, step), lambda t, s: (0, 0, skip + t))] * len(parts)
            + [
                pl.BlockSpec((2, HEAD, step), lambda t, s: (0, 0, t)),
                pl.BlockSpec((tokens, HEAD), lambda t, s: (0, 0)),
                pl.BlockSpec((tokens, HEAD), lambda t, s: (0, 0)),
            ],
            out_specs=[
                pl.BlockSpec((step, 2 * HEAD), lambda t, s: (t, 0)),
                pl.BlockSpec((2 * HEAD, step), lambda t, s: (0, t)),
            ],
            scratch_shapes=[pltpu.VMEM((chip_len, HEAD), F32)],
        ),
        out_shape=[
            jax.ShapeDtypeStruct((chip_len, 2 * HEAD), BF),
            jax.ShapeDtypeStruct((2 * HEAD, chip_len), BF),
        ],
        compiler_params=params(),
        cost_estimate=cost(chip_len * HEAD * 64, chip_len * HEAD * 16),
        name="kv_finish",
    )(core, *parts, far, tab_own, tab_oth)


def wgrad_kernel(s_ref, actt_ref, x_own, x_oth, g_own, g_oth, out_ref):
    tokens = x_own.shape[0]
    own, oth = span(s_ref[0], tokens), span(1 - s_ref[0], tokens)
    out_ref[0] = (dot_nn(actt_ref[1, :, own], x_own[...]) + dot_nn(actt_ref[1, :, oth], x_oth[...])).astype(BF)
    out_ref[1] = (dot_nn(actt_ref[0, :, own], g_own[...]) + dot_nn(actt_ref[0, :, oth], g_oth[...])).astype(BF)


def wgrad(core, actt, x_own, x_oth, g_own, g_oth):
    tokens, width = x_own.shape
    step = 512
    piece = pl.BlockSpec((tokens, step), lambda n, s: (0, n))
    return pl.pallas_call(
        wgrad_kernel,
        grid_spec=pltpu.PrefetchScalarGridSpec(
            num_scalar_prefetch=1,
            grid=(width // step,),
            in_specs=[pl.BlockSpec((2, WIDE, 2 * tokens), lambda n, s: (0, 0, 0)), piece, piece, piece, piece],
            out_specs=pl.BlockSpec((2, WIDE, step), lambda n, s: (0, 0, n)),
        ),
        out_shape=jax.ShapeDtypeStruct((2, WIDE, width), BF),
        compiler_params=params(),
        cost_estimate=cost(8 * tokens * width * WIDE, 8 * tokens * width),
        name="wgrad",
    )(core, actt, x_own, x_oth, g_own, g_oth)


def kvgrad_kernel(s_ref, dkvt_ref, x_own, x_oth, out_ref):
    tokens = x_own.shape[0]
    own, oth = span(s_ref[0], tokens), span(1 - s_ref[0], tokens)
    out_ref[...] = (dot_nn(dkvt_ref[:, own], x_own[...]) + dot_nn(dkvt_ref[:, oth], x_oth[...])).astype(BF)


def kvgrad(core, dkvt, x_own, x_oth):
    tokens, width = x_own.shape
    step = 512
    piece = pl.BlockSpec((tokens, step), lambda n, s: (0, n))
    return pl.pallas_call(
        kvgrad_kernel,
        grid_spec=pltpu.PrefetchScalarGridSpec(
            num_scalar_prefetch=1,
            grid=(width // step,),
            in_specs=[pl.BlockSpec((2 * HEAD, 2 * tokens), lambda n, s: (0, 0)), piece, piece],
            out_specs=pl.BlockSpec((2 * HEAD, step), lambda n, s: (0, n)),
        ),
        out_shape=jax.ShapeDtypeStruct((2 * HEAD, width), BF),
        compiler_params=params(),
        cost_estimate=cost(4 * tokens * width * 2 * HEAD, 4 * tokens * width),
        name="kvgrad",
    )(core, dkvt, x_own, x_oth)


def kv_combine_kernel(s_ref, a_ref, b_ref, c_ref, d_ref, gk_ref, gv_ref):
    for place, u_ref, v_ref in ((s_ref[0], a_ref, b_ref), (1 - s_ref[0], c_ref, d_ref)):
        total = u_ref[...].astype(F32) + v_ref[...].astype(F32)
        where = span(place, HEAD)
        gk_ref[:, where] = total[:HEAD, :].T
        gv_ref[:, where] = total[HEAD:, :].T


def kv_combine(core, parts):
    rows, width = parts[0].shape
    step = 512
    out = jax.ShapeDtypeStruct((width, rows), F32)
    return pl.pallas_call(
        kv_combine_kernel,
        grid_spec=pltpu.PrefetchScalarGridSpec(
            num_scalar_prefetch=1,
            grid=(width // step,),
            in_specs=[pl.BlockSpec((rows, step), lambda n, s: (0, n))] * 4,
            out_specs=[pl.BlockSpec((step, rows), lambda n, s: (n, 0))] * 2,
        ),
        out_shape=[out, out],
        compiler_params=params(),
        cost_estimate=cost(16 * width * rows * 16, 16 * width * rows),
        name="kv_combine",
    )(core, *parts)


def combine_kernel(s_ref, a_ref, b_ref, c_ref, d_ref, *rest):
    gq_ref, go_ref = rest[-2:]

    def put(u_ref, v_ref):
        gq_ref[...] = (u_ref[0].astype(F32) + v_ref[0].astype(F32)).T
        go_ref[...] = u_ref[1].astype(F32) + v_ref[1].astype(F32)

    @pl.when(pl.program_id(0) == 0)
    def _():
        put(a_ref, b_ref)

    @pl.when(pl.program_id(0) == 1)
    def _():
        put(c_ref, d_ref)


def combine(core, chunk, n_chunks, parts, prev):
    width = parts[0].shape[2]
    step = 512
    last = width // step - 1
    near = pl.BlockSpec((2, WIDE, step), lambda w, r, s: (0, 0, r + w * (last - r)))
    far = pl.BlockSpec((2, WIDE, step), lambda w, r, s: (0, 0, r * w))

    def place(w, s):
        return (s[0] + w - 2 * s[0] * w) * n_chunks + chunk

    shape = jax.ShapeDtypeStruct((width, 2 * n_chunks * WIDE), F32)
    shape_o = jax.ShapeDtypeStruct((2 * n_chunks * WIDE, width), F32)
    extra = [] if prev is None else list(prev)
    return pl.pallas_call(
        combine_kernel,
        grid_spec=pltpu.PrefetchScalarGridSpec(
            num_scalar_prefetch=1,
            grid=(2, width // step),
            in_specs=[near, near, far, far] + [pl.BlockSpec(memory_space=pl.ANY)] * len(extra),
            out_specs=[
                pl.BlockSpec((step, WIDE), lambda w, r, s: (r, place(w, s))),
                pl.BlockSpec((WIDE, step), lambda w, r, s: (place(w, s), r)),
            ],
        ),
        out_shape=[shape, shape_o],
        input_output_aliases={} if prev is None else {5: 0, 6: 1},
        compiler_params=params(),
        cost_estimate=cost(16 * width * WIDE * 64, 32 * width * WIDE),
        name="combine",
    )(core, *parts, *extra)


def fill_heads(core, own_refs, oth_refs, lhs):
    n = len(own_refs)
    for j in range(n):
        lhs[:, pl.ds(pl.multiple_of((core * n + j) * WIDE, WIDE), WIDE)] = own_refs[j][0]
        lhs[:, pl.ds(pl.multiple_of(((1 - core) * n + j) * WIDE, WIDE), WIDE)] = oth_refs[j][0]


def attn_out_kernel(n, s_ref, *refs):
    own_refs, oth_refs = refs[:n], refs[n:2 * n]
    wo_ref, out_ref, lhs = refs[2 * n:]

    @pl.when(pl.program_id(0) == 0)
    def _():
        fill_heads(s_ref[0], own_refs, oth_refs, lhs)

    out_ref[...] = dot_nn(lhs[...], wo_ref[...]).astype(BF)


def attn_out(core, own, oth, w_o):
    n = len(own)
    tokens = own[0].shape[1] // 2
    heads, width = w_o.shape
    step = 512
    return pl.pallas_call(
        functools.partial(attn_out_kernel, n),
        grid_spec=pltpu.PrefetchScalarGridSpec(
            num_scalar_prefetch=1,
            grid=(width // step,),
            in_specs=[pl.BlockSpec((1, tokens, WIDE), lambda k, s: (0, s[0], 0))] * (2 * n)
            + [pl.BlockSpec((heads, step), lambda k, s: (0, k))],
            out_specs=pl.BlockSpec((tokens, step), lambda k, s: (0, k)),
            scratch_shapes=[pltpu.VMEM((tokens, heads), BF)],
        ),
        out_shape=jax.ShapeDtypeStruct((tokens, width), BF),
        compiler_params=params(),
        cost_estimate=cost(2 * tokens * heads * width, 2 * heads * width + 4 * tokens * width),
        name="attn_out",
    )(core, *own, *oth, w_o)


def hidden_kernel(n, s_ref, *refs):
    own_refs, oth_refs = refs[:n], refs[n:2 * n]
    kv_own, kv_oth, wq_ref, wk_ref, wv_ref, out_ref, lhs, klhs, vlhs = refs[2 * n:]
    core = s_ref[0]

    @pl.when(pl.program_id(0) == 0)
    def _():
        fill_heads(core, own_refs, oth_refs, lhs)
        for place, ref in ((core, kv_own), (1 - core, kv_oth)):
            where = pl.ds(pl.multiple_of(place * HEAD, HEAD), HEAD)
            klhs[:, where] = ref[:, :HEAD]
            vlhs[:, where] = ref[:, HEAD:]

    out_ref[...] = (
        dot_nt(lhs[...], wq_ref[...]) + dot_nt(klhs[...], wk_ref[...]) + dot_nt(vlhs[...], wv_ref[...])
    ).astype(BF)


def grad_hidden(core, own, oth, kv_own, kv_oth, w_q, w_k, w_v):
    n = len(own)
    tokens = own[0].shape[1] // 2
    width, heads = w_q.shape
    kv_cols = w_k.shape[1]
    step = 512
    return pl.pallas_call(
        functools.partial(hidden_kernel, n),
        grid_spec=pltpu.PrefetchScalarGridSpec(
            num_scalar_prefetch=1,
            grid=(width // step,),
            in_specs=[pl.BlockSpec((1, tokens, WIDE), lambda k, s: (1, s[0], 0))] * (2 * n)
            + [pl.BlockSpec((tokens, 2 * HEAD), lambda k, s: (s[0], 0))] * 2
            + [
                pl.BlockSpec((step, heads), lambda k, s: (k, 0)),
                pl.BlockSpec((step, kv_cols), lambda k, s: (k, 0)),
                pl.BlockSpec((step, kv_cols), lambda k, s: (k, 0)),
            ],
            out_specs=pl.BlockSpec((tokens, step), lambda k, s: (0, k)),
            scratch_shapes=[
                pltpu.VMEM((tokens, heads), BF),
                pltpu.VMEM((tokens, kv_cols), BF),
                pltpu.VMEM((tokens, kv_cols), BF),
            ],
        ),
        out_shape=jax.ShapeDtypeStruct((tokens, width), BF),
        compiler_params=params(),
        cost_estimate=cost(2 * tokens * (heads + 2 * kv_cols) * width, 2 * heads * width + 4 * tokens * width),
        name="grad_hidden",
    )(core, *own, *oth, kv_own, kv_oth, w_q, w_k, w_v)


def solution(mesh):
    n_dev = mesh.shape["sp"]
    n_chunks = 4
    near_perm = [(d, d ^ 1) for d in range(n_dev)]
    far_perm = [(d, d ^ 2) for d in range(n_dev)]
    down_perm = [(0, 2), (1, 3)]
    up_perm = [(2, 0), (3, 1)]

    def near(v):
        return lax.ppermute(v, "sp", near_perm)

    def far(v):
        return lax.ppermute(v, "sp", far_perm)

    def device_step(hidden, grad_out, positions, doc_ids, w_q, w_k, w_v, w_o):
        tokens = hidden.shape[0]
        chip_len = 2 * tokens
        assert n_chunks == w_q.shape[1] // (2 * WIDE)
        place = lax.axis_index("sp")
        core_id, chip_id = place & 1, place >> 1
        core = core_id.astype(jnp.int32)[None]
        sel_own = jnp.stack([core_id, core_id]).astype(jnp.int32)
        sel_oth = jnp.stack([core_id, 1 - core_id]).astype(jnp.int32)

        doc_oth = near(doc_ids)
        x_oth = near(hidden)
        g_oth = near(grad_out)
        tab_own = rope_table(positions)
        tab_oth = near(tab_own)
        kv_own = kv_proj(core, hidden, w_k, w_v, tab_own)
        kvp_own = lax.ppermute(kv_own, "sp", down_perm)
        q = q_proj(sel_own, hidden, w_q, tab_own, None)
        doc_chip = jnp.where(
            core_id == 0, jnp.concatenate([doc_ids, doc_oth]), jnp.concatenate([doc_oth, doc_ids])
        )
        doc_far = far(doc_chip)
        kv_oth = kv_proj(core, x_oth, w_k, w_v, tab_oth)
        kvp_oth = lax.ppermute(kv_oth, "sp", down_perm)
        dctx = dctx_proj(sel_own, grad_out, w_o, None)
        q = q_proj(sel_oth, x_oth, w_q, tab_oth, q)
        dctx = dctx_proj(sel_oth, g_oth, w_o, dctx)

        heads_doc = doc_chip[::BQ]
        lo = jnp.sum(doc_chip[None, :] < heads_doc[:, None], axis=1, dtype=jnp.int32)
        lo_far = jnp.sum(doc_far[None, :] < heads_doc[:, None], axis=1, dtype=jnp.int32)
        lo = lo + jnp.where(chip_id == 0, chip_len, lo_far)
        lo = (lo >> (ALIGN.bit_length() - 1)) << (ALIGN.bit_length() - 1)
        end = chip_len + BQ * (1 + jnp.arange(chip_len // BQ, dtype=jnp.int32))
        n_blocks = (end - lo + BK - 1) >> (BK.bit_length() - 1)
        kdoc = jnp.concatenate([doc_far, doc_chip, jnp.zeros((BK,), jnp.int32)])[None, :]

        acts, acts_oth, dkvs, sums = [], [], [], None
        q_in = q
        for j in range(n_chunks):
            act, actt, dkv = attention(
                j, core, lo, n_blocks, q_in, dctx, kdoc, tab_own, tab_oth, (kvp_own, kvp_oth), (kv_own, kv_oth)
            )
            acts.append(act)
            dkvs.append(dkv)
            if j == n_chunks - 1:
                dkv_up = sum(d[:, :, :chip_len].astype(F32) for d in dkvs).astype(BF)
                dkv_far = lax.ppermute(dkv_up, "sp", up_perm)
            acts_oth.append(near(act))
            part = wgrad(core, actt, hidden, x_oth, grad_out, g_oth)
            part_far = far(part)
            part_near = near(part)
            part_far_near = near(part_far)
            sums = combine(core, j, n_chunks, (part, part_far, part_near, part_far_near), sums)
        grad_wq, grad_wo = sums

        dkv, dkvt = kv_finish(core, dkvs, dkv_far, tab_own, tab_oth)
        dkv_oth = near(dkv)
        kv_part = kvgrad(core, dkvt, hidden, x_oth)
        kv_part_far = far(kv_part)
        kv_part_near = near(kv_part)
        kv_part_far_near = near(kv_part_far)
        grad_wk, grad_wv = kv_combine(core, (kv_part, kv_part_far, kv_part_near, kv_part_far_near))
        out = attn_out(core, acts, acts_oth, w_o)
        g_hidden = grad_hidden(core, acts, acts_oth, dkv, dkv_oth, w_q, w_k, w_v)
        return out, g_hidden, grad_wq, grad_wk, grad_wv, grad_wo

    tok_spec = P(("dp", "sp"), None)
    vec_spec = P(("dp", "sp"))
    rep_spec = P(None, None)
    part_spec = P("dp", None)


    return jax.shard_map(
        device_step,
        mesh=mesh,
        in_specs=(tok_spec, tok_spec, vec_spec, vec_spec, rep_spec, rep_spec, rep_spec, rep_spec),
        out_specs=(tok_spec, tok_spec, part_spec, part_spec, part_spec, part_spec),
        check_vma=False,
    )
```

time: 570 us -> 556 us (0.975)
  starting transfers between devices: 28 us -> 67.9 us
  waiting for transfers between devices: 208 us -> 172 us
  Pallas kernels: 306 us -> 297 us
  other arithmetic: 14.6 us -> 7.74 us
  local copies, waits for them, and re-layouts: 11.1 us -> 4.27 us
    ppermute x1, waiting for transfers between devices: 71.8 us -> 12 us  [device_step(): dkv_far = lax.ppermute(dkv_up, 'sp', up_perm)]
    ppermute x6, starting transfers between devices: 20.6 us -> 54.7 us  [far(): return lax.ppermute(v, 'sp', far_perm)]
    ppermute x6, waiting for transfers between devices: 130 us -> 153 us  [far(): return lax.ppermute(v, 'sp', far_perm)]
    pallas_call x7 -> x6, Pallas kernels: 137 us -> 124 us  [the longest x4 113 us: attention(): pl.pallas_call(attn_kernel, grid_spec=pltpu.PrefetchScalarGridSpec(num_sc...]
  transfers between devices with their start and end apart: 25 -> 28, of which waited for: 5 -> 8; matrix products, arithmetic and copies ran while one was open for 4% -> 1% of each run, Pallas kernels for 45% -> 32%
where the time goes in v2:
time: 556 us; the launch traced here: 550 us
  Pallas kernels  297 us (53%)
  waiting for transfers between devices  172 us (31%)
  starting transfers between devices  67.9 us (12%)
  other arithmetic  7.74 us (1%)
    ppermute x6, waiting for transfers between devices, far(): return lax.ppermute(v, 'sp', far_perm)  153 us
    pallas_call x4, Pallas kernels, attention(): pl.pallas_call(attn_kernel, grid_spec=pltpu.PrefetchScalarGridSpec(num_sc...  113 us
    ppermute x6, starting transfers between devices, far(): return lax.ppermute(v, 'sp', far_perm)  54.7 us
    pallas_call x4, Pallas kernels, wgrad(): pl.pallas_call(wgrad_kernel, grid_spec=pltpu.PrefetchScalarGridSpec(num_s...  44.2 us
    pallas_call x4, Pallas kernels, combine(): pl.pallas_call(combine_kernel, grid_spec=pltpu.PrefetchScalarGridSpec(num...  39.4 us
    pallas_call x2, Pallas kernels, q_proj(): pl.pallas_call(q_kernel, grid_spec=pltpu.PrefetchScalarGridSpec(num_scala...  21.3 us
    pallas_call x2, Pallas kernels, dctx_proj(): pl.pallas_call(dctx_kernel, grid_spec=pltpu.PrefetchScalarGridSpec(num_sc...  20.4 us
    pallas_call x1, Pallas kernels, grad_hidden(): pl.pallas_call(functools.partial(hidden_kernel, n), grid_spec=pltpu.Prefe...  17 us
  transfers between devices with their start and end apart: 28, of which 8 were waited for; matrix products, arithmetic and copies ran while one was open for 1% of the time, Pallas kernels for 32%

profile of v2, /device:TPU:0, one launch (start us, length us, event | category | flops | bytes accessed | tf_op | source)
XLA Modules:
  0.0 550.4 jit_solution(2375374729065792470)
XLA Ops:
  5.1 5.4 kv_proj.2.kvc_own
  10.5 4.9 collective-permute-start.5
  16.0 10.7 %q_proj.2.rest_0_ = bf16[2048,1024]{1,0:T(8,128)(2,1)} custom-call(s32[2]{0:T(128)} %pad_add_fusion.2.s_ref, bf16[1024,2048]{1,0:T(8,128)(2,1)} %x_own.9, bf16[2048,2048]{1,0:T(8,128)(2,1)} %refs_10_.1, f32[1024,128]{1,0:T(8,128)} %copy-done), custom_call_target="tpu_custom_call" | custom-call | flops 4294967296 | bytes 8388608 | tf_op jit(solution)/shard_map/q_proj/pallas_call | solution.py:127
  26.7 10.2 %dctx_proj.2.rest_0_ = bf16[2048,1024]{1,0:T(8,128)(2,1)} custom-call(s32[2]{0:T(128)} %pad_add_fusion.2.s_ref, bf16[1024,2048]{1,0:T(8,128)(2,1)} %g_own.7, bf16[2048,2048]{1,0:T(8,128)(2,1)} %refs_8_.1), custom_call_target="tpu_custom_call" | custom-call | flops 4294967296 | bytes 8388608 | tf_op jit(solution)/shard_map/dctx_proj/pallas_call | solution.py:159
  37.6 3.0 collective-permute-done.1
  42.8 5.4 kv_proj.3.kvc_oth
  50.6 10.7 %q_proj.3.q_ref = bf16[2048,1024]{1,0:T(8,128)(2,1)} custom-call(s32[2]{0:T(128)} %pad_add_fusion.1.s_ref, bf16[1024,2048]{1,0:T(8,128)(2,1)} %collective-permute-done.2.x_ref.x_oth, bf16[2048,2048]{1,0:T(8,128)(2,1)} %refs_10_.1, f32[1024,128]{1,0:T(8,128)} %copy-done.1, bf16[2048,1024]{1,0:T(8,128)(2,1)} %q_proj.2.rest_0_), custom_call_target="tpu_custom_call", output_to_operand_aliasing={{}: (4, {})} | custom-call | flops 4294967296 | bytes 8388608 | tf_op jit(solution)/shard_map/q_proj/pallas_call | solution.py:127
  61.3 10.2 %dctx_proj.3.do_ref = bf16[2048,1024]{1,0:T(8,128)(2,1)} custom-call(s32[2]{0:T(128)} %pad_add_fusion.1.s_ref, bf16[1024,2048]{1,0:T(8,128)(2,1)} %collective-permute-done.4.g_ref.g_oth, bf16[2048,2048]{1,0:T(8,128)(2,1)} %refs_8_.1, bf16[2048,1024]{1,0:T(8,128)(2,1)} %dctx_proj.2.rest_0_), custom_call_target="tpu_custom_call", output_to_operand_aliasing={{}: (3, {})} | custom-call | flops 4294967296 | bytes 8388608 | tf_op jit(solution)/shard_map/dctx_proj/pallas_call | solution.py:159
  72.5 28.2 %attention.7 = (bf16[2,2048,256]{2,1,0:T(8,128)(2,1)}, bf16[2,256,2048]{2,1,0:T(8,128)(2,1)}, bf16[2,128,4096]{2,1,0:T(8,128)(2,1)}) custom-call(s32[1]{0:T(128)} %bitcast.s_ref.core_ref, s32[4]{0:T(128)} %get-tuple-element.57.lo_ref, s32[4]{0:T(128)} %get-tuple-element.56.nb_ref, bf16[2048,1024]{1,0:T(8,128)(2,1)} %q_proj.3.q_ref, ...), custom_call_target="tpu_custom_call" | custom-call | flops 17179869184 | bytes 12582912 | tf_op jit(solution)/shard_map/attention/pallas_call | solution.py:300
  100.8 28.2 %attention.6 = (bf16[2,2048,256]{2,1,0:T(8,128)(2,1)}, bf16[2,256,2048]{2,1,0:T(8,128)(2,1)}, bf16[2,128,4096]{2,1,0:T(8,128)(2,1)}) custom-call(s32[1]{0:T(128)} %bitcast.s_ref.core_ref, s32[4]{0:T(128)} %get-tuple-element.57.lo_ref, s32[4]{0:T(128)} %get-tuple-element.56.nb_ref, bf16[2048,1024]{1,0:T(8,128)(2,1)} %q_proj.3.q_ref, ...), custom_call_target="tpu_custom_call" | custom-call | flops 17179869184 | bytes 12582912 | tf_op jit(solution)/shard_map/attention/pallas_call | solution.py:300
  129.0 28.4 %attention.5 = (bf16[2,2048,256]{2,1,0:T(8,128)(2,1)}, bf16[2,256,2048]{2,1,0:T(8,128)(2,1)}, bf16[2,128,4096]{2,1,0:T(8,128)(2,1)}) custom-call(s32[1]{0:T(128)} %bitcast.s_ref.core_ref, s32[4]{0:T(128)} %get-tuple-element.57.lo_ref, s32[4]{0:T(128)} %get-tuple-element.56.nb_ref, bf16[2048,1024]{1,0:T(8,128)(2,1)} %q_proj.3.q_ref, ...), custom_call_target="tpu_custom_call" | custom-call | flops 17179869184 | bytes 12582912 | tf_op jit(solution)/shard_map/attention/pallas_call | solution.py:300
  157.5 28.2 %attention.4 = (bf16[2,2048,256]{2,1,0:T(8,128)(2,1)}, bf16[2,256,2048]{2,1,0:T(8,128)(2,1)}, bf16[2,128,4096]{2,1,0:T(8,128)(2,1)}) custom-call(s32[1]{0:T(128)} %bitcast.s_ref.core_ref, s32[4]{0:T(128)} %get-tuple-element.57.lo_ref, s32[4]{0:T(128)} %get-tuple-element.56.nb_ref, bf16[2048,1024]{1,0:T(8,128)(2,1)} %q_proj.3.q_ref, ...), custom_call_target="tpu_custom_call" | custom-call | flops 17179869184 | bytes 12582912 | tf_op jit(solution)/shard_map/attention/pallas_call | solution.py:300
  189.9 11.1 %wgrad.7.a_ref = bf16[2,256,2048]{2,1,0:T(8,128)(2,1)} custom-call(s32[1]{0:T(128)} %bitcast.s_ref.core_ref, bf16[2,256,2048]{2,1,0:T(8,128)(2,1)} %get-tuple-element.42.actt_ref, bf16[1024,2048]{1,0:T(8,128)(2,1)} %x_own.9, bf16[1024,2048]{1,0:T(8,128)(2,1)} %collective-permute-done.2.x_ref.x_oth, bf16[1024,2048]{1,0:T(8,128)(2,1)} %g_own.7, ...), custom_call_target="tpu_custom_call" | custom-call | flops 4294967296 | bytes 16777216 | tf_op jit(solution)/shard_map/wgrad/pallas_call | solution.py:412
  201.0 51.0 %collective-permute-start.22 = (bf16[2,256,2048]{2,1,0:T(8,128)(2,1)}, bf16[2,256,2048]{2,1,0:T(8,128)(2,1)}, u32[]{:S(2)}, u32[]{:S(2)}) collective-permute-start(bf16[2,256,2048]{2,1,0:T(8,128)(2,1)} %wgrad.7.a_ref), channel_id=1, source_target_pairs={{0,2},{1,3},{2,0},{3,1},{4,6},{5,7},{6,4},{7,5}} | collective-permute-start | bytes 6291464 | tf_op jit(solution)/shard_map/ppermute | solution.py:629
  252.0 12.0 %collective-permute-done.11.refs_4_ = bf16[2,128,2048]{2,1,0:T(8,128)(2,1)} collective-permute-done((bf16[2,128,2048]{2,1,0:T(8,128)(2,1)S(1)}, bf16[2,128,2048]{2,1,0:T(8,128)(2,1)}, u32[]{:S(2)}, u32[]{:S(2)}) %collective-permute-start.11) | collective-permute-done | bytes 1048608 | tf_op jit(solution)/shard_map/ppermute | solution.py:678
  264.0 5.5 kv_finish.1
  269.5 6.6 %kvgrad.1.a_ref = bf16[256,2048]{1,0:T(8,128)(2,1)} custom-call(s32[1]{0:T(128)} %bitcast.s_ref.core_ref, bf16[256,2048]{1,0:T(8,128)(2,1)} %get-tuple-element.50.dkvt_ref, bf16[1024,2048]{1,0:T(8,128)(2,1)} %x_own.9, bf16[1024,2048]{1,0:T(8,128)(2,1)} %collective-permute-done.2.x_ref.x_oth), custom_call_target="tpu_custom_call" | custom-call | flops 2147483648 | bytes 8388608 | tf_op jit(solution)/shard_map/kvgrad/pallas_call | solution.py:437
  276.6 11.0 %wgrad.6.a_ref = bf16[2,256,2048]{2,1,0:T(8,128)(2,1)} custom-call(s32[1]{0:T(128)} %bitcast.s_ref.core_ref, bf16[2,256,2048]{2,1,0:T(8,128)(2,1)} %get-tuple-element.41.actt_ref, bf16[1024,2048]{1,0:T(8,128)(2,1)} %x_own.9, bf16[1024,2048]{1,0:T(8,128)(2,1)} %collective-permute-done.2.x_ref.x_oth, bf16[1024,2048]{1,0:T(8,128)(2,1)} %g_own.7, ...), custom_call_target="tpu_custom_call" | custom-call | flops 4294967296 | bytes 16777216 | tf_op jit(solution)/shard_map/wgrad/pallas_call | solution.py:412
  289.6 10.9 %wgrad.5.a_ref = bf16[2,256,2048]{2,1,0:T(8,128)(2,1)} custom-call(s32[1]{0:T(128)} %bitcast.s_ref.core_ref, bf16[2,256,2048]{2,1,0:T(8,128)(2,1)} %get-tuple-element.40.actt_ref, bf16[1024,2048]{1,0:T(8,128)(2,1)} %x_own.9, bf16[1024,2048]{1,0:T(8,128)(2,1)} %collective-permute-done.2.x_ref.x_oth, bf16[1024,2048]{1,0:T(8,128)(2,1)} %g_own.7, ...), custom_call_target="tpu_custom_call" | custom-call | flops 4294967296 | bytes 16777216 | tf_op jit(solution)/shard_map/wgrad/pallas_call | solution.py:412
  300.5 30.8 %collective-permute-done.25.b_ref = bf16[256,2048]{1,0:T(8,128)(2,1)S(1)} collective-permute-done((bf16[256,2048]{1,0:T(8,128)(2,1)}, bf16[256,2048]{1,0:T(8,128)(2,1)S(1)}, u32[]{:S(2)}, u32[]{:S(2)}) %collective-permute-start.25) | collective-permute-done | bytes 1048608 | tf_op jit(solution)/shard_map/ppermute | solution.py:629
  331.3 11.2 %wgrad.4.a_ref = bf16[2,256,2048]{2,1,0:T(8,128)(2,1)} custom-call(s32[1]{0:T(128)} %bitcast.s_ref.core_ref, bf16[2,256,2048]{2,1,0:T(8,128)(2,1)} %get-tuple-element.39.actt_ref, bf16[1024,2048]{1,0:T(8,128)(2,1)} %x_own.9, bf16[1024,2048]{1,0:T(8,128)(2,1)} %collective-permute-done.2.x_ref.x_oth, bf16[1024,2048]{1,0:T(8,128)(2,1)} %g_own.7, ...), custom_call_target="tpu_custom_call" | custom-call | flops 4294967296 | bytes 16777216 | tf_op jit(solution)/shard_map/wgrad/pallas_call | solution.py:412
  344.3 32.1 %collective-permute-done.19.b_ref = bf16[2,256,2048]{2,1,0:T(8,128)(2,1)} collective-permute-done((bf16[2,256,2048]{2,1,0:T(8,128)(2,1)}, bf16[2,256,2048]{2,1,0:T(8,128)(2,1)}, u32[]{:S(2)}, u32[]{:S(2)}) %collective-permute-start.19) | collective-permute-done | bytes 2097184 | tf_op jit(solution)/shard_map/ppermute | solution.py:629
  376.9 44.4 %collective-permute-done.16.b_ref = bf16[2,256,2048]{2,1,0:T(8,128)(2,1)} collective-permute-done((bf16[2,256,2048]{2,1,0:T(8,128)(2,1)}, bf16[2,256,2048]{2,1,0:T(8,128)(2,1)}, u32[]{:S(2)}, u32[]{:S(2)}) %collective-permute-start.16) | collective-permute-done | bytes 2097184 | tf_op jit(solution)/shard_map/ppermute | solution.py:629
  421.3 43.1 %collective-permute-done.13.b_ref = bf16[2,256,2048]{2,1,0:T(8,128)(2,1)} collective-permute-done((bf16[2,256,2048]{2,1,0:T(8,128)(2,1)}, bf16[2,256,2048]{2,1,0:T(8,128)(2,1)}, u32[]{:S(2)}, u32[]{:S(2)}) %collective-permute-start.13) | collective-permute-done | bytes 2097184 | tf_op jit(solution)/shard_map/ppermute | solution.py:629
  468.9 4.4 collective-permute-done.27.d_ref
  474.8 13.9 %attn_out.1 = bf16[1024,2048]{1,0:T(8,128)(2,1)} custom-call(s32[1]{0:T(128)} %bitcast.s_ref.core_ref, bf16[2,2048,256]{2,1,0:T(8,128)(2,1)} %get-tuple-element.30.refs_0_, bf16[2,2048,256]{2,1,0:T(8,128)(2,1)} %get-tuple-element.31.refs_1_, bf16[2,2048,256]{2,1,0:T(8,128)(2,1)} %get-tuple-element.32.refs_2_, ...), custom_call_target="tpu_custom_call" | custom-call | flops 8589934592 | bytes 16777216 | tf_op jit(solution)/shard_map/attn_out/pallas_call | solution.py:550
  488.7 17.0 %grad_hidden.1 = bf16[1024,2048]{1,0:T(8,128)(2,1)} custom-call(s32[1]{0:T(128)} %bitcast.s_ref.core_ref, bf16[2,2048,256]{2,1,0:T(8,128)(2,1)} %get-tuple-element.30.refs_0_, bf16[2,2048,256]{2,1,0:T(8,128)(2,1)} %get-tuple-element.31.refs_1_, bf16[2,2048,256]{2,1,0:T(8,128)(2,1)} %get-tuple-element.32.refs_2_, ...), custom_call_target="tpu_custom_call" | custom-call | flops 10737418240 | bytes 16777216 | tf_op jit(solution)/shard_map/grad_hidden/pallas_call | solution.py:591
  505.7 5.1 kv_combine.1
  510.7 9.8 %combine.4 = (f32[2048,2048]{1,0:T(8,128)}, f32[2048,2048]{1,0:T(8,128)}) custom-call(s32[1]{0:T(128)} %bitcast.s_ref.core_ref, bf16[2,256,2048]{2,1,0:T(8,128)(2,1)} %wgrad.7.a_ref, bf16[2,256,2048]{2,1,0:T(8,128)(2,1)} %collective-permute-done.22.b_ref, bf16[2,256,2048]{2,1,0:T(8,128)(2,1)} %collective-permute-done.23.c_ref, ...), custom_call_target="tpu_custom_call" | custom-call | flops 536870912 | bytes 16777216 | tf_op jit(solution)/shard_map/combine/pallas_call | solution.py:508
  520.6 9.9 %combine.5 = (f32[2048,2048]{1,0:T(8,128)}, f32[2048,2048]{1,0:T(8,128)}) custom-call(s32[1]{0:T(128)} %bitcast.s_ref.core_ref, bf16[2,256,2048]{2,1,0:T(8,128)(2,1)} %wgrad.6.a_ref, bf16[2,256,2048]{2,1,0:T(8,128)(2,1)} %collective-permute-done.19.b_ref, ...), custom_call_target="tpu_custom_call", output_to_operand_aliasing={{0}: (5, {}), {1}: (6, {})} | custom-call | flops 536870912 | bytes 16777216 | tf_op jit(solution)/shard_map/combine/pallas_call | solution.py:508
  530.5 9.9 %combine.6 = (f32[2048,2048]{1,0:T(8,128)}, f32[2048,2048]{1,0:T(8,128)}) custom-call(s32[1]{0:T(128)} %bitcast.s_ref.core_ref, bf16[2,256,2048]{2,1,0:T(8,128)(2,1)} %wgrad.5.a_ref, bf16[2,256,2048]{2,1,0:T(8,128)(2,1)} %collective-permute-done.16.b_ref, ...), custom_call_target="tpu_custom_call", output_to_operand_aliasing={{0}: (5, {}), {1}: (6, {})} | custom-call | flops 536870912 | bytes 16777216 | tf_op jit(solution)/shard_map/combine/pallas_call | solution.py:508
  540.3 9.9 %combine.7 = (f32[2048,2048]{1,0:T(8,128)}, f32[2048,2048]{1,0:T(8,128)}) custom-call(s32[1]{0:T(128)} %bitcast.s_ref.core_ref, bf16[2,256,2048]{2,1,0:T(8,128)(2,1)} %wgrad.4.a_ref, bf16[2,256,2048]{2,1,0:T(8,128)(2,1)} %collective-permute-done.13.b_ref, ...), custom_call_target="tpu_custom_call", output_to_operand_aliasing={{0}: (5, {}), {1}: (6, {})} | custom-call | flops 536870912 | bytes 16777216 | tf_op jit(solution)/shard_map/combine/pallas_call | solution.py:508
  (83 shorter events, 26.5 us)
Async XLA Ops:
  0.6 41.4 %collective-permute-start.2 = (bf16[1024,2048]{1,0:T(8,128)(2,1)}, bf16[1024,2048]{1,0:T(8,128)(2,1)}, u32[]{:S(2)}, u32[]{:S(2)}) collective-permute-start(bf16[1024,2048]{1,0:T(8,128)(2,1)} %x_own.9), channel_id=1, source_target_pairs={{0,1},{1,0},{2,3},{3,2},{4,5},{5,4},{6,7},{7,6}} | collective-permute-start | bytes 12582920 | tf_op jit(solution)/shard_map/ppermute | solution.py:626
  1.5 59.8 %collective-permute-start.4 = (bf16[1024,2048]{1,0:T(8,128)(2,1)}, bf16[1024,2048]{1,0:T(8,128)(2,1)}, u32[]{:S(2)}, u32[]{:S(2)}) collective-permute-start(bf16[1024,2048]{1,0:T(8,128)(2,1)} %g_own.7), channel_id=1, source_target_pairs={{0,1},{1,0},{2,3},{3,2},{4,5},{5,4},{6,7},{7,6}} | collective-permute-start | bytes 12582920 | tf_op jit(solution)/shard_map/ppermute | solution.py:626
  4.4 37.6 %collective-permute-start.3 = (f32[1024,128]{1,0:T(8,128)S(1)}, f32[1024,128]{1,0:T(8,128)S(1)}, u32[]{:S(2)}, u32[]{:S(2)}) collective-permute-start(f32[1024,128]{1,0:T(8,128)S(1)} %pad_maximum_fusion.tab_ref.tab_own.refs_5_), channel_id=1, source_target_pairs={{0,1},{1,0},{2,3},{3,2},{4,5},{5,4},{6,7},{7,6}} | collective-permute-start | bytes 1572872 | tf_op jit(solution)/shard_map/ppermute | solution.py:626
  4.9 32.0 %collective-permute-start = (s32[1024]{0:T(1024)S(1)}, s32[1024]{0:T(1024)S(1)}, u32[]{:S(2)}, u32[]{:S(2)}) collective-permute-start(s32[1024]{0:T(1024)S(1)} %copy-done.4), channel_id=1, source_target_pairs={{0,1},{1,0},{2,3},{3,2},{4,5},{5,4},{6,7},{7,6}} | collective-permute-start | bytes 12296 | tf_op jit(solution)/shard_map/ppermute | solution.py:626
  10.5 61.0 %collective-permute-start.5 = (bf16[1024,256]{1,0:T(8,128)(2,1)}, bf16[1024,256]{1,0:T(8,128)(2,1)S(1)}, u32[]{:S(2)}, u32[]{:S(2)}) collective-permute-start(bf16[1024,256]{1,0:T(8,128)(2,1)} %kv_proj.2.kvc_own), channel_id=1, source_target_pairs={{0,2},{1,3},{4,6},{5,7}} | collective-permute-start | bytes 1572872 | tf_op jit(solution)/shard_map/ppermute | solution.py:647
  36.9 3.7 collective-permute-start.1
  48.2 23.3 %collective-permute-start.6 = (bf16[1024,256]{1,0:T(8,128)(2,1)}, bf16[1024,256]{1,0:T(8,128)(2,1)S(1)}, u32[]{:S(2)}, u32[]{:S(2)}) collective-permute-start(bf16[1024,256]{1,0:T(8,128)(2,1)} %kv_proj.3.kvc_oth), channel_id=1, source_target_pairs={{0,2},{1,3},{4,6},{5,7}} | collective-permute-start | bytes 1572872 | tf_op jit(solution)/shard_map/ppermute | solution.py:654
  188.6 75.4 %collective-permute-start.11 = (bf16[2,128,2048]{2,1,0:T(8,128)(2,1)S(1)}, bf16[2,128,2048]{2,1,0:T(8,128)(2,1)}, u32[]{:S(2)}, u32[]{:S(2)}) collective-permute-start(bf16[2,128,2048]{2,1,0:T(8,128)(2,1)S(1)} %add_convert_fusion), channel_id=1, source_target_pairs={{2,0},{3,1},{6,4},{7,5}} | collective-permute-start | bytes 3145736 | tf_op jit(solution)/shard_map/ppermute | solution.py:678
  201.0 141.6 %collective-permute-start.22 = (bf16[2,256,2048]{2,1,0:T(8,128)(2,1)}, bf16[2,256,2048]{2,1,0:T(8,128)(2,1)}, u32[]{:S(2)}, u32[]{:S(2)}) collective-permute-start(bf16[2,256,2048]{2,1,0:T(8,128)(2,1)} %wgrad.7.a_ref), channel_id=1, source_target_pairs={{0,2},{1,3},{2,0},{3,1},{4,6},{5,7},{6,4},{7,5}} | collective-permute-start | bytes 6291464 | tf_op jit(solution)/shard_map/ppermute | solution.py:629
  276.1 55.2 %collective-permute-start.25 = (bf16[256,2048]{1,0:T(8,128)(2,1)}, bf16[256,2048]{1,0:T(8,128)(2,1)S(1)}, u32[]{:S(2)}, u32[]{:S(2)}) collective-permute-start(bf16[256,2048]{1,0:T(8,128)(2,1)} %kvgrad.1.a_ref), channel_id=1, source_target_pairs={{0,2},{1,3},{2,0},{3,1},{4,6},{5,7},{6,4},{7,5}} | collective-permute-start | bytes 3145736 | tf_op jit(solution)/shard_map/ppermute | solution.py:629
  276.1 55.2 %collective-permute-start.26 = (bf16[256,2048]{1,0:T(8,128)(2,1)}, bf16[256,2048]{1,0:T(8,128)(2,1)}, u32[]{:S(2)}, u32[]{:S(2)}) collective-permute-start(bf16[256,2048]{1,0:T(8,128)(2,1)} %kvgrad.1.a_ref), channel_id=1, source_target_pairs={{0,1},{1,0},{2,3},{3,2},{4,5},{5,4},{6,7},{7,6}} | collective-permute-start | bytes 3145736 | tf_op jit(solution)/shard_map/ppermute | solution.py:626
  276.1 68.1 %collective-permute-start.23 = (bf16[2,256,2048]{2,1,0:T(8,128)(2,1)}, bf16[2,256,2048]{2,1,0:T(8,128)(2,1)}, u32[]{:S(2)}, u32[]{:S(2)}) collective-permute-start(bf16[2,256,2048]{2,1,0:T(8,128)(2,1)} %wgrad.7.a_ref), channel_id=1, source_target_pairs={{0,1},{1,0},{2,3},{3,2},{4,5},{5,4},{6,7},{7,6}} | collective-permute-start | bytes 6291464 | tf_op jit(solution)/shard_map/ppermute | solution.py:626
  287.6 88.7 %collective-permute-start.19 = (bf16[2,256,2048]{2,1,0:T(8,128)(2,1)}, bf16[2,256,2048]{2,1,0:T(8,128)(2,1)}, u32[]{:S(2)}, u32[]{:S(2)}) collective-permute-start(bf16[2,256,2048]{2,1,0:T(8,128)(2,1)} %wgrad.6.a_ref), channel_id=1, source_target_pairs={{0,2},{1,3},{2,0},{3,1},{4,6},{5,7},{6,4},{7,5}} | collective-permute-start | bytes 6291464 | tf_op jit(solution)/shard_map/ppermute | solution.py:629
  331.3 134.2 %copy-start.2 = (bf16[256,2048]{1,0:T(8,128)(2,1)}, bf16[256,2048]{1,0:T(8,128)(2,1)S(1)}, u32[]{:S(2)}) copy-start(bf16[256,2048]{1,0:T(8,128)(2,1)S(1)} %collective-permute-done.25.b_ref) | copy-start | bytes 3145732
  331.3 45.1 %collective-permute-start.20 = (bf16[2,256,2048]{2,1,0:T(8,128)(2,1)}, bf16[2,256,2048]{2,1,0:T(8,128)(2,1)}, u32[]{:S(2)}, u32[]{:S(2)}) collective-permute-start(bf16[2,256,2048]{2,1,0:T(8,128)(2,1)} %wgrad.6.a_ref), channel_id=1, source_target_pairs={{0,1},{1,0},{2,3},{3,2},{4,5},{5,4},{6,7},{7,6}} | collective-permute-start | bytes 6291464 | tf_op jit(solution)/shard_map/ppermute | solution.py:626
  331.3 90.0 %collective-permute-start.16 = (bf16[2,256,2048]{2,1,0:T(8,128)(2,1)}, bf16[2,256,2048]{2,1,0:T(8,128)(2,1)}, u32[]{:S(2)}, u32[]{:S(2)}) collective-permute-start(bf16[2,256,2048]{2,1,0:T(8,128)(2,1)} %wgrad.5.a_ref), channel_id=1, source_target_pairs={{0,2},{1,3},{2,0},{3,1},{4,6},{5,7},{6,4},{7,5}} | collective-permute-start | bytes 6291464 | tf_op jit(solution)/shard_map/ppermute | solution.py:629
  342.6 121.8 %collective-permute-start.13 = (bf16[2,256,2048]{2,1,0:T(8,128)(2,1)}, bf16[2,256,2048]{2,1,0:T(8,128)(2,1)}, u32[]{:S(2)}, u32[]{:S(2)}) collective-permute-start(bf16[2,256,2048]{2,1,0:T(8,128)(2,1)} %wgrad.4.a_ref), channel_id=1, source_target_pairs={{0,2},{1,3},{2,0},{3,1},{4,6},{5,7},{6,4},{7,5}} | collective-permute-start | bytes 6291464 | tf_op jit(solution)/shard_map/ppermute | solution.py:629
  344.3 121.2 %collective-permute-start.10 = (bf16[2,2048,256]{2,1,0:T(8,128)(2,1)}, bf16[2,2048,256]{2,1,0:T(8,128)(2,1)}, u32[]{:S(2)}, u32[]{:S(2)}) collective-permute-start(bf16[2,2048,256]{2,1,0:T(8,128)(2,1)} %get-tuple-element.33.refs_3_), channel_id=1, source_target_pairs={{0,1},{1,0},{2,3},{3,2},{4,5},{5,4},{6,7},{7,6}} | collective-permute-start | bytes 6291464 | tf_op jit(solution)/shard_map/ppermute | solution.py:626
  376.3 88.1 %collective-permute-start.12 = (bf16[2048,256]{1,0:T(8,128)(2,1)}, bf16[2048,256]{1,0:T(8,128)(2,1)S(1)}, u32[]{:S(2)}, u32[]{:S(2)}) collective-permute-start(bf16[2048,256]{1,0:T(8,128)(2,1)} %get-tuple-element.38.refs_8_), channel_id=1, source_target_pairs={{0,1},{1,0},{2,3},{3,2},{4,5},{5,4},{6,7},{7,6}} | collective-permute-start | bytes 3145736 | tf_op jit(solution)/shard_map/ppermute | solution.py:626
  376.4 89.6 %collective-permute-start.9 = (bf16[2,2048,256]{2,1,0:T(8,128)(2,1)}, bf16[2,2048,256]{2,1,0:T(8,128)(2,1)S(1)}, u32[]{:S(2)}, u32[]{:S(2)}) collective-permute-start(bf16[2,2048,256]{2,1,0:T(8,128)(2,1)} %get-tuple-element.32.refs_2_), channel_id=1, source_target_pairs={{0,1},{1,0},{2,3},{3,2},{4,5},{5,4},{6,7},{7,6}} | collective-permute-start | bytes 6291464 | tf_op jit(solution)/shard_map/ppermute | solution.py:626
  421.3 44.7 %collective-permute-start.8 = (bf16[2,2048,256]{2,1,0:T(8,128)(2,1)}, bf16[2,2048,256]{2,1,0:T(8,128)(2,1)S(1)}, u32[]{:S(2)}, u32[]{:S(2)}) collective-permute-start(bf16[2,2048,256]{2,1,0:T(8,128)(2,1)} %get-tuple-element.31.refs_1_), channel_id=1, source_target_pairs={{0,1},{1,0},{2,3},{3,2},{4,5},{5,4},{6,7},{7,6}} | collective-permute-start | bytes 6291464 | tf_op jit(solution)/shard_map/ppermute | solution.py:626
  464.4 4.4 collective-permute-start.7
  464.4 10.0 %collective-permute-start.24 = (bf16[2,256,2048]{2,1,0:T(8,128)(2,1)}, bf16[2,256,2048]{2,1,0:T(8,128)(2,1)}, u32[]{:S(2)}, u32[]{:S(2)}) collective-permute-start(bf16[2,256,2048]{2,1,0:T(8,128)(2,1)} %collective-permute-done.22.b_ref), channel_id=1, source_target_pairs={{0,1},{1,0},{2,3},{3,2},{4,5},{5,4},{6,7},{7,6}} | collective-permute-start | bytes 6291464 | tf_op jit(solution)/shard_map/ppermute | solution.py:626
  465.5 7.8 %collective-permute-start.27 = (bf16[256,2048]{1,0:T(8,128)(2,1)S(1)}, bf16[256,2048]{1,0:T(8,128)(2,1)S(1)}, u32[]{:S(2)}, u32[]{:S(2)}) collective-permute-start(bf16[256,2048]{1,0:T(8,128)(2,1)S(1)} %collective-permute-done.25.b_ref), channel_id=1, source_target_pairs={{0,1},{1,0},{2,3},{3,2},{4,5},{5,4},{6,7},{7,6}} | collective-permute-start | bytes 3145736 | tf_op jit(solution)/shard_map/ppermute | solution.py:626
  466.0 8.5 %copy-start.5 = (bf16[2,2048,256]{2,1,0:T(8,128)(2,1)}, bf16[2,2048,256]{2,1,0:T(8,128)(2,1)S(1)}, u32[]{:S(2)}) copy-start(bf16[2,2048,256]{2,1,0:T(8,128)(2,1)S(1)} %collective-permute-done.9.refs_6_) | copy-start | bytes 6291460
  466.0 54.6 %collective-permute-start.21 = (bf16[2,256,2048]{2,1,0:T(8,128)(2,1)}, bf16[2,256,2048]{2,1,0:T(8,128)(2,1)}, u32[]{:S(2)}, u32[]{:S(2)}) collective-permute-start(bf16[2,256,2048]{2,1,0:T(8,128)(2,1)} %collective-permute-done.19.b_ref), channel_id=1, source_target_pairs={{0,1},{1,0},{2,3},{3,2},{4,5},{5,4},{6,7},{7,6}} | collective-permute-start | bytes 6291464 | tf_op jit(solution)/shard_map/ppermute | solution.py:626
  466.0 8.4 %copy-start.6 = (bf16[2,2048,256]{2,1,0:T(8,128)(2,1)}, bf16[2,2048,256]{2,1,0:T(8,128)(2,1)S(1)}, u32[]{:S(2)}) copy-start(bf16[2,2048,256]{2,1,0:T(8,128)(2,1)S(1)} %collective-permute-done.8.refs_5_) | copy-start | bytes 6291460
  466.0 64.4 %collective-permute-start.17 = (bf16[2,256,2048]{2,1,0:T(8,128)(2,1)}, bf16[2,256,2048]{2,1,0:T(8,128)(2,1)}, u32[]{:S(2)}, u32[]{:S(2)}) collective-permute-start(bf16[2,256,2048]{2,1,0:T(8,128)(2,1)} %wgrad.5.a_ref), channel_id=1, source_target_pairs={{0,1},{1,0},{2,3},{3,2},{4,5},{5,4},{6,7},{7,6}} | collective-permute-start | bytes 6291464 | tf_op jit(solution)/shard_map/ppermute | solution.py:626
  468.8 5.6 %copy-start.7 = (bf16[2,2048,256]{2,1,0:T(8,128)(2,1)}, bf16[2,2048,256]{2,1,0:T(8,128)(2,1)S(1)}, u32[]{:S(2)}) copy-start(bf16[2,2048,256]{2,1,0:T(8,128)(2,1)S(1)} %collective-permute-done.7.refs_4_) | copy-start | bytes 6291460
  468.8 61.6 %collective-permute-start.18 = (bf16[2,256,2048]{2,1,0:T(8,128)(2,1)}, bf16[2,256,2048]{2,1,0:T(8,128)(2,1)}, u32[]{:S(2)}, u32[]{:S(2)}) collective-permute-start(bf16[2,256,2048]{2,1,0:T(8,128)(2,1)} %collective-permute-done.16.b_ref), channel_id=1, source_target_pairs={{0,1},{1,0},{2,3},{3,2},{4,5},{5,4},{6,7},{7,6}} | collective-permute-start | bytes 6291464 | tf_op jit(solution)/shard_map/ppermute | solution.py:626
  474.3 66.0 %collective-permute-start.14 = (bf16[2,256,2048]{2,1,0:T(8,128)(2,1)}, bf16[2,256,2048]{2,1,0:T(8,128)(2,1)}, u32[]{:S(2)}, u32[]{:S(2)}) collective-permute-start(bf16[2,256,2048]{2,1,0:T(8,128)(2,1)} %wgrad.4.a_ref), channel_id=1, source_target_pairs={{0,1},{1,0},{2,3},{3,2},{4,5},{5,4},{6,7},{7,6}} | collective-permute-start | bytes 6291464 | tf_op jit(solution)/shard_map/ppermute | solution.py:626
  474.4 65.9 %collective-permute-start.15 = (bf16[2,256,2048]{2,1,0:T(8,128)(2,1)}, bf16[2,256,2048]{2,1,0:T(8,128)(2,1)}, u32[]{:S(2)}, u32[]{:S(2)}) collective-permute-start(bf16[2,256,2048]{2,1,0:T(8,128)(2,1)} %collective-permute-done.13.b_ref), channel_id=1, source_target_pairs={{0,1},{1,0},{2,3},{3,2},{4,5},{5,4},{6,7},{7,6}} | collective-permute-start | bytes 6291464 | tf_op jit(solution)/shard_map/ppermute | solution.py:626
  (7 other events, 9.6 us)

commit v3 on v2

--- a/solution.py
+++ b/solution.py
@@ -64,139 +64,176 @@
 
 
 def params(**kw):
-    return pltpu.CompilerParams(vmem_limit_bytes=62 * 1024 * 1024, **kw)
+    return pltpu.CompilerParams(vmem_limit_bytes=67_000_000, **kw)
+
+
+def by_rows(rows, body, size=16):
+    def step(r, carry):
+        body(span(r, size))
+        return carry
+
+    lax.fori_loop(0, rows // size, step, 0)
 
 
 def span(index, size):
     return pl.ds(pl.multiple_of(index * size, size), size)
 
 
-def kv_kernel(s_ref, x_ref, wk_ref, wv_ref, tab_ref, out_ref, w_s):
+def qkv_kernel(s_ref, x_ref, wq_ref, wk_ref, wv_ref, tab_ref, *rest):
+    kv_ref, q_ref, w_s = rest[-3:]
+
     @pl.when(pl.program_id(0) == 0)
     def _():
         w_s[:, :HEAD] = wk_ref[...]
         w_s[:, HEAD:] = wv_ref[...]
 
-    kv = dot_nn(x_ref[...], w_s[...])
+    x = x_ref[...]
     cos_t, sin_t = spread_table(tab_ref[...])
+    kv = dot_nn(x, w_s[...])
     k = kv[:, :HEAD]
-    out_ref[:, :HEAD] = (k * cos_t + swap_halves(k) * sin_t).astype(BF)
-    out_ref[:, HEAD:] = kv[:, HEAD:].astype(BF)
-
-
-def kv_proj(core, x, w_k, w_v, tab):
+    kv_ref[:, :HEAD] = (k * cos_t + swap_halves(k) * sin_t).astype(BF)
+    kv_ref[:, HEAD:] = kv[:, HEAD:].astype(BF)
+    step = 4 * HEAD
+    for n in range(wq_ref.shape[1] // step):
+        q = dot_nn(x, wq_ref[:, n * step:(n + 1) * step])
+        for h in range(step // HEAD):
+            part = q[:, h * HEAD:(h + 1) * HEAD]
+            at = n * step + h * HEAD
+            q_ref[:, at:at + HEAD] = (part * cos_t + swap_halves(part) * sin_t).astype(BF)
+
+
+def qkv_proj(sel, x, w_q, w_k, w_v, tab, prev):
     tokens, width = x.shape
-    step = tokens // 4
-    return pl.pallas_call(
-        kv_kernel,
+    cols = w_q.shape[1] // 2
+    rows = tokens // 2
+    extra = [] if prev is None else [prev]
+    return pl.pallas_call(
+        qkv_kernel,
         grid_spec=pltpu.PrefetchScalarGridSpec(
             num_scalar_prefetch=1,
-            grid=(tokens // step,),
+            grid=(2,),
             in_specs=[
-                pl.BlockSpec((step, width), lambda m, s: (m, 0)),
+                pl.BlockSpec((rows, width), lambda m, s: (m, 0)),
+                pl.BlockSpec((width, cols), lambda m, s: (0, s[0])),
                 pl.BlockSpec((width, HEAD), lambda m, s: (0, s[0])),
                 pl.BlockSpec((width, HEAD), lambda m, s: (0, s[0])),
-                pl.BlockSpec((step, HEAD), lambda m, s: (m, 0)),
-            ],
-            out_specs=pl.BlockSpec((step, 2 * HEAD), lambda m, s: (m, 0)),
+                pl.BlockSpec((rows, HEAD), lambda m, s: (m, 0)),
+            ] + [pl.BlockSpec(memory_space=pl.ANY)] * len(extra),
+            out_specs=[
+                pl.BlockSpec((rows, 2 * HEAD), lambda m, s: (m, 0)),
+                pl.BlockSpec((rows, cols), lambda m, s: (s[1] * 2 + m, 0)),
+            ],
             scratch_shapes=[pltpu.VMEM((width, 2 * HEAD), BF)],
         ),
-        out_shape=jax.ShapeDtypeStruct((tokens, 2 * HEAD), BF),
-        compiler_params=params(),
-        cost_estimate=cost(2 * tokens * width * 2 * HEAD, tokens * width * 2),
-        name="kv_proj",
-    )(core, x, w_k, w_v, tab)
-
-
-def q_kernel(s_ref, x_ref, wq_ref, tab_ref, *rest):
-    out_ref = rest[-1]
-    q = dot_nn(x_ref[...], wq_ref[...])
-    cos_t, sin_t = spread_table(tab_ref[...])
-    for h in range(wq_ref.shape[1] // HEAD):
-        part = q[:, h * HEAD:(h + 1) * HEAD]
-        out_ref[:, h * HEAD:(h + 1) * HEAD] = (part * cos_t + swap_halves(part) * sin_t).astype(BF)
-
-
-def q_proj(sel, x, w_q, tab, prev):
-    tokens, width = x.shape
-    cols = w_q.shape[1] // 2
-    step = 512
+        out_shape=[
+            jax.ShapeDtypeStruct((tokens, 2 * HEAD), BF),
+            jax.ShapeDtypeStruct((2 * tokens, cols), BF),
+        ],
+        input_output_aliases={} if prev is None else {6: 1},
+        compiler_params=params(),
+        cost_estimate=cost(2 * tokens * width * (cols + 2 * HEAD), tokens * width * 2 + cols * width * 2),
+        name="qkv_proj",
+    )(sel, x, w_q, w_k, w_v, tab, *extra)
+
+
+def dctx_kernel(s_ref, own_ref, oth_ref, wo_ref, out_ref):
+    def put(ref):
+        step = 4 * HEAD
+        for n in range(wo_ref.shape[0] // step):
+            out_ref[:, n * step:(n + 1) * step] = dot_nt(ref[...], wo_ref[n * step:(n + 1) * step, :]).astype(BF)
+
+    @pl.when(pl.program_id(0) < 2)
+    def _():
+        put(own_ref)
+
+    @pl.when(pl.program_id(0) >= 2)
+    def _():
+        put(oth_ref)
+
+
+def dctx_proj(core, own, oth, w_o):
+    tokens, width = own.shape
+    cols = w_o.shape[0] // 2
     rows = tokens // 2
-    n = cols // step
-    extra = [] if prev is None else [prev]
-    return pl.pallas_call(
-        q_kernel,
+
+    def place(m, s):
+        far = m // 2
+        return (s[0] + far - 2 * s[0] * far) * 2 + m % 2
+
+    return pl.pallas_call(
+        dctx_kernel,
         grid_spec=pltpu.PrefetchScalarGridSpec(
             num_scalar_prefetch=1,
-            grid=(n, 2),
+            grid=(4,),
             in_specs=[
-                pl.BlockSpec((rows, width), lambda j, m, s: (m, 0)),
-                pl.BlockSpec((width, step), lambda j, m, s: (0, s[0] * n + j)),
-                pl.BlockSpec((rows, HEAD), lambda j, m, s: (m, 0)),
-            ] + [pl.BlockSpec(memory_space=pl.ANY)] * len(extra),
-            out_specs=pl.BlockSpec((rows, step), lambda j, m, s: (s[1] * 2 + m, j)),
+                pl.BlockSpec((rows, width), lambda m, s: (jnp.minimum(m, 1), 0)),
+                pl.BlockSpec((rows, width), lambda m, s: (jnp.maximum(m - 2, 0), 0)),
+                pl.BlockSpec((cols, width), lambda m, s: (s[0], 0)),
+            ],
+            out_specs=pl.BlockSpec((rows, cols), lambda m, s: (place(m, s), 0)),
         ),
         out_shape=jax.ShapeDtypeStruct((2 * tokens, cols), BF),
-        input_output_aliases={} if prev is None else {4: 0},
-        compiler_params=params(),
-        cost_estimate=cost(2 * tokens * width * cols, tokens * width * 2 + cols * width * 2),
-        name="q_proj",
-    )(sel, x, w_q, tab, *extra)
-
-
-def dctx_kernel(s_ref, g_ref, wo_ref, *rest):
-    out_ref = rest[-1]
-    out_ref[...] = dot_nt(g_ref[...], wo_ref[...]).astype(BF)
-
-
-def dctx_proj(sel, g, w_o, prev):
-    tokens, width = g.shape
-    cols = w_o.shape[0] // 2
-    step = 512
-    rows = tokens // 2
-    n = cols // step
-    extra = [] if prev is None else [prev]
-    return pl.pallas_call(
-        dctx_kernel,
-        grid_spec=pltpu.PrefetchScalarGridSpec(
-            num_scalar_prefetch=1,
-            grid=(n, 2),
-            in_specs=[
-                pl.BlockSpec((rows, width), lambda j, m, s: (m, 0)),
-                pl.BlockSpec((step, width), lambda j, m, s: (s[0] * n + j, 0)),
-            ] + [pl.BlockSpec(memory_space=pl.ANY)] * len(extra),
-            out_specs=pl.BlockSpec((rows, step), lambda j, m, s: (s[1] * 2 + m, j)),
-        ),
-        out_shape=jax.ShapeDtypeStruct((2 * tokens, cols), BF),
-        input_output_aliases={} if prev is None else {3: 0},
-        compiler_params=params(),
-        cost_estimate=cost(2 * tokens * width * cols, tokens * width * 2 + cols * width * 2),
+        compiler_params=params(),
+        cost_estimate=cost(4 * tokens * width * cols, tokens * width * 4 + cols * width * 2),
         name="dctx_proj",
-    )(sel, g, w_o, *extra)
+    )(core, own, oth, w_o)
 
 
 def attn_kernel(
     core_ref, lo_ref, nb_ref, q_ref, do_ref, kdoc_ref, tab_own, tab_oth, kvp_own, kvp_oth, kvc_own, kvc_oth,
-    act_ref, actt_ref, dkv_ref,
+    x_own, x_oth, g_own, g_oth, act_ref, part_ref, dkv_ref,
     k_s, v_s, s_s, dp_s, m_s, l_s, d_s, qd_s, ctx_s, dq_s, q_s, do_s, qt_s, dot_s, tab_s, dk_s, dv_s,
+    x_s, g_s, at_s, w_s, init_sem, row_sem, out_sem,
 ):
     i = pl.program_id(0)
     tokens = kvc_own.shape[0]
     chip_len = 2 * tokens
     core = core_ref[0]
+    per_half = tokens // BQ
+    rows_here = span(i % per_half, BQ)
+
+    def row_copies(x, g):
+        return (
+            pltpu.make_async_copy(x.at[rows_here, :], x_s, row_sem.at[0]),
+            pltpu.make_async_copy(g.at[rows_here, :], g_s, row_sem.at[1]),
+        )
+
+    @pl.when(i // per_half == core)
+    def _():
+        for copy in row_copies(x_own, g_own):
+            copy.start()
+
+    @pl.when(i // per_half != core)
+    def _():
+        for copy in row_copies(x_oth, g_oth):
+            copy.start()
 
     @pl.when(i == 0)
     def _():
+        copies = []
         for base, place, ref in ((0, core, kvp_own), (0, 1 - core, kvp_oth), (2, core, kvc_own), (2, 1 - core, kvc_oth)):
             where = span(base + place, tokens)
-            k_s[where, :] = ref[:, :HEAD]
-            v_s[where, :] = ref[:, HEAD:]
+            copies.append((ref.at[:, pl.ds(0, HEAD)], k_s.at[where, :]))
+            copies.append((ref.at[:, pl.ds(HEAD, HEAD)], v_s.at[where, :]))
+        copies.append((tab_own, tab_s.at[span(core, tokens), :]))
+        copies.append((tab_oth, tab_s.at[span(1 - core, tokens), :]))
+        copies = [pltpu.make_async_copy(src, dst, init_sem.at[n]) for n, (src, dst) in enumerate(copies)]
+        for copy in copies:
+            copy.start()
         k_s[2 * chip_len:, :] = jnp.zeros((BK, HEAD), BF)
         v_s[2 * chip_len:, :] = jnp.zeros((BK, HEAD), BF)
-        tab_s[span(core, tokens), :] = tab_own[...]
-        tab_s[span(1 - core, tokens), :] = tab_oth[...]
-        dk_s[...] = jnp.zeros_like(dk_s)
-        dv_s[...] = jnp.zeros_like(dv_s)
+
+        def clear(r):
+            w_s[r, :] = jnp.zeros((16, w_s.shape[1]), F32)
+
+        def clear_kv(r):
+            dk_s[r, :] = jnp.zeros((16, dk_s.shape[1]), F32)
+            dv_s[r, :] = jnp.zeros((16, dv_s.shape[1]), F32)
+
+        by_rows(w_s.shape[0], clear)
+        by_rows(HEAD, clear_kv)
+        for copy in copies:
+            copy.wait()
 
     for h in range(PAIR):
         rows = slice(h * BQ, (h + 1) * BQ)
@@ -277,23 +314,55 @@
         cols = slice(h * HEAD, (h + 1) * HEAD)
         ctx = ctx_s[rows, :].astype(BF)
         act_ref[0, :, cols] = ctx
-        actt_ref[0, cols, :] = ctx.T
+        at_s[WIDE + h * HEAD:WIDE + (h + 1) * HEAD, :] = ctx.T
         dq = dq_s[rows, :].astype(BF).astype(F32)
         dq = (dq * cos_t - swap_halves(dq) * sin_t).astype(BF)
         act_ref[1, :, cols] = dq
-        actt_ref[1, cols, :] = dq.T
+        at_s[h * HEAD:(h + 1) * HEAD, :] = dq.T
+    step = 4 * HEAD
+    for copy in row_copies(x_own, g_own):
+        copy.wait()
+
+    def products(c, carry):
+        cols = span(c, step)
+        w_s[:WIDE, cols] += dot_nn(at_s[:WIDE, :], x_s[:, cols])
+        w_s[WIDE:, cols] += dot_nn(at_s[WIDE:, :], g_s[:, cols])
+        return carry
+
+    lax.fori_loop(0, x_s.shape[1] // step, products, 0)
 
     @pl.when(i == pl.num_programs(0) - 1)
     def _():
-        dkv_ref[0] = dk_s[:, :2 * chip_len].astype(BF)
-        dkv_ref[1] = dv_s[:, :2 * chip_len].astype(BF)
-
-
-def attention(chunk, core, lo, n_blocks, q, dctx, kdoc, tab_own, tab_oth, kv_prev, kv_chip):
+        def narrow(r):
+            x_s[r, :] = w_s[r, :].astype(BF)
+
+        by_rows(w_s.shape[0], narrow)
+
+        def narrow_kv(r, carry):
+            rows = span(r, 16)
+            for n, acc in enumerate((dk_s, dv_s)):
+                for side in range(2):
+                    at = pl.ds(pl.multiple_of((2 * n + side) * HEAD + r * 16, 16), 16)
+                    g_s[at, :] = acc[rows, side * chip_len:(side + 1) * chip_len].astype(BF)
+            return carry
+
+        lax.fori_loop(0, HEAD // 16, narrow_kv, 0)
+        copies = (
+            pltpu.make_async_copy(x_s, part_ref, out_sem.at[0]),
+            pltpu.make_async_copy(g_s, dkv_ref, out_sem.at[1]),
+        )
+        for copy in copies:
+            copy.start()
+        for copy in copies:
+            copy.wait()
+
+
+def attention(chunk, core, lo, n_blocks, q, dctx, kdoc, tabs, kv_prev, kv_chip, xs, gs):
     chip_len = q.shape[0]
-    tokens = chip_len // 2
+    width = xs[0].shape[1]
+    assert 2 * WIDE == BQ == 4 * HEAD and width == chip_len
     padded = 2 * chip_len + BK
-    max_blocks = 2 * chip_len // BK + 1
+    max_blocks = 2 * chip_len // BK
     rows = PAIR * BQ
     full = lambda shape: pl.BlockSpec(shape, lambda i, *s: (0,) * len(shape))
     pairs = chip_len * chip_len * PAIR
@@ -306,11 +375,11 @@
                 pl.BlockSpec((BQ, WIDE), lambda i, *s: (i, chunk)),
                 pl.BlockSpec((BQ, WIDE), lambda i, *s: (i, chunk)),
                 full((1, padded)),
-            ] + [full((tokens, HEAD))] * 2 + [full((tokens, 2 * HEAD))] * 4,
+            ] + [pl.BlockSpec(memory_space=pl.ANY)] * 10,
             out_specs=[
                 pl.BlockSpec((2, BQ, WIDE), lambda i, *s: (0, i, 0)),
-                pl.BlockSpec((2, WIDE, BQ), lambda i, *s: (0, 0, i)),
-                full((2, HEAD, 2 * chip_len)),
+                pl.BlockSpec(memory_space=pl.ANY),
+                pl.BlockSpec(memory_space=pl.ANY),
             ],
             scratch_shapes=[
                 pltpu.VMEM((padded, HEAD), BF),
@@ -330,17 +399,24 @@
                 pltpu.VMEM((chip_len, HEAD), F32),
                 pltpu.VMEM((HEAD, padded), F32),
                 pltpu.VMEM((HEAD, padded), F32),
+                pltpu.VMEM((BQ, width), BF),
+                pltpu.VMEM((BQ, width), BF),
+                pltpu.VMEM((2 * WIDE, BQ), BF),
+                pltpu.VMEM((2 * WIDE, width), F32),
+                pltpu.SemaphoreType.DMA((10,)),
+                pltpu.SemaphoreType.DMA((2,)),
+                pltpu.SemaphoreType.DMA((2,)),
             ],
         ),
         out_shape=[
             jax.ShapeDtypeStruct((2, chip_len, WIDE), BF),
-            jax.ShapeDtypeStruct((2, WIDE, chip_len), BF),
-            jax.ShapeDtypeStruct((2, HEAD, 2 * chip_len), BF),
+            jax.ShapeDtypeStruct((2 * WIDE, width), BF),
+            jax.ShapeDtypeStruct((4 * HEAD, chip_len), BF),
         ],
         compiler_params=params(),
         cost_estimate=cost(pairs * HEAD * 2 * 8, 12 * 1024 * 1024, pairs),
         name="attention",
-    )(core, lo, n_blocks, q, dctx, kdoc, tab_own, tab_oth, *kv_prev, *kv_chip)
+    )(core, lo, n_blocks, q, dctx, kdoc, *tabs, *kv_prev, *kv_chip, *xs, *gs)
 
 
 def kv_finish_kernel(n, s_ref, *refs):
@@ -355,7 +431,7 @@
 
     total = far_ref[...].astype(F32)
     for ref in refs[:n]:
-        total = total + ref[...].astype(F32)
+        total = total + ref[:, 0].astype(F32)
     cos_t, sin_t = spread_table(tab_s[span(pl.program_id(0), step), :])
     dk = total[0].astype(BF).astype(F32).T
     dk = (dk * cos_t - swap_halves(dk) * sin_t).astype(BF)
@@ -370,13 +446,12 @@
     tokens = tab_own.shape[0]
     chip_len = 2 * tokens
     step = 512
-    skip = chip_len // step
     return pl.pallas_call(
         functools.partial(kv_finish_kernel, len(parts)),
         grid_spec=pltpu.PrefetchScalarGridSpec(
             num_scalar_prefetch=1,
             grid=(chip_len // step,),
-            in_specs=[pl.BlockSpec((2, HEAD, step), lambda t, s: (0, 0, skip + t))] * len(parts)
+            in_specs=[pl.BlockSpec((2, 1, HEAD, step), lambda t, s: (0, 1, 0, t))] * len(parts)
             + [
                 pl.BlockSpec((2, HEAD, step), lambda t, s: (0, 0, t)),
                 pl.BlockSpec((tokens, HEAD), lambda t, s: (0, 0)),
@@ -396,32 +471,6 @@
         cost_estimate=cost(chip_len * HEAD * 64, chip_len * HEAD * 16),
         name="kv_finish",
     )(core, *parts, far, tab_own, tab_oth)
-
-
-def wgrad_kernel(s_ref, actt_ref, x_own, x_oth, g_own, g_oth, out_ref):
-    tokens = x_own.shape[0]
-    own, oth = span(s_ref[0], tokens), span(1 - s_ref[0], tokens)
-    out_ref[0] = (dot_nn(actt_ref[1, :, own], x_own[...]) + dot_nn(actt_ref[1, :, oth], x_oth[...])).astype(BF)
-    out_ref[1] = (dot_nn(actt_ref[0, :, own], g_own[...]) + dot_nn(actt_ref[0, :, oth], g_oth[...])).astype(BF)
-
-
-def wgrad(core, actt, x_own, x_oth, g_own, g_oth):
-    tokens, width = x_own.shape
-    step = 512
-    piece = pl.BlockSpec((tokens, step), lambda n, s: (0, n))
-    return pl.pallas_call(
-        wgrad_kernel,
-        grid_spec=pltpu.PrefetchScalarGridSpec(
-            num_scalar_prefetch=1,
-            grid=(width // step,),
-            in_specs=[pl.BlockSpec((2, WIDE, 2 * tokens), lambda n, s: (0, 0, 0)), piece, piece, piece, piece],
-            out_specs=pl.BlockSpec((2, WIDE, step), lambda n, s: (0, 0, n)),
-        ),
-        out_shape=jax.ShapeDtypeStruct((2, WIDE, width), BF),
-        compiler_params=params(),
-        cost_estimate=cost(8 * tokens * width * WIDE, 8 * tokens * width),
-        name="wgrad",
-    )(core, actt, x_own, x_oth, g_own, g_oth)
 
 
 def kvgrad_kernel(s_ref, dkvt_ref, x_own, x_oth, out_ref):
@@ -643,18 +692,15 @@
         g_oth = near(grad_out)
         tab_own = rope_table(positions)
         tab_oth = near(tab_own)
-        kv_own = kv_proj(core, hidden, w_k, w_v, tab_own)
+        kv_own, q = qkv_proj(sel_own, hidden, w_q, w_k, w_v, tab_own, None)
         kvp_own = lax.ppermute(kv_own, "sp", down_perm)
-        q = q_proj(sel_own, hidden, w_q, tab_own, None)
         doc_chip = jnp.where(
             core_id == 0, jnp.concatenate([doc_ids, doc_oth]), jnp.concatenate([doc_oth, doc_ids])
         )
         doc_far = far(doc_chip)
-        kv_oth = kv_proj(core, x_oth, w_k, w_v, tab_oth)
+        kv_oth, q = qkv_proj(sel_oth, x_oth, w_q, w_k, w_v, tab_oth, q)
         kvp_oth = lax.ppermute(kv_oth, "sp", down_perm)
-        dctx = dctx_proj(sel_own, grad_out, w_o, None)
-        q = q_proj(sel_oth, x_oth, w_q, tab_oth, q)
-        dctx = dctx_proj(sel_oth, g_oth, w_o, dctx)
+        dctx = dctx_proj(core, grad_out, g_oth, w_o)
 
         heads_doc = doc_chip[::BQ]
         lo = jnp.sum(doc_chip[None, :] < heads_doc[:, None], axis=1, dtype=jnp.int32)
@@ -666,18 +712,18 @@
         kdoc = jnp.concatenate([doc_far, doc_chip, jnp.zeros((BK,), jnp.int32)])[None, :]
 
         acts, acts_oth, dkvs, sums = [], [], [], None
-        q_in = q
         for j in range(n_chunks):
-            act, actt, dkv = attention(
-                j, core, lo, n_blocks, q_in, dctx, kdoc, tab_own, tab_oth, (kvp_own, kvp_oth), (kv_own, kv_oth)
+            act, part, dkv = attention(
+                j, core, lo, n_blocks, q, dctx, kdoc, (tab_own, tab_oth), (kvp_own, kvp_oth), (kv_own, kv_oth),
+                (hidden, x_oth), (grad_out, g_oth),
             )
+            part = part.reshape(2, WIDE, -1)
             acts.append(act)
-            dkvs.append(dkv)
+            dkvs.append(dkv.reshape(2, 2, HEAD, chip_len))
             if j == n_chunks - 1:
-                dkv_up = sum(d[:, :, :chip_len].astype(F32) for d in dkvs).astype(BF)
+                dkv_up = sum(d[:, 0].astype(F32) for d in dkvs).astype(BF)
                 dkv_far = lax.ppermute(dkv_up, "sp", up_perm)
             acts_oth.append(near(act))
-            part = wgrad(core, actt, hidden, x_oth, grad_out, g_oth)
             part_far = far(part)
             part_near = near(part)
             part_far_near = near(part_far)

time: 556 us -> 584 us (1.050)
  waiting for transfers between devices: 172 us -> 224 us
  Pallas kernels: 297 us -> 277 us
    pallas_call x8 -> x2, Pallas kernels: 76.4 us -> 22.3 us  [qkv_proj(): pl.pallas_call(qkv_kernel, grid_spec=pltpu.PrefetchScalarGridSpec(num_sca...]
    ppermute x6, waiting for transfers between devices: 153 us -> 194 us  [far(): return lax.ppermute(v, 'sp', far_perm)]
    pallas_call x4, Pallas kernels: 113 us -> 153 us  [attention(): pl.pallas_call(attn_kernel, grid_spec=pltpu.PrefetchScalarGridSpec(num_sc...]
    ppermute x1, waiting for transfers between devices: 12 us -> 23.1 us  [device_step(): dkv_far = lax.ppermute(dkv_up, 'sp', up_perm)]
    pallas_call x2 -> x1, Pallas kernels: 20.4 us -> 14.2 us  [dctx_proj(): pl.pallas_call(dctx_kernel, grid_spec=pltpu.PrefetchScalarGridSpec(num_sc...]
  transfers between devices with their start and end apart: 28 -> 28, of which waited for: 8 -> 8; matrix products, arithmetic and copies ran while one was open for 1% -> 1% of each run, Pallas kernels for 32% -> 20%
where the time goes in v3:
time: 584 us; the launch traced here: 583 us
  Pallas kernels  277 us (47%)
  waiting for transfers between devices  224 us (38%)
  starting transfers between devices  71 us (12%)
  other arithmetic  8.5 us (1%)
    ppermute x6, waiting for transfers between devices, far(): return lax.ppermute(v, 'sp', far_perm)  194 us
    pallas_call x4, Pallas kernels, attention(): pl.pallas_call(attn_kernel, grid_spec=pltpu.PrefetchScalarGridSpec(num_sc...  153 us
    ppermute x6, starting transfers between devices, far(): return lax.ppermute(v, 'sp', far_perm)  54.5 us
    pallas_call x4, Pallas kernels, combine(): pl.pallas_call(combine_kernel, grid_spec=pltpu.PrefetchScalarGridSpec(num...  39.4 us
    ppermute x1, waiting for transfers between devices, device_step(): dkv_far = lax.ppermute(dkv_up, 'sp', up_perm)  23.1 us
    pallas_call x2, Pallas kernels, qkv_proj(): pl.pallas_call(qkv_kernel, grid_spec=pltpu.PrefetchScalarGridSpec(num_sca...  22.3 us
    pallas_call x1, Pallas kernels, grad_hidden(): pl.pallas_call(functools.partial(hidden_kernel, n), grid_spec=pltpu.Prefe...  17 us
    pallas_call x1, Pallas kernels, dctx_proj(): pl.pallas_call(dctx_kernel, grid_spec=pltpu.PrefetchScalarGridSpec(num_sc...  14.2 us
  transfers between devices with their start and end apart: 28, of which 8 were waited for; matrix products, arithmetic and copies ran while one was open for 1% of the time, Pallas kernels for 20%

profile of v3, /device:TPU:0, one launch (start us, length us, event | category | flops | bytes accessed | tf_op | source)
XLA Modules:
  0.0 583.0 jit_solution(2519321782540828484)
XLA Ops:
  2.2 1.9 multiply_cosine_fusion
  6.3 11.2 %qkv_proj.2 = (bf16[1024,256]{1,0:T(8,128)(2,1)}, bf16[2048,1024]{1,0:T(8,128)(2,1)}) custom-call(s32[2]{0:T(128)} %pad_add_fusion.2.s_ref, bf16[1024,2048]{1,0:T(8,128)(2,1)} %x_own.9, bf16[2048,2048]{1,0:T(8,128)(2,1)} %refs_10_.1, bf16[2048,256]{1,0:T(8,128)(2,1)} %refs_11_.1, bf16[2048,256]{1,0:T(8,128)(2,1)} %refs_12_.1, ...), custom_call_target="tpu_custom_call" | custom-call | flops 5368709120 | bytes 8388608 | tf_op jit(solution)/shard_map/qkv_proj/pallas_call | solution.py:110
  17.4 5.6 collective-permute-start.5
  23.8 10.3 %collective-permute-done.1 = s32[2048]{0:T(1024)S(1)} collective-permute-done((s32[2048]{0:T(1024)S(1)}, s32[2048]{0:T(1024)S(1)}, u32[]{:S(2)}, u32[]{:S(2)}) %collective-permute-start.1) | collective-permute-done | bytes 8224 | tf_op jit(solution)/shard_map/ppermute | solution.py:678
  35.5 11.2 %qkv_proj.3 = (bf16[1024,256]{1,0:T(8,128)(2,1)}, bf16[2048,1024]{1,0:T(8,128)(2,1)}) custom-call(s32[2]{0:T(128)} %pad_add_fusion.1.s_ref, bf16[1024,2048]{1,0:T(8,128)(2,1)} %collective-permute-done.2.x_ref.x_oth, bf16[2048,2048]{1,0:T(8,128)(2,1)} %refs_10_.1, bf16[2048,256]{1,0:T(8,128)(2,1)} %refs_11_.1, ...), custom_call_target="tpu_custom_call", output_to_operand_aliasing={{1}: (6, {})} | custom-call | flops 5368709120 | bytes 8388608 | tf_op jit(solution)/shard_map/qkv_proj/pallas_call | solution.py:110
  46.6 5.2 collective-permute-start.6
  51.8 14.2 %dctx_proj.1.do_ref = bf16[2048,1024]{1,0:T(8,128)(2,1)} custom-call(s32[1]{0:T(128)} %bitcast.s_ref.core_ref, bf16[1024,2048]{1,0:T(8,128)(2,1)} %g_own.7, bf16[1024,2048]{1,0:T(8,128)(2,1)} %collective-permute-done.4.oth_ref.g_oth, bf16[2048,2048]{1,0:T(8,128)(2,1)} %refs_8_.1), custom_call_target="tpu_custom_call" | custom-call | flops 8589934592 | bytes 12582912 | tf_op jit(solution)/shard_map/dctx_proj/pallas_call | solution.py:163
  66.0 38.2 %attention.7 = (bf16[2,2048,256]{2,1,0:T(8,128)(2,1)}, bf16[512,2048]{1,0:T(8,128)(2,1)}, bf16[512,2048]{1,0:T(8,128)(2,1)}) custom-call(s32[1]{0:T(128)} %bitcast.s_ref.core_ref, s32[4]{0:T(128)} %get-tuple-element.65.lo_ref, s32[4]{0:T(128)} %get-tuple-element.64.nb_ref, bf16[2048,1024]{1,0:T(8,128)(2,1)} %get-tuple-element.35.q_ref, ...), custom_call_target="tpu_custom_call" | custom-call | flops 17179869184 | bytes 12582912 | tf_op jit(solution)/shard_map/attention/pallas_call | solution.py:369
  104.3 38.2 %attention.6 = (bf16[2,2048,256]{2,1,0:T(8,128)(2,1)}, bf16[512,2048]{1,0:T(8,128)(2,1)}, bf16[512,2048]{1,0:T(8,128)(2,1)}) custom-call(s32[1]{0:T(128)} %bitcast.s_ref.core_ref, s32[4]{0:T(128)} %get-tuple-element.65.lo_ref, s32[4]{0:T(128)} %get-tuple-element.64.nb_ref, bf16[2048,1024]{1,0:T(8,128)(2,1)} %get-tuple-element.35.q_ref, ...), custom_call_target="tpu_custom_call" | custom-call | flops 17179869184 | bytes 12582912 | tf_op jit(solution)/shard_map/attention/pallas_call | solution.py:369
  142.5 38.4 %attention.5 = (bf16[2,2048,256]{2,1,0:T(8,128)(2,1)}, bf16[512,2048]{1,0:T(8,128)(2,1)}, bf16[512,2048]{1,0:T(8,128)(2,1)}) custom-call(s32[1]{0:T(128)} %bitcast.s_ref.core_ref, s32[4]{0:T(128)} %get-tuple-element.65.lo_ref, s32[4]{0:T(128)} %get-tuple-element.64.nb_ref, bf16[2048,1024]{1,0:T(8,128)(2,1)} %get-tuple-element.35.q_ref, ...), custom_call_target="tpu_custom_call" | custom-call | flops 17179869184 | bytes 12582912 | tf_op jit(solution)/shard_map/attention/pallas_call | solution.py:369
  180.9 38.2 %attention.4 = (bf16[2,2048,256]{2,1,0:T(8,128)(2,1)}, bf16[512,2048]{1,0:T(8,128)(2,1)}, bf16[512,2048]{1,0:T(8,128)(2,1)}) custom-call(s32[1]{0:T(128)} %bitcast.s_ref.core_ref, s32[4]{0:T(128)} %get-tuple-element.65.lo_ref, s32[4]{0:T(128)} %get-tuple-element.64.nb_ref, bf16[2048,1024]{1,0:T(8,128)(2,1)} %get-tuple-element.35.q_ref, ...), custom_call_target="tpu_custom_call" | custom-call | flops 17179869184 | bytes 12582912 | tf_op jit(solution)/shard_map/attention/pallas_call | solution.py:369
  219.1 2.9 fusion
  222.0 1.3 collective-permute-start.11
  223.3 50.4 %collective-permute-start.22 = (bf16[2,256,2048]{2,1,0:T(8,128)(2,1)}, bf16[2,256,2048]{2,1,0:T(8,128)(2,1)}, u32[]{:S(2)}, u32[]{:S(2)}) collective-permute-start(bf16[2,256,2048]{2,1,0:T(8,128)(2,1)} %bitcast.10.a_ref), channel_id=1, source_target_pairs={{0,2},{1,3},{2,0},{3,1},{4,6},{5,7},{6,4},{7,5}} | collective-permute-start | bytes 6291464 | tf_op jit(solution)/shard_map/ppermute | solution.py:678
  273.7 23.1 %collective-permute-done.11.refs_4_ = bf16[2,128,2048]{2,1,0:T(8,128)(2,1)} collective-permute-done((bf16[2,128,2048]{2,1,0:T(8,128)(2,1)S(1)}, bf16[2,128,2048]{2,1,0:T(8,128)(2,1)}, u32[]{:S(2)}, u32[]{:S(2)}) %collective-permute-start.11) | collective-permute-done | bytes 1048608 | tf_op jit(solution)/shard_map/ppermute | solution.py:725
  296.8 5.3 kv_finish.1
  302.2 6.6 %kvgrad.1.a_ref = bf16[256,2048]{1,0:T(8,128)(2,1)} custom-call(s32[1]{0:T(128)} %bitcast.s_ref.core_ref, bf16[256,2048]{1,0:T(8,128)(2,1)} %get-tuple-element.58.dkvt_ref, bf16[1024,2048]{1,0:T(8,128)(2,1)} %x_own.9, bf16[1024,2048]{1,0:T(8,128)(2,1)} %collective-permute-done.2.x_ref.x_oth), custom_call_target="tpu_custom_call" | custom-call | flops 2147483648 | bytes 8388608 | tf_op jit(solution)/shard_map/kvgrad/pallas_call | solution.py:486
  309.2 2.0 collective-permute-start.19
  311.3 52.9 %collective-permute-done.25.b_ref = bf16[256,2048]{1,0:T(8,128)(2,1)S(1)} collective-permute-done((bf16[256,2048]{1,0:T(8,128)(2,1)}, bf16[256,2048]{1,0:T(8,128)(2,1)S(1)}, u32[]{:S(2)}, u32[]{:S(2)}) %collective-permute-start.25) | collective-permute-done | bytes 1048608 | tf_op jit(solution)/shard_map/ppermute | solution.py:678
  364.2 2.0 collective-permute-start.13
  366.2 43.0 %collective-permute-done.19.b_ref = bf16[2,256,2048]{2,1,0:T(8,128)(2,1)} collective-permute-done((bf16[2,256,2048]{2,1,0:T(8,128)(2,1)}, bf16[2,256,2048]{2,1,0:T(8,128)(2,1)}, u32[]{:S(2)}, u32[]{:S(2)}) %collective-permute-start.19) | collective-permute-done | bytes 2097184 | tf_op jit(solution)/shard_map/ppermute | solution.py:678
  409.7 44.4 %collective-permute-done.16.b_ref = bf16[2,256,2048]{2,1,0:T(8,128)(2,1)} collective-permute-done((bf16[2,256,2048]{2,1,0:T(8,128)(2,1)}, bf16[2,256,2048]{2,1,0:T(8,128)(2,1)}, u32[]{:S(2)}, u32[]{:S(2)}) %collective-permute-start.16) | collective-permute-done | bytes 2097184 | tf_op jit(solution)/shard_map/ppermute | solution.py:678
  454.1 43.5 %collective-permute-done.13.b_ref = bf16[2,256,2048]{2,1,0:T(8,128)(2,1)} collective-permute-done((bf16[2,256,2048]{2,1,0:T(8,128)(2,1)}, bf16[2,256,2048]{2,1,0:T(8,128)(2,1)}, u32[]{:S(2)}, u32[]{:S(2)}) %collective-permute-start.13) | collective-permute-done | bytes 2097184 | tf_op jit(solution)/shard_map/ppermute | solution.py:678
  499.7 2.3 collective-permute-done.7.refs_4_
  502.2 4.4 collective-permute-done.27.d_ref
  507.7 13.9 %attn_out.1 = bf16[1024,2048]{1,0:T(8,128)(2,1)} custom-call(s32[1]{0:T(128)} %bitcast.s_ref.core_ref, bf16[2,2048,256]{2,1,0:T(8,128)(2,1)} %get-tuple-element.38.refs_0_, bf16[2,2048,256]{2,1,0:T(8,128)(2,1)} %get-tuple-element.39.refs_1_, bf16[2,2048,256]{2,1,0:T(8,128)(2,1)} %get-tuple-element.40.refs_2_, ...), custom_call_target="tpu_custom_call" | custom-call | flops 8589934592 | bytes 16777216 | tf_op jit(solution)/shard_map/attn_out/pallas_call | solution.py:599
  521.6 17.0 %grad_hidden.1 = bf16[1024,2048]{1,0:T(8,128)(2,1)} custom-call(s32[1]{0:T(128)} %bitcast.s_ref.core_ref, bf16[2,2048,256]{2,1,0:T(8,128)(2,1)} %get-tuple-element.38.refs_0_, bf16[2,2048,256]{2,1,0:T(8,128)(2,1)} %get-tuple-element.39.refs_1_, bf16[2,2048,256]{2,1,0:T(8,128)(2,1)} %get-tuple-element.40.refs_2_, ...), custom_call_target="tpu_custom_call" | custom-call | flops 10737418240 | bytes 16777216 | tf_op jit(solution)/shard_map/grad_hidden/pallas_call | solution.py:640
  538.5 5.1 kv_combine.1
  543.6 9.8 %combine.4 = (f32[2048,2048]{1,0:T(8,128)}, f32[2048,2048]{1,0:T(8,128)}) custom-call(s32[1]{0:T(128)} %bitcast.s_ref.core_ref, bf16[2,256,2048]{2,1,0:T(8,128)(2,1)} %bitcast.10.a_ref, bf16[2,256,2048]{2,1,0:T(8,128)(2,1)} %collective-permute-done.22.b_ref, bf16[2,256,2048]{2,1,0:T(8,128)(2,1)} %collective-permute-done.23.c_ref, ...), custom_call_target="tpu_custom_call" | custom-call | flops 536870912 | bytes 16777216 | tf_op jit(solution)/shard_map/combine/pallas_call | solution.py:557
  553.5 9.9 %combine.5 = (f32[2048,2048]{1,0:T(8,128)}, f32[2048,2048]{1,0:T(8,128)}) custom-call(s32[1]{0:T(128)} %bitcast.s_ref.core_ref, bf16[2,256,2048]{2,1,0:T(8,128)(2,1)} %bitcast.44, bf16[2,256,2048]{2,1,0:T(8,128)(2,1)} %collective-permute-done.19.b_ref, ...), custom_call_target="tpu_custom_call", output_to_operand_aliasing={{0}: (5, {}), {1}: (6, {})} | custom-call | flops 536870912 | bytes 16777216 | tf_op jit(solution)/shard_map/combine/pallas_call | solution.py:557
  563.3 9.9 %combine.6 = (f32[2048,2048]{1,0:T(8,128)}, f32[2048,2048]{1,0:T(8,128)}) custom-call(s32[1]{0:T(128)} %bitcast.s_ref.core_ref, bf16[2,256,2048]{2,1,0:T(8,128)(2,1)} %bitcast.41, bf16[2,256,2048]{2,1,0:T(8,128)(2,1)} %collective-permute-done.16.b_ref, ...), custom_call_target="tpu_custom_call", output_to_operand_aliasing={{0}: (5, {}), {1}: (6, {})} | custom-call | flops 536870912 | bytes 16777216 | tf_op jit(solution)/shard_map/combine/pallas_call | solution.py:557
  573.2 9.9 %combine.7 = (f32[2048,2048]{1,0:T(8,128)}, f32[2048,2048]{1,0:T(8,128)}) custom-call(s32[1]{0:T(128)} %bitcast.s_ref.core_ref, bf16[2,256,2048]{2,1,0:T(8,128)(2,1)} %bitcast.38, bf16[2,256,2048]{2,1,0:T(8,128)(2,1)} %collective-permute-done.13.b_ref, ...), custom_call_target="tpu_custom_call", output_to_operand_aliasing={{0}: (5, {}), {1}: (6, {})} | custom-call | flops 536870912 | bytes 16777216 | tf_op jit(solution)/shard_map/combine/pallas_call | solution.py:557
  (70 shorter events, 10.2 us)
Async XLA Ops:
  0.6 34.8 %collective-permute-start.2 = (bf16[1024,2048]{1,0:T(8,128)(2,1)}, bf16[1024,2048]{1,0:T(8,128)(2,1)}, u32[]{:S(2)}, u32[]{:S(2)}) collective-permute-start(bf16[1024,2048]{1,0:T(8,128)(2,1)} %x_own.9), channel_id=1, source_target_pairs={{0,1},{1,0},{2,3},{3,2},{4,5},{5,4},{6,7},{7,6}} | collective-permute-start | bytes 12582920 | tf_op jit(solution)/shard_map/ppermute | solution.py:675
  1.5 50.3 %collective-permute-start.4 = (bf16[1024,2048]{1,0:T(8,128)(2,1)}, bf16[1024,2048]{1,0:T(8,128)(2,1)}, u32[]{:S(2)}, u32[]{:S(2)}) collective-permute-start(bf16[1024,2048]{1,0:T(8,128)(2,1)} %g_own.7), channel_id=1, source_target_pairs={{0,1},{1,0},{2,3},{3,2},{4,5},{5,4},{6,7},{7,6}} | collective-permute-start | bytes 12582920 | tf_op jit(solution)/shard_map/ppermute | solution.py:675
  5.2 30.3 %collective-permute-start.3 = (f32[1024,128]{1,0:T(8,128)}, f32[1024,128]{1,0:T(8,128)}, u32[]{:S(2)}, u32[]{:S(2)}) collective-permute-start(f32[1024,128]{1,0:T(8,128)} %pad_maximum_fusion.tab_ref.tab_own.refs_5_), channel_id=1, source_target_pairs={{0,1},{1,0},{2,3},{3,2},{4,5},{5,4},{6,7},{7,6}} | collective-permute-start | bytes 1572872 | tf_op jit(solution)/shard_map/ppermute | solution.py:675
  5.7 17.4 %collective-permute-start = (s32[1024]{0:T(1024)S(1)}, s32[1024]{0:T(1024)S(1)}, u32[]{:S(2)}, u32[]{:S(2)}) collective-permute-start(s32[1024]{0:T(1024)S(1)} %copy-done.3), channel_id=1, source_target_pairs={{0,1},{1,0},{2,3},{3,2},{4,5},{5,4},{6,7},{7,6}} | collective-permute-start | bytes 12296 | tf_op jit(solution)/shard_map/ppermute | solution.py:675
  17.4 48.6 %collective-permute-start.5 = (bf16[1024,256]{1,0:T(8,128)(2,1)}, bf16[1024,256]{1,0:T(8,128)(2,1)}, u32[]{:S(2)}, u32[]{:S(2)}) collective-permute-start(bf16[1024,256]{1,0:T(8,128)(2,1)} %get-tuple-element.36.kvc_own), channel_id=1, source_target_pairs={{0,2},{1,3},{4,6},{5,7}} | collective-permute-start | bytes 1572872 | tf_op jit(solution)/shard_map/ppermute | solution.py:696
  23.1 11.0 %collective-permute-start.1 = (s32[2048]{0:T(1024)S(1)}, s32[2048]{0:T(1024)S(1)}, u32[]{:S(2)}, u32[]{:S(2)}) collective-permute-start(s32[2048]{0:T(1024)S(1)} %add_select_fusion), channel_id=1, source_target_pairs={{0,2},{1,3},{2,0},{3,1},{4,6},{5,7},{6,4},{7,5}} | collective-permute-start | bytes 24584 | tf_op jit(solution)/shard_map/ppermute | solution.py:678
  46.6 19.4 %collective-permute-start.6 = (bf16[1024,256]{1,0:T(8,128)(2,1)}, bf16[1024,256]{1,0:T(8,128)(2,1)}, u32[]{:S(2)}, u32[]{:S(2)}) collective-permute-start(bf16[1024,256]{1,0:T(8,128)(2,1)} %get-tuple-element.37.kvc_oth), channel_id=1, source_target_pairs={{0,2},{1,3},{4,6},{5,7}} | collective-permute-start | bytes 1572872 | tf_op jit(solution)/shard_map/ppermute | solution.py:702
  222.0 74.8 %collective-permute-start.11 = (bf16[2,128,2048]{2,1,0:T(8,128)(2,1)S(1)}, bf16[2,128,2048]{2,1,0:T(8,128)(2,1)}, u32[]{:S(2)}, u32[]{:S(2)}) collective-permute-start(bf16[2,128,2048]{2,1,0:T(8,128)(2,1)S(1)} %fusion), channel_id=1, source_target_pairs={{2,0},{3,1},{6,4},{7,5}} | collective-permute-start | bytes 3145736 | tf_op jit(solution)/shard_map/ppermute | solution.py:725
  223.3 140.9 %collective-permute-start.22 = (bf16[2,256,2048]{2,1,0:T(8,128)(2,1)}, bf16[2,256,2048]{2,1,0:T(8,128)(2,1)}, u32[]{:S(2)}, u32[]{:S(2)}) collective-permute-start(bf16[2,256,2048]{2,1,0:T(8,128)(2,1)} %bitcast.10.a_ref), channel_id=1, source_target_pairs={{0,2},{1,3},{2,0},{3,1},{4,6},{5,7},{6,4},{7,5}} | collective-permute-start | bytes 6291464 | tf_op jit(solution)/shard_map/ppermute | solution.py:678
  308.7 55.4 %collective-permute-start.25 = (bf16[256,2048]{1,0:T(8,128)(2,1)}, bf16[256,2048]{1,0:T(8,128)(2,1)S(1)}, u32[]{:S(2)}, u32[]{:S(2)}) collective-permute-start(bf16[256,2048]{1,0:T(8,128)(2,1)} %kvgrad.1.a_ref), channel_id=1, source_target_pairs={{0,2},{1,3},{2,0},{3,1},{4,6},{5,7},{6,4},{7,5}} | collective-permute-start | bytes 3145736 | tf_op jit(solution)/shard_map/ppermute | solution.py:678
  308.7 55.4 %collective-permute-start.26 = (bf16[256,2048]{1,0:T(8,128)(2,1)}, bf16[256,2048]{1,0:T(8,128)(2,1)S(1)}, u32[]{:S(2)}, u32[]{:S(2)}) collective-permute-start(bf16[256,2048]{1,0:T(8,128)(2,1)} %kvgrad.1.a_ref), channel_id=1, source_target_pairs={{0,1},{1,0},{2,3},{3,2},{4,5},{5,4},{6,7},{7,6}} | collective-permute-start | bytes 3145736 | tf_op jit(solution)/shard_map/ppermute | solution.py:675
  308.7 57.5 %collective-permute-start.23 = (bf16[2,256,2048]{2,1,0:T(8,128)(2,1)}, bf16[2,256,2048]{2,1,0:T(8,128)(2,1)}, u32[]{:S(2)}, u32[]{:S(2)}) collective-permute-start(bf16[2,256,2048]{2,1,0:T(8,128)(2,1)} %bitcast.10.a_ref), channel_id=1, source_target_pairs={{0,1},{1,0},{2,3},{3,2},{4,5},{5,4},{6,7},{7,6}} | collective-permute-start | bytes 6291464 | tf_op jit(solution)/shard_map/ppermute | solution.py:675
  309.2 99.9 %collective-permute-start.19 = (bf16[2,256,2048]{2,1,0:T(8,128)(2,1)}, bf16[2,256,2048]{2,1,0:T(8,128)(2,1)}, u32[]{:S(2)}, u32[]{:S(2)}) collective-permute-start(bf16[2,256,2048]{2,1,0:T(8,128)(2,1)} %bitcast.42), channel_id=1, source_target_pairs={{0,2},{1,3},{2,0},{3,1},{4,6},{5,7},{6,4},{7,5}} | collective-permute-start | bytes 6291464 | tf_op jit(solution)/shard_map/ppermute | solution.py:678
  364.1 134.5 %copy-start = (bf16[256,2048]{1,0:T(8,128)(2,1)}, bf16[256,2048]{1,0:T(8,128)(2,1)S(1)}, u32[]{:S(2)}) copy-start(bf16[256,2048]{1,0:T(8,128)(2,1)S(1)} %collective-permute-done.25.b_ref) | copy-start | bytes 3145732
  364.1 45.1 %collective-permute-start.20 = (bf16[2,256,2048]{2,1,0:T(8,128)(2,1)}, bf16[2,256,2048]{2,1,0:T(8,128)(2,1)}, u32[]{:S(2)}, u32[]{:S(2)}) collective-permute-start(bf16[2,256,2048]{2,1,0:T(8,128)(2,1)} %bitcast.43), channel_id=1, source_target_pairs={{0,1},{1,0},{2,3},{3,2},{4,5},{5,4},{6,7},{7,6}} | collective-permute-start | bytes 6291464 | tf_op jit(solution)/shard_map/ppermute | solution.py:675
  364.1 142.4 %copy-start.1 = (bf16[256,2048]{1,0:T(8,128)(2,1)}, bf16[256,2048]{1,0:T(8,128)(2,1)S(1)}, u32[]{:S(2)}) copy-start(bf16[256,2048]{1,0:T(8,128)(2,1)S(1)} %collective-permute-done.26.c_ref) | copy-start | bytes 3145732
  364.2 90.0 %collective-permute-start.16 = (bf16[2,256,2048]{2,1,0:T(8,128)(2,1)}, bf16[2,256,2048]{2,1,0:T(8,128)(2,1)}, u32[]{:S(2)}, u32[]{:S(2)}) collective-permute-start(bf16[2,256,2048]{2,1,0:T(8,128)(2,1)} %bitcast.39), channel_id=1, source_target_pairs={{0,2},{1,3},{2,0},{3,1},{4,6},{5,7},{6,4},{7,5}} | collective-permute-start | bytes 6291464 | tf_op jit(solution)/shard_map/ppermute | solution.py:678
  364.2 133.4 %collective-permute-start.13 = (bf16[2,256,2048]{2,1,0:T(8,128)(2,1)}, bf16[2,256,2048]{2,1,0:T(8,128)(2,1)}, u32[]{:S(2)}, u32[]{:S(2)}) collective-permute-start(bf16[2,256,2048]{2,1,0:T(8,128)(2,1)} %bitcast.36), channel_id=1, source_target_pairs={{0,2},{1,3},{2,0},{3,1},{4,6},{5,7},{6,4},{7,5}} | collective-permute-start | bytes 6291464 | tf_op jit(solution)/shard_map/ppermute | solution.py:678
  366.2 132.5 %collective-permute-start.10 = (bf16[2,2048,256]{2,1,0:T(8,128)(2,1)}, bf16[2,2048,256]{2,1,0:T(8,128)(2,1)}, u32[]{:S(2)}, u32[]{:S(2)}) collective-permute-start(bf16[2,2048,256]{2,1,0:T(8,128)(2,1)} %get-tuple-element.41.refs_3_), channel_id=1, source_target_pairs={{0,1},{1,0},{2,3},{3,2},{4,5},{5,4},{6,7},{7,6}} | collective-permute-start | bytes 6291464 | tf_op jit(solution)/shard_map/ppermute | solution.py:675
  409.2 88.5 %collective-permute-start.12 = (bf16[2048,256]{1,0:T(8,128)(2,1)}, bf16[2048,256]{1,0:T(8,128)(2,1)S(1)}, u32[]{:S(2)}, u32[]{:S(2)}) collective-permute-start(bf16[2048,256]{1,0:T(8,128)(2,1)} %get-tuple-element.46.refs_8_), channel_id=1, source_target_pairs={{0,1},{1,0},{2,3},{3,2},{4,5},{5,4},{6,7},{7,6}} | collective-permute-start | bytes 3145736 | tf_op jit(solution)/shard_map/ppermute | solution.py:675
  409.2 90.0 %collective-permute-start.9 = (bf16[2,2048,256]{2,1,0:T(8,128)(2,1)}, bf16[2,2048,256]{2,1,0:T(8,128)(2,1)S(1)}, u32[]{:S(2)}, u32[]{:S(2)}) collective-permute-start(bf16[2,2048,256]{2,1,0:T(8,128)(2,1)} %get-tuple-element.40.refs_2_), channel_id=1, source_target_pairs={{0,1},{1,0},{2,3},{3,2},{4,5},{5,4},{6,7},{7,6}} | collective-permute-start | bytes 6291464 | tf_op jit(solution)/shard_map/ppermute | solution.py:675
  454.1 45.1 %collective-permute-start.8 = (bf16[2,2048,256]{2,1,0:T(8,128)(2,1)}, bf16[2,2048,256]{2,1,0:T(8,128)(2,1)S(1)}, u32[]{:S(2)}, u32[]{:S(2)}) collective-permute-start(bf16[2,2048,256]{2,1,0:T(8,128)(2,1)} %get-tuple-element.39.refs_1_), channel_id=1, source_target_pairs={{0,1},{1,0},{2,3},{3,2},{4,5},{5,4},{6,7},{7,6}} | collective-permute-start | bytes 6291464 | tf_op jit(solution)/shard_map/ppermute | solution.py:675
  497.6 4.4 collective-permute-start.7
  497.7 9.8 %collective-permute-start.24 = (bf16[2,256,2048]{2,1,0:T(8,128)(2,1)}, bf16[2,256,2048]{2,1,0:T(8,128)(2,1)}, u32[]{:S(2)}, u32[]{:S(2)}) collective-permute-start(bf16[2,256,2048]{2,1,0:T(8,128)(2,1)} %collective-permute-done.22.b_ref), channel_id=1, source_target_pairs={{0,1},{1,0},{2,3},{3,2},{4,5},{5,4},{6,7},{7,6}} | collective-permute-start | bytes 6291464 | tf_op jit(solution)/shard_map/ppermute | solution.py:675
  498.7 7.8 %collective-permute-start.27 = (bf16[256,2048]{1,0:T(8,128)(2,1)S(1)}, bf16[256,2048]{1,0:T(8,128)(2,1)S(1)}, u32[]{:S(2)}, u32[]{:S(2)}) collective-permute-start(bf16[256,2048]{1,0:T(8,128)(2,1)S(1)} %collective-permute-done.25.b_ref), channel_id=1, source_target_pairs={{0,1},{1,0},{2,3},{3,2},{4,5},{5,4},{6,7},{7,6}} | collective-permute-start | bytes 3145736 | tf_op jit(solution)/shard_map/ppermute | solution.py:675
  499.2 8.3 %copy-start.4 = (bf16[2,2048,256]{2,1,0:T(8,128)(2,1)}, bf16[2,2048,256]{2,1,0:T(8,128)(2,1)S(1)}, u32[]{:S(2)}) copy-start(bf16[2,2048,256]{2,1,0:T(8,128)(2,1)S(1)} %collective-permute-done.9.refs_6_) | copy-start | bytes 6291460
  499.2 54.3 %collective-permute-start.21 = (bf16[2,256,2048]{2,1,0:T(8,128)(2,1)}, bf16[2,256,2048]{2,1,0:T(8,128)(2,1)}, u32[]{:S(2)}, u32[]{:S(2)}) collective-permute-start(bf16[2,256,2048]{2,1,0:T(8,128)(2,1)} %collective-permute-done.19.b_ref), channel_id=1, source_target_pairs={{0,1},{1,0},{2,3},{3,2},{4,5},{5,4},{6,7},{7,6}} | collective-permute-start | bytes 6291464 | tf_op jit(solution)/shard_map/ppermute | solution.py:675
  499.2 8.3 %copy-start.5 = (bf16[2,2048,256]{2,1,0:T(8,128)(2,1)}, bf16[2,2048,256]{2,1,0:T(8,128)(2,1)S(1)}, u32[]{:S(2)}) copy-start(bf16[2,2048,256]{2,1,0:T(8,128)(2,1)S(1)} %collective-permute-done.8.refs_5_) | copy-start | bytes 6291460
  499.2 64.1 %collective-permute-start.17 = (bf16[2,256,2048]{2,1,0:T(8,128)(2,1)}, bf16[2,256,2048]{2,1,0:T(8,128)(2,1)}, u32[]{:S(2)}, u32[]{:S(2)}) collective-permute-start(bf16[2,256,2048]{2,1,0:T(8,128)(2,1)} %bitcast.40), channel_id=1, source_target_pairs={{0,1},{1,0},{2,3},{3,2},{4,5},{5,4},{6,7},{7,6}} | collective-permute-start | bytes 6291464 | tf_op jit(solution)/shard_map/ppermute | solution.py:675
  502.0 61.3 %collective-permute-start.18 = (bf16[2,256,2048]{2,1,0:T(8,128)(2,1)}, bf16[2,256,2048]{2,1,0:T(8,128)(2,1)}, u32[]{:S(2)}, u32[]{:S(2)}) collective-permute-start(bf16[2,256,2048]{2,1,0:T(8,128)(2,1)} %collective-permute-done.16.b_ref), channel_id=1, source_target_pairs={{0,1},{1,0},{2,3},{3,2},{4,5},{5,4},{6,7},{7,6}} | collective-permute-start | bytes 6291464 | tf_op jit(solution)/shard_map/ppermute | solution.py:675
  506.5 66.7 %collective-permute-start.14 = (bf16[2,256,2048]{2,1,0:T(8,128)(2,1)}, bf16[2,256,2048]{2,1,0:T(8,128)(2,1)}, u32[]{:S(2)}, u32[]{:S(2)}) collective-permute-start(bf16[2,256,2048]{2,1,0:T(8,128)(2,1)} %bitcast.37), channel_id=1, source_target_pairs={{0,1},{1,0},{2,3},{3,2},{4,5},{5,4},{6,7},{7,6}} | collective-permute-start | bytes 6291464 | tf_op jit(solution)/shard_map/ppermute | solution.py:675
  507.5 65.7 %collective-permute-start.15 = (bf16[2,256,2048]{2,1,0:T(8,128)(2,1)}, bf16[2,256,2048]{2,1,0:T(8,128)(2,1)}, u32[]{:S(2)}, u32[]{:S(2)}) collective-permute-start(bf16[2,256,2048]{2,1,0:T(8,128)(2,1)} %collective-permute-done.13.b_ref), channel_id=1, source_target_pairs={{0,1},{1,0},{2,3},{3,2},{4,5},{5,4},{6,7},{7,6}} | collective-permute-start | bytes 6291464 | tf_op jit(solution)/shard_map/ppermute | solution.py:675
  (4 other events, 12.5 us)

commit v4 on v3

--- a/solution.py
+++ b/solution.py
@@ -198,27 +198,25 @@
             pltpu.make_async_copy(g.at[rows_here, :], g_s, row_sem.at[1]),
         )
 
-    @pl.when(i // per_half == core)
-    def _():
-        for copy in row_copies(x_own, g_own):
-            copy.start()
-
-    @pl.when(i // per_half != core)
-    def _():
-        for copy in row_copies(x_oth, g_oth):
-            copy.start()
+    def init_copies():
+        moves = []
+        for base, place, ref in ((0, core, kvp_own), (0, 1 - core, kvp_oth), (2, core, kvc_own), (2, 1 - core, kvc_oth)):
+            moves.append((ref.at[:, pl.ds(0, HEAD)], k_s.at[span(base + place, tokens), :]))
+        for base, place, ref in ((0, core, kvp_own), (0, 1 - core, kvp_oth), (2, core, kvc_own), (2, 1 - core, kvc_oth)):
+            moves.append((ref.at[:, pl.ds(HEAD, HEAD)], v_s.at[span(base + place, tokens), :]))
+        moves.append((tab_own, tab_s.at[span(core, tokens), :]))
+        moves.append((tab_oth, tab_s.at[span(1 - core, tokens), :]))
+        return [pltpu.make_async_copy(src, dst, init_sem.at[n]) for n, (src, dst) in enumerate(moves)]
+
+    def arrive(first, last):
+        @pl.when(i == 0)
+        def _():
+            for copy in init_copies()[first:last]:
+                copy.wait()
 
     @pl.when(i == 0)
     def _():
-        copies = []
-        for base, place, ref in ((0, core, kvp_own), (0, 1 - core, kvp_oth), (2, core, kvc_own), (2, 1 - core, kvc_oth)):
-            where = span(base + place, tokens)
-            copies.append((ref.at[:, pl.ds(0, HEAD)], k_s.at[where, :]))
-            copies.append((ref.at[:, pl.ds(HEAD, HEAD)], v_s.at[where, :]))
-        copies.append((tab_own, tab_s.at[span(core, tokens), :]))
-        copies.append((tab_oth, tab_s.at[span(1 - core, tokens), :]))
-        copies = [pltpu.make_async_copy(src, dst, init_sem.at[n]) for n, (src, dst) in enumerate(copies)]
-        for copy in copies:
+        for copy in init_copies():
             copy.start()
         k_s[2 * chip_len:, :] = jnp.zeros((BK, HEAD), BF)
         v_s[2 * chip_len:, :] = jnp.zeros((BK, HEAD), BF)
@@ -232,8 +230,16 @@
 
         by_rows(w_s.shape[0], clear)
         by_rows(HEAD, clear_kv)
-        for copy in copies:
-            copy.wait()
+
+    @pl.when(i // per_half == core)
+    def _():
+        for copy in row_copies(x_own, g_own):
+            copy.start()
+
+    @pl.when(i // per_half != core)
+    def _():
+        for copy in row_copies(x_oth, g_oth):
+            copy.start()
 
     for h in range(PAIR):
         rows = slice(h * BQ, (h + 1) * BQ)
@@ -278,6 +284,7 @@
             m_s[rows, :] = jnp.maximum(m_s[rows, :], fold(sh, jnp.maximum))
         return carry
 
+    arrive(0, 4)
     lax.fori_loop(0, n_blocks, scores, 0)
     m_s[...] = jnp.broadcast_to(jnp.max(m_s[...], axis=1, keepdims=True), m_s.shape)
 
@@ -290,6 +297,7 @@
         d_s[...] += fold(e * dp, jnp.add)
         return carry
 
+    arrive(4, 10)
     lax.fori_loop(0, n_blocks, weights, 0)
     inv = 1.0 / jnp.sum(l_s[...], axis=1, keepdims=True)
     delta = jnp.sum(d_s[...], axis=1, keepdims=True) * inv
@@ -337,6 +345,8 @@
             x_s[r, :] = w_s[r, :].astype(BF)
 
         by_rows(w_s.shape[0], narrow)
+        part_copy = pltpu.make_async_copy(x_s, part_ref, out_sem.at[0])
+        part_copy.start()
 
         def narrow_kv(r, carry):
             rows = span(r, 16)
@@ -347,14 +357,10 @@
             return carry
 
         lax.fori_loop(0, HEAD // 16, narrow_kv, 0)
-        copies = (
-            pltpu.make_async_copy(x_s, part_ref, out_sem.at[0]),
-            pltpu.make_async_copy(g_s, dkv_ref, out_sem.at[1]),
-        )
-        for copy in copies:
-            copy.start()
-        for copy in copies:
-            copy.wait()
+        dkv_copy = pltpu.make_async_copy(g_s, dkv_ref, out_sem.at[1])
+        dkv_copy.start()
+        part_copy.wait()
+        dkv_copy.wait()
 
 
 def attention(chunk, core, lo, n_blocks, q, dctx, kdoc, tabs, kv_prev, kv_chip, xs, gs):
@@ -688,16 +694,19 @@
         sel_oth = jnp.stack([core_id, 1 - core_id]).astype(jnp.int32)
 
         doc_oth = near(doc_ids)
+        doc_far = far(doc_ids)
+        doc_far_oth = lax.ppermute(doc_ids, "sp", [(d, d ^ 3) for d in range(n_dev)])
         x_oth = near(hidden)
         g_oth = near(grad_out)
         tab_own = rope_table(positions)
         tab_oth = near(tab_own)
         kv_own, q = qkv_proj(sel_own, hidden, w_q, w_k, w_v, tab_own, None)
         kvp_own = lax.ppermute(kv_own, "sp", down_perm)
-        doc_chip = jnp.where(
-            core_id == 0, jnp.concatenate([doc_ids, doc_oth]), jnp.concatenate([doc_oth, doc_ids])
-        )
-        doc_far = far(doc_chip)
+
+        def in_order(own, oth):
+            return jnp.where(core_id == 0, jnp.concatenate([own, oth]), jnp.concatenate([oth, own]))
+
+        doc_chip, doc_far = in_order(doc_ids, doc_oth), in_order(doc_far, doc_far_oth)
         kv_oth, q = qkv_proj(sel_oth, x_oth, w_q, w_k, w_v, tab_oth, q)
         kvp_oth = lax.ppermute(kv_oth, "sp", down_perm)
         dctx = dctx_proj(core, grad_out, g_oth, w_o)

time: 584 us -> 563 us (0.964)
  Pallas kernels: 277 us -> 267 us
  waiting for transfers between devices: 224 us -> 214 us
    ppermute x6, waiting for transfers between devices: 194 us -> 184 us  [far(): return lax.ppermute(v, 'sp', far_perm)]
    pallas_call x4, Pallas kernels: 153 us -> 143 us  [attention(): pl.pallas_call(attn_kernel, grid_spec=pltpu.PrefetchScalarGridSpec(num_sc...]
  transfers between devices with their start and end apart: 28 -> 29, of which waited for: 8 -> 7; matrix products, arithmetic and copies ran while one was open for 1% -> 1% of each run, Pallas kernels for 20% -> 20%
where the time goes in v4:
time: 563 us; the launch traced here: 562 us
  Pallas kernels  267 us (47%)
  waiting for transfers between devices  214 us (38%)
  starting transfers between devices  70.2 us (12%)
  other arithmetic  8.5 us (2%)
    ppermute x6, waiting for transfers between devices, far(): return lax.ppermute(v, 'sp', far_perm)  184 us
    pallas_call x4, Pallas kernels, attention(): pl.pallas_call(attn_kernel, grid_spec=pltpu.PrefetchScalarGridSpec(num_sc...  143 us
    ppermute x6, starting transfers between devices, far(): return lax.ppermute(v, 'sp', far_perm)  57.6 us
    pallas_call x4, Pallas kernels, combine(): pl.pallas_call(combine_kernel, grid_spec=pltpu.PrefetchScalarGridSpec(num...  39.4 us
    ppermute x1, waiting for transfers between devices, device_step(): dkv_far = lax.ppermute(dkv_up, 'sp', up_perm)  23.1 us
    pallas_call x2, Pallas kernels, qkv_proj(): pl.pallas_call(qkv_kernel, grid_spec=pltpu.PrefetchScalarGridSpec(num_sca...  22.5 us
    pallas_call x1, Pallas kernels, grad_hidden(): pl.pallas_call(functools.partial(hidden_kernel, n), grid_spec=pltpu.Prefe...  17 us
    pallas_call x1, Pallas kernels, dctx_proj(): pl.pallas_call(dctx_kernel, grid_spec=pltpu.PrefetchScalarGridSpec(num_sc...  14.2 us
  transfers between devices with their start and end apart: 29, of which 7 were waited for; matrix products, arithmetic and copies ran while one was open for 1% of the time, Pallas kernels for 20%

profile of v4, /device:TPU:0, one launch (start us, length us, event | category | flops | bytes accessed | tf_op | source)
XLA Modules:
  0.0 562.1 jit_solution(4129063147749038849)
XLA Ops:
  2.0 2.5 collective-permute-start.1
  5.2 1.9 multiply_cosine_fusion
  8.9 11.3 %qkv_proj.2 = (bf16[1024,256]{1,0:T(8,128)(2,1)}, bf16[2048,1024]{1,0:T(8,128)(2,1)}) custom-call(s32[2]{0:T(128)} %pad_add_fusion.2.s_ref, bf16[1024,2048]{1,0:T(8,128)(2,1)} %x_own.9, bf16[2048,2048]{1,0:T(8,128)(2,1)} %refs_10_.1, bf16[2048,256]{1,0:T(8,128)(2,1)} %refs_11_.1, bf16[2048,256]{1,0:T(8,128)(2,1)} %refs_12_.1, ...), custom_call_target="tpu_custom_call" | custom-call | flops 5368709120 | bytes 8388608 | tf_op jit(solution)/shard_map/qkv_proj/pallas_call | solution.py:110
  20.9 4.6 collective-permute-start.6
  27.0 11.2 %qkv_proj.3 = (bf16[1024,256]{1,0:T(8,128)(2,1)}, bf16[2048,1024]{1,0:T(8,128)(2,1)}) custom-call(s32[2]{0:T(128)} %pad_add_fusion.1.s_ref, bf16[1024,2048]{1,0:T(8,128)(2,1)} %collective-permute-done.3.x_ref.x_oth, bf16[2048,2048]{1,0:T(8,128)(2,1)} %refs_10_.1, bf16[2048,256]{1,0:T(8,128)(2,1)} %refs_11_.1, ...), custom_call_target="tpu_custom_call", output_to_operand_aliasing={{1}: (6, {})} | custom-call | flops 5368709120 | bytes 8388608 | tf_op jit(solution)/shard_map/qkv_proj/pallas_call | solution.py:110
  38.2 2.1 collective-permute-start.7
  40.3 14.2 %dctx_proj.1.do_ref = bf16[2048,1024]{1,0:T(8,128)(2,1)} custom-call(s32[1]{0:T(128)} %bitcast.s_ref.core_ref, bf16[1024,2048]{1,0:T(8,128)(2,1)} %g_own.7, bf16[1024,2048]{1,0:T(8,128)(2,1)} %collective-permute-done.5.oth_ref.g_oth, bf16[2048,2048]{1,0:T(8,128)(2,1)} %refs_8_.1), custom_call_target="tpu_custom_call" | custom-call | flops 8589934592 | bytes 12582912 | tf_op jit(solution)/shard_map/dctx_proj/pallas_call | solution.py:163
  54.4 35.7 %attention.7 = (bf16[2,2048,256]{2,1,0:T(8,128)(2,1)}, bf16[512,2048]{1,0:T(8,128)(2,1)}, bf16[512,2048]{1,0:T(8,128)(2,1)}) custom-call(s32[1]{0:T(128)} %bitcast.s_ref.core_ref, s32[4]{0:T(128)} %get-tuple-element.65.lo_ref, s32[4]{0:T(128)} %get-tuple-element.64.nb_ref, bf16[2048,1024]{1,0:T(8,128)(2,1)} %get-tuple-element.35.q_ref, ...), custom_call_target="tpu_custom_call" | custom-call | flops 17179869184 | bytes 12582912 | tf_op jit(solution)/shard_map/attention/pallas_call | solution.py:375
  90.2 35.7 %attention.6 = (bf16[2,2048,256]{2,1,0:T(8,128)(2,1)}, bf16[512,2048]{1,0:T(8,128)(2,1)}, bf16[512,2048]{1,0:T(8,128)(2,1)}) custom-call(s32[1]{0:T(128)} %bitcast.s_ref.core_ref, s32[4]{0:T(128)} %get-tuple-element.65.lo_ref, s32[4]{0:T(128)} %get-tuple-element.64.nb_ref, bf16[2048,1024]{1,0:T(8,128)(2,1)} %get-tuple-element.35.q_ref, ...), custom_call_target="tpu_custom_call" | custom-call | flops 17179869184 | bytes 12582912 | tf_op jit(solution)/shard_map/attention/pallas_call | solution.py:375
  125.8 35.9 %attention.5 = (bf16[2,2048,256]{2,1,0:T(8,128)(2,1)}, bf16[512,2048]{1,0:T(8,128)(2,1)}, bf16[512,2048]{1,0:T(8,128)(2,1)}) custom-call(s32[1]{0:T(128)} %bitcast.s_ref.core_ref, s32[4]{0:T(128)} %get-tuple-element.65.lo_ref, s32[4]{0:T(128)} %get-tuple-element.64.nb_ref, bf16[2048,1024]{1,0:T(8,128)(2,1)} %get-tuple-element.35.q_ref, ...), custom_call_target="tpu_custom_call" | custom-call | flops 17179869184 | bytes 12582912 | tf_op jit(solution)/shard_map/attention/pallas_call | solution.py:375
  161.7 35.7 %attention.4 = (bf16[2,2048,256]{2,1,0:T(8,128)(2,1)}, bf16[512,2048]{1,0:T(8,128)(2,1)}, bf16[512,2048]{1,0:T(8,128)(2,1)}) custom-call(s32[1]{0:T(128)} %bitcast.s_ref.core_ref, s32[4]{0:T(128)} %get-tuple-element.65.lo_ref, s32[4]{0:T(128)} %get-tuple-element.64.nb_ref, bf16[2048,1024]{1,0:T(8,128)(2,1)} %get-tuple-element.35.q_ref, ...), custom_call_target="tpu_custom_call" | custom-call | flops 17179869184 | bytes 12582912 | tf_op jit(solution)/shard_map/attention/pallas_call | solution.py:375
  197.4 2.9 fusion
  200.3 1.3 collective-permute-start.12
  201.6 51.1 %collective-permute-start.23 = (bf16[2,256,2048]{2,1,0:T(8,128)(2,1)}, bf16[2,256,2048]{2,1,0:T(8,128)(2,1)}, u32[]{:S(2)}, u32[]{:S(2)}) collective-permute-start(bf16[2,256,2048]{2,1,0:T(8,128)(2,1)} %bitcast.10.a_ref), channel_id=1, source_target_pairs={{0,2},{1,3},{2,0},{3,1},{4,6},{5,7},{6,4},{7,5}} | collective-permute-start | bytes 6291464 | tf_op jit(solution)/shard_map/ppermute | solution.py:684
  252.6 23.1 %collective-permute-done.12.refs_4_ = bf16[2,128,2048]{2,1,0:T(8,128)(2,1)} collective-permute-done((bf16[2,128,2048]{2,1,0:T(8,128)(2,1)S(1)}, bf16[2,128,2048]{2,1,0:T(8,128)(2,1)}, u32[]{:S(2)}, u32[]{:S(2)}) %collective-permute-start.12) | collective-permute-done | bytes 1048608 | tf_op jit(solution)/shard_map/ppermute | solution.py:734
  275.8 5.3 kv_finish.1
  281.1 6.6 %kvgrad.1.a_ref = bf16[256,2048]{1,0:T(8,128)(2,1)} custom-call(s32[1]{0:T(128)} %bitcast.s_ref.core_ref, bf16[256,2048]{1,0:T(8,128)(2,1)} %get-tuple-element.58.dkvt_ref, bf16[1024,2048]{1,0:T(8,128)(2,1)} %x_own.9, bf16[1024,2048]{1,0:T(8,128)(2,1)} %collective-permute-done.3.x_ref.x_oth), custom_call_target="tpu_custom_call" | custom-call | flops 2147483648 | bytes 8388608 | tf_op jit(solution)/shard_map/kvgrad/pallas_call | solution.py:492
  288.3 2.0 collective-permute-start.20
  290.3 52.8 %collective-permute-done.26.b_ref = bf16[256,2048]{1,0:T(8,128)(2,1)S(1)} collective-permute-done((bf16[256,2048]{1,0:T(8,128)(2,1)}, bf16[256,2048]{1,0:T(8,128)(2,1)S(1)}, u32[]{:S(2)}, u32[]{:S(2)}) %collective-permute-start.26) | collective-permute-done | bytes 1048608 | tf_op jit(solution)/shard_map/ppermute | solution.py:684
  343.1 2.0 collective-permute-start.14
  345.2 43.0 %collective-permute-done.20.b_ref = bf16[2,256,2048]{2,1,0:T(8,128)(2,1)} collective-permute-done((bf16[2,256,2048]{2,1,0:T(8,128)(2,1)}, bf16[2,256,2048]{2,1,0:T(8,128)(2,1)}, u32[]{:S(2)}, u32[]{:S(2)}) %collective-permute-start.20) | collective-permute-done | bytes 2097184 | tf_op jit(solution)/shard_map/ppermute | solution.py:684
  388.6 44.4 %collective-permute-done.17.b_ref = bf16[2,256,2048]{2,1,0:T(8,128)(2,1)} collective-permute-done((bf16[2,256,2048]{2,1,0:T(8,128)(2,1)}, bf16[2,256,2048]{2,1,0:T(8,128)(2,1)}, u32[]{:S(2)}, u32[]{:S(2)}) %collective-permute-start.17) | collective-permute-done | bytes 2097184 | tf_op jit(solution)/shard_map/ppermute | solution.py:684
  433.1 43.6 %collective-permute-done.14.b_ref = bf16[2,256,2048]{2,1,0:T(8,128)(2,1)} collective-permute-done((bf16[2,256,2048]{2,1,0:T(8,128)(2,1)}, bf16[2,256,2048]{2,1,0:T(8,128)(2,1)}, u32[]{:S(2)}, u32[]{:S(2)}) %collective-permute-start.14) | collective-permute-done | bytes 2097184 | tf_op jit(solution)/shard_map/ppermute | solution.py:684
  478.7 2.3 collective-permute-done.8.refs_4_
  481.2 4.4 collective-permute-done.28.d_ref
  486.7 13.9 %attn_out.1 = bf16[1024,2048]{1,0:T(8,128)(2,1)} custom-call(s32[1]{0:T(128)} %bitcast.s_ref.core_ref, bf16[2,2048,256]{2,1,0:T(8,128)(2,1)} %get-tuple-element.38.refs_0_, bf16[2,2048,256]{2,1,0:T(8,128)(2,1)} %get-tuple-element.39.refs_1_, bf16[2,2048,256]{2,1,0:T(8,128)(2,1)} %get-tuple-element.40.refs_2_, ...), custom_call_target="tpu_custom_call" | custom-call | flops 8589934592 | bytes 16777216 | tf_op jit(solution)/shard_map/attn_out/pallas_call | solution.py:605
  500.6 17.0 %grad_hidden.1 = bf16[1024,2048]{1,0:T(8,128)(2,1)} custom-call(s32[1]{0:T(128)} %bitcast.s_ref.core_ref, bf16[2,2048,256]{2,1,0:T(8,128)(2,1)} %get-tuple-element.38.refs_0_, bf16[2,2048,256]{2,1,0:T(8,128)(2,1)} %get-tuple-element.39.refs_1_, bf16[2,2048,256]{2,1,0:T(8,128)(2,1)} %get-tuple-element.40.refs_2_, ...), custom_call_target="tpu_custom_call" | custom-call | flops 10737418240 | bytes 16777216 | tf_op jit(solution)/shard_map/grad_hidden/pallas_call | solution.py:646
  517.6 5.1 kv_combine.1
  522.6 9.8 %combine.4 = (f32[2048,2048]{1,0:T(8,128)}, f32[2048,2048]{1,0:T(8,128)}) custom-call(s32[1]{0:T(128)} %bitcast.s_ref.core_ref, bf16[2,256,2048]{2,1,0:T(8,128)(2,1)} %bitcast.10.a_ref, bf16[2,256,2048]{2,1,0:T(8,128)(2,1)} %collective-permute-done.23.b_ref, bf16[2,256,2048]{2,1,0:T(8,128)(2,1)} %collective-permute-done.24.c_ref, ...), custom_call_target="tpu_custom_call" | custom-call | flops 536870912 | bytes 16777216 | tf_op jit(solution)/shard_map/combine/pallas_call | solution.py:563
  532.5 9.9 %combine.5 = (f32[2048,2048]{1,0:T(8,128)}, f32[2048,2048]{1,0:T(8,128)}) custom-call(s32[1]{0:T(128)} %bitcast.s_ref.core_ref, bf16[2,256,2048]{2,1,0:T(8,128)(2,1)} %bitcast.44, bf16[2,256,2048]{2,1,0:T(8,128)(2,1)} %collective-permute-done.20.b_ref, ...), custom_call_target="tpu_custom_call", output_to_operand_aliasing={{0}: (5, {}), {1}: (6, {})} | custom-call | flops 536870912 | bytes 16777216 | tf_op jit(solution)/shard_map/combine/pallas_call | solution.py:563
  542.3 9.9 %combine.6 = (f32[2048,2048]{1,0:T(8,128)}, f32[2048,2048]{1,0:T(8,128)}) custom-call(s32[1]{0:T(128)} %bitcast.s_ref.core_ref, bf16[2,256,2048]{2,1,0:T(8,128)(2,1)} %bitcast.41, bf16[2,256,2048]{2,1,0:T(8,128)(2,1)} %collective-permute-done.17.b_ref, ...), custom_call_target="tpu_custom_call", output_to_operand_aliasing={{0}: (5, {}), {1}: (6, {})} | custom-call | flops 536870912 | bytes 16777216 | tf_op jit(solution)/shard_map/combine/pallas_call | solution.py:563
  552.2 9.9 %combine.7 = (f32[2048,2048]{1,0:T(8,128)}, f32[2048,2048]{1,0:T(8,128)}) custom-call(s32[1]{0:T(128)} %bitcast.s_ref.core_ref, bf16[2,256,2048]{2,1,0:T(8,128)(2,1)} %bitcast.38, bf16[2,256,2048]{2,1,0:T(8,128)(2,1)} %collective-permute-done.14.b_ref, ...), custom_call_target="tpu_custom_call", output_to_operand_aliasing={{0}: (5, {}), {1}: (6, {})} | custom-call | flops 536870912 | bytes 16777216 | tf_op jit(solution)/shard_map/combine/pallas_call | solution.py:563
  (73 shorter events, 10.4 us)
Async XLA Ops:
  0.6 26.4 %collective-permute-start.3 = (bf16[1024,2048]{1,0:T(8,128)(2,1)}, bf16[1024,2048]{1,0:T(8,128)(2,1)}, u32[]{:S(2)}, u32[]{:S(2)}) collective-permute-start(bf16[1024,2048]{1,0:T(8,128)(2,1)} %x_own.9), channel_id=1, source_target_pairs={{0,1},{1,0},{2,3},{3,2},{4,5},{5,4},{6,7},{7,6}} | collective-permute-start | bytes 12582920 | tf_op jit(solution)/shard_map/ppermute | solution.py:681
  1.5 38.8 %collective-permute-start.5 = (bf16[1024,2048]{1,0:T(8,128)(2,1)}, bf16[1024,2048]{1,0:T(8,128)(2,1)}, u32[]{:S(2)}, u32[]{:S(2)}) collective-permute-start(bf16[1024,2048]{1,0:T(8,128)(2,1)} %g_own.7), channel_id=1, source_target_pairs={{0,1},{1,0},{2,3},{3,2},{4,5},{5,4},{6,7},{7,6}} | collective-permute-start | bytes 12582920 | tf_op jit(solution)/shard_map/ppermute | solution.py:681
  1.5 19.3 %collective-permute-start = (s32[1024]{0:T(1024)}, s32[1024]{0:T(1024)S(1)}, u32[]{:S(2)}, u32[]{:S(2)}) collective-permute-start(s32[1024]{0:T(1024)} %param.11), channel_id=1, source_target_pairs={{0,1},{1,0},{2,3},{3,2},{4,5},{5,4},{6,7},{7,6}} | collective-permute-start | bytes 12296 | tf_op jit(solution)/shard_map/ppermute | solution.py:681
  2.0 18.9 %collective-permute-start.1 = (s32[1024]{0:T(1024)}, s32[1024]{0:T(1024)S(1)}, u32[]{:S(2)}, u32[]{:S(2)}) collective-permute-start(s32[1024]{0:T(1024)} %param.11), channel_id=1, source_target_pairs={{0,2},{1,3},{2,0},{3,1},{4,6},{5,7},{6,4},{7,5}} | collective-permute-start | bytes 12296 | tf_op jit(solution)/shard_map/ppermute | solution.py:684
  8.2 18.8 %collective-permute-start.4 = (f32[1024,128]{1,0:T(8,128)}, f32[1024,128]{1,0:T(8,128)}, u32[]{:S(2)}, u32[]{:S(2)}) collective-permute-start(f32[1024,128]{1,0:T(8,128)} %pad_maximum_fusion.tab_ref.tab_own.refs_5_), channel_id=1, source_target_pairs={{0,1},{1,0},{2,3},{3,2},{4,5},{5,4},{6,7},{7,6}} | collective-permute-start | bytes 1572872 | tf_op jit(solution)/shard_map/ppermute | solution.py:681
  8.9 11.9 %copy-start.3 = (s32[1024]{0:T(1024)S(1)}, s32[1024]{0:T(1024)}, u32[]{:S(2)}) copy-start(s32[1024]{0:T(1024)} %param.11) | copy-start | bytes 12292
  20.8 4.7 collective-permute-start.2
  20.9 33.5 %collective-permute-start.6 = (bf16[1024,256]{1,0:T(8,128)(2,1)}, bf16[1024,256]{1,0:T(8,128)(2,1)}, u32[]{:S(2)}, u32[]{:S(2)}) collective-permute-start(bf16[1024,256]{1,0:T(8,128)(2,1)} %get-tuple-element.36.kvc_own), channel_id=1, source_target_pairs={{0,2},{1,3},{4,6},{5,7}} | collective-permute-start | bytes 1572872 | tf_op jit(solution)/shard_map/ppermute | solution.py:704
  38.2 16.3 %collective-permute-start.7 = (bf16[1024,256]{1,0:T(8,128)(2,1)}, bf16[1024,256]{1,0:T(8,128)(2,1)}, u32[]{:S(2)}, u32[]{:S(2)}) collective-permute-start(bf16[1024,256]{1,0:T(8,128)(2,1)} %get-tuple-element.37.kvc_oth), channel_id=1, source_target_pairs={{0,2},{1,3},{4,6},{5,7}} | collective-permute-start | bytes 1572872 | tf_op jit(solution)/shard_map/ppermute | solution.py:711
  200.3 75.5 %collective-permute-start.12 = (bf16[2,128,2048]{2,1,0:T(8,128)(2,1)S(1)}, bf16[2,128,2048]{2,1,0:T(8,128)(2,1)}, u32[]{:S(2)}, u32[]{:S(2)}) collective-permute-start(bf16[2,128,2048]{2,1,0:T(8,128)(2,1)S(1)} %fusion), channel_id=1, source_target_pairs={{2,0},{3,1},{6,4},{7,5}} | collective-permute-start | bytes 3145736 | tf_op jit(solution)/shard_map/ppermute | solution.py:734
  201.6 141.5 %collective-permute-start.23 = (bf16[2,256,2048]{2,1,0:T(8,128)(2,1)}, bf16[2,256,2048]{2,1,0:T(8,128)(2,1)}, u32[]{:S(2)}, u32[]{:S(2)}) collective-permute-start(bf16[2,256,2048]{2,1,0:T(8,128)(2,1)} %bitcast.10.a_ref), channel_id=1, source_target_pairs={{0,2},{1,3},{2,0},{3,1},{4,6},{5,7},{6,4},{7,5}} | collective-permute-start | bytes 6291464 | tf_op jit(solution)/shard_map/ppermute | solution.py:684
  287.7 55.3 %collective-permute-start.26 = (bf16[256,2048]{1,0:T(8,128)(2,1)}, bf16[256,2048]{1,0:T(8,128)(2,1)S(1)}, u32[]{:S(2)}, u32[]{:S(2)}) collective-permute-start(bf16[256,2048]{1,0:T(8,128)(2,1)} %kvgrad.1.a_ref), channel_id=1, source_target_pairs={{0,2},{1,3},{2,0},{3,1},{4,6},{5,7},{6,4},{7,5}} | collective-permute-start | bytes 3145736 | tf_op jit(solution)/shard_map/ppermute | solution.py:684
  287.7 55.3 %collective-permute-start.27 = (bf16[256,2048]{1,0:T(8,128)(2,1)}, bf16[256,2048]{1,0:T(8,128)(2,1)S(1)}, u32[]{:S(2)}, u32[]{:S(2)}) collective-permute-start(bf16[256,2048]{1,0:T(8,128)(2,1)} %kvgrad.1.a_ref), channel_id=1, source_target_pairs={{0,1},{1,0},{2,3},{3,2},{4,5},{5,4},{6,7},{7,6}} | collective-permute-start | bytes 3145736 | tf_op jit(solution)/shard_map/ppermute | solution.py:681
  287.8 57.4 %collective-permute-start.24 = (bf16[2,256,2048]{2,1,0:T(8,128)(2,1)}, bf16[2,256,2048]{2,1,0:T(8,128)(2,1)}, u32[]{:S(2)}, u32[]{:S(2)}) collective-permute-start(bf16[2,256,2048]{2,1,0:T(8,128)(2,1)} %bitcast.10.a_ref), channel_id=1, source_target_pairs={{0,1},{1,0},{2,3},{3,2},{4,5},{5,4},{6,7},{7,6}} | collective-permute-start | bytes 6291464 | tf_op jit(solution)/shard_map/ppermute | solution.py:681
  288.3 99.9 %collective-permute-start.20 = (bf16[2,256,2048]{2,1,0:T(8,128)(2,1)}, bf16[2,256,2048]{2,1,0:T(8,128)(2,1)}, u32[]{:S(2)}, u32[]{:S(2)}) collective-permute-start(bf16[2,256,2048]{2,1,0:T(8,128)(2,1)} %bitcast.42), channel_id=1, source_target_pairs={{0,2},{1,3},{2,0},{3,1},{4,6},{5,7},{6,4},{7,5}} | collective-permute-start | bytes 6291464 | tf_op jit(solution)/shard_map/ppermute | solution.py:684
  343.1 134.6 %copy-start = (bf16[256,2048]{1,0:T(8,128)(2,1)}, bf16[256,2048]{1,0:T(8,128)(2,1)S(1)}, u32[]{:S(2)}) copy-start(bf16[256,2048]{1,0:T(8,128)(2,1)S(1)} %collective-permute-done.26.b_ref) | copy-start | bytes 3145732
  343.1 45.1 %collective-permute-start.21 = (bf16[2,256,2048]{2,1,0:T(8,128)(2,1)}, bf16[2,256,2048]{2,1,0:T(8,128)(2,1)}, u32[]{:S(2)}, u32[]{:S(2)}) collective-permute-start(bf16[2,256,2048]{2,1,0:T(8,128)(2,1)} %bitcast.43), channel_id=1, source_target_pairs={{0,1},{1,0},{2,3},{3,2},{4,5},{5,4},{6,7},{7,6}} | collective-permute-start | bytes 6291464 | tf_op jit(solution)/shard_map/ppermute | solution.py:681
  343.1 142.5 %copy-start.1 = (bf16[256,2048]{1,0:T(8,128)(2,1)}, bf16[256,2048]{1,0:T(8,128)(2,1)S(1)}, u32[]{:S(2)}) copy-start(bf16[256,2048]{1,0:T(8,128)(2,1)S(1)} %collective-permute-done.27.c_ref) | copy-start | bytes 3145732
  343.1 90.0 %collective-permute-start.17 = (bf16[2,256,2048]{2,1,0:T(8,128)(2,1)}, bf16[2,256,2048]{2,1,0:T(8,128)(2,1)}, u32[]{:S(2)}, u32[]{:S(2)}) collective-permute-start(bf16[2,256,2048]{2,1,0:T(8,128)(2,1)} %bitcast.39), channel_id=1, source_target_pairs={{0,2},{1,3},{2,0},{3,1},{4,6},{5,7},{6,4},{7,5}} | collective-permute-start | bytes 6291464 | tf_op jit(solution)/shard_map/ppermute | solution.py:684
  343.1 133.5 %collective-permute-start.14 = (bf16[2,256,2048]{2,1,0:T(8,128)(2,1)}, bf16[2,256,2048]{2,1,0:T(8,128)(2,1)}, u32[]{:S(2)}, u32[]{:S(2)}) collective-permute-start(bf16[2,256,2048]{2,1,0:T(8,128)(2,1)} %bitcast.36), channel_id=1, source_target_pairs={{0,2},{1,3},{2,0},{3,1},{4,6},{5,7},{6,4},{7,5}} | collective-permute-start | bytes 6291464 | tf_op jit(solution)/shard_map/ppermute | solution.py:684
  345.1 132.5 %collective-permute-start.11 = (bf16[2,2048,256]{2,1,0:T(8,128)(2,1)}, bf16[2,2048,256]{2,1,0:T(8,128)(2,1)}, u32[]{:S(2)}, u32[]{:S(2)}) collective-permute-start(bf16[2,2048,256]{2,1,0:T(8,128)(2,1)} %get-tuple-element.41.refs_3_), channel_id=1, source_target_pairs={{0,1},{1,0},{2,3},{3,2},{4,5},{5,4},{6,7},{7,6}} | collective-permute-start | bytes 6291464 | tf_op jit(solution)/shard_map/ppermute | solution.py:681
  388.1 88.5 %collective-permute-start.13 = (bf16[2048,256]{1,0:T(8,128)(2,1)}, bf16[2048,256]{1,0:T(8,128)(2,1)S(1)}, u32[]{:S(2)}, u32[]{:S(2)}) collective-permute-start(bf16[2048,256]{1,0:T(8,128)(2,1)} %get-tuple-element.46.refs_8_), channel_id=1, source_target_pairs={{0,1},{1,0},{2,3},{3,2},{4,5},{5,4},{6,7},{7,6}} | collective-permute-start | bytes 3145736 | tf_op jit(solution)/shard_map/ppermute | solution.py:681
  388.1 90.1 %collective-permute-start.10 = (bf16[2,2048,256]{2,1,0:T(8,128)(2,1)}, bf16[2,2048,256]{2,1,0:T(8,128)(2,1)S(1)}, u32[]{:S(2)}, u32[]{:S(2)}) collective-permute-start(bf16[2,2048,256]{2,1,0:T(8,128)(2,1)} %get-tuple-element.40.refs_2_), channel_id=1, source_target_pairs={{0,1},{1,0},{2,3},{3,2},{4,5},{5,4},{6,7},{7,6}} | collective-permute-start | bytes 6291464 | tf_op jit(solution)/shard_map/ppermute | solution.py:681
  433.1 45.2 %collective-permute-start.9 = (bf16[2,2048,256]{2,1,0:T(8,128)(2,1)}, bf16[2,2048,256]{2,1,0:T(8,128)(2,1)S(1)}, u32[]{:S(2)}, u32[]{:S(2)}) collective-permute-start(bf16[2,2048,256]{2,1,0:T(8,128)(2,1)} %get-tuple-element.39.refs_1_), channel_id=1, source_target_pairs={{0,1},{1,0},{2,3},{3,2},{4,5},{5,4},{6,7},{7,6}} | collective-permute-start | bytes 6291464 | tf_op jit(solution)/shard_map/ppermute | solution.py:681
  476.7 4.4 collective-permute-start.8
  476.7 9.8 %collective-permute-start.25 = (bf16[2,256,2048]{2,1,0:T(8,128)(2,1)}, bf16[2,256,2048]{2,1,0:T(8,128)(2,1)}, u32[]{:S(2)}, u32[]{:S(2)}) collective-permute-start(bf16[2,256,2048]{2,1,0:T(8,128)(2,1)} %collective-permute-done.23.b_ref), channel_id=1, source_target_pairs={{0,1},{1,0},{2,3},{3,2},{4,5},{5,4},{6,7},{7,6}} | collective-permute-start | bytes 6291464 | tf_op jit(solution)/shard_map/ppermute | solution.py:681
  477.7 7.8 %collective-permute-start.28 = (bf16[256,2048]{1,0:T(8,128)(2,1)S(1)}, bf16[256,2048]{1,0:T(8,128)(2,1)S(1)}, u32[]{:S(2)}, u32[]{:S(2)}) collective-permute-start(bf16[256,2048]{1,0:T(8,128)(2,1)S(1)} %collective-permute-done.26.b_ref), channel_id=1, source_target_pairs={{0,1},{1,0},{2,3},{3,2},{4,5},{5,4},{6,7},{7,6}} | collective-permute-start | bytes 3145736 | tf_op jit(solution)/shard_map/ppermute | solution.py:681
  478.2 54.3 %collective-permute-start.22 = (bf16[2,256,2048]{2,1,0:T(8,128)(2,1)}, bf16[2,256,2048]{2,1,0:T(8,128)(2,1)}, u32[]{:S(2)}, u32[]{:S(2)}) collective-permute-start(bf16[2,256,2048]{2,1,0:T(8,128)(2,1)} %collective-permute-done.20.b_ref), channel_id=1, source_target_pairs={{0,1},{1,0},{2,3},{3,2},{4,5},{5,4},{6,7},{7,6}} | collective-permute-start | bytes 6291464 | tf_op jit(solution)/shard_map/ppermute | solution.py:681
  478.2 64.1 %collective-permute-start.18 = (bf16[2,256,2048]{2,1,0:T(8,128)(2,1)}, bf16[2,256,2048]{2,1,0:T(8,128)(2,1)}, u32[]{:S(2)}, u32[]{:S(2)}) collective-permute-start(bf16[2,256,2048]{2,1,0:T(8,128)(2,1)} %bitcast.40), channel_id=1, source_target_pairs={{0,1},{1,0},{2,3},{3,2},{4,5},{5,4},{6,7},{7,6}} | collective-permute-start | bytes 6291464 | tf_op jit(solution)/shard_map/ppermute | solution.py:681
  481.0 61.3 %collective-permute-start.19 = (bf16[2,256,2048]{2,1,0:T(8,128)(2,1)}, bf16[2,256,2048]{2,1,0:T(8,128)(2,1)}, u32[]{:S(2)}, u32[]{:S(2)}) collective-permute-start(bf16[2,256,2048]{2,1,0:T(8,128)(2,1)} %collective-permute-done.17.b_ref), channel_id=1, source_target_pairs={{0,1},{1,0},{2,3},{3,2},{4,5},{5,4},{6,7},{7,6}} | collective-permute-start | bytes 6291464 | tf_op jit(solution)/shard_map/ppermute | solution.py:681
  485.5 66.7 %collective-permute-start.15 = (bf16[2,256,2048]{2,1,0:T(8,128)(2,1)}, bf16[2,256,2048]{2,1,0:T(8,128)(2,1)}, u32[]{:S(2)}, u32[]{:S(2)}) collective-permute-start(bf16[2,256,2048]{2,1,0:T(8,128)(2,1)} %bitcast.37), channel_id=1, source_target_pairs={{0,1},{1,0},{2,3},{3,2},{4,5},{5,4},{6,7},{7,6}} | collective-permute-start | bytes 6291464 | tf_op jit(solution)/shard_map/ppermute | solution.py:681
  486.5 65.7 %collective-permute-start.16 = (bf16[2,256,2048]{2,1,0:T(8,128)(2,1)}, bf16[2,256,2048]{2,1,0:T(8,128)(2,1)}, u32[]{:S(2)}, u32[]{:S(2)}) collective-permute-start(bf16[2,256,2048]{2,1,0:T(8,128)(2,1)} %collective-permute-done.14.b_ref), channel_id=1, source_target_pairs={{0,1},{1,0},{2,3},{3,2},{4,5},{5,4},{6,7},{7,6}} | collective-permute-start | bytes 6291464 | tf_op jit(solution)/shard_map/ppermute | solution.py:681
  (5 other events, 24.1 us)

commit v5 on v4

--- a/solution.py
+++ b/solution.py
@@ -79,104 +79,161 @@
     return pl.ds(pl.multiple_of(index * size, size), size)
 
 
-def qkv_kernel(s_ref, x_ref, wq_ref, wk_ref, wv_ref, tab_ref, *rest):
+def qkv_kernel(s_ref, x_ref, wk_ref, wv_ref, wq_ref, tab_ref, *rest):
     kv_ref, q_ref, w_s = rest[-3:]
 
     @pl.when(pl.program_id(0) == 0)
     def _():
         w_s[:, :HEAD] = wk_ref[...]
-        w_s[:, HEAD:] = wv_ref[...]
-
-    x = x_ref[...]
+        w_s[:, HEAD:2 * HEAD] = wv_ref[...]
+        w_s[:, 2 * HEAD:] = wq_ref[...]
+
+    out = dot_nn(x_ref[...], w_s[...])
     cos_t, sin_t = spread_table(tab_ref[...])
-    kv = dot_nn(x, w_s[...])
-    k = kv[:, :HEAD]
-    kv_ref[:, :HEAD] = (k * cos_t + swap_halves(k) * sin_t).astype(BF)
-    kv_ref[:, HEAD:] = kv[:, HEAD:].astype(BF)
-    step = 4 * HEAD
-    for n in range(wq_ref.shape[1] // step):
-        q = dot_nn(x, wq_ref[:, n * step:(n + 1) * step])
-        for h in range(step // HEAD):
-            part = q[:, h * HEAD:(h + 1) * HEAD]
-            at = n * step + h * HEAD
-            q_ref[:, at:at + HEAD] = (part * cos_t + swap_halves(part) * sin_t).astype(BF)
+
+    def turned(n):
+        part = out[:, n * HEAD:(n + 1) * HEAD]
+        return (part * cos_t + swap_halves(part) * sin_t).astype(BF)
+
+    kv_ref[:, :HEAD] = turned(0)
+    kv_ref[:, HEAD:] = out[:, HEAD:2 * HEAD].astype(BF)
+    for h in range(PAIR):
+        q_ref[:, h * HEAD:(h + 1) * HEAD] = turned(2 + h)
 
 
 def qkv_proj(sel, x, w_q, w_k, w_v, tab, prev):
     tokens, width = x.shape
-    cols = w_q.shape[1] // 2
-    rows = tokens // 2
+    n = w_q.shape[1] // 2 // WIDE
+    rows = tokens // 4
     extra = [] if prev is None else [prev]
     return pl.pallas_call(
         qkv_kernel,
         grid_spec=pltpu.PrefetchScalarGridSpec(
             num_scalar_prefetch=1,
-            grid=(2,),
+            grid=(4,),
             in_specs=[
                 pl.BlockSpec((rows, width), lambda m, s: (m, 0)),
-                pl.BlockSpec((width, cols), lambda m, s: (0, s[0])),
                 pl.BlockSpec((width, HEAD), lambda m, s: (0, s[0])),
                 pl.BlockSpec((width, HEAD), lambda m, s: (0, s[0])),
+                pl.BlockSpec((width, WIDE), lambda m, s: (0, s[0] * n)),
                 pl.BlockSpec((rows, HEAD), lambda m, s: (m, 0)),
             ] + [pl.BlockSpec(memory_space=pl.ANY)] * len(extra),
             out_specs=[
                 pl.BlockSpec((rows, 2 * HEAD), lambda m, s: (m, 0)),
-                pl.BlockSpec((rows, cols), lambda m, s: (s[1] * 2 + m, 0)),
-            ],
-            scratch_shapes=[pltpu.VMEM((width, 2 * HEAD), BF)],
+                pl.BlockSpec((rows, WIDE), lambda m, s: (s[1] * 4 + m, 0)),
+            ],
+            scratch_shapes=[pltpu.VMEM((width, 2 * HEAD + WIDE), BF)],
         ),
         out_shape=[
             jax.ShapeDtypeStruct((tokens, 2 * HEAD), BF),
-            jax.ShapeDtypeStruct((2 * tokens, cols), BF),
+            jax.ShapeDtypeStruct((2 * tokens, WIDE), BF),
         ],
         input_output_aliases={} if prev is None else {6: 1},
         compiler_params=params(),
-        cost_estimate=cost(2 * tokens * width * (cols + 2 * HEAD), tokens * width * 2 + cols * width * 2),
+        cost_estimate=cost(2 * tokens * width * (WIDE + 2 * HEAD), tokens * width * 2),
         name="qkv_proj",
-    )(sel, x, w_q, w_k, w_v, tab, *extra)
-
-
-def dctx_kernel(s_ref, own_ref, oth_ref, wo_ref, out_ref):
-    def put(ref):
-        step = 4 * HEAD
-        for n in range(wo_ref.shape[0] // step):
-            out_ref[:, n * step:(n + 1) * step] = dot_nt(ref[...], wo_ref[n * step:(n + 1) * step, :]).astype(BF)
-
-    @pl.when(pl.program_id(0) < 2)
-    def _():
-        put(own_ref)
-
-    @pl.when(pl.program_id(0) >= 2)
-    def _():
-        put(oth_ref)
-
-
-def dctx_proj(core, own, oth, w_o):
+    )(sel, x, w_k, w_v, w_q, tab, *extra)
+
+
+def by_half(rows_per_step, width, steps=2):
+    own = pl.BlockSpec((rows_per_step, width), lambda m, s: (jnp.minimum(m, steps - 1), 0))
+    oth = pl.BlockSpec((rows_per_step, width), lambda m, s: (jnp.maximum(m - steps, 0), 0))
+
+    def place(m, s):
+        far = m // steps
+        return (s[0] + far - 2 * s[0] * far) * steps + m % steps
+
+    return own, oth, place
+
+
+def on_half(put, own_refs, oth_refs, steps=2):
+    @pl.when(pl.program_id(0) < steps)
+    def _():
+        put(*own_refs)
+
+    @pl.when(pl.program_id(0) >= steps)
+    def _():
+        put(*oth_refs)
+
+
+def q_rest_kernel(n, s_ref, own_ref, oth_ref, tab_own, tab_oth, *rest):
+    w_refs, (out_ref, w_s) = rest[:n], rest[n:]
+
+    @pl.when(pl.program_id(0) == 0)
+    def _():
+        for r in range(n):
+            w_s[:, r * WIDE:(r + 1) * WIDE] = w_refs[r][...]
+
+    def put(ref, tab_ref):
+        cos_t, sin_t = spread_table(tab_ref[...])
+        q = dot_nn(ref[...], w_s[...])
+        for h in range(q.shape[1] // HEAD):
+            part = q[:, h * HEAD:(h + 1) * HEAD]
+            out_ref[:, h * HEAD:(h + 1) * HEAD] = (part * cos_t + swap_halves(part) * sin_t).astype(BF)
+
+    on_half(put, (own_ref, tab_own), (oth_ref, tab_oth))
+
+
+def q_rest(core, own, oth, tab_own, tab_oth, w_q):
     tokens, width = own.shape
-    cols = w_o.shape[0] // 2
+    chunks = w_q.shape[1] // 2 // WIDE
+    n = chunks - 1
     rows = tokens // 2
-
-    def place(m, s):
-        far = m // 2
-        return (s[0] + far - 2 * s[0] * far) * 2 + m % 2
-
-    return pl.pallas_call(
-        dctx_kernel,
+    spec_own, spec_oth, place = by_half(rows, width)
+    t_own, t_oth, _ = by_half(rows, HEAD)
+    return pl.pallas_call(
+        functools.partial(q_rest_kernel, n),
         grid_spec=pltpu.PrefetchScalarGridSpec(
             num_scalar_prefetch=1,
             grid=(4,),
-            in_specs=[
-                pl.BlockSpec((rows, width), lambda m, s: (jnp.minimum(m, 1), 0)),
-                pl.BlockSpec((rows, width), lambda m, s: (jnp.maximum(m - 2, 0), 0)),
-                pl.BlockSpec((cols, width), lambda m, s: (s[0], 0)),
-            ],
-            out_specs=pl.BlockSpec((rows, cols), lambda m, s: (place(m, s), 0)),
-        ),
-        out_shape=jax.ShapeDtypeStruct((2 * tokens, cols), BF),
-        compiler_params=params(),
-        cost_estimate=cost(4 * tokens * width * cols, tokens * width * 4 + cols * width * 2),
+            in_specs=[spec_own, spec_oth, t_own, t_oth] + [
+                pl.BlockSpec((width, WIDE), lambda m, s, r=r: (0, s[0] * chunks + 1 + r)) for r in range(n)
+            ],
+            out_specs=pl.BlockSpec((rows, n * WIDE), lambda m, s: (place(m, s), 0)),
+            scratch_shapes=[pltpu.VMEM((width, n * WIDE), BF)],
+        ),
+        out_shape=jax.ShapeDtypeStruct((2 * tokens, n * WIDE), BF),
+        compiler_params=params(),
+        cost_estimate=cost(4 * tokens * width * n * WIDE, tokens * width * 4),
+        name="q_rest",
+    )(core, own, oth, tab_own, tab_oth, *([w_q] * n))
+
+
+def dctx_kernel(n, s_ref, own_ref, oth_ref, *rest):
+    w_refs, (out_ref, w_s) = rest[:n], rest[n:]
+
+    @pl.when(pl.program_id(0) == 0)
+    def _():
+        for r in range(n):
+            w_s[r * WIDE:(r + 1) * WIDE, :] = w_refs[r][...]
+
+    def put(ref):
+        out_ref[...] = dot_nt(ref[...], w_s[...]).astype(BF)
+
+    on_half(put, (own_ref,), (oth_ref,))
+
+
+def dctx_proj(core, own, oth, w_o, first, n):
+    tokens, width = own.shape
+    chunks = w_o.shape[0] // 2 // WIDE
+    rows = tokens // 2
+    spec_own, spec_oth, place = by_half(rows, width)
+    return pl.pallas_call(
+        functools.partial(dctx_kernel, n),
+        grid_spec=pltpu.PrefetchScalarGridSpec(
+            num_scalar_prefetch=1,
+            grid=(4,),
+            in_specs=[spec_own, spec_oth] + [
+                pl.BlockSpec((WIDE, width), lambda m, s, r=r: (s[0] * chunks + first + r, 0)) for r in range(n)
+            ],
+            out_specs=pl.BlockSpec((rows, n * WIDE), lambda m, s: (place(m, s), 0)),
+            scratch_shapes=[pltpu.VMEM((n * WIDE, width), BF)],
+        ),
+        out_shape=jax.ShapeDtypeStruct((2 * tokens, n * WIDE), BF),
+        compiler_params=params(),
+        cost_estimate=cost(4 * tokens * width * n * WIDE, tokens * width * 4),
         name="dctx_proj",
-    )(core, own, oth, w_o)
+    )(core, own, oth, *([w_o] * n))
 
 
 def attn_kernel(
@@ -700,16 +757,18 @@
         g_oth = near(grad_out)
         tab_own = rope_table(positions)
         tab_oth = near(tab_own)
-        kv_own, q = qkv_proj(sel_own, hidden, w_q, w_k, w_v, tab_own, None)
+        kv_own, q_first = qkv_proj(sel_own, hidden, w_q, w_k, w_v, tab_own, None)
         kvp_own = lax.ppermute(kv_own, "sp", down_perm)
 
         def in_order(own, oth):
             return jnp.where(core_id == 0, jnp.concatenate([own, oth]), jnp.concatenate([oth, own]))
 
         doc_chip, doc_far = in_order(doc_ids, doc_oth), in_order(doc_far, doc_far_oth)
-        kv_oth, q = qkv_proj(sel_oth, x_oth, w_q, w_k, w_v, tab_oth, q)
+        kv_oth, q_first = qkv_proj(sel_oth, x_oth, w_q, w_k, w_v, tab_oth, q_first)
         kvp_oth = lax.ppermute(kv_oth, "sp", down_perm)
-        dctx = dctx_proj(core, grad_out, g_oth, w_o)
+        dctx_first = dctx_proj(core, grad_out, g_oth, w_o, 0, 1)
+        q_more = q_rest(core, hidden, x_oth, tab_own, tab_oth, w_q)
+        dctx_more = dctx_proj(core, grad_out, g_oth, w_o, 1, n_chunks - 1)
 
         heads_doc = doc_chip[::BQ]
         lo = jnp.sum(doc_chip[None, :] < heads_doc[:, None], axis=1, dtype=jnp.int32)
@@ -723,7 +782,7 @@
         acts, acts_oth, dkvs, sums = [], [], [], None
         for j in range(n_chunks):
             act, part, dkv = attention(
-                j, core, lo, n_blocks, q, dctx, kdoc, (tab_own, tab_oth), (kvp_own, kvp_oth), (kv_own, kv_oth),
+                max(j - 1, 0), core, lo, n_blocks, q_more if j else q_first, dctx_more if j else dctx_first, kdoc, (tab_own, tab_oth), (kvp_own, kvp_oth), (kv_own, kv_oth),
                 (hidden, x_oth), (grad_out, g_oth),
             )
             part = part.reshape(2, WIDE, -1)

time: 563 us -> 574 us (1.020)
  Pallas kernels: 267 us -> 277 us
    pallas_call x1 -> x3, Pallas kernels: 14.2 us -> 31.9 us  [the longest x2 19.2 us: dctx_proj(): pl.pallas_call(functools.partial(dctx_kernel, n), grid_spec=pltpu.Prefetc...]
    pallas_call x2, Pallas kernels: 22.5 us -> 15.1 us  [qkv_proj(): pl.pallas_call(qkv_kernel, grid_spec=pltpu.PrefetchScalarGridSpec(num_sca...]
  transfers between devices with their start and end apart: 29 -> 29, of which waited for: 7 -> 7; matrix products, arithmetic and copies ran while one was open for 1% -> 1% of each run, Pallas kernels for 20% -> 22%
where the time goes in v5:
time: 574 us; the launch traced here: 572 us
  Pallas kernels  277 us (48%)
  waiting for transfers between devices  214 us (37%)
  starting transfers between devices  69.2 us (12%)
  other arithmetic  8.46 us (1%)
    ppermute x6, waiting for transfers between devices, far(): return lax.ppermute(v, 'sp', far_perm)  185 us
    pallas_call x4, Pallas kernels, attention(): pl.pallas_call(attn_kernel, grid_spec=pltpu.PrefetchScalarGridSpec(num_sc...  143 us
    ppermute x6, starting transfers between devices, far(): return lax.ppermute(v, 'sp', far_perm)  56.3 us
    pallas_call x4, Pallas kernels, combine(): pl.pallas_call(combine_kernel, grid_spec=pltpu.PrefetchScalarGridSpec(num...  39.4 us
    ppermute x1, waiting for transfers between devices, device_step(): dkv_far = lax.ppermute(dkv_up, 'sp', up_perm)  23.1 us
    pallas_call x2, Pallas kernels, dctx_proj(): pl.pallas_call(functools.partial(dctx_kernel, n), grid_spec=pltpu.Prefetc...  19.2 us
    pallas_call x1, Pallas kernels, grad_hidden(): pl.pallas_call(functools.partial(hidden_kernel, n), grid_spec=pltpu.Prefe...  17 us
    pallas_call x2, Pallas kernels, qkv_proj(): pl.pallas_call(qkv_kernel, grid_spec=pltpu.PrefetchScalarGridSpec(num_sca...  15.1 us
  transfers between devices with their start and end apart: 29, of which 7 were waited for; matrix products, arithmetic and copies ran while one was open for 1% of the time, Pallas kernels for 22%

profile of v5, /device:TPU:0, one launch (start us, length us, event | category | flops | bytes accessed | tf_op | source)
XLA Modules:
  0.0 572.2 jit_solution(2886938078903987990)
XLA Ops:
  2.0 2.5 collective-permute-start.1
  8.9 7.6 %qkv_proj.2 = (bf16[1024,256]{1,0:T(8,128)(2,1)}, bf16[2048,256]{1,0:T(8,128)(2,1)}) custom-call(s32[2]{0:T(128)} %pad_add_fusion.2.s_ref, bf16[1024,2048]{1,0:T(8,128)(2,1)} %x_own.9, bf16[2048,256]{1,0:T(8,128)(2,1)} %refs_11_.1, bf16[2048,256]{1,0:T(8,128)(2,1)} %refs_12_.1, bf16[2048,2048]{1,0:T(8,128)(2,1)} %refs_10_.1, ...), custom_call_target="tpu_custom_call" | custom-call | flops 2147483648 | bytes 4194304 | tf_op jit(solution)/shard_map/qkv_proj/pallas_call | solution.py:109
  17.3 4.6 collective-permute-start.6
  23.3 7.5 %qkv_proj.3 = (bf16[1024,256]{1,0:T(8,128)(2,1)}, bf16[2048,256]{1,0:T(8,128)(2,1)}) custom-call(s32[2]{0:T(128)} %pad_add_fusion.1.s_ref, bf16[1024,2048]{1,0:T(8,128)(2,1)} %collective-permute-done.3.x_ref.x_oth.oth_ref, bf16[2048,256]{1,0:T(8,128)(2,1)} %refs_11_.1, bf16[2048,256]{1,0:T(8,128)(2,1)} %refs_12_.1, ...), custom_call_target="tpu_custom_call", output_to_operand_aliasing={{1}: (6, {})} | custom-call | flops 2147483648 | bytes 4194304 | tf_op jit(solution)/shard_map/qkv_proj/pallas_call | solution.py:109
  30.8 2.1 collective-permute-start.7
  32.9 12.7 %q_rest.1.q_ref = bf16[2048,768]{1,0:T(8,128)(2,1)} custom-call(s32[1]{0:T(128)} %bitcast.s_ref.core_ref, bf16[1024,2048]{1,0:T(8,128)(2,1)} %x_own.9, bf16[1024,2048]{1,0:T(8,128)(2,1)} %collective-permute-done.3.x_ref.x_oth.oth_ref, f32[1024,128]{1,0:T(8,128)} %pad_maximum_fusion.tab_ref.tab_own.refs_5_, ...), custom_call_target="tpu_custom_call" | custom-call | flops 6442450944 | bytes 8388608 | tf_op jit(solution)/shard_map/q_rest/pallas_call | solution.py:184
  45.6 7.3 %dctx_proj.2.do_ref = bf16[2048,256]{1,0:T(8,128)(2,1)} custom-call(s32[1]{0:T(128)} %bitcast.s_ref.core_ref, bf16[1024,2048]{1,0:T(8,128)(2,1)} %g_own.7, bf16[1024,2048]{1,0:T(8,128)(2,1)} %collective-permute-done.5.oth_ref.g_oth, bf16[2048,2048]{1,0:T(8,128)(2,1)} %refs_8_.1), custom_call_target="tpu_custom_call" | custom-call | flops 2147483648 | bytes 8388608 | tf_op jit(solution)/shard_map/dctx_proj/pallas_call | solution.py:221
  53.0 11.8 %dctx_proj.3.do_ref = bf16[2048,768]{1,0:T(8,128)(2,1)} custom-call(s32[1]{0:T(128)} %bitcast.s_ref.core_ref, bf16[1024,2048]{1,0:T(8,128)(2,1)} %g_own.7, bf16[1024,2048]{1,0:T(8,128)(2,1)} %collective-permute-done.5.oth_ref.g_oth, bf16[2048,2048]{1,0:T(8,128)(2,1)} %refs_8_.1, bf16[2048,2048]{1,0:T(8,128)(2,1)} %refs_8_.1, bf16[2048,2048]{1,0:T(8,128)(2,1)} %refs_8_.1), custom_call_target="tpu_custom_call" | custom-call | flops 6442450944 | bytes 8388608 | tf_op jit(solution)/shard_map/dctx_proj/pallas_call | solution.py:221
  64.8 35.7 %attention.7 = (bf16[2,2048,256]{2,1,0:T(8,128)(2,1)}, bf16[512,2048]{1,0:T(8,128)(2,1)}, bf16[512,2048]{1,0:T(8,128)(2,1)}) custom-call(s32[1]{0:T(128)} %bitcast.s_ref.core_ref, s32[4]{0:T(128)} %get-tuple-element.65.lo_ref, s32[4]{0:T(128)} %get-tuple-element.64.nb_ref, bf16[2048,768]{1,0:T(8,128)(2,1)} %q_rest.1.q_ref, ...), custom_call_target="tpu_custom_call" | custom-call | flops 17179869184 | bytes 12582912 | tf_op jit(solution)/shard_map/attention/pallas_call | solution.py:432
  100.5 35.9 %attention.6 = (bf16[2,2048,256]{2,1,0:T(8,128)(2,1)}, bf16[512,2048]{1,0:T(8,128)(2,1)}, bf16[512,2048]{1,0:T(8,128)(2,1)}) custom-call(s32[1]{0:T(128)} %bitcast.s_ref.core_ref, s32[4]{0:T(128)} %get-tuple-element.65.lo_ref, s32[4]{0:T(128)} %get-tuple-element.64.nb_ref, bf16[2048,768]{1,0:T(8,128)(2,1)} %q_rest.1.q_ref, ...), custom_call_target="tpu_custom_call" | custom-call | flops 17179869184 | bytes 12582912 | tf_op jit(solution)/shard_map/attention/pallas_call | solution.py:432
  136.4 35.7 %attention.5 = (bf16[2,2048,256]{2,1,0:T(8,128)(2,1)}, bf16[512,2048]{1,0:T(8,128)(2,1)}, bf16[512,2048]{1,0:T(8,128)(2,1)}) custom-call(s32[1]{0:T(128)} %bitcast.s_ref.core_ref, s32[4]{0:T(128)} %get-tuple-element.65.lo_ref, s32[4]{0:T(128)} %get-tuple-element.64.nb_ref, bf16[2048,768]{1,0:T(8,128)(2,1)} %q_rest.1.q_ref, ...), custom_call_target="tpu_custom_call" | custom-call | flops 17179869184 | bytes 12582912 | tf_op jit(solution)/shard_map/attention/pallas_call | solution.py:432
  172.1 35.7 %attention.4 = (bf16[2,2048,256]{2,1,0:T(8,128)(2,1)}, bf16[512,2048]{1,0:T(8,128)(2,1)}, bf16[512,2048]{1,0:T(8,128)(2,1)}) custom-call(s32[1]{0:T(128)} %bitcast.s_ref.core_ref, s32[4]{0:T(128)} %get-tuple-element.65.lo_ref, s32[4]{0:T(128)} %get-tuple-element.64.nb_ref, bf16[2048,256]{1,0:T(8,128)(2,1)} %get-tuple-element.35.q_ref, ...), custom_call_target="tpu_custom_call" | custom-call | flops 17179869184 | bytes 12582912 | tf_op jit(solution)/shard_map/attention/pallas_call | solution.py:432
  207.8 2.9 fusion
  212.2 49.8 %collective-permute-start.23 = (bf16[2,256,2048]{2,1,0:T(8,128)(2,1)}, bf16[2,256,2048]{2,1,0:T(8,128)(2,1)}, u32[]{:S(2)}, u32[]{:S(2)}) collective-permute-start(bf16[2,256,2048]{2,1,0:T(8,128)(2,1)} %bitcast.10.a_ref), channel_id=1, source_target_pairs={{0,2},{1,3},{2,0},{3,1},{4,6},{5,7},{6,4},{7,5}} | collective-permute-start | bytes 6291464 | tf_op jit(solution)/shard_map/ppermute | solution.py:741
  262.0 23.1 %collective-permute-done.12.refs_4_ = bf16[2,128,2048]{2,1,0:T(8,128)(2,1)} collective-permute-done((bf16[2,128,2048]{2,1,0:T(8,128)(2,1)S(1)}, bf16[2,128,2048]{2,1,0:T(8,128)(2,1)}, u32[]{:S(2)}, u32[]{:S(2)}) %collective-permute-start.12) | collective-permute-done | bytes 1048608 | tf_op jit(solution)/shard_map/ppermute | solution.py:793
  285.1 5.3 kv_finish.1
  290.4 6.6 %kvgrad.1.a_ref = bf16[256,2048]{1,0:T(8,128)(2,1)} custom-call(s32[1]{0:T(128)} %bitcast.s_ref.core_ref, bf16[256,2048]{1,0:T(8,128)(2,1)} %get-tuple-element.58.dkvt_ref, bf16[1024,2048]{1,0:T(8,128)(2,1)} %x_own.9, bf16[1024,2048]{1,0:T(8,128)(2,1)} %collective-permute-done.3.x_ref.x_oth.oth_ref), custom_call_target="tpu_custom_call" | custom-call | flops 2147483648 | bytes 8388608 | tf_op jit(solution)/shard_map/kvgrad/pallas_call | solution.py:549
  297.6 2.0 collective-permute-start.20
  299.6 52.8 %collective-permute-done.26.b_ref = bf16[256,2048]{1,0:T(8,128)(2,1)S(1)} collective-permute-done((bf16[256,2048]{1,0:T(8,128)(2,1)}, bf16[256,2048]{1,0:T(8,128)(2,1)S(1)}, u32[]{:S(2)}, u32[]{:S(2)}) %collective-permute-start.26) | collective-permute-done | bytes 1048608 | tf_op jit(solution)/shard_map/ppermute | solution.py:741
  352.5 2.0 collective-permute-start.14
  354.5 43.0 %collective-permute-done.20.b_ref = bf16[2,256,2048]{2,1,0:T(8,128)(2,1)} collective-permute-done((bf16[2,256,2048]{2,1,0:T(8,128)(2,1)}, bf16[2,256,2048]{2,1,0:T(8,128)(2,1)}, u32[]{:S(2)}, u32[]{:S(2)}) %collective-permute-start.20) | collective-permute-done | bytes 2097184 | tf_op jit(solution)/shard_map/ppermute | solution.py:741
  398.0 44.4 %collective-permute-done.17.b_ref = bf16[2,256,2048]{2,1,0:T(8,128)(2,1)} collective-permute-done((bf16[2,256,2048]{2,1,0:T(8,128)(2,1)}, bf16[2,256,2048]{2,1,0:T(8,128)(2,1)}, u32[]{:S(2)}, u32[]{:S(2)}) %collective-permute-start.17) | collective-permute-done | bytes 2097184 | tf_op jit(solution)/shard_map/ppermute | solution.py:741
  442.4 44.4 %collective-permute-done.14.b_ref = bf16[2,256,2048]{2,1,0:T(8,128)(2,1)} collective-permute-done((bf16[2,256,2048]{2,1,0:T(8,128)(2,1)}, bf16[2,256,2048]{2,1,0:T(8,128)(2,1)}, u32[]{:S(2)}, u32[]{:S(2)}) %collective-permute-start.14) | collective-permute-done | bytes 2097184 | tf_op jit(solution)/shard_map/ppermute | solution.py:741
  488.9 2.3 collective-permute-done.8.refs_4_
  491.3 4.4 collective-permute-done.28.d_ref
  496.9 13.9 %attn_out.1 = bf16[1024,2048]{1,0:T(8,128)(2,1)} custom-call(s32[1]{0:T(128)} %bitcast.s_ref.core_ref, bf16[2,2048,256]{2,1,0:T(8,128)(2,1)} %get-tuple-element.38.refs_0_, bf16[2,2048,256]{2,1,0:T(8,128)(2,1)} %get-tuple-element.39.refs_1_, bf16[2,2048,256]{2,1,0:T(8,128)(2,1)} %get-tuple-element.40.refs_2_, ...), custom_call_target="tpu_custom_call" | custom-call | flops 8589934592 | bytes 16777216 | tf_op jit(solution)/shard_map/attn_out/pallas_call | solution.py:662
  510.8 17.0 %grad_hidden.1 = bf16[1024,2048]{1,0:T(8,128)(2,1)} custom-call(s32[1]{0:T(128)} %bitcast.s_ref.core_ref, bf16[2,2048,256]{2,1,0:T(8,128)(2,1)} %get-tuple-element.38.refs_0_, bf16[2,2048,256]{2,1,0:T(8,128)(2,1)} %get-tuple-element.39.refs_1_, bf16[2,2048,256]{2,1,0:T(8,128)(2,1)} %get-tuple-element.40.refs_2_, ...), custom_call_target="tpu_custom_call" | custom-call | flops 10737418240 | bytes 16777216 | tf_op jit(solution)/shard_map/grad_hidden/pallas_call | solution.py:703
  527.7 5.1 kv_combine.1
  532.8 9.8 %combine.4 = (f32[2048,2048]{1,0:T(8,128)}, f32[2048,2048]{1,0:T(8,128)}) custom-call(s32[1]{0:T(128)} %bitcast.s_ref.core_ref, bf16[2,256,2048]{2,1,0:T(8,128)(2,1)} %bitcast.10.a_ref, bf16[2,256,2048]{2,1,0:T(8,128)(2,1)} %collective-permute-done.23.b_ref, bf16[2,256,2048]{2,1,0:T(8,128)(2,1)} %collective-permute-done.24.c_ref, ...), custom_call_target="tpu_custom_call" | custom-call | flops 536870912 | bytes 16777216 | tf_op jit(solution)/shard_map/combine/pallas_call | solution.py:620
  542.6 9.9 %combine.5 = (f32[2048,2048]{1,0:T(8,128)}, f32[2048,2048]{1,0:T(8,128)}) custom-call(s32[1]{0:T(128)} %bitcast.s_ref.core_ref, bf16[2,256,2048]{2,1,0:T(8,128)(2,1)} %bitcast.44, bf16[2,256,2048]{2,1,0:T(8,128)(2,1)} %collective-permute-done.20.b_ref, ...), custom_call_target="tpu_custom_call", output_to_operand_aliasing={{0}: (5, {}), {1}: (6, {})} | custom-call | flops 536870912 | bytes 16777216 | tf_op jit(solution)/shard_map/combine/pallas_call | solution.py:620
  552.5 9.9 %combine.6 = (f32[2048,2048]{1,0:T(8,128)}, f32[2048,2048]{1,0:T(8,128)}) custom-call(s32[1]{0:T(128)} %bitcast.s_ref.core_ref, bf16[2,256,2048]{2,1,0:T(8,128)(2,1)} %bitcast.41, bf16[2,256,2048]{2,1,0:T(8,128)(2,1)} %collective-permute-done.17.b_ref, ...), custom_call_target="tpu_custom_call", output_to_operand_aliasing={{0}: (5, {}), {1}: (6, {})} | custom-call | flops 536870912 | bytes 16777216 | tf_op jit(solution)/shard_map/combine/pallas_call | solution.py:620
  562.4 9.9 %combine.7 = (f32[2048,2048]{1,0:T(8,128)}, f32[2048,2048]{1,0:T(8,128)}) custom-call(s32[1]{0:T(128)} %bitcast.s_ref.core_ref, bf16[2,256,2048]{2,1,0:T(8,128)(2,1)} %bitcast.38, bf16[2,256,2048]{2,1,0:T(8,128)(2,1)} %collective-permute-done.14.b_ref, ...), custom_call_target="tpu_custom_call", output_to_operand_aliasing={{0}: (5, {}), {1}: (6, {})} | custom-call | flops 536870912 | bytes 16777216 | tf_op jit(solution)/shard_map/combine/pallas_call | solution.py:620
  (75 shorter events, 13.9 us)
Async XLA Ops:
  0.6 22.7 %collective-permute-start.3 = (bf16[1024,2048]{1,0:T(8,128)(2,1)}, bf16[1024,2048]{1,0:T(8,128)(2,1)}, u32[]{:S(2)}, u32[]{:S(2)}) collective-permute-start(bf16[1024,2048]{1,0:T(8,128)(2,1)} %x_own.9), channel_id=1, source_target_pairs={{0,1},{1,0},{2,3},{3,2},{4,5},{5,4},{6,7},{7,6}} | collective-permute-start | bytes 12582920 | tf_op jit(solution)/shard_map/ppermute | solution.py:738
  1.5 44.1 %collective-permute-start.5 = (bf16[1024,2048]{1,0:T(8,128)(2,1)}, bf16[1024,2048]{1,0:T(8,128)(2,1)}, u32[]{:S(2)}, u32[]{:S(2)}) collective-permute-start(bf16[1024,2048]{1,0:T(8,128)(2,1)} %g_own.7), channel_id=1, source_target_pairs={{0,1},{1,0},{2,3},{3,2},{4,5},{5,4},{6,7},{7,6}} | collective-permute-start | bytes 12582920 | tf_op jit(solution)/shard_map/ppermute | solution.py:738
  1.5 15.6 %collective-permute-start = (s32[1024]{0:T(1024)}, s32[1024]{0:T(1024)S(1)}, u32[]{:S(2)}, u32[]{:S(2)}) collective-permute-start(s32[1024]{0:T(1024)} %param.11), channel_id=1, source_target_pairs={{0,1},{1,0},{2,3},{3,2},{4,5},{5,4},{6,7},{7,6}} | collective-permute-start | bytes 12296 | tf_op jit(solution)/shard_map/ppermute | solution.py:738
  2.0 15.3 %collective-permute-start.1 = (s32[1024]{0:T(1024)}, s32[1024]{0:T(1024)S(1)}, u32[]{:S(2)}, u32[]{:S(2)}) collective-permute-start(s32[1024]{0:T(1024)} %param.11), channel_id=1, source_target_pairs={{0,2},{1,3},{2,0},{3,1},{4,6},{5,7},{6,4},{7,5}} | collective-permute-start | bytes 12296 | tf_op jit(solution)/shard_map/ppermute | solution.py:741
  8.1 15.2 %collective-permute-start.4 = (f32[1024,128]{1,0:T(8,128)}, f32[1024,128]{1,0:T(8,128)}, u32[]{:S(2)}, u32[]{:S(2)}) collective-permute-start(f32[1024,128]{1,0:T(8,128)} %pad_maximum_fusion.tab_ref.tab_own.refs_5_), channel_id=1, source_target_pairs={{0,1},{1,0},{2,3},{3,2},{4,5},{5,4},{6,7},{7,6}} | collective-permute-start | bytes 1572872 | tf_op jit(solution)/shard_map/ppermute | solution.py:738
  17.1 4.8 collective-permute-start.2
  17.3 47.5 %collective-permute-start.6 = (bf16[1024,256]{1,0:T(8,128)(2,1)}, bf16[1024,256]{1,0:T(8,128)(2,1)}, u32[]{:S(2)}, u32[]{:S(2)}) collective-permute-start(bf16[1024,256]{1,0:T(8,128)(2,1)} %get-tuple-element.36.kvc_own), channel_id=1, source_target_pairs={{0,2},{1,3},{4,6},{5,7}} | collective-permute-start | bytes 1572872 | tf_op jit(solution)/shard_map/ppermute | solution.py:761
  30.8 34.0 %collective-permute-start.7 = (bf16[1024,256]{1,0:T(8,128)(2,1)}, bf16[1024,256]{1,0:T(8,128)(2,1)}, u32[]{:S(2)}, u32[]{:S(2)}) collective-permute-start(bf16[1024,256]{1,0:T(8,128)(2,1)} %get-tuple-element.37.kvc_oth), channel_id=1, source_target_pairs={{0,2},{1,3},{4,6},{5,7}} | collective-permute-start | bytes 1572872 | tf_op jit(solution)/shard_map/ppermute | solution.py:768
  210.6 74.5 %collective-permute-start.12 = (bf16[2,128,2048]{2,1,0:T(8,128)(2,1)S(1)}, bf16[2,128,2048]{2,1,0:T(8,128)(2,1)}, u32[]{:S(2)}, u32[]{:S(2)}) collective-permute-start(bf16[2,128,2048]{2,1,0:T(8,128)(2,1)S(1)} %fusion), channel_id=1, source_target_pairs={{2,0},{3,1},{6,4},{7,5}} | collective-permute-start | bytes 3145736 | tf_op jit(solution)/shard_map/ppermute | solution.py:793
  212.2 140.3 %collective-permute-start.23 = (bf16[2,256,2048]{2,1,0:T(8,128)(2,1)}, bf16[2,256,2048]{2,1,0:T(8,128)(2,1)}, u32[]{:S(2)}, u32[]{:S(2)}) collective-permute-start(bf16[2,256,2048]{2,1,0:T(8,128)(2,1)} %bitcast.10.a_ref), channel_id=1, source_target_pairs={{0,2},{1,3},{2,0},{3,1},{4,6},{5,7},{6,4},{7,5}} | collective-permute-start | bytes 6291464 | tf_op jit(solution)/shard_map/ppermute | solution.py:741
  297.1 55.3 %collective-permute-start.26 = (bf16[256,2048]{1,0:T(8,128)(2,1)}, bf16[256,2048]{1,0:T(8,128)(2,1)S(1)}, u32[]{:S(2)}, u32[]{:S(2)}) collective-permute-start(bf16[256,2048]{1,0:T(8,128)(2,1)} %kvgrad.1.a_ref), channel_id=1, source_target_pairs={{0,2},{1,3},{2,0},{3,1},{4,6},{5,7},{6,4},{7,5}} | collective-permute-start | bytes 3145736 | tf_op jit(solution)/shard_map/ppermute | solution.py:741
  297.1 55.3 %collective-permute-start.27 = (bf16[256,2048]{1,0:T(8,128)(2,1)}, bf16[256,2048]{1,0:T(8,128)(2,1)S(1)}, u32[]{:S(2)}, u32[]{:S(2)}) collective-permute-start(bf16[256,2048]{1,0:T(8,128)(2,1)} %kvgrad.1.a_ref), channel_id=1, source_target_pairs={{0,1},{1,0},{2,3},{3,2},{4,5},{5,4},{6,7},{7,6}} | collective-permute-start | bytes 3145736 | tf_op jit(solution)/shard_map/ppermute | solution.py:738
  297.1 57.4 %collective-permute-start.24 = (bf16[2,256,2048]{2,1,0:T(8,128)(2,1)}, bf16[2,256,2048]{2,1,0:T(8,128)(2,1)}, u32[]{:S(2)}, u32[]{:S(2)}) collective-permute-start(bf16[2,256,2048]{2,1,0:T(8,128)(2,1)} %bitcast.10.a_ref), channel_id=1, source_target_pairs={{0,1},{1,0},{2,3},{3,2},{4,5},{5,4},{6,7},{7,6}} | collective-permute-start | bytes 6291464 | tf_op jit(solution)/shard_map/ppermute | solution.py:738
  297.6 99.9 %collective-permute-start.20 = (bf16[2,256,2048]{2,1,0:T(8,128)(2,1)}, bf16[2,256,2048]{2,1,0:T(8,128)(2,1)}, u32[]{:S(2)}, u32[]{:S(2)}) collective-permute-start(bf16[2,256,2048]{2,1,0:T(8,128)(2,1)} %bitcast.42), channel_id=1, source_target_pairs={{0,2},{1,3},{2,0},{3,1},{4,6},{5,7},{6,4},{7,5}} | collective-permute-start | bytes 6291464 | tf_op jit(solution)/shard_map/ppermute | solution.py:741
  352.4 135.4 %copy-start = (bf16[256,2048]{1,0:T(8,128)(2,1)}, bf16[256,2048]{1,0:T(8,128)(2,1)S(1)}, u32[]{:S(2)}) copy-start(bf16[256,2048]{1,0:T(8,128)(2,1)S(1)} %collective-permute-done.26.b_ref) | copy-start | bytes 3145732
  352.4 45.1 %collective-permute-start.21 = (bf16[2,256,2048]{2,1,0:T(8,128)(2,1)}, bf16[2,256,2048]{2,1,0:T(8,128)(2,1)}, u32[]{:S(2)}, u32[]{:S(2)}) collective-permute-start(bf16[2,256,2048]{2,1,0:T(8,128)(2,1)} %bitcast.43), channel_id=1, source_target_pairs={{0,1},{1,0},{2,3},{3,2},{4,5},{5,4},{6,7},{7,6}} | collective-permute-start | bytes 6291464 | tf_op jit(solution)/shard_map/ppermute | solution.py:738
  352.4 143.3 %copy-start.1 = (bf16[256,2048]{1,0:T(8,128)(2,1)}, bf16[256,2048]{1,0:T(8,128)(2,1)S(1)}, u32[]{:S(2)}) copy-start(bf16[256,2048]{1,0:T(8,128)(2,1)S(1)} %collective-permute-done.27.c_ref) | copy-start | bytes 3145732
  352.4 90.0 %collective-permute-start.17 = (bf16[2,256,2048]{2,1,0:T(8,128)(2,1)}, bf16[2,256,2048]{2,1,0:T(8,128)(2,1)}, u32[]{:S(2)}, u32[]{:S(2)}) collective-permute-start(bf16[2,256,2048]{2,1,0:T(8,128)(2,1)} %bitcast.39), channel_id=1, source_target_pairs={{0,2},{1,3},{2,0},{3,1},{4,6},{5,7},{6,4},{7,5}} | collective-permute-start | bytes 6291464 | tf_op jit(solution)/shard_map/ppermute | solution.py:741
  352.5 134.3 %collective-permute-start.14 = (bf16[2,256,2048]{2,1,0:T(8,128)(2,1)}, bf16[2,256,2048]{2,1,0:T(8,128)(2,1)}, u32[]{:S(2)}, u32[]{:S(2)}) collective-permute-start(bf16[2,256,2048]{2,1,0:T(8,128)(2,1)} %bitcast.36), channel_id=1, source_target_pairs={{0,2},{1,3},{2,0},{3,1},{4,6},{5,7},{6,4},{7,5}} | collective-permute-start | bytes 6291464 | tf_op jit(solution)/shard_map/ppermute | solution.py:741
  354.5 133.4 %collective-permute-start.11 = (bf16[2,2048,256]{2,1,0:T(8,128)(2,1)}, bf16[2,2048,256]{2,1,0:T(8,128)(2,1)}, u32[]{:S(2)}, u32[]{:S(2)}) collective-permute-start(bf16[2,2048,256]{2,1,0:T(8,128)(2,1)} %get-tuple-element.41.refs_3_), channel_id=1, source_target_pairs={{0,1},{1,0},{2,3},{3,2},{4,5},{5,4},{6,7},{7,6}} | collective-permute-start | bytes 6291464 | tf_op jit(solution)/shard_map/ppermute | solution.py:738
  397.5 89.4 %collective-permute-start.13 = (bf16[2048,256]{1,0:T(8,128)(2,1)}, bf16[2048,256]{1,0:T(8,128)(2,1)S(1)}, u32[]{:S(2)}, u32[]{:S(2)}) collective-permute-start(bf16[2048,256]{1,0:T(8,128)(2,1)} %get-tuple-element.46.refs_8_), channel_id=1, source_target_pairs={{0,1},{1,0},{2,3},{3,2},{4,5},{5,4},{6,7},{7,6}} | collective-permute-start | bytes 3145736 | tf_op jit(solution)/shard_map/ppermute | solution.py:738
  397.5 90.9 %collective-permute-start.10 = (bf16[2,2048,256]{2,1,0:T(8,128)(2,1)}, bf16[2,2048,256]{2,1,0:T(8,128)(2,1)S(1)}, u32[]{:S(2)}, u32[]{:S(2)}) collective-permute-start(bf16[2,2048,256]{2,1,0:T(8,128)(2,1)} %get-tuple-element.40.refs_2_), channel_id=1, source_target_pairs={{0,1},{1,0},{2,3},{3,2},{4,5},{5,4},{6,7},{7,6}} | collective-permute-start | bytes 6291464 | tf_op jit(solution)/shard_map/ppermute | solution.py:738
  442.4 46.0 %collective-permute-start.9 = (bf16[2,2048,256]{2,1,0:T(8,128)(2,1)}, bf16[2,2048,256]{2,1,0:T(8,128)(2,1)S(1)}, u32[]{:S(2)}, u32[]{:S(2)}) collective-permute-start(bf16[2,2048,256]{2,1,0:T(8,128)(2,1)} %get-tuple-element.39.refs_1_), channel_id=1, source_target_pairs={{0,1},{1,0},{2,3},{3,2},{4,5},{5,4},{6,7},{7,6}} | collective-permute-start | bytes 6291464 | tf_op jit(solution)/shard_map/ppermute | solution.py:738
  486.8 4.4 collective-permute-start.8
  486.8 9.8 %collective-permute-start.25 = (bf16[2,256,2048]{2,1,0:T(8,128)(2,1)}, bf16[2,256,2048]{2,1,0:T(8,128)(2,1)}, u32[]{:S(2)}, u32[]{:S(2)}) collective-permute-start(bf16[2,256,2048]{2,1,0:T(8,128)(2,1)} %collective-permute-done.23.b_ref), channel_id=1, source_target_pairs={{0,1},{1,0},{2,3},{3,2},{4,5},{5,4},{6,7},{7,6}} | collective-permute-start | bytes 6291464 | tf_op jit(solution)/shard_map/ppermute | solution.py:738
  487.8 7.8 %collective-permute-start.28 = (bf16[256,2048]{1,0:T(8,128)(2,1)S(1)}, bf16[256,2048]{1,0:T(8,128)(2,1)S(1)}, u32[]{:S(2)}, u32[]{:S(2)}) collective-permute-start(bf16[256,2048]{1,0:T(8,128)(2,1)S(1)} %collective-permute-done.26.b_ref), channel_id=1, source_target_pairs={{0,1},{1,0},{2,3},{3,2},{4,5},{5,4},{6,7},{7,6}} | collective-permute-start | bytes 3145736 | tf_op jit(solution)/shard_map/ppermute | solution.py:738
  488.4 8.3 %copy-start.4 = (bf16[2,2048,256]{2,1,0:T(8,128)(2,1)}, bf16[2,2048,256]{2,1,0:T(8,128)(2,1)S(1)}, u32[]{:S(2)}) copy-start(bf16[2,2048,256]{2,1,0:T(8,128)(2,1)S(1)} %collective-permute-done.10.refs_6_) | copy-start | bytes 6291460
  488.4 54.3 %collective-permute-start.22 = (bf16[2,256,2048]{2,1,0:T(8,128)(2,1)}, bf16[2,256,2048]{2,1,0:T(8,128)(2,1)}, u32[]{:S(2)}, u32[]{:S(2)}) collective-permute-start(bf16[2,256,2048]{2,1,0:T(8,128)(2,1)} %collective-permute-done.20.b_ref), channel_id=1, source_target_pairs={{0,1},{1,0},{2,3},{3,2},{4,5},{5,4},{6,7},{7,6}} | collective-permute-start | bytes 6291464 | tf_op jit(solution)/shard_map/ppermute | solution.py:738
  488.4 64.1 %collective-permute-start.18 = (bf16[2,256,2048]{2,1,0:T(8,128)(2,1)}, bf16[2,256,2048]{2,1,0:T(8,128)(2,1)}, u32[]{:S(2)}, u32[]{:S(2)}) collective-permute-start(bf16[2,256,2048]{2,1,0:T(8,128)(2,1)} %bitcast.40), channel_id=1, source_target_pairs={{0,1},{1,0},{2,3},{3,2},{4,5},{5,4},{6,7},{7,6}} | collective-permute-start | bytes 6291464 | tf_op jit(solution)/shard_map/ppermute | solution.py:738
  491.2 61.3 %collective-permute-start.19 = (bf16[2,256,2048]{2,1,0:T(8,128)(2,1)}, bf16[2,256,2048]{2,1,0:T(8,128)(2,1)}, u32[]{:S(2)}, u32[]{:S(2)}) collective-permute-start(bf16[2,256,2048]{2,1,0:T(8,128)(2,1)} %collective-permute-done.17.b_ref), channel_id=1, source_target_pairs={{0,1},{1,0},{2,3},{3,2},{4,5},{5,4},{6,7},{7,6}} | collective-permute-start | bytes 6291464 | tf_op jit(solution)/shard_map/ppermute | solution.py:738
  495.7 66.7 %collective-permute-start.15 = (bf16[2,256,2048]{2,1,0:T(8,128)(2,1)}, bf16[2,256,2048]{2,1,0:T(8,128)(2,1)}, u32[]{:S(2)}, u32[]{:S(2)}) collective-permute-start(bf16[2,256,2048]{2,1,0:T(8,128)(2,1)} %bitcast.37), channel_id=1, source_target_pairs={{0,1},{1,0},{2,3},{3,2},{4,5},{5,4},{6,7},{7,6}} | collective-permute-start | bytes 6291464 | tf_op jit(solution)/shard_map/ppermute | solution.py:738
  496.7 65.7 %collective-permute-start.16 = (bf16[2,256,2048]{2,1,0:T(8,128)(2,1)}, bf16[2,256,2048]{2,1,0:T(8,128)(2,1)}, u32[]{:S(2)}, u32[]{:S(2)}) collective-permute-start(bf16[2,256,2048]{2,1,0:T(8,128)(2,1)} %collective-permute-done.14.b_ref), channel_id=1, source_target_pairs={{0,1},{1,0},{2,3},{3,2},{4,5},{5,4},{6,7},{7,6}} | collective-permute-start | bytes 6291464 | tf_op jit(solution)/shard_map/ppermute | solution.py:738
  (5 other events, 23.9 us)

commit v6 on v4

--- a/solution.py
+++ b/solution.py
@@ -13,7 +13,7 @@
 ROPE_LOW = 1.0
 ROPE_HIGH = 4.0
 ROPE_OLD_CTX = 8192.0
-NEG_BIG = -1.0e30
+NEG_BIG = float("-inf")
 SCALE = HEAD ** -0.5
 LOG2E = 1.4426950408889634
 
@@ -21,6 +21,7 @@
 WIDE = PAIR * HEAD
 BQ = 512
 BK = 512
+MIX = 16
 ALIGN = 128
 BF = jnp.bfloat16
 F32 = jnp.float32
@@ -182,7 +183,7 @@
 def attn_kernel(
     core_ref, lo_ref, nb_ref, q_ref, do_ref, kdoc_ref, tab_own, tab_oth, kvp_own, kvp_oth, kvc_own, kvc_oth,
     x_own, x_oth, g_own, g_oth, act_ref, part_ref, dkv_ref,
-    k_s, v_s, s_s, dp_s, m_s, l_s, d_s, qd_s, ctx_s, dq_s, q_s, do_s, qt_s, dot_s, tab_s, dk_s, dv_s,
+    k_s, v_s, s_s, dp_s, m_s, l_s, d_s, qd_s, ahead_s, ctx_s, dq_s, q_s, do_s, qt_s, dot_s, tab_s, dk_s, dv_s,
     x_s, g_s, at_s, w_s, init_sem, row_sem, out_sem,
 ):
     i = pl.program_id(0)
@@ -228,6 +229,11 @@
             dk_s[r, :] = jnp.zeros((16, dk_s.shape[1]), F32)
             dv_s[r, :] = jnp.zeros((16, dv_s.shape[1]), F32)
 
+        def order(r):
+            row = lax.broadcasted_iota(jnp.int32, (16, BK), 0)
+            ahead_s[r, :] = lax.broadcasted_iota(jnp.int32, (16, BK), 1) - row - r.start
+
+        by_rows(BQ, order)
         by_rows(w_s.shape[0], clear)
         by_rows(HEAD, clear_kv)
 
@@ -241,13 +247,18 @@
         for copy in row_copies(x_oth, g_oth):
             copy.start()
 
-    for h in range(PAIR):
-        rows = slice(h * BQ, (h + 1) * BQ)
-        cols = slice(h * HEAD, (h + 1) * HEAD)
-        q_s[rows, :] = q_ref[:, cols]
-        do_s[rows, :] = do_ref[:, cols]
-        qt_s[:, rows] = q_ref[:, cols].T
-        dot_s[:, rows] = do_ref[:, cols].T
+    def mixed(ref):
+        parts = [ref[:, h * HEAD:(h + 1) * HEAD].reshape(BQ // MIX, 1, MIX, HEAD) for h in range(PAIR)]
+        return jnp.concatenate(parts, axis=1).reshape(PAIR * BQ, HEAD)
+
+    def apart(v, h):
+        return v.reshape(BQ // MIX, PAIR, MIX, HEAD)[:, h].reshape(BQ, HEAD)
+
+    q_mix, do_mix = mixed(q_ref), mixed(do_ref)
+    q_s[...] = q_mix
+    do_s[...] = do_mix
+    qt_s[...] = q_mix.T
+    dot_s[...] = do_mix.T
     qdoc = kdoc_ref[:, pl.ds(pl.multiple_of(chip_len + i * BQ, BQ), BQ)]
     qd_s[...] = jnp.broadcast_to(qdoc, (HEAD, BQ)).T
     m_s[...] = jnp.full(m_s.shape, NEG_BIG, F32)
@@ -274,14 +285,17 @@
     def scores(b, carry):
         off = offset(b)
         s = dot_nt(q_s[...], k_s[pl.ds(off, BK), :])
-        key = off + lax.broadcasted_iota(jnp.int32, (BQ, BK), 1)
-        query = chip_len + i * BQ + lax.broadcasted_iota(jnp.int32, (BQ, BK), 0)
-        keep = (key <= query) & (kdoc_ref[:, pl.ds(off, BK)] == spread(qd_s[...]))
-        for h in range(PAIR):
-            rows = slice(h * BQ, (h + 1) * BQ)
-            sh = jnp.where(keep, s[rows, :], NEG_BIG)
-            s_s[b, rows, :] = sh
-            m_s[rows, :] = jnp.maximum(m_s[rows, :], fold(sh, jnp.maximum))
+        limit = chip_len + i * BQ - off
+        key_doc = kdoc_ref[:, pl.ds(off, BK)]
+        for c in range(BQ // MIX):
+            here = slice(c * MIX, (c + 1) * MIX)
+            keep = (ahead_s[here, :] <= limit) & (key_doc == spread(qd_s[here, :]))
+            shift = jnp.where(keep, 0.0, NEG_BIG)
+            for h in range(PAIR):
+                rows = slice((c * PAIR + h) * MIX, (c * PAIR + h + 1) * MIX)
+                sh = s[rows, :] * (SCALE * LOG2E) + shift
+                s_s[b, rows, :] = sh
+                m_s[rows, :] = jnp.maximum(m_s[rows, :], fold(sh, jnp.maximum))
         return carry
 
     arrive(0, 4)
@@ -290,7 +304,7 @@
 
     def weights(b, carry):
         dp = dot_nt(do_s[...], v_s[pl.ds(offset(b), BK), :])
-        e = jnp.exp2((s_s[b] - spread(m_s[...])) * (SCALE * LOG2E))
+        e = jnp.exp2(s_s[b] - spread(m_s[...]))
         s_s[b] = e
         dp_s[b] = dp
         l_s[...] += fold(e, jnp.add)
@@ -317,13 +331,13 @@
 
     lax.fori_loop(0, n_blocks, grads, 0)
     cos_t, sin_t = spread_table(tab_s[span(i, BQ), :])
+    ctx_all, dq_all = ctx_s[...].astype(BF), dq_s[...].astype(BF).astype(F32)
     for h in range(PAIR):
-        rows = slice(h * BQ, (h + 1) * BQ)
         cols = slice(h * HEAD, (h + 1) * HEAD)
-        ctx = ctx_s[rows, :].astype(BF)
+        ctx = apart(ctx_all, h)
         act_ref[0, :, cols] = ctx
         at_s[WIDE + h * HEAD:WIDE + (h + 1) * HEAD, :] = ctx.T
-        dq = dq_s[rows, :].astype(BF).astype(F32)
+        dq = apart(dq_all, h)
         dq = (dq * cos_t - swap_halves(dq) * sin_t).astype(BF)
         act_ref[1, :, cols] = dq
         at_s[h * HEAD:(h + 1) * HEAD, :] = dq.T
@@ -396,6 +410,7 @@
                 pltpu.VMEM((rows, HEAD), F32),
                 pltpu.VMEM((rows, HEAD), F32),
                 pltpu.VMEM((BQ, HEAD), jnp.int32),
+                pltpu.VMEM((BQ, BK), jnp.int32),
                 pltpu.VMEM((rows, HEAD), F32),
                 pltpu.VMEM((rows, HEAD), F32),
                 pltpu.VMEM((rows, HEAD), BF),
@@ -514,7 +529,7 @@
 
 def kv_combine(core, parts):
     rows, width = parts[0].shape
-    step = 512
+    step = 1024
     out = jax.ShapeDtypeStruct((width, rows), F32)
     return pl.pallas_call(
         kv_combine_kernel,
@@ -535,8 +550,13 @@
     gq_ref, go_ref = rest[-2:]
 
     def put(u_ref, v_ref):
-        gq_ref[...] = (u_ref[0].astype(F32) + v_ref[0].astype(F32)).T
-        go_ref[...] = u_ref[1].astype(F32) + v_ref[1].astype(F32)
+        def part(c, carry):
+            cols = span(c, 256)
+            gq_ref[cols, :] = (u_ref[0, :, cols].astype(F32) + v_ref[0, :, cols].astype(F32)).T
+            go_ref[:, cols] = u_ref[1, :, cols].astype(F32) + v_ref[1, :, cols].astype(F32)
+            return carry
+
+        lax.fori_loop(0, u_ref.shape[2] // 256, part, 0)
 
     @pl.when(pl.program_id(0) == 0)
     def _():
@@ -549,7 +569,7 @@
 
 def combine(core, chunk, n_chunks, parts, prev):
     width = parts[0].shape[2]
-    step = 512
+    step = 1024
     last = width // step - 1
     near = pl.BlockSpec((2, WIDE, step), lambda w, r, s: (0, 0, r + w * (last - r)))
     far = pl.BlockSpec((2, WIDE, step), lambda w, r, s: (0, 0, r * w))
@@ -730,8 +750,10 @@
             acts.append(act)
             dkvs.append(dkv.reshape(2, 2, HEAD, chip_len))
             if j == n_chunks - 1:
-                dkv_up = sum(d[:, 0].astype(F32) for d in dkvs).astype(BF)
+                dkv_up = (dkv_early + dkvs[j][:, 0].astype(F32)).astype(BF)
                 dkv_far = lax.ppermute(dkv_up, "sp", up_perm)
+            if j == n_chunks - 2:
+                dkv_early = lax.optimization_barrier(sum(d[:, 0].astype(F32) for d in dkvs))
             acts_oth.append(near(act))
             part_far = far(part)
             part_near = near(part)

time: 563 us -> 553 us (0.982)
  Pallas kernels: 267 us -> 257 us
where the time goes in v6:
time: 553 us; the launch traced here: 552 us
  Pallas kernels  257 us (46%)
  waiting for transfers between devices  214 us (39%)
  starting transfers between devices  67.3 us (12%)
  other arithmetic  11.4 us (2%)
    ppermute x6, waiting for transfers between devices, far(): return lax.ppermute(v, 'sp', far_perm)  184 us
    pallas_call x4, Pallas kernels, attention(): pl.pallas_call(attn_kernel, grid_spec=pltpu.PrefetchScalarGridSpec(num_sc...  139 us
    ppermute x6, starting transfers between devices, far(): return lax.ppermute(v, 'sp', far_perm)  54.7 us
    pallas_call x4, Pallas kernels, combine(): pl.pallas_call(combine_kernel, grid_spec=pltpu.PrefetchScalarGridSpec(num...  33.9 us
    ppermute x1, waiting for transfers between devices, device_step(): dkv_far = lax.ppermute(dkv_up, 'sp', up_perm)  23.1 us
    pallas_call x2, Pallas kernels, qkv_proj(): pl.pallas_call(qkv_kernel, grid_spec=pltpu.PrefetchScalarGridSpec(num_sca...  22.4 us
    pallas_call x1, Pallas kernels, grad_hidden(): pl.pallas_call(functools.partial(hidden_kernel, n), grid_spec=pltpu.Prefe...  17 us
    pallas_call x1, Pallas kernels, dctx_proj(): pl.pallas_call(dctx_kernel, grid_spec=pltpu.PrefetchScalarGridSpec(num_sc...  14.2 us
  transfers between devices with their start and end apart: 29, of which 7 were waited for; matrix products, arithmetic and copies ran while one was open for 1% of the time, Pallas kernels for 20%

profile of v6, /device:TPU:0, one launch (start us, length us, event | category | flops | bytes accessed | tf_op | source)
XLA Modules:
  0.0 552.0 jit_solution(15476552461782855362)
XLA Ops:
  2.0 2.5 collective-permute-start.1
  5.2 1.9 multiply_cosine_fusion
  8.9 11.3 %qkv_proj.2 = (bf16[1024,256]{1,0:T(8,128)(2,1)}, bf16[2048,1024]{1,0:T(8,128)(2,1)}) custom-call(s32[2]{0:T(128)} %pad_add_fusion.2.s_ref, bf16[1024,2048]{1,0:T(8,128)(2,1)} %x_own.9, bf16[2048,2048]{1,0:T(8,128)(2,1)} %refs_10_.1, bf16[2048,256]{1,0:T(8,128)(2,1)} %refs_11_.1, bf16[2048,256]{1,0:T(8,128)(2,1)} %refs_12_.1, ...), custom_call_target="tpu_custom_call" | custom-call | flops 5368709120 | bytes 8388608 | tf_op jit(solution)/shard_map/qkv_proj/pallas_call | solution.py:111
  20.9 4.7 collective-permute-start.6
  27.0 11.2 %qkv_proj.3 = (bf16[1024,256]{1,0:T(8,128)(2,1)}, bf16[2048,1024]{1,0:T(8,128)(2,1)}) custom-call(s32[2]{0:T(128)} %pad_add_fusion.1.s_ref, bf16[1024,2048]{1,0:T(8,128)(2,1)} %collective-permute-done.3.x_ref.x_oth, bf16[2048,2048]{1,0:T(8,128)(2,1)} %refs_10_.1, bf16[2048,256]{1,0:T(8,128)(2,1)} %refs_11_.1, ...), custom_call_target="tpu_custom_call", output_to_operand_aliasing={{1}: (6, {})} | custom-call | flops 5368709120 | bytes 8388608 | tf_op jit(solution)/shard_map/qkv_proj/pallas_call | solution.py:111
  38.1 2.1 collective-permute-start.7
  40.2 14.2 %dctx_proj.1.do_ref = bf16[2048,1024]{1,0:T(8,128)(2,1)} custom-call(s32[1]{0:T(128)} %bitcast.s_ref.core_ref, bf16[1024,2048]{1,0:T(8,128)(2,1)} %g_own.7, bf16[1024,2048]{1,0:T(8,128)(2,1)} %collective-permute-done.5.oth_ref.g_oth, bf16[2048,2048]{1,0:T(8,128)(2,1)} %refs_8_.1), custom_call_target="tpu_custom_call" | custom-call | flops 8589934592 | bytes 12582912 | tf_op jit(solution)/shard_map/dctx_proj/pallas_call | solution.py:164
  54.4 34.8 %attention.6 = (bf16[2,2048,256]{2,1,0:T(8,128)(2,1)}, bf16[512,2048]{1,0:T(8,128)(2,1)}, bf16[512,2048]{1,0:T(8,128)(2,1)}) custom-call(s32[1]{0:T(128)} %bitcast.s_ref.core_ref, s32[4]{0:T(128)} %get-tuple-element.65.lo_ref, s32[4]{0:T(128)} %get-tuple-element.64.nb_ref, bf16[2048,1024]{1,0:T(8,128)(2,1)} %get-tuple-element.35.q_ref, ...), custom_call_target="tpu_custom_call" | custom-call | flops 17179869184 | bytes 12582912 | tf_op jit(solution)/shard_map/attention/pallas_call | solution.py:389
  89.2 34.8 %attention.5 = (bf16[2,2048,256]{2,1,0:T(8,128)(2,1)}, bf16[512,2048]{1,0:T(8,128)(2,1)}, bf16[512,2048]{1,0:T(8,128)(2,1)}) custom-call(s32[1]{0:T(128)} %bitcast.s_ref.core_ref, s32[4]{0:T(128)} %get-tuple-element.65.lo_ref, s32[4]{0:T(128)} %get-tuple-element.64.nb_ref, bf16[2048,1024]{1,0:T(8,128)(2,1)} %get-tuple-element.35.q_ref, ...), custom_call_target="tpu_custom_call" | custom-call | flops 17179869184 | bytes 12582912 | tf_op jit(solution)/shard_map/attention/pallas_call | solution.py:389
  124.0 35.0 %attention.4 = (bf16[2,2048,256]{2,1,0:T(8,128)(2,1)}, bf16[512,2048]{1,0:T(8,128)(2,1)}, bf16[512,2048]{1,0:T(8,128)(2,1)}) custom-call(s32[1]{0:T(128)} %bitcast.s_ref.core_ref, s32[4]{0:T(128)} %get-tuple-element.65.lo_ref, s32[4]{0:T(128)} %get-tuple-element.64.nb_ref, bf16[2048,1024]{1,0:T(8,128)(2,1)} %get-tuple-element.35.q_ref, ...), custom_call_target="tpu_custom_call" | custom-call | flops 17179869184 | bytes 12582912 | tf_op jit(solution)/shard_map/attention/pallas_call | solution.py:389
  159.0 3.7 add_bitcast_fusion
  162.7 34.7 %attention.7 = (bf16[2,2048,256]{2,1,0:T(8,128)(2,1)}, bf16[512,2048]{1,0:T(8,128)(2,1)}, bf16[512,2048]{1,0:T(8,128)(2,1)}) custom-call(s32[1]{0:T(128)} %bitcast.s_ref.core_ref, s32[4]{0:T(128)} %get-tuple-element.65.lo_ref, s32[4]{0:T(128)} %get-tuple-element.64.nb_ref, bf16[2048,1024]{1,0:T(8,128)(2,1)} %get-tuple-element.35.q_ref, ...), custom_call_target="tpu_custom_call" | custom-call | flops 17179869184 | bytes 12582912 | tf_op jit(solution)/shard_map/attention/pallas_call | solution.py:389
  197.5 2.1 fusion
  200.9 48.1 %collective-permute-start.23 = (bf16[2,256,2048]{2,1,0:T(8,128)(2,1)}, bf16[2,256,2048]{2,1,0:T(8,128)(2,1)}, u32[]{:S(2)}, u32[]{:S(2)}) collective-permute-start(bf16[2,256,2048]{2,1,0:T(8,128)(2,1)} %bitcast.11.a_ref), channel_id=1, source_target_pairs={{0,2},{1,3},{2,0},{3,1},{4,6},{5,7},{6,4},{7,5}} | collective-permute-start | bytes 6291464 | tf_op jit(solution)/shard_map/ppermute | solution.py:704
  249.1 23.1 %collective-permute-done.12.refs_4_ = bf16[2,128,2048]{2,1,0:T(8,128)(2,1)} collective-permute-done((bf16[2,128,2048]{2,1,0:T(8,128)(2,1)S(1)}, bf16[2,128,2048]{2,1,0:T(8,128)(2,1)}, u32[]{:S(2)}, u32[]{:S(2)}) %collective-permute-start.12) | collective-permute-done | bytes 1048608 | tf_op jit(solution)/shard_map/ppermute | solution.py:754
  272.2 5.3 kv_finish.1
  277.5 6.6 %kvgrad.1.a_ref = bf16[256,2048]{1,0:T(8,128)(2,1)} custom-call(s32[1]{0:T(128)} %bitcast.s_ref.core_ref, bf16[256,2048]{1,0:T(8,128)(2,1)} %get-tuple-element.58.dkvt_ref, bf16[1024,2048]{1,0:T(8,128)(2,1)} %x_own.9, bf16[1024,2048]{1,0:T(8,128)(2,1)} %collective-permute-done.3.x_ref.x_oth), custom_call_target="tpu_custom_call" | custom-call | flops 2147483648 | bytes 8388608 | tf_op jit(solution)/shard_map/kvgrad/pallas_call | solution.py:507
  284.7 2.0 collective-permute-start.20
  286.7 52.8 %collective-permute-done.26.b_ref = bf16[256,2048]{1,0:T(8,128)(2,1)S(1)} collective-permute-done((bf16[256,2048]{1,0:T(8,128)(2,1)}, bf16[256,2048]{1,0:T(8,128)(2,1)S(1)}, u32[]{:S(2)}, u32[]{:S(2)}) %collective-permute-start.26) | collective-permute-done | bytes 1048608 | tf_op jit(solution)/shard_map/ppermute | solution.py:704
  339.6 2.0 collective-permute-start.14
  341.6 43.0 %collective-permute-done.20.b_ref = bf16[2,256,2048]{2,1,0:T(8,128)(2,1)} collective-permute-done((bf16[2,256,2048]{2,1,0:T(8,128)(2,1)}, bf16[2,256,2048]{2,1,0:T(8,128)(2,1)}, u32[]{:S(2)}, u32[]{:S(2)}) %collective-permute-start.20) | collective-permute-done | bytes 2097184 | tf_op jit(solution)/shard_map/ppermute | solution.py:704
  385.0 44.4 %collective-permute-done.17.b_ref = bf16[2,256,2048]{2,1,0:T(8,128)(2,1)} collective-permute-done((bf16[2,256,2048]{2,1,0:T(8,128)(2,1)}, bf16[2,256,2048]{2,1,0:T(8,128)(2,1)}, u32[]{:S(2)}, u32[]{:S(2)}) %collective-permute-start.17) | collective-permute-done | bytes 2097184 | tf_op jit(solution)/shard_map/ppermute | solution.py:704
  429.5 43.6 %collective-permute-done.14.b_ref = bf16[2,256,2048]{2,1,0:T(8,128)(2,1)} collective-permute-done((bf16[2,256,2048]{2,1,0:T(8,128)(2,1)}, bf16[2,256,2048]{2,1,0:T(8,128)(2,1)}, u32[]{:S(2)}, u32[]{:S(2)}) %collective-permute-start.14) | collective-permute-done | bytes 2097184 | tf_op jit(solution)/shard_map/ppermute | solution.py:704
  475.1 2.3 collective-permute-done.8.refs_4_
  477.6 4.4 collective-permute-done.28.d_ref
  483.1 13.9 %attn_out.1 = bf16[1024,2048]{1,0:T(8,128)(2,1)} custom-call(s32[1]{0:T(128)} %bitcast.s_ref.core_ref, bf16[2,2048,256]{2,1,0:T(8,128)(2,1)} %get-tuple-element.38.refs_0_, bf16[2,2048,256]{2,1,0:T(8,128)(2,1)} %get-tuple-element.39.refs_1_, bf16[2,2048,256]{2,1,0:T(8,128)(2,1)} %get-tuple-element.40.refs_2_, ...), custom_call_target="tpu_custom_call" | custom-call | flops 8589934592 | bytes 16777216 | tf_op jit(solution)/shard_map/attn_out/pallas_call | solution.py:625
  497.0 17.0 %grad_hidden.1 = bf16[1024,2048]{1,0:T(8,128)(2,1)} custom-call(s32[1]{0:T(128)} %bitcast.s_ref.core_ref, bf16[2,2048,256]{2,1,0:T(8,128)(2,1)} %get-tuple-element.38.refs_0_, bf16[2,2048,256]{2,1,0:T(8,128)(2,1)} %get-tuple-element.39.refs_1_, bf16[2,2048,256]{2,1,0:T(8,128)(2,1)} %get-tuple-element.40.refs_2_, ...), custom_call_target="tpu_custom_call" | custom-call | flops 10737418240 | bytes 16777216 | tf_op jit(solution)/shard_map/grad_hidden/pallas_call | solution.py:666
  514.0 4.1 kv_combine.1
  518.0 8.5 %combine.4 = (f32[2048,2048]{1,0:T(8,128)}, f32[2048,2048]{1,0:T(8,128)}) custom-call(s32[1]{0:T(128)} %bitcast.s_ref.core_ref, bf16[2,256,2048]{2,1,0:T(8,128)(2,1)} %bitcast.11.a_ref, bf16[2,256,2048]{2,1,0:T(8,128)(2,1)} %collective-permute-done.23.b_ref, bf16[2,256,2048]{2,1,0:T(8,128)(2,1)} %collective-permute-done.24.c_ref, ...), custom_call_target="tpu_custom_call" | custom-call | flops 536870912 | bytes 16777216 | tf_op jit(solution)/shard_map/combine/pallas_call | solution.py:583
  526.5 8.5 %combine.5 = (f32[2048,2048]{1,0:T(8,128)}, f32[2048,2048]{1,0:T(8,128)}) custom-call(s32[1]{0:T(128)} %bitcast.s_ref.core_ref, bf16[2,256,2048]{2,1,0:T(8,128)(2,1)} %bitcast.47, bf16[2,256,2048]{2,1,0:T(8,128)(2,1)} %collective-permute-done.20.b_ref, ...), custom_call_target="tpu_custom_call", output_to_operand_aliasing={{0}: (5, {}), {1}: (6, {})} | custom-call | flops 536870912 | bytes 16777216 | tf_op jit(solution)/shard_map/combine/pallas_call | solution.py:583
  535.0 8.5 %combine.6 = (f32[2048,2048]{1,0:T(8,128)}, f32[2048,2048]{1,0:T(8,128)}) custom-call(s32[1]{0:T(128)} %bitcast.s_ref.core_ref, bf16[2,256,2048]{2,1,0:T(8,128)(2,1)} %bitcast.44, bf16[2,256,2048]{2,1,0:T(8,128)(2,1)} %collective-permute-done.17.b_ref, ...), custom_call_target="tpu_custom_call", output_to_operand_aliasing={{0}: (5, {}), {1}: (6, {})} | custom-call | flops 536870912 | bytes 16777216 | tf_op jit(solution)/shard_map/combine/pallas_call | solution.py:583
  543.5 8.5 %combine.7 = (f32[2048,2048]{1,0:T(8,128)}, f32[2048,2048]{1,0:T(8,128)}) custom-call(s32[1]{0:T(128)} %bitcast.s_ref.core_ref, bf16[2,256,2048]{2,1,0:T(8,128)(2,1)} %bitcast.41, bf16[2,256,2048]{2,1,0:T(8,128)(2,1)} %collective-permute-done.14.b_ref, ...), custom_call_target="tpu_custom_call", output_to_operand_aliasing={{0}: (5, {}), {1}: (6, {})} | custom-call | flops 536870912 | bytes 16777216 | tf_op jit(solution)/shard_map/combine/pallas_call | solution.py:583
  (74 shorter events, 11.7 us)
Async XLA Ops:
  0.6 26.4 %collective-permute-start.3 = (bf16[1024,2048]{1,0:T(8,128)(2,1)}, bf16[1024,2048]{1,0:T(8,128)(2,1)}, u32[]{:S(2)}, u32[]{:S(2)}) collective-permute-start(bf16[1024,2048]{1,0:T(8,128)(2,1)} %x_own.9), channel_id=1, source_target_pairs={{0,1},{1,0},{2,3},{3,2},{4,5},{5,4},{6,7},{7,6}} | collective-permute-start | bytes 12582920 | tf_op jit(solution)/shard_map/ppermute | solution.py:701
  1.5 38.8 %collective-permute-start.5 = (bf16[1024,2048]{1,0:T(8,128)(2,1)}, bf16[1024,2048]{1,0:T(8,128)(2,1)}, u32[]{:S(2)}, u32[]{:S(2)}) collective-permute-start(bf16[1024,2048]{1,0:T(8,128)(2,1)} %g_own.7), channel_id=1, source_target_pairs={{0,1},{1,0},{2,3},{3,2},{4,5},{5,4},{6,7},{7,6}} | collective-permute-start | bytes 12582920 | tf_op jit(solution)/shard_map/ppermute | solution.py:701
  1.5 19.2 %collective-permute-start = (s32[1024]{0:T(1024)}, s32[1024]{0:T(1024)S(1)}, u32[]{:S(2)}, u32[]{:S(2)}) collective-permute-start(s32[1024]{0:T(1024)} %param.11), channel_id=1, source_target_pairs={{0,1},{1,0},{2,3},{3,2},{4,5},{5,4},{6,7},{7,6}} | collective-permute-start | bytes 12296 | tf_op jit(solution)/shard_map/ppermute | solution.py:701
  2.0 18.9 %collective-permute-start.1 = (s32[1024]{0:T(1024)}, s32[1024]{0:T(1024)S(1)}, u32[]{:S(2)}, u32[]{:S(2)}) collective-permute-start(s32[1024]{0:T(1024)} %param.11), channel_id=1, source_target_pairs={{0,2},{1,3},{2,0},{3,1},{4,6},{5,7},{6,4},{7,5}} | collective-permute-start | bytes 12296 | tf_op jit(solution)/shard_map/ppermute | solution.py:704
  8.1 18.9 %collective-permute-start.4 = (f32[1024,128]{1,0:T(8,128)}, f32[1024,128]{1,0:T(8,128)}, u32[]{:S(2)}, u32[]{:S(2)}) collective-permute-start(f32[1024,128]{1,0:T(8,128)} %pad_maximum_fusion.tab_ref.tab_own.refs_5_), channel_id=1, source_target_pairs={{0,1},{1,0},{2,3},{3,2},{4,5},{5,4},{6,7},{7,6}} | collective-permute-start | bytes 1572872 | tf_op jit(solution)/shard_map/ppermute | solution.py:701
  8.9 11.9 %copy-start.3 = (s32[1024]{0:T(1024)S(1)}, s32[1024]{0:T(1024)}, u32[]{:S(2)}) copy-start(s32[1024]{0:T(1024)} %param.11) | copy-start | bytes 12292
  20.8 4.8 collective-permute-start.2
  20.9 33.5 %collective-permute-start.6 = (bf16[1024,256]{1,0:T(8,128)(2,1)}, bf16[1024,256]{1,0:T(8,128)(2,1)}, u32[]{:S(2)}, u32[]{:S(2)}) collective-permute-start(bf16[1024,256]{1,0:T(8,128)(2,1)} %get-tuple-element.36.kvc_own), channel_id=1, source_target_pairs={{0,2},{1,3},{4,6},{5,7}} | collective-permute-start | bytes 1572872 | tf_op jit(solution)/shard_map/ppermute | solution.py:724
  38.1 16.3 %collective-permute-start.7 = (bf16[1024,256]{1,0:T(8,128)(2,1)}, bf16[1024,256]{1,0:T(8,128)(2,1)}, u32[]{:S(2)}, u32[]{:S(2)}) collective-permute-start(bf16[1024,256]{1,0:T(8,128)(2,1)} %get-tuple-element.37.kvc_oth), channel_id=1, source_target_pairs={{0,2},{1,3},{4,6},{5,7}} | collective-permute-start | bytes 1572872 | tf_op jit(solution)/shard_map/ppermute | solution.py:731
  199.6 72.6 %collective-permute-start.12 = (bf16[2,128,2048]{2,1,0:T(8,128)(2,1)S(1)}, bf16[2,128,2048]{2,1,0:T(8,128)(2,1)}, u32[]{:S(2)}, u32[]{:S(2)}) collective-permute-start(bf16[2,128,2048]{2,1,0:T(8,128)(2,1)S(1)} %fusion), channel_id=1, source_target_pairs={{2,0},{3,1},{6,4},{7,5}} | collective-permute-start | bytes 3145736 | tf_op jit(solution)/shard_map/ppermute | solution.py:754
  200.9 138.6 %collective-permute-start.23 = (bf16[2,256,2048]{2,1,0:T(8,128)(2,1)}, bf16[2,256,2048]{2,1,0:T(8,128)(2,1)}, u32[]{:S(2)}, u32[]{:S(2)}) collective-permute-start(bf16[2,256,2048]{2,1,0:T(8,128)(2,1)} %bitcast.11.a_ref), channel_id=1, source_target_pairs={{0,2},{1,3},{2,0},{3,1},{4,6},{5,7},{6,4},{7,5}} | collective-permute-start | bytes 6291464 | tf_op jit(solution)/shard_map/ppermute | solution.py:704
  284.2 55.3 %collective-permute-start.26 = (bf16[256,2048]{1,0:T(8,128)(2,1)}, bf16[256,2048]{1,0:T(8,128)(2,1)S(1)}, u32[]{:S(2)}, u32[]{:S(2)}) collective-permute-start(bf16[256,2048]{1,0:T(8,128)(2,1)} %kvgrad.1.a_ref), channel_id=1, source_target_pairs={{0,2},{1,3},{2,0},{3,1},{4,6},{5,7},{6,4},{7,5}} | collective-permute-start | bytes 3145736 | tf_op jit(solution)/shard_map/ppermute | solution.py:704
  284.2 55.3 %collective-permute-start.27 = (bf16[256,2048]{1,0:T(8,128)(2,1)}, bf16[256,2048]{1,0:T(8,128)(2,1)S(1)}, u32[]{:S(2)}, u32[]{:S(2)}) collective-permute-start(bf16[256,2048]{1,0:T(8,128)(2,1)} %kvgrad.1.a_ref), channel_id=1, source_target_pairs={{0,1},{1,0},{2,3},{3,2},{4,5},{5,4},{6,7},{7,6}} | collective-permute-start | bytes 3145736 | tf_op jit(solution)/shard_map/ppermute | solution.py:701
  284.2 57.4 %collective-permute-start.24 = (bf16[2,256,2048]{2,1,0:T(8,128)(2,1)}, bf16[2,256,2048]{2,1,0:T(8,128)(2,1)}, u32[]{:S(2)}, u32[]{:S(2)}) collective-permute-start(bf16[2,256,2048]{2,1,0:T(8,128)(2,1)} %bitcast.11.a_ref), channel_id=1, source_target_pairs={{0,1},{1,0},{2,3},{3,2},{4,5},{5,4},{6,7},{7,6}} | collective-permute-start | bytes 6291464 | tf_op jit(solution)/shard_map/ppermute | solution.py:701
  284.7 99.9 %collective-permute-start.20 = (bf16[2,256,2048]{2,1,0:T(8,128)(2,1)}, bf16[2,256,2048]{2,1,0:T(8,128)(2,1)}, u32[]{:S(2)}, u32[]{:S(2)}) collective-permute-start(bf16[2,256,2048]{2,1,0:T(8,128)(2,1)} %bitcast.45), channel_id=1, source_target_pairs={{0,2},{1,3},{2,0},{3,1},{4,6},{5,7},{6,4},{7,5}} | collective-permute-start | bytes 6291464 | tf_op jit(solution)/shard_map/ppermute | solution.py:704
  339.5 134.6 %copy-start = (bf16[256,2048]{1,0:T(8,128)(2,1)}, bf16[256,2048]{1,0:T(8,128)(2,1)S(1)}, u32[]{:S(2)}) copy-start(bf16[256,2048]{1,0:T(8,128)(2,1)S(1)} %collective-permute-done.26.b_ref) | copy-start | bytes 3145732
  339.5 45.1 %collective-permute-start.21 = (bf16[2,256,2048]{2,1,0:T(8,128)(2,1)}, bf16[2,256,2048]{2,1,0:T(8,128)(2,1)}, u32[]{:S(2)}, u32[]{:S(2)}) collective-permute-start(bf16[2,256,2048]{2,1,0:T(8,128)(2,1)} %bitcast.46), channel_id=1, source_target_pairs={{0,1},{1,0},{2,3},{3,2},{4,5},{5,4},{6,7},{7,6}} | collective-permute-start | bytes 6291464 | tf_op jit(solution)/shard_map/ppermute | solution.py:701
  339.5 142.4 %copy-start.1 = (bf16[256,2048]{1,0:T(8,128)(2,1)}, bf16[256,2048]{1,0:T(8,128)(2,1)S(1)}, u32[]{:S(2)}) copy-start(bf16[256,2048]{1,0:T(8,128)(2,1)S(1)} %collective-permute-done.27.c_ref) | copy-start | bytes 3145732
  339.5 90.0 %collective-permute-start.17 = (bf16[2,256,2048]{2,1,0:T(8,128)(2,1)}, bf16[2,256,2048]{2,1,0:T(8,128)(2,1)}, u32[]{:S(2)}, u32[]{:S(2)}) collective-permute-start(bf16[2,256,2048]{2,1,0:T(8,128)(2,1)} %bitcast.42), channel_id=1, source_target_pairs={{0,2},{1,3},{2,0},{3,1},{4,6},{5,7},{6,4},{7,5}} | collective-permute-start | bytes 6291464 | tf_op jit(solution)/shard_map/ppermute | solution.py:704
  339.6 133.5 %collective-permute-start.14 = (bf16[2,256,2048]{2,1,0:T(8,128)(2,1)}, bf16[2,256,2048]{2,1,0:T(8,128)(2,1)}, u32[]{:S(2)}, u32[]{:S(2)}) collective-permute-start(bf16[2,256,2048]{2,1,0:T(8,128)(2,1)} %bitcast.39), channel_id=1, source_target_pairs={{0,2},{1,3},{2,0},{3,1},{4,6},{5,7},{6,4},{7,5}} | collective-permute-start | bytes 6291464 | tf_op jit(solution)/shard_map/ppermute | solution.py:704
  341.6 132.5 %collective-permute-start.11 = (bf16[2,2048,256]{2,1,0:T(8,128)(2,1)}, bf16[2,2048,256]{2,1,0:T(8,128)(2,1)}, u32[]{:S(2)}, u32[]{:S(2)}) collective-permute-start(bf16[2,2048,256]{2,1,0:T(8,128)(2,1)} %get-tuple-element.41.refs_3_), channel_id=1, source_target_pairs={{0,1},{1,0},{2,3},{3,2},{4,5},{5,4},{6,7},{7,6}} | collective-permute-start | bytes 6291464 | tf_op jit(solution)/shard_map/ppermute | solution.py:701
  384.5 88.5 %collective-permute-start.13 = (bf16[2048,256]{1,0:T(8,128)(2,1)}, bf16[2048,256]{1,0:T(8,128)(2,1)S(1)}, u32[]{:S(2)}, u32[]{:S(2)}) collective-permute-start(bf16[2048,256]{1,0:T(8,128)(2,1)} %get-tuple-element.46.refs_8_), channel_id=1, source_target_pairs={{0,1},{1,0},{2,3},{3,2},{4,5},{5,4},{6,7},{7,6}} | collective-permute-start | bytes 3145736 | tf_op jit(solution)/shard_map/ppermute | solution.py:701
  384.5 90.1 %collective-permute-start.10 = (bf16[2,2048,256]{2,1,0:T(8,128)(2,1)}, bf16[2,2048,256]{2,1,0:T(8,128)(2,1)S(1)}, u32[]{:S(2)}, u32[]{:S(2)}) collective-permute-start(bf16[2,2048,256]{2,1,0:T(8,128)(2,1)} %get-tuple-element.40.refs_2_), channel_id=1, source_target_pairs={{0,1},{1,0},{2,3},{3,2},{4,5},{5,4},{6,7},{7,6}} | collective-permute-start | bytes 6291464 | tf_op jit(solution)/shard_map/ppermute | solution.py:701
  429.5 45.2 %collective-permute-start.9 = (bf16[2,2048,256]{2,1,0:T(8,128)(2,1)}, bf16[2,2048,256]{2,1,0:T(8,128)(2,1)S(1)}, u32[]{:S(2)}, u32[]{:S(2)}) collective-permute-start(bf16[2,2048,256]{2,1,0:T(8,128)(2,1)} %get-tuple-element.39.refs_1_), channel_id=1, source_target_pairs={{0,1},{1,0},{2,3},{3,2},{4,5},{5,4},{6,7},{7,6}} | collective-permute-start | bytes 6291464 | tf_op jit(solution)/shard_map/ppermute | solution.py:701
  473.1 4.4 collective-permute-start.8
  473.1 9.8 %collective-permute-start.25 = (bf16[2,256,2048]{2,1,0:T(8,128)(2,1)}, bf16[2,256,2048]{2,1,0:T(8,128)(2,1)}, u32[]{:S(2)}, u32[]{:S(2)}) collective-permute-start(bf16[2,256,2048]{2,1,0:T(8,128)(2,1)} %collective-permute-done.23.b_ref), channel_id=1, source_target_pairs={{0,1},{1,0},{2,3},{3,2},{4,5},{5,4},{6,7},{7,6}} | collective-permute-start | bytes 6291464 | tf_op jit(solution)/shard_map/ppermute | solution.py:701
  474.1 7.8 %collective-permute-start.28 = (bf16[256,2048]{1,0:T(8,128)(2,1)S(1)}, bf16[256,2048]{1,0:T(8,128)(2,1)S(1)}, u32[]{:S(2)}, u32[]{:S(2)}) collective-permute-start(bf16[256,2048]{1,0:T(8,128)(2,1)S(1)} %collective-permute-done.26.b_ref), channel_id=1, source_target_pairs={{0,1},{1,0},{2,3},{3,2},{4,5},{5,4},{6,7},{7,6}} | collective-permute-start | bytes 3145736 | tf_op jit(solution)/shard_map/ppermute | solution.py:701
  474.6 51.9 %collective-permute-start.22 = (bf16[2,256,2048]{2,1,0:T(8,128)(2,1)}, bf16[2,256,2048]{2,1,0:T(8,128)(2,1)}, u32[]{:S(2)}, u32[]{:S(2)}) collective-permute-start(bf16[2,256,2048]{2,1,0:T(8,128)(2,1)} %collective-permute-done.20.b_ref), channel_id=1, source_target_pairs={{0,1},{1,0},{2,3},{3,2},{4,5},{5,4},{6,7},{7,6}} | collective-permute-start | bytes 6291464 | tf_op jit(solution)/shard_map/ppermute | solution.py:701
  474.6 60.3 %collective-permute-start.18 = (bf16[2,256,2048]{2,1,0:T(8,128)(2,1)}, bf16[2,256,2048]{2,1,0:T(8,128)(2,1)}, u32[]{:S(2)}, u32[]{:S(2)}) collective-permute-start(bf16[2,256,2048]{2,1,0:T(8,128)(2,1)} %bitcast.43), channel_id=1, source_target_pairs={{0,1},{1,0},{2,3},{3,2},{4,5},{5,4},{6,7},{7,6}} | collective-permute-start | bytes 6291464 | tf_op jit(solution)/shard_map/ppermute | solution.py:701
  477.4 57.5 %collective-permute-start.19 = (bf16[2,256,2048]{2,1,0:T(8,128)(2,1)}, bf16[2,256,2048]{2,1,0:T(8,128)(2,1)}, u32[]{:S(2)}, u32[]{:S(2)}) collective-permute-start(bf16[2,256,2048]{2,1,0:T(8,128)(2,1)} %collective-permute-done.17.b_ref), channel_id=1, source_target_pairs={{0,1},{1,0},{2,3},{3,2},{4,5},{5,4},{6,7},{7,6}} | collective-permute-start | bytes 6291464 | tf_op jit(solution)/shard_map/ppermute | solution.py:701
  481.9 61.5 %collective-permute-start.15 = (bf16[2,256,2048]{2,1,0:T(8,128)(2,1)}, bf16[2,256,2048]{2,1,0:T(8,128)(2,1)}, u32[]{:S(2)}, u32[]{:S(2)}) collective-permute-start(bf16[2,256,2048]{2,1,0:T(8,128)(2,1)} %bitcast.40), channel_id=1, source_target_pairs={{0,1},{1,0},{2,3},{3,2},{4,5},{5,4},{6,7},{7,6}} | collective-permute-start | bytes 6291464 | tf_op jit(solution)/shard_map/ppermute | solution.py:701
  482.9 60.6 %collective-permute-start.16 = (bf16[2,256,2048]{2,1,0:T(8,128)(2,1)}, bf16[2,256,2048]{2,1,0:T(8,128)(2,1)}, u32[]{:S(2)}, u32[]{:S(2)}) collective-permute-start(bf16[2,256,2048]{2,1,0:T(8,128)(2,1)} %collective-permute-done.14.b_ref), channel_id=1, source_target_pairs={{0,1},{1,0},{2,3},{3,2},{4,5},{5,4},{6,7},{7,6}} | collective-permute-start | bytes 6291464 | tf_op jit(solution)/shard_map/ppermute | solution.py:701
  (5 other events, 24.1 us)

commit v7 on v6

--- a/solution.py
+++ b/solution.py
@@ -82,47 +82,56 @@
 
 def qkv_kernel(s_ref, x_ref, wq_ref, wk_ref, wv_ref, tab_ref, *rest):
     kv_ref, q_ref, w_s = rest[-3:]
-
-    @pl.when(pl.program_id(0) == 0)
+    part = pl.program_id(0)
+
+    @pl.when((part == 0) & (pl.program_id(1) == 0))
     def _():
         w_s[:, :HEAD] = wk_ref[...]
         w_s[:, HEAD:] = wv_ref[...]
 
-    x = x_ref[...]
-    cos_t, sin_t = spread_table(tab_ref[...])
-    kv = dot_nn(x, w_s[...])
-    k = kv[:, :HEAD]
-    kv_ref[:, :HEAD] = (k * cos_t + swap_halves(k) * sin_t).astype(BF)
-    kv_ref[:, HEAD:] = kv[:, HEAD:].astype(BF)
-    step = 4 * HEAD
-    for n in range(wq_ref.shape[1] // step):
-        q = dot_nn(x, wq_ref[:, n * step:(n + 1) * step])
-        for h in range(step // HEAD):
-            part = q[:, h * HEAD:(h + 1) * HEAD]
-            at = n * step + h * HEAD
-            q_ref[:, at:at + HEAD] = (part * cos_t + swap_halves(part) * sin_t).astype(BF)
-
-
-def qkv_proj(sel, x, w_q, w_k, w_v, tab, prev):
+    @pl.when(part == 0)
+    def _():
+        kv = dot_nn(x_ref[...], w_s[...])
+        cos_t, sin_t = spread_table(tab_ref[...])
+        k = kv[:, :HEAD]
+        kv_ref[:, :HEAD] = (k * cos_t + swap_halves(k) * sin_t).astype(BF)
+        kv_ref[:, HEAD:] = kv[:, HEAD:].astype(BF)
+
+    @pl.when(part > 0)
+    def _():
+        q = dot_nn(x_ref[...], wq_ref[...])
+        cos_t, sin_t = spread_table(tab_ref[...])
+        for h in range(wq_ref.shape[1] // HEAD):
+            head = q[:, h * HEAD:(h + 1) * HEAD]
+            q_ref[:, h * HEAD:(h + 1) * HEAD] = (head * cos_t + swap_halves(head) * sin_t).astype(BF)
+
+
+def qkv_proj(own, core, x, w_q, w_k, w_v, tab, prev):
     tokens, width = x.shape
     cols = w_q.shape[1] // 2
-    rows = tokens // 2
+    step, rows = 512, 256
+    n, m_all = cols // step, tokens // rows
     extra = [] if prev is None else [prev]
+
+    def q_place(p, m, s):
+        half = s[0] if own else 1 - s[0]
+        return half * m_all + jnp.where(p == 0, 0, m), jnp.maximum(p - 1, 0)
+
     return pl.pallas_call(
         qkv_kernel,
         grid_spec=pltpu.PrefetchScalarGridSpec(
             num_scalar_prefetch=1,
-            grid=(2,),
+            grid=(n + 1, m_all),
             in_specs=[
-                pl.BlockSpec((rows, width), lambda m, s: (m, 0)),
-                pl.BlockSpec((width, cols), lambda m, s: (0, s[0])),
-                pl.BlockSpec((width, HEAD), lambda m, s: (0, s[0])),
-                pl.BlockSpec((width, HEAD), lambda m, s: (0, s[0])),
-                pl.BlockSpec((rows, HEAD), lambda m, s: (m, 0)),
+                pl.BlockSpec((rows, width), lambda p, m, s: (m, 0)),
+                pl.BlockSpec((width, step), lambda p, m, s: (0, s[0] * n + jnp.maximum(p - 1, 0))),
+                pl.BlockSpec((width, HEAD), lambda p, m, s: (0, s[0])),
+                pl.BlockSpec((width, HEAD), lambda p, m, s: (0, s[0])),
+                pl.BlockSpec((rows, HEAD), lambda p, m, s: (m, 0)),
             ] + [pl.BlockSpec(memory_space=pl.ANY)] * len(extra),
             out_specs=[
-                pl.BlockSpec((rows, 2 * HEAD), lambda m, s: (m, 0)),
-                pl.BlockSpec((rows, cols), lambda m, s: (s[1] * 2 + m, 0)),
+                pl.BlockSpec((rows, 2 * HEAD), lambda p, m, s: (jnp.where(p == 0, m, m_all - 1), 0)),
+                pl.BlockSpec((rows, step), q_place),
             ],
             scratch_shapes=[pltpu.VMEM((width, 2 * HEAD), BF)],
         ),
@@ -134,44 +143,40 @@
         compiler_params=params(),
         cost_estimate=cost(2 * tokens * width * (cols + 2 * HEAD), tokens * width * 2 + cols * width * 2),
         name="qkv_proj",
-    )(sel, x, w_q, w_k, w_v, tab, *extra)
-
-
-def dctx_kernel(s_ref, own_ref, oth_ref, wo_ref, out_ref):
-    def put(ref):
-        step = 4 * HEAD
-        for n in range(wo_ref.shape[0] // step):
-            out_ref[:, n * step:(n + 1) * step] = dot_nt(ref[...], wo_ref[n * step:(n + 1) * step, :]).astype(BF)
-
-    @pl.when(pl.program_id(0) < 2)
-    def _():
-        put(own_ref)
-
-    @pl.when(pl.program_id(0) >= 2)
-    def _():
-        put(oth_ref)
+    )(core, x, w_q, w_k, w_v, tab, *extra)
+
+
+def dctx_kernel(steps, s_ref, own_ref, oth_ref, wo_ref, out_ref):
+    @pl.when(pl.program_id(1) < steps)
+    def _():
+        out_ref[...] = dot_nt(own_ref[...], wo_ref[...]).astype(BF)
+
+    @pl.when(pl.program_id(1) >= steps)
+    def _():
+        out_ref[...] = dot_nt(oth_ref[...], wo_ref[...]).astype(BF)
 
 
 def dctx_proj(core, own, oth, w_o):
     tokens, width = own.shape
     cols = w_o.shape[0] // 2
-    rows = tokens // 2
+    step, rows = 512, 256
+    n, m_all = cols // step, tokens // rows
 
     def place(m, s):
-        far = m // 2
-        return (s[0] + far - 2 * s[0] * far) * 2 + m % 2
-
-    return pl.pallas_call(
-        dctx_kernel,
+        far = m // m_all
+        return (s[0] + far - 2 * s[0] * far) * m_all + m % m_all
+
+    return pl.pallas_call(
+        functools.partial(dctx_kernel, m_all),
         grid_spec=pltpu.PrefetchScalarGridSpec(
             num_scalar_prefetch=1,
-            grid=(4,),
+            grid=(n, 2 * m_all),
             in_specs=[
-                pl.BlockSpec((rows, width), lambda m, s: (jnp.minimum(m, 1), 0)),
-                pl.BlockSpec((rows, width), lambda m, s: (jnp.maximum(m - 2, 0), 0)),
-                pl.BlockSpec((cols, width), lambda m, s: (s[0], 0)),
-            ],
-            out_specs=pl.BlockSpec((rows, cols), lambda m, s: (place(m, s), 0)),
+                pl.BlockSpec((rows, width), lambda p, m, s: (jnp.minimum(m, m_all - 1), 0)),
+                pl.BlockSpec((rows, width), lambda p, m, s: (jnp.maximum(m - m_all, 0), 0)),
+                pl.BlockSpec((step, width), lambda p, m, s: (s[0] * n + p, 0)),
+            ],
+            out_specs=pl.BlockSpec((rows, step), lambda p, m, s: (place(m, s), p)),
         ),
         out_shape=jax.ShapeDtypeStruct((2 * tokens, cols), BF),
         compiler_params=params(),
@@ -181,11 +186,12 @@
 
 
 def attn_kernel(
-    core_ref, lo_ref, nb_ref, q_ref, do_ref, kdoc_ref, tab_own, tab_oth, kvp_own, kvp_oth, kvc_own, kvc_oth,
-    x_own, x_oth, g_own, g_oth, act_ref, part_ref, dkv_ref,
+    first, core_ref, lo_ref, nb_ref, q_ref, do_ref, kdoc_ref, tab_own, tab_oth, kvp_own, kvp_oth, kvc_own, kvc_oth,
+    x_own, x_oth, g_own, g_oth, before_ref, act_ref, part_ref, dkv_ref,
     k_s, v_s, s_s, dp_s, m_s, l_s, d_s, qd_s, ahead_s, ctx_s, dq_s, q_s, do_s, qt_s, dot_s, tab_s, dk_s, dv_s,
-    x_s, g_s, at_s, w_s, init_sem, row_sem, out_sem,
+    x_s, g_s, at_s, w_s, before_s, init_sem, row_sem, out_sem,
 ):
+    before_copy = pltpu.make_async_copy(before_ref, before_s, out_sem.at[2])
     i = pl.program_id(0)
     tokens = kvc_own.shape[0]
     chip_len = 2 * tokens
@@ -219,6 +225,8 @@
     def _():
         for copy in init_copies():
             copy.start()
+        if not first:
+            before_copy.start()
         k_s[2 * chip_len:, :] = jnp.zeros((BK, HEAD), BF)
         v_s[2 * chip_len:, :] = jnp.zeros((BK, HEAD), BF)
 
@@ -361,13 +369,18 @@
         by_rows(w_s.shape[0], narrow)
         part_copy = pltpu.make_async_copy(x_s, part_ref, out_sem.at[0])
         part_copy.start()
+        if not first:
+            before_copy.wait()
 
         def narrow_kv(r, carry):
             rows = span(r, 16)
             for n, acc in enumerate((dk_s, dv_s)):
                 for side in range(2):
-                    at = pl.ds(pl.multiple_of((2 * n + side) * HEAD + r * 16, 16), 16)
-                    g_s[at, :] = acc[rows, side * chip_len:(side + 1) * chip_len].astype(BF)
+                    at = pl.ds(pl.multiple_of((n + 2 * side) * HEAD + r * 16, 16), 16)
+                    total = acc[rows, side * chip_len:(side + 1) * chip_len]
+                    if not first:
+                        total = total + before_s[at, :].astype(F32)
+                    g_s[at, :] = total.astype(BF)
             return carry
 
         lax.fori_loop(0, HEAD // 16, narrow_kv, 0)
@@ -377,7 +390,8 @@
         dkv_copy.wait()
 
 
-def attention(chunk, core, lo, n_blocks, q, dctx, kdoc, tabs, kv_prev, kv_chip, xs, gs):
+def attention(chunk, core, lo, n_blocks, q, dctx, kdoc, tabs, kv_prev, kv_chip, xs, gs, before):
+    first = before is None
     chip_len = q.shape[0]
     width = xs[0].shape[1]
     assert 2 * WIDE == BQ == 4 * HEAD and width == chip_len
@@ -387,7 +401,7 @@
     full = lambda shape: pl.BlockSpec(shape, lambda i, *s: (0,) * len(shape))
     pairs = chip_len * chip_len * PAIR
     return pl.pallas_call(
-        attn_kernel,
+        functools.partial(attn_kernel, first),
         grid_spec=pltpu.PrefetchScalarGridSpec(
             num_scalar_prefetch=3,
             grid=(chip_len // BQ,),
@@ -395,7 +409,7 @@
                 pl.BlockSpec((BQ, WIDE), lambda i, *s: (i, chunk)),
                 pl.BlockSpec((BQ, WIDE), lambda i, *s: (i, chunk)),
                 full((1, padded)),
-            ] + [pl.BlockSpec(memory_space=pl.ANY)] * 10,
+            ] + [pl.BlockSpec(memory_space=pl.ANY)] * 11,
             out_specs=[
                 pl.BlockSpec((2, BQ, WIDE), lambda i, *s: (0, i, 0)),
                 pl.BlockSpec(memory_space=pl.ANY),
@@ -424,9 +438,10 @@
                 pltpu.VMEM((BQ, width), BF),
                 pltpu.VMEM((2 * WIDE, BQ), BF),
                 pltpu.VMEM((2 * WIDE, width), F32),
+                pltpu.VMEM((4 * HEAD, chip_len), BF),
                 pltpu.SemaphoreType.DMA((10,)),
                 pltpu.SemaphoreType.DMA((2,)),
-                pltpu.SemaphoreType.DMA((2,)),
+                pltpu.SemaphoreType.DMA((3,)),
             ],
         ),
         out_shape=[
@@ -437,11 +452,10 @@
         compiler_params=params(),
         cost_estimate=cost(pairs * HEAD * 2 * 8, 12 * 1024 * 1024, pairs),
         name="attention",
-    )(core, lo, n_blocks, q, dctx, kdoc, *tabs, *kv_prev, *kv_chip, *xs, *gs)
-
-
-def kv_finish_kernel(n, s_ref, *refs):
-    far_ref, tab_own, tab_oth, out_ref, outt_ref, tab_s = refs[n:]
+    )(core, lo, n_blocks, q, dctx, kdoc, *tabs, *kv_prev, *kv_chip, *xs, *gs, gs[0] if first else before)
+
+
+def kv_finish_kernel(s_ref, near_ref, far_ref, tab_own, tab_oth, out_ref, outt_ref, tab_s):
     tokens = tab_own.shape[0]
     step = out_ref.shape[0]
 
@@ -450,31 +464,29 @@
         tab_s[span(s_ref[0], tokens), :] = tab_own[...]
         tab_s[span(1 - s_ref[0], tokens), :] = tab_oth[...]
 
-    total = far_ref[...].astype(F32)
-    for ref in refs[:n]:
-        total = total + ref[:, 0].astype(F32)
+    total = near_ref[...].astype(F32) + far_ref[...].astype(F32)
     cos_t, sin_t = spread_table(tab_s[span(pl.program_id(0), step), :])
-    dk = total[0].astype(BF).astype(F32).T
+    dk = total[:HEAD].astype(BF).astype(F32).T
     dk = (dk * cos_t - swap_halves(dk) * sin_t).astype(BF)
-    dvt = total[1].astype(BF)
+    dvt = total[HEAD:].astype(BF)
     out_ref[:, :HEAD] = dk
     out_ref[:, HEAD:] = dvt.T
     outt_ref[:HEAD, :] = dk.T
     outt_ref[HEAD:, :] = dvt
 
 
-def kv_finish(core, parts, far, tab_own, tab_oth):
+def kv_finish(core, near, far, tab_own, tab_oth):
     tokens = tab_own.shape[0]
     chip_len = 2 * tokens
     step = 512
     return pl.pallas_call(
-        functools.partial(kv_finish_kernel, len(parts)),
+        kv_finish_kernel,
         grid_spec=pltpu.PrefetchScalarGridSpec(
             num_scalar_prefetch=1,
             grid=(chip_len // step,),
-            in_specs=[pl.BlockSpec((2, 1, HEAD, step), lambda t, s: (0, 1, 0, t))] * len(parts)
-            + [
-                pl.BlockSpec((2, HEAD, step), lambda t, s: (0, 0, t)),
+            in_specs=[
+                pl.BlockSpec((2 * HEAD, step), lambda t, s: (1, t)),
+                pl.BlockSpec((2 * HEAD, step), lambda t, s: (0, t)),
                 pl.BlockSpec((tokens, HEAD), lambda t, s: (0, 0)),
                 pl.BlockSpec((tokens, HEAD), lambda t, s: (0, 0)),
             ],
@@ -491,7 +503,7 @@
         compiler_params=params(),
         cost_estimate=cost(chip_len * HEAD * 64, chip_len * HEAD * 16),
         name="kv_finish",
-    )(core, *parts, far, tab_own, tab_oth)
+    )(core, near, far, tab_own, tab_oth)
 
 
 def kvgrad_kernel(s_ref, dkvt_ref, x_own, x_oth, out_ref):
@@ -710,8 +722,6 @@
         place = lax.axis_index("sp")
         core_id, chip_id = place & 1, place >> 1
         core = core_id.astype(jnp.int32)[None]
-        sel_own = jnp.stack([core_id, core_id]).astype(jnp.int32)
-        sel_oth = jnp.stack([core_id, 1 - core_id]).astype(jnp.int32)
 
         doc_oth = near(doc_ids)
         doc_far = far(doc_ids)
@@ -720,14 +730,14 @@
         g_oth = near(grad_out)
         tab_own = rope_table(positions)
         tab_oth = near(tab_own)
-        kv_own, q = qkv_proj(sel_own, hidden, w_q, w_k, w_v, tab_own, None)
+        kv_own, q = qkv_proj(True, core, hidden, w_q, w_k, w_v, tab_own, None)
         kvp_own = lax.ppermute(kv_own, "sp", down_perm)
 
         def in_order(own, oth):
             return jnp.where(core_id == 0, jnp.concatenate([own, oth]), jnp.concatenate([oth, own]))
 
         doc_chip, doc_far = in_order(doc_ids, doc_oth), in_order(doc_far, doc_far_oth)
-        kv_oth, q = qkv_proj(sel_oth, x_oth, w_q, w_k, w_v, tab_oth, q)
+        kv_oth, q = qkv_proj(False, core, x_oth, w_q, w_k, w_v, tab_oth, q)
         kvp_oth = lax.ppermute(kv_oth, "sp", down_perm)
         dctx = dctx_proj(core, grad_out, g_oth, w_o)
 
@@ -740,20 +750,18 @@
         n_blocks = (end - lo + BK - 1) >> (BK.bit_length() - 1)
         kdoc = jnp.concatenate([doc_far, doc_chip, jnp.zeros((BK,), jnp.int32)])[None, :]
 
-        acts, acts_oth, dkvs, sums = [], [], [], None
+        acts, acts_oth, dkv_sum, sums = [], [], None, None
         for j in range(n_chunks):
             act, part, dkv = attention(
                 j, core, lo, n_blocks, q, dctx, kdoc, (tab_own, tab_oth), (kvp_own, kvp_oth), (kv_own, kv_oth),
-                (hidden, x_oth), (grad_out, g_oth),
+                (hidden, x_oth), (grad_out, g_oth), dkv_sum,
             )
             part = part.reshape(2, WIDE, -1)
             acts.append(act)
-            dkvs.append(dkv.reshape(2, 2, HEAD, chip_len))
+            dkv_sum = dkv
             if j == n_chunks - 1:
-                dkv_up = (dkv_early + dkvs[j][:, 0].astype(F32)).astype(BF)
+                dkv_up = dkv[:2 * HEAD]
                 dkv_far = lax.ppermute(dkv_up, "sp", up_perm)
-            if j == n_chunks - 2:
-                dkv_early = lax.optimization_barrier(sum(d[:, 0].astype(F32) for d in dkvs))
             acts_oth.append(near(act))
             part_far = far(part)
             part_near = near(part)
@@ -761,7 +769,7 @@
             sums = combine(core, j, n_chunks, (part, part_far, part_near, part_far_near), sums)
         grad_wq, grad_wo = sums
 
-        dkv, dkvt = kv_finish(core, dkvs, dkv_far, tab_own, tab_oth)
+        dkv, dkvt = kv_finish(core, dkv_sum, dkv_far, tab_own, tab_oth)
         dkv_oth = near(dkv)
         kv_part = kvgrad(core, dkvt, hidden, x_oth)
         kv_part_far = far(kv_part)

time: 553 us -> 563 us (1.018)
  Pallas kernels: 257 us -> 271 us
  other arithmetic: 11.4 us -> 4.42 us
    pallas_call x2, Pallas kernels: 22.4 us -> 32.1 us  [qkv_proj(): pl.pallas_call(qkv_kernel, grid_spec=pltpu.PrefetchScalarGridSpec(num_sca...]
  transfers between devices with their start and end apart: 29 -> 29, of which waited for: 7 -> 7; matrix products, arithmetic and copies ran while one was open for 1% -> 1% of each run, Pallas kernels for 20% -> 22%
where the time goes in v7:
time: 563 us; the launch traced here: 561 us
  Pallas kernels  271 us (48%)
  waiting for transfers between devices  215 us (38%)
  starting transfers between devices  66 us (12%)
    ppermute x6, waiting for transfers between devices, far(): return lax.ppermute(v, 'sp', far_perm)  185 us
    pallas_call x4, Pallas kernels, attention(): pl.pallas_call(functools.partial(attn_kernel, first), grid_spec=pltpu.Pre...  139 us
    ppermute x6, starting transfers between devices, far(): return lax.ppermute(v, 'sp', far_perm)  53.4 us
    pallas_call x4, Pallas kernels, combine(): pl.pallas_call(combine_kernel, grid_spec=pltpu.PrefetchScalarGridSpec(num...  33.9 us
    pallas_call x2, Pallas kernels, qkv_proj(): pl.pallas_call(qkv_kernel, grid_spec=pltpu.PrefetchScalarGridSpec(num_sca...  32.1 us
    ppermute x1, waiting for transfers between devices, device_step(): dkv_far = lax.ppermute(dkv_up, 'sp', up_perm)  23.1 us
    pallas_call x1, Pallas kernels, dctx_proj(): pl.pallas_call(functools.partial(dctx_kernel, m_all), grid_spec=pltpu.Pre...  20.2 us
    pallas_call x1, Pallas kernels, grad_hidden(): pl.pallas_call(functools.partial(hidden_kernel, n), grid_spec=pltpu.Prefe...  17 us
  transfers between devices with their start and end apart: 29, of which 7 were waited for; matrix products, arithmetic and copies ran while one was open for 1% of the time, Pallas kernels for 22%

profile of v7, /device:TPU:0, one launch (start us, length us, event | category | flops | bytes accessed | tf_op | source)
XLA Modules:
  0.0 561.3 jit_solution(17550707546889605058)
XLA Ops:
  2.0 2.5 collective-permute-start.1
  5.2 1.9 multiply_cosine_fusion
  8.3 16.0 %qkv_proj.2 = (bf16[1024,256]{1,0:T(8,128)(2,1)}, bf16[2048,1024]{1,0:T(8,128)(2,1)}) custom-call(s32[1]{0:T(128)} %bitcast.s_ref.core_ref, bf16[1024,2048]{1,0:T(8,128)(2,1)} %x_own.9, bf16[2048,2048]{1,0:T(8,128)(2,1)} %refs_10_.1, bf16[2048,256]{1,0:T(8,128)(2,1)} %refs_11_.1, bf16[2048,256]{1,0:T(8,128)(2,1)} %refs_12_.1, ...), custom_call_target="tpu_custom_call" | custom-call | flops 5368709120 | bytes 8388608 | tf_op jit(solution)/shard_map/qkv_proj/pallas_call | solution.py:120
  24.5 4.6 collective-permute-start.6
  30.6 16.0 %qkv_proj.3 = (bf16[1024,256]{1,0:T(8,128)(2,1)}, bf16[2048,1024]{1,0:T(8,128)(2,1)}) custom-call(s32[1]{0:T(128)} %bitcast.s_ref.core_ref, bf16[1024,2048]{1,0:T(8,128)(2,1)} %collective-permute-done.3.x_ref.x_oth, bf16[2048,2048]{1,0:T(8,128)(2,1)} %refs_10_.1, bf16[2048,256]{1,0:T(8,128)(2,1)} %refs_11_.1, ...), custom_call_target="tpu_custom_call", output_to_operand_aliasing={{1}: (6, {})} | custom-call | flops 5368709120 | bytes 8388608 | tf_op jit(solution)/shard_map/qkv_proj/pallas_call | solution.py:120
  46.6 2.1 collective-permute-start.7
  48.7 20.2 %dctx_proj.1.do_ref = bf16[2048,1024]{1,0:T(8,128)(2,1)} custom-call(s32[1]{0:T(128)} %bitcast.s_ref.core_ref, bf16[1024,2048]{1,0:T(8,128)(2,1)} %g_own.7, bf16[1024,2048]{1,0:T(8,128)(2,1)} %collective-permute-done.5.oth_ref.g_oth, bf16[2048,2048]{1,0:T(8,128)(2,1)} %refs_8_.1), custom_call_target="tpu_custom_call" | custom-call | flops 8589934592 | bytes 12582912 | tf_op jit(solution)/shard_map/dctx_proj/pallas_call | solution.py:169
  68.9 34.8 %attention.4 = (bf16[2,2048,256]{2,1,0:T(8,128)(2,1)}, bf16[512,2048]{1,0:T(8,128)(2,1)}, bf16[512,2048]{1,0:T(8,128)(2,1)}) custom-call(s32[1]{0:T(128)} %bitcast.s_ref.core_ref, s32[4]{0:T(128)} %get-tuple-element.65.lo_ref, s32[4]{0:T(128)} %get-tuple-element.64.nb_ref, bf16[2048,1024]{1,0:T(8,128)(2,1)} %get-tuple-element.35.q_ref, ...), custom_call_target="tpu_custom_call" | custom-call | flops 17179869184 | bytes 12582912 | tf_op jit(solution)/shard_map/attention/pallas_call | solution.py:403
  103.7 34.8 %attention.5 = (bf16[2,2048,256]{2,1,0:T(8,128)(2,1)}, bf16[512,2048]{1,0:T(8,128)(2,1)}, bf16[512,2048]{1,0:T(8,128)(2,1)}) custom-call(s32[1]{0:T(128)} %bitcast.s_ref.core_ref, s32[4]{0:T(128)} %get-tuple-element.65.lo_ref, s32[4]{0:T(128)} %get-tuple-element.64.nb_ref, bf16[2048,1024]{1,0:T(8,128)(2,1)} %get-tuple-element.35.q_ref, ...), custom_call_target="tpu_custom_call" | custom-call | flops 17179869184 | bytes 12582912 | tf_op jit(solution)/shard_map/attention/pallas_call | solution.py:403
  138.4 34.9 %attention.6 = (bf16[2,2048,256]{2,1,0:T(8,128)(2,1)}, bf16[512,2048]{1,0:T(8,128)(2,1)}, bf16[512,2048]{1,0:T(8,128)(2,1)}) custom-call(s32[1]{0:T(128)} %bitcast.s_ref.core_ref, s32[4]{0:T(128)} %get-tuple-element.65.lo_ref, s32[4]{0:T(128)} %get-tuple-element.64.nb_ref, bf16[2048,1024]{1,0:T(8,128)(2,1)} %get-tuple-element.35.q_ref, ...), custom_call_target="tpu_custom_call" | custom-call | flops 17179869184 | bytes 12582912 | tf_op jit(solution)/shard_map/attention/pallas_call | solution.py:403
  173.4 34.7 %attention.7 = (bf16[2,2048,256]{2,1,0:T(8,128)(2,1)}, bf16[512,2048]{1,0:T(8,128)(2,1)}, bf16[512,2048]{1,0:T(8,128)(2,1)}) custom-call(s32[1]{0:T(128)} %bitcast.s_ref.core_ref, s32[4]{0:T(128)} %get-tuple-element.65.lo_ref, s32[4]{0:T(128)} %get-tuple-element.64.nb_ref, bf16[2048,1024]{1,0:T(8,128)(2,1)} %get-tuple-element.35.q_ref, ...), custom_call_target="tpu_custom_call" | custom-call | flops 17179869184 | bytes 12582912 | tf_op jit(solution)/shard_map/attention/pallas_call | solution.py:403
  208.1 1.3 slice.7
  209.4 1.3 collective-permute-start.12
  210.7 46.9 %collective-permute-start.23 = (bf16[2,256,2048]{2,1,0:T(8,128)(2,1)}, bf16[2,256,2048]{2,1,0:T(8,128)(2,1)}, u32[]{:S(2)}, u32[]{:S(2)}) collective-permute-start(bf16[2,256,2048]{2,1,0:T(8,128)(2,1)} %bitcast.4.a_ref), channel_id=1, source_target_pairs={{0,2},{1,3},{2,0},{3,1},{4,6},{5,7},{6,4},{7,5}} | collective-permute-start | bytes 6291464 | tf_op jit(solution)/shard_map/ppermute | solution.py:716
  257.6 23.1 %collective-permute-done.12.far_ref = bf16[256,2048]{1,0:T(8,128)(2,1)} collective-permute-done((bf16[256,2048]{1,0:T(8,128)(2,1)S(1)}, bf16[256,2048]{1,0:T(8,128)(2,1)}, u32[]{:S(2)}, u32[]{:S(2)}) %collective-permute-start.12) | collective-permute-done | bytes 1048608 | tf_op jit(solution)/shard_map/ppermute | solution.py:764
  280.7 4.6 kv_finish.1
  285.3 6.6 %kvgrad.1.a_ref = bf16[256,2048]{1,0:T(8,128)(2,1)} custom-call(s32[1]{0:T(128)} %bitcast.s_ref.core_ref, bf16[256,2048]{1,0:T(8,128)(2,1)} %get-tuple-element.58.dkvt_ref, bf16[1024,2048]{1,0:T(8,128)(2,1)} %x_own.9, bf16[1024,2048]{1,0:T(8,128)(2,1)} %collective-permute-done.3.x_ref.x_oth), custom_call_target="tpu_custom_call" | custom-call | flops 2147483648 | bytes 8388608 | tf_op jit(solution)/shard_map/kvgrad/pallas_call | solution.py:519
  292.4 2.0 collective-permute-start.20
  294.4 53.6 %collective-permute-done.26.b_ref = bf16[256,2048]{1,0:T(8,128)(2,1)S(1)} collective-permute-done((bf16[256,2048]{1,0:T(8,128)(2,1)}, bf16[256,2048]{1,0:T(8,128)(2,1)S(1)}, u32[]{:S(2)}, u32[]{:S(2)}) %collective-permute-start.26) | collective-permute-done | bytes 1048608 | tf_op jit(solution)/shard_map/ppermute | solution.py:716
  348.1 2.0 collective-permute-start.14
  350.1 43.0 %collective-permute-done.20.b_ref = bf16[2,256,2048]{2,1,0:T(8,128)(2,1)} collective-permute-done((bf16[2,256,2048]{2,1,0:T(8,128)(2,1)}, bf16[2,256,2048]{2,1,0:T(8,128)(2,1)}, u32[]{:S(2)}, u32[]{:S(2)}) %collective-permute-start.20) | collective-permute-done | bytes 2097184 | tf_op jit(solution)/shard_map/ppermute | solution.py:716
  393.6 44.4 %collective-permute-done.17.b_ref = bf16[2,256,2048]{2,1,0:T(8,128)(2,1)} collective-permute-done((bf16[2,256,2048]{2,1,0:T(8,128)(2,1)}, bf16[2,256,2048]{2,1,0:T(8,128)(2,1)}, u32[]{:S(2)}, u32[]{:S(2)}) %collective-permute-start.17) | collective-permute-done | bytes 2097184 | tf_op jit(solution)/shard_map/ppermute | solution.py:716
  438.0 44.4 %collective-permute-done.14.b_ref = bf16[2,256,2048]{2,1,0:T(8,128)(2,1)} collective-permute-done((bf16[2,256,2048]{2,1,0:T(8,128)(2,1)}, bf16[2,256,2048]{2,1,0:T(8,128)(2,1)}, u32[]{:S(2)}, u32[]{:S(2)}) %collective-permute-start.14) | collective-permute-done | bytes 2097184 | tf_op jit(solution)/shard_map/ppermute | solution.py:716
  484.5 2.3 collective-permute-done.8.refs_4_
  487.0 4.4 collective-permute-done.28.d_ref
  492.5 13.8 %attn_out.1 = bf16[1024,2048]{1,0:T(8,128)(2,1)} custom-call(s32[1]{0:T(128)} %bitcast.s_ref.core_ref, bf16[2,2048,256]{2,1,0:T(8,128)(2,1)} %get-tuple-element.38.refs_0_, bf16[2,2048,256]{2,1,0:T(8,128)(2,1)} %get-tuple-element.40.refs_1_, bf16[2,2048,256]{2,1,0:T(8,128)(2,1)} %get-tuple-element.42.refs_2_, ...), custom_call_target="tpu_custom_call" | custom-call | flops 8589934592 | bytes 16777216 | tf_op jit(solution)/shard_map/attn_out/pallas_call | solution.py:637
  506.3 17.0 %grad_hidden.1 = bf16[1024,2048]{1,0:T(8,128)(2,1)} custom-call(s32[1]{0:T(128)} %bitcast.s_ref.core_ref, bf16[2,2048,256]{2,1,0:T(8,128)(2,1)} %get-tuple-element.38.refs_0_, bf16[2,2048,256]{2,1,0:T(8,128)(2,1)} %get-tuple-element.40.refs_1_, bf16[2,2048,256]{2,1,0:T(8,128)(2,1)} %get-tuple-element.42.refs_2_, ...), custom_call_target="tpu_custom_call" | custom-call | flops 10737418240 | bytes 16777216 | tf_op jit(solution)/shard_map/grad_hidden/pallas_call | solution.py:678
  523.3 4.1 kv_combine.1
  527.4 8.5 %combine.4 = (f32[2048,2048]{1,0:T(8,128)}, f32[2048,2048]{1,0:T(8,128)}) custom-call(s32[1]{0:T(128)} %bitcast.s_ref.core_ref, bf16[2,256,2048]{2,1,0:T(8,128)(2,1)} %bitcast.4.a_ref, bf16[2,256,2048]{2,1,0:T(8,128)(2,1)} %collective-permute-done.23.b_ref, bf16[2,256,2048]{2,1,0:T(8,128)(2,1)} %collective-permute-done.24.c_ref, ...), custom_call_target="tpu_custom_call" | custom-call | flops 536870912 | bytes 16777216 | tf_op jit(solution)/shard_map/combine/pallas_call | solution.py:595
  535.8 8.5 %combine.5 = (f32[2048,2048]{1,0:T(8,128)}, f32[2048,2048]{1,0:T(8,128)}) custom-call(s32[1]{0:T(128)} %bitcast.s_ref.core_ref, bf16[2,256,2048]{2,1,0:T(8,128)(2,1)} %bitcast.13, bf16[2,256,2048]{2,1,0:T(8,128)(2,1)} %collective-permute-done.20.b_ref, ...), custom_call_target="tpu_custom_call", output_to_operand_aliasing={{0}: (5, {}), {1}: (6, {})} | custom-call | flops 536870912 | bytes 16777216 | tf_op jit(solution)/shard_map/combine/pallas_call | solution.py:595
  544.3 8.5 %combine.6 = (f32[2048,2048]{1,0:T(8,128)}, f32[2048,2048]{1,0:T(8,128)}) custom-call(s32[1]{0:T(128)} %bitcast.s_ref.core_ref, bf16[2,256,2048]{2,1,0:T(8,128)(2,1)} %bitcast.10, bf16[2,256,2048]{2,1,0:T(8,128)(2,1)} %collective-permute-done.17.b_ref, ...), custom_call_target="tpu_custom_call", output_to_operand_aliasing={{0}: (5, {}), {1}: (6, {})} | custom-call | flops 536870912 | bytes 16777216 | tf_op jit(solution)/shard_map/combine/pallas_call | solution.py:595
  552.8 8.5 %combine.7 = (f32[2048,2048]{1,0:T(8,128)}, f32[2048,2048]{1,0:T(8,128)}) custom-call(s32[1]{0:T(128)} %bitcast.s_ref.core_ref, bf16[2,256,2048]{2,1,0:T(8,128)(2,1)} %bitcast.7, bf16[2,256,2048]{2,1,0:T(8,128)(2,1)} %collective-permute-done.14.b_ref, ...), custom_call_target="tpu_custom_call", output_to_operand_aliasing={{0}: (5, {}), {1}: (6, {})} | custom-call | flops 536870912 | bytes 16777216 | tf_op jit(solution)/shard_map/combine/pallas_call | solution.py:595
  (71 shorter events, 9.3 us)
Async XLA Ops:
  0.6 30.0 %collective-permute-start.3 = (bf16[1024,2048]{1,0:T(8,128)(2,1)}, bf16[1024,2048]{1,0:T(8,128)(2,1)}, u32[]{:S(2)}, u32[]{:S(2)}) collective-permute-start(bf16[1024,2048]{1,0:T(8,128)(2,1)} %x_own.9), channel_id=1, source_target_pairs={{0,1},{1,0},{2,3},{3,2},{4,5},{5,4},{6,7},{7,6}} | collective-permute-start | bytes 12582920 | tf_op jit(solution)/shard_map/ppermute | solution.py:713
  1.5 47.2 %collective-permute-start.5 = (bf16[1024,2048]{1,0:T(8,128)(2,1)}, bf16[1024,2048]{1,0:T(8,128)(2,1)}, u32[]{:S(2)}, u32[]{:S(2)}) collective-permute-start(bf16[1024,2048]{1,0:T(8,128)(2,1)} %g_own.7), channel_id=1, source_target_pairs={{0,1},{1,0},{2,3},{3,2},{4,5},{5,4},{6,7},{7,6}} | collective-permute-start | bytes 12582920 | tf_op jit(solution)/shard_map/ppermute | solution.py:713
  1.5 22.8 %collective-permute-start = (s32[1024]{0:T(1024)}, s32[1024]{0:T(1024)S(1)}, u32[]{:S(2)}, u32[]{:S(2)}) collective-permute-start(s32[1024]{0:T(1024)} %param.11), channel_id=1, source_target_pairs={{0,1},{1,0},{2,3},{3,2},{4,5},{5,4},{6,7},{7,6}} | collective-permute-start | bytes 12296 | tf_op jit(solution)/shard_map/ppermute | solution.py:713
  2.0 22.5 %collective-permute-start.1 = (s32[1024]{0:T(1024)}, s32[1024]{0:T(1024)S(1)}, u32[]{:S(2)}, u32[]{:S(2)}) collective-permute-start(s32[1024]{0:T(1024)} %param.11), channel_id=1, source_target_pairs={{0,2},{1,3},{2,0},{3,1},{4,6},{5,7},{6,4},{7,5}} | collective-permute-start | bytes 12296 | tf_op jit(solution)/shard_map/ppermute | solution.py:716
  8.1 22.4 %collective-permute-start.4 = (f32[1024,128]{1,0:T(8,128)}, f32[1024,128]{1,0:T(8,128)}, u32[]{:S(2)}, u32[]{:S(2)}) collective-permute-start(f32[1024,128]{1,0:T(8,128)} %pad_maximum_fusion.tab_ref.tab_own), channel_id=1, source_target_pairs={{0,1},{1,0},{2,3},{3,2},{4,5},{5,4},{6,7},{7,6}} | collective-permute-start | bytes 1572872 | tf_op jit(solution)/shard_map/ppermute | solution.py:713
  8.3 16.0 %copy-start.3 = (s32[1024]{0:T(1024)S(1)}, s32[1024]{0:T(1024)}, u32[]{:S(2)}) copy-start(s32[1024]{0:T(1024)} %param.11) | copy-start | bytes 12292
  24.4 4.8 collective-permute-start.2
  24.5 44.4 %collective-permute-start.6 = (bf16[1024,256]{1,0:T(8,128)(2,1)}, bf16[1024,256]{1,0:T(8,128)(2,1)}, u32[]{:S(2)}, u32[]{:S(2)}) collective-permute-start(bf16[1024,256]{1,0:T(8,128)(2,1)} %get-tuple-element.36.kvc_own), channel_id=1, source_target_pairs={{0,2},{1,3},{4,6},{5,7}} | collective-permute-start | bytes 1572872 | tf_op jit(solution)/shard_map/ppermute | solution.py:734
  46.6 22.3 %collective-permute-start.7 = (bf16[1024,256]{1,0:T(8,128)(2,1)}, bf16[1024,256]{1,0:T(8,128)(2,1)}, u32[]{:S(2)}, u32[]{:S(2)}) collective-permute-start(bf16[1024,256]{1,0:T(8,128)(2,1)} %get-tuple-element.37.kvc_oth), channel_id=1, source_target_pairs={{0,2},{1,3},{4,6},{5,7}} | collective-permute-start | bytes 1572872 | tf_op jit(solution)/shard_map/ppermute | solution.py:741
  209.4 71.3 %collective-permute-start.12 = (bf16[256,2048]{1,0:T(8,128)(2,1)S(1)}, bf16[256,2048]{1,0:T(8,128)(2,1)}, u32[]{:S(2)}, u32[]{:S(2)}) collective-permute-start(bf16[256,2048]{1,0:T(8,128)(2,1)S(1)} %slice.7), channel_id=1, source_target_pairs={{2,0},{3,1},{6,4},{7,5}} | collective-permute-start | bytes 3145736 | tf_op jit(solution)/shard_map/ppermute | solution.py:764
  210.7 137.4 %collective-permute-start.23 = (bf16[2,256,2048]{2,1,0:T(8,128)(2,1)}, bf16[2,256,2048]{2,1,0:T(8,128)(2,1)}, u32[]{:S(2)}, u32[]{:S(2)}) collective-permute-start(bf16[2,256,2048]{2,1,0:T(8,128)(2,1)} %bitcast.4.a_ref), channel_id=1, source_target_pairs={{0,2},{1,3},{2,0},{3,1},{4,6},{5,7},{6,4},{7,5}} | collective-permute-start | bytes 6291464 | tf_op jit(solution)/shard_map/ppermute | solution.py:716
  291.9 56.1 %collective-permute-start.26 = (bf16[256,2048]{1,0:T(8,128)(2,1)}, bf16[256,2048]{1,0:T(8,128)(2,1)S(1)}, u32[]{:S(2)}, u32[]{:S(2)}) collective-permute-start(bf16[256,2048]{1,0:T(8,128)(2,1)} %kvgrad.1.a_ref), channel_id=1, source_target_pairs={{0,2},{1,3},{2,0},{3,1},{4,6},{5,7},{6,4},{7,5}} | collective-permute-start | bytes 3145736 | tf_op jit(solution)/shard_map/ppermute | solution.py:716
  291.9 56.1 %collective-permute-start.27 = (bf16[256,2048]{1,0:T(8,128)(2,1)}, bf16[256,2048]{1,0:T(8,128)(2,1)S(1)}, u32[]{:S(2)}, u32[]{:S(2)}) collective-permute-start(bf16[256,2048]{1,0:T(8,128)(2,1)} %kvgrad.1.a_ref), channel_id=1, source_target_pairs={{0,1},{1,0},{2,3},{3,2},{4,5},{5,4},{6,7},{7,6}} | collective-permute-start | bytes 3145736 | tf_op jit(solution)/shard_map/ppermute | solution.py:713
  291.9 58.2 %collective-permute-start.24 = (bf16[2,256,2048]{2,1,0:T(8,128)(2,1)}, bf16[2,256,2048]{2,1,0:T(8,128)(2,1)}, u32[]{:S(2)}, u32[]{:S(2)}) collective-permute-start(bf16[2,256,2048]{2,1,0:T(8,128)(2,1)} %bitcast.4.a_ref), channel_id=1, source_target_pairs={{0,1},{1,0},{2,3},{3,2},{4,5},{5,4},{6,7},{7,6}} | collective-permute-start | bytes 6291464 | tf_op jit(solution)/shard_map/ppermute | solution.py:713
  292.4 100.6 %collective-permute-start.20 = (bf16[2,256,2048]{2,1,0:T(8,128)(2,1)}, bf16[2,256,2048]{2,1,0:T(8,128)(2,1)}, u32[]{:S(2)}, u32[]{:S(2)}) collective-permute-start(bf16[2,256,2048]{2,1,0:T(8,128)(2,1)} %bitcast.11), channel_id=1, source_target_pairs={{0,2},{1,3},{2,0},{3,1},{4,6},{5,7},{6,4},{7,5}} | collective-permute-start | bytes 6291464 | tf_op jit(solution)/shard_map/ppermute | solution.py:716
  348.0 135.5 %copy-start = (bf16[256,2048]{1,0:T(8,128)(2,1)}, bf16[256,2048]{1,0:T(8,128)(2,1)S(1)}, u32[]{:S(2)}) copy-start(bf16[256,2048]{1,0:T(8,128)(2,1)S(1)} %collective-permute-done.26.b_ref) | copy-start | bytes 3145732
  348.0 45.1 %collective-permute-start.21 = (bf16[2,256,2048]{2,1,0:T(8,128)(2,1)}, bf16[2,256,2048]{2,1,0:T(8,128)(2,1)}, u32[]{:S(2)}, u32[]{:S(2)}) collective-permute-start(bf16[2,256,2048]{2,1,0:T(8,128)(2,1)} %bitcast.12), channel_id=1, source_target_pairs={{0,1},{1,0},{2,3},{3,2},{4,5},{5,4},{6,7},{7,6}} | collective-permute-start | bytes 6291464 | tf_op jit(solution)/shard_map/ppermute | solution.py:713
  348.0 143.3 %copy-start.1 = (bf16[256,2048]{1,0:T(8,128)(2,1)}, bf16[256,2048]{1,0:T(8,128)(2,1)S(1)}, u32[]{:S(2)}) copy-start(bf16[256,2048]{1,0:T(8,128)(2,1)S(1)} %collective-permute-done.27.c_ref) | copy-start | bytes 3145732
  348.0 90.0 %collective-permute-start.17 = (bf16[2,256,2048]{2,1,0:T(8,128)(2,1)}, bf16[2,256,2048]{2,1,0:T(8,128)(2,1)}, u32[]{:S(2)}, u32[]{:S(2)}) collective-permute-start(bf16[2,256,2048]{2,1,0:T(8,128)(2,1)} %bitcast.8), channel_id=1, source_target_pairs={{0,2},{1,3},{2,0},{3,1},{4,6},{5,7},{6,4},{7,5}} | collective-permute-start | bytes 6291464 | tf_op jit(solution)/shard_map/ppermute | solution.py:716
  348.1 134.4 %collective-permute-start.14 = (bf16[2,256,2048]{2,1,0:T(8,128)(2,1)}, bf16[2,256,2048]{2,1,0:T(8,128)(2,1)}, u32[]{:S(2)}, u32[]{:S(2)}) collective-permute-start(bf16[2,256,2048]{2,1,0:T(8,128)(2,1)} %bitcast.5), channel_id=1, source_target_pairs={{0,2},{1,3},{2,0},{3,1},{4,6},{5,7},{6,4},{7,5}} | collective-permute-start | bytes 6291464 | tf_op jit(solution)/shard_map/ppermute | solution.py:716
  350.1 133.4 %collective-permute-start.11 = (bf16[2,2048,256]{2,1,0:T(8,128)(2,1)}, bf16[2,2048,256]{2,1,0:T(8,128)(2,1)}, u32[]{:S(2)}, u32[]{:S(2)}) collective-permute-start(bf16[2,2048,256]{2,1,0:T(8,128)(2,1)} %get-tuple-element.44.refs_3_), channel_id=1, source_target_pairs={{0,1},{1,0},{2,3},{3,2},{4,5},{5,4},{6,7},{7,6}} | collective-permute-start | bytes 6291464 | tf_op jit(solution)/shard_map/ppermute | solution.py:713
  393.1 89.4 %collective-permute-start.13 = (bf16[2048,256]{1,0:T(8,128)(2,1)}, bf16[2048,256]{1,0:T(8,128)(2,1)S(1)}, u32[]{:S(2)}, u32[]{:S(2)}) collective-permute-start(bf16[2048,256]{1,0:T(8,128)(2,1)} %get-tuple-element.46.refs_8_), channel_id=1, source_target_pairs={{0,1},{1,0},{2,3},{3,2},{4,5},{5,4},{6,7},{7,6}} | collective-permute-start | bytes 3145736 | tf_op jit(solution)/shard_map/ppermute | solution.py:713
  393.1 90.9 %collective-permute-start.10 = (bf16[2,2048,256]{2,1,0:T(8,128)(2,1)}, bf16[2,2048,256]{2,1,0:T(8,128)(2,1)S(1)}, u32[]{:S(2)}, u32[]{:S(2)}) collective-permute-start(bf16[2,2048,256]{2,1,0:T(8,128)(2,1)} %get-tuple-element.42.refs_2_), channel_id=1, source_target_pairs={{0,1},{1,0},{2,3},{3,2},{4,5},{5,4},{6,7},{7,6}} | collective-permute-start | bytes 6291464 | tf_op jit(solution)/shard_map/ppermute | solution.py:713
  438.0 46.0 %collective-permute-start.9 = (bf16[2,2048,256]{2,1,0:T(8,128)(2,1)}, bf16[2,2048,256]{2,1,0:T(8,128)(2,1)S(1)}, u32[]{:S(2)}, u32[]{:S(2)}) collective-permute-start(bf16[2,2048,256]{2,1,0:T(8,128)(2,1)} %get-tuple-element.40.refs_1_), channel_id=1, source_target_pairs={{0,1},{1,0},{2,3},{3,2},{4,5},{5,4},{6,7},{7,6}} | collective-permute-start | bytes 6291464 | tf_op jit(solution)/shard_map/ppermute | solution.py:713
  482.4 4.4 collective-permute-start.8
  482.5 9.8 %collective-permute-start.25 = (bf16[2,256,2048]{2,1,0:T(8,128)(2,1)}, bf16[2,256,2048]{2,1,0:T(8,128)(2,1)}, u32[]{:S(2)}, u32[]{:S(2)}) collective-permute-start(bf16[2,256,2048]{2,1,0:T(8,128)(2,1)} %collective-permute-done.23.b_ref), channel_id=1, source_target_pairs={{0,1},{1,0},{2,3},{3,2},{4,5},{5,4},{6,7},{7,6}} | collective-permute-start | bytes 6291464 | tf_op jit(solution)/shard_map/ppermute | solution.py:713
  483.5 7.8 %collective-permute-start.28 = (bf16[256,2048]{1,0:T(8,128)(2,1)S(1)}, bf16[256,2048]{1,0:T(8,128)(2,1)S(1)}, u32[]{:S(2)}, u32[]{:S(2)}) collective-permute-start(bf16[256,2048]{1,0:T(8,128)(2,1)S(1)} %collective-permute-done.26.b_ref), channel_id=1, source_target_pairs={{0,1},{1,0},{2,3},{3,2},{4,5},{5,4},{6,7},{7,6}} | collective-permute-start | bytes 3145736 | tf_op jit(solution)/shard_map/ppermute | solution.py:713
  484.0 51.8 %collective-permute-start.22 = (bf16[2,256,2048]{2,1,0:T(8,128)(2,1)}, bf16[2,256,2048]{2,1,0:T(8,128)(2,1)}, u32[]{:S(2)}, u32[]{:S(2)}) collective-permute-start(bf16[2,256,2048]{2,1,0:T(8,128)(2,1)} %collective-permute-done.20.b_ref), channel_id=1, source_target_pairs={{0,1},{1,0},{2,3},{3,2},{4,5},{5,4},{6,7},{7,6}} | collective-permute-start | bytes 6291464 | tf_op jit(solution)/shard_map/ppermute | solution.py:713
  484.0 60.3 %collective-permute-start.18 = (bf16[2,256,2048]{2,1,0:T(8,128)(2,1)}, bf16[2,256,2048]{2,1,0:T(8,128)(2,1)}, u32[]{:S(2)}, u32[]{:S(2)}) collective-permute-start(bf16[2,256,2048]{2,1,0:T(8,128)(2,1)} %bitcast.9), channel_id=1, source_target_pairs={{0,1},{1,0},{2,3},{3,2},{4,5},{5,4},{6,7},{7,6}} | collective-permute-start | bytes 6291464 | tf_op jit(solution)/shard_map/ppermute | solution.py:713
  486.8 57.5 %collective-permute-start.19 = (bf16[2,256,2048]{2,1,0:T(8,128)(2,1)}, bf16[2,256,2048]{2,1,0:T(8,128)(2,1)}, u32[]{:S(2)}, u32[]{:S(2)}) collective-permute-start(bf16[2,256,2048]{2,1,0:T(8,128)(2,1)} %collective-permute-done.17.b_ref), channel_id=1, source_target_pairs={{0,1},{1,0},{2,3},{3,2},{4,5},{5,4},{6,7},{7,6}} | collective-permute-start | bytes 6291464 | tf_op jit(solution)/shard_map/ppermute | solution.py:713
  491.3 61.5 %collective-permute-start.15 = (bf16[2,256,2048]{2,1,0:T(8,128)(2,1)}, bf16[2,256,2048]{2,1,0:T(8,128)(2,1)}, u32[]{:S(2)}, u32[]{:S(2)}) collective-permute-start(bf16[2,256,2048]{2,1,0:T(8,128)(2,1)} %bitcast.6), channel_id=1, source_target_pairs={{0,1},{1,0},{2,3},{3,2},{4,5},{5,4},{6,7},{7,6}} | collective-permute-start | bytes 6291464 | tf_op jit(solution)/shard_map/ppermute | solution.py:713
  492.3 60.5 %collective-permute-start.16 = (bf16[2,256,2048]{2,1,0:T(8,128)(2,1)}, bf16[2,256,2048]{2,1,0:T(8,128)(2,1)}, u32[]{:S(2)}, u32[]{:S(2)}) collective-permute-start(bf16[2,256,2048]{2,1,0:T(8,128)(2,1)} %collective-permute-done.14.b_ref), channel_id=1, source_target_pairs={{0,1},{1,0},{2,3},{3,2},{4,5},{5,4},{6,7},{7,6}} | collective-permute-start | bytes 6291464 | tf_op jit(solution)/shard_map/ppermute | solution.py:713
  (5 other events, 24.1 us)

commit v8 on v6

--- a/solution.py
+++ b/solution.py
@@ -103,7 +103,7 @@
             q_ref[:, at:at + HEAD] = (part * cos_t + swap_halves(part) * sin_t).astype(BF)
 
 
-def qkv_proj(sel, x, w_q, w_k, w_v, tab, prev):
+def qkv_proj(own, core, x, w_q, w_k, w_v, tab, prev):
     tokens, width = x.shape
     cols = w_q.shape[1] // 2
     rows = tokens // 2
@@ -122,7 +122,7 @@
             ] + [pl.BlockSpec(memory_space=pl.ANY)] * len(extra),
             out_specs=[
                 pl.BlockSpec((rows, 2 * HEAD), lambda m, s: (m, 0)),
-                pl.BlockSpec((rows, cols), lambda m, s: (s[1] * 2 + m, 0)),
+                pl.BlockSpec((rows, cols), lambda m, s: ((s[0] if own else 1 - s[0]) * 2 + m, 0)),
             ],
             scratch_shapes=[pltpu.VMEM((width, 2 * HEAD), BF)],
         ),
@@ -134,7 +134,7 @@
         compiler_params=params(),
         cost_estimate=cost(2 * tokens * width * (cols + 2 * HEAD), tokens * width * 2 + cols * width * 2),
         name="qkv_proj",
-    )(sel, x, w_q, w_k, w_v, tab, *extra)
+    )(core, x, w_q, w_k, w_v, tab, *extra)
 
 
 def dctx_kernel(s_ref, own_ref, oth_ref, wo_ref, out_ref):
@@ -181,11 +181,18 @@
 
 
 def attn_kernel(
-    core_ref, lo_ref, nb_ref, q_ref, do_ref, kdoc_ref, tab_own, tab_oth, kvp_own, kvp_oth, kvc_own, kvc_oth,
-    x_own, x_oth, g_own, g_oth, act_ref, part_ref, dkv_ref,
-    k_s, v_s, s_s, dp_s, m_s, l_s, d_s, qd_s, ahead_s, ctx_s, dq_s, q_s, do_s, qt_s, dot_s, tab_s, dk_s, dv_s,
-    x_s, g_s, at_s, w_s, init_sem, row_sem, out_sem,
+    first, core_ref, lo_ref, nb_ref, q_ref, do_ref, kdoc_ref, tab_own, tab_oth, kvp_own, kvp_oth, kvc_own, kvc_oth,
+    x_own, x_oth, g_own, g_oth, before_up, before_here, act_ref, part_ref, up_ref, here_ref,
+    kv_s, s_s, dp_s, m_s, l_s, d_s, qd_s, ahead_s, ctx_s, dq_s, q_s, do_s, qt_s, dot_s, tab_s, dk_s, dv_s,
+    x_s, g_s, at_s, w_s, before_s, init_sem, row_sem, out_sem,
 ):
+
+    def before_copies():
+        return (
+            pltpu.make_async_copy(before_up, before_s.at[pl.ds(0, 2 * HEAD), :], out_sem.at[3]),
+            pltpu.make_async_copy(before_here, before_s.at[pl.ds(2 * HEAD, 2 * HEAD), :], out_sem.at[4]),
+        )
+
     i = pl.program_id(0)
     tokens = kvc_own.shape[0]
     chip_len = 2 * tokens
@@ -202,9 +209,7 @@
     def init_copies():
         moves = []
         for base, place, ref in ((0, core, kvp_own), (0, 1 - core, kvp_oth), (2, core, kvc_own), (2, 1 - core, kvc_oth)):
-            moves.append((ref.at[:, pl.ds(0, HEAD)], k_s.at[span(base + place, tokens), :]))
-        for base, place, ref in ((0, core, kvp_own), (0, 1 - core, kvp_oth), (2, core, kvc_own), (2, 1 - core, kvc_oth)):
-            moves.append((ref.at[:, pl.ds(HEAD, HEAD)], v_s.at[span(base + place, tokens), :]))
+            moves.append((ref, kv_s.at[span(base + place, tokens), :]))
         moves.append((tab_own, tab_s.at[span(core, tokens), :]))
         moves.append((tab_oth, tab_s.at[span(1 - core, tokens), :]))
         return [pltpu.make_async_copy(src, dst, init_sem.at[n]) for n, (src, dst) in enumerate(moves)]
@@ -219,8 +224,10 @@
     def _():
         for copy in init_copies():
             copy.start()
-        k_s[2 * chip_len:, :] = jnp.zeros((BK, HEAD), BF)
-        v_s[2 * chip_len:, :] = jnp.zeros((BK, HEAD), BF)
+        if not first:
+            for copy in before_copies():
+                copy.start()
+        kv_s[2 * chip_len:, :] = jnp.zeros((BK, 2 * HEAD), BF)
 
         def clear(r):
             w_s[r, :] = jnp.zeros((16, w_s.shape[1]), F32)
@@ -284,7 +291,7 @@
 
     def scores(b, carry):
         off = offset(b)
-        s = dot_nt(q_s[...], k_s[pl.ds(off, BK), :])
+        s = dot_nt(q_s[...], kv_s[pl.ds(off, BK), :HEAD])
         limit = chip_len + i * BQ - off
         key_doc = kdoc_ref[:, pl.ds(off, BK)]
         for c in range(BQ // MIX):
@@ -303,7 +310,7 @@
     m_s[...] = jnp.broadcast_to(jnp.max(m_s[...], axis=1, keepdims=True), m_s.shape)
 
     def weights(b, carry):
-        dp = dot_nt(do_s[...], v_s[pl.ds(offset(b), BK), :])
+        dp = dot_nt(do_s[...], kv_s[pl.ds(offset(b), BK), HEAD:])
         e = jnp.exp2(s_s[b] - spread(m_s[...]))
         s_s[b] = e
         dp_s[b] = dp
@@ -311,7 +318,7 @@
         d_s[...] += fold(e * dp, jnp.add)
         return carry
 
-    arrive(4, 10)
+    arrive(4, 6)
     lax.fori_loop(0, n_blocks, weights, 0)
     inv = 1.0 / jnp.sum(l_s[...], axis=1, keepdims=True)
     delta = jnp.sum(d_s[...], axis=1, keepdims=True) * inv
@@ -323,8 +330,8 @@
         p = s_s[b] * spread(l_s[...])
         pb = p.astype(BF)
         ds = (p * (dp_s[b] - spread(d_s[...])) * SCALE).astype(BF)
-        ctx_s[...] += dot_nn(pb, v_s[pl.ds(off, BK), :])
-        dq_s[...] += dot_nn(ds, k_s[pl.ds(off, BK), :])
+        ctx_s[...] += dot_nn(pb, kv_s[pl.ds(off, BK), HEAD:])
+        dq_s[...] += dot_nn(ds, kv_s[pl.ds(off, BK), :HEAD])
         dv_s[:, pl.ds(off, BK)] += dot_nn(dot_s[...], pb)
         dk_s[:, pl.ds(off, BK)] += dot_nn(qt_s[...], ds)
         return carry
@@ -361,23 +368,33 @@
         by_rows(w_s.shape[0], narrow)
         part_copy = pltpu.make_async_copy(x_s, part_ref, out_sem.at[0])
         part_copy.start()
+        if not first:
+            for copy in before_copies():
+                copy.wait()
 
         def narrow_kv(r, carry):
             rows = span(r, 16)
             for n, acc in enumerate((dk_s, dv_s)):
                 for side in range(2):
-                    at = pl.ds(pl.multiple_of((2 * n + side) * HEAD + r * 16, 16), 16)
-                    g_s[at, :] = acc[rows, side * chip_len:(side + 1) * chip_len].astype(BF)
+                    at = pl.ds(pl.multiple_of((n + 2 * side) * HEAD + r * 16, 16), 16)
+                    total = acc[rows, side * chip_len:(side + 1) * chip_len]
+                    if not first:
+                        total = total + before_s[at, :].astype(F32)
+                    g_s[at, :] = total.astype(BF)
             return carry
 
         lax.fori_loop(0, HEAD // 16, narrow_kv, 0)
-        dkv_copy = pltpu.make_async_copy(g_s, dkv_ref, out_sem.at[1])
-        dkv_copy.start()
+        up_copy = pltpu.make_async_copy(g_s.at[pl.ds(0, 2 * HEAD), :], up_ref, out_sem.at[1])
+        here_copy = pltpu.make_async_copy(g_s.at[pl.ds(2 * HEAD, 2 * HEAD), :], here_ref, out_sem.at[2])
+        up_copy.start()
+        here_copy.start()
         part_copy.wait()
-        dkv_copy.wait()
-
-
-def attention(chunk, core, lo, n_blocks, q, dctx, kdoc, tabs, kv_prev, kv_chip, xs, gs):
+        up_copy.wait()
+        here_copy.wait()
+
+
+def attention(chunk, core, lo, n_blocks, q, dctx, kdoc, tabs, kv_prev, kv_chip, xs, gs, before):
+    first = before is None
     chip_len = q.shape[0]
     width = xs[0].shape[1]
     assert 2 * WIDE == BQ == 4 * HEAD and width == chip_len
@@ -387,7 +404,7 @@
     full = lambda shape: pl.BlockSpec(shape, lambda i, *s: (0,) * len(shape))
     pairs = chip_len * chip_len * PAIR
     return pl.pallas_call(
-        attn_kernel,
+        functools.partial(attn_kernel, first),
         grid_spec=pltpu.PrefetchScalarGridSpec(
             num_scalar_prefetch=3,
             grid=(chip_len // BQ,),
@@ -395,15 +412,15 @@
                 pl.BlockSpec((BQ, WIDE), lambda i, *s: (i, chunk)),
                 pl.BlockSpec((BQ, WIDE), lambda i, *s: (i, chunk)),
                 full((1, padded)),
-            ] + [pl.BlockSpec(memory_space=pl.ANY)] * 10,
+            ] + [pl.BlockSpec(memory_space=pl.ANY)] * 12,
             out_specs=[
                 pl.BlockSpec((2, BQ, WIDE), lambda i, *s: (0, i, 0)),
                 pl.BlockSpec(memory_space=pl.ANY),
                 pl.BlockSpec(memory_space=pl.ANY),
+                pl.BlockSpec(memory_space=pl.ANY),
             ],
             scratch_shapes=[
-                pltpu.VMEM((padded, HEAD), BF),
-                pltpu.VMEM((padded, HEAD), BF),
+                pltpu.VMEM((padded, 2 * HEAD), BF),
                 pltpu.VMEM((max_blocks, rows, BK), F32),
                 pltpu.VMEM((max_blocks, rows, BK), F32),
                 pltpu.VMEM((rows, HEAD), F32),
@@ -424,24 +441,25 @@
                 pltpu.VMEM((BQ, width), BF),
                 pltpu.VMEM((2 * WIDE, BQ), BF),
                 pltpu.VMEM((2 * WIDE, width), F32),
-                pltpu.SemaphoreType.DMA((10,)),
+                pltpu.VMEM((4 * HEAD, chip_len), BF),
+                pltpu.SemaphoreType.DMA((6,)),
                 pltpu.SemaphoreType.DMA((2,)),
-                pltpu.SemaphoreType.DMA((2,)),
+                pltpu.SemaphoreType.DMA((5,)),
             ],
         ),
         out_shape=[
             jax.ShapeDtypeStruct((2, chip_len, WIDE), BF),
             jax.ShapeDtypeStruct((2 * WIDE, width), BF),
-            jax.ShapeDtypeStruct((4 * HEAD, chip_len), BF),
+            jax.ShapeDtypeStruct((2 * HEAD, chip_len), BF),
+            jax.ShapeDtypeStruct((2 * HEAD, chip_len), BF),
         ],
         compiler_params=params(),
         cost_estimate=cost(pairs * HEAD * 2 * 8, 12 * 1024 * 1024, pairs),
         name="attention",
-    )(core, lo, n_blocks, q, dctx, kdoc, *tabs, *kv_prev, *kv_chip, *xs, *gs)
-
-
-def kv_finish_kernel(n, s_ref, *refs):
-    far_ref, tab_own, tab_oth, out_ref, outt_ref, tab_s = refs[n:]
+    )(core, lo, n_blocks, q, dctx, kdoc, *tabs, *kv_prev, *kv_chip, *xs, *gs, *(gs if first else before))
+
+
+def kv_finish_kernel(s_ref, near_ref, far_ref, tab_own, tab_oth, out_ref, outt_ref, tab_s):
     tokens = tab_own.shape[0]
     step = out_ref.shape[0]
 
@@ -450,31 +468,29 @@
         tab_s[span(s_ref[0], tokens), :] = tab_own[...]
         tab_s[span(1 - s_ref[0], tokens), :] = tab_oth[...]
 
-    total = far_ref[...].astype(F32)
-    for ref in refs[:n]:
-        total = total + ref[:, 0].astype(F32)
+    total = near_ref[...].astype(F32) + far_ref[...].astype(F32)
     cos_t, sin_t = spread_table(tab_s[span(pl.program_id(0), step), :])
-    dk = total[0].astype(BF).astype(F32).T
+    dk = total[:HEAD].astype(BF).astype(F32).T
     dk = (dk * cos_t - swap_halves(dk) * sin_t).astype(BF)
-    dvt = total[1].astype(BF)
+    dvt = total[HEAD:].astype(BF)
     out_ref[:, :HEAD] = dk
     out_ref[:, HEAD:] = dvt.T
     outt_ref[:HEAD, :] = dk.T
     outt_ref[HEAD:, :] = dvt
 
 
-def kv_finish(core, parts, far, tab_own, tab_oth):
+def kv_finish(core, near, far, tab_own, tab_oth):
     tokens = tab_own.shape[0]
     chip_len = 2 * tokens
     step = 512
     return pl.pallas_call(
-        functools.partial(kv_finish_kernel, len(parts)),
+        kv_finish_kernel,
         grid_spec=pltpu.PrefetchScalarGridSpec(
             num_scalar_prefetch=1,
             grid=(chip_len // step,),
-            in_specs=[pl.BlockSpec((2, 1, HEAD, step), lambda t, s: (0, 1, 0, t))] * len(parts)
-            + [
-                pl.BlockSpec((2, HEAD, step), lambda t, s: (0, 0, t)),
+            in_specs=[
+                pl.BlockSpec((2 * HEAD, step), lambda t, s: (0, t)),
+                pl.BlockSpec((2 * HEAD, step), lambda t, s: (0, t)),
                 pl.BlockSpec((tokens, HEAD), lambda t, s: (0, 0)),
                 pl.BlockSpec((tokens, HEAD), lambda t, s: (0, 0)),
             ],
@@ -491,7 +507,7 @@
         compiler_params=params(),
         cost_estimate=cost(chip_len * HEAD * 64, chip_len * HEAD * 16),
         name="kv_finish",
-    )(core, *parts, far, tab_own, tab_oth)
+    )(core, near, far, tab_own, tab_oth)
 
 
 def kvgrad_kernel(s_ref, dkvt_ref, x_own, x_oth, out_ref):
@@ -710,8 +726,6 @@
         place = lax.axis_index("sp")
         core_id, chip_id = place & 1, place >> 1
         core = core_id.astype(jnp.int32)[None]
-        sel_own = jnp.stack([core_id, core_id]).astype(jnp.int32)
-        sel_oth = jnp.stack([core_id, 1 - core_id]).astype(jnp.int32)
 
         doc_oth = near(doc_ids)
         doc_far = far(doc_ids)
@@ -720,14 +734,14 @@
         g_oth = near(grad_out)
         tab_own = rope_table(positions)
         tab_oth = near(tab_own)
-        kv_own, q = qkv_proj(sel_own, hidden, w_q, w_k, w_v, tab_own, None)
+        kv_own, q = qkv_proj(True, core, hidden, w_q, w_k, w_v, tab_own, None)
         kvp_own = lax.ppermute(kv_own, "sp", down_perm)
 
         def in_order(own, oth):
             return jnp.where(core_id == 0, jnp.concatenate([own, oth]), jnp.concatenate([oth, own]))
 
         doc_chip, doc_far = in_order(doc_ids, doc_oth), in_order(doc_far, doc_far_oth)
-        kv_oth, q = qkv_proj(sel_oth, x_oth, w_q, w_k, w_v, tab_oth, q)
+        kv_oth, q = qkv_proj(False, core, x_oth, w_q, w_k, w_v, tab_oth, q)
         kvp_oth = lax.ppermute(kv_oth, "sp", down_perm)
         dctx = dctx_proj(core, grad_out, g_oth, w_o)
 
@@ -740,20 +754,17 @@
         n_blocks = (end - lo + BK - 1) >> (BK.bit_length() - 1)
         kdoc = jnp.concatenate([doc_far, doc_chip, jnp.zeros((BK,), jnp.int32)])[None, :]
 
-        acts, acts_oth, dkvs, sums = [], [], [], None
+        acts, acts_oth, dkv_sum, sums = [], [], None, None
         for j in range(n_chunks):
-            act, part, dkv = attention(
+            act, part, dkv_up, dkv_here = attention(
                 j, core, lo, n_blocks, q, dctx, kdoc, (tab_own, tab_oth), (kvp_own, kvp_oth), (kv_own, kv_oth),
-                (hidden, x_oth), (grad_out, g_oth),
+                (hidden, x_oth), (grad_out, g_oth), dkv_sum,
             )
             part = part.reshape(2, WIDE, -1)
             acts.append(act)
-            dkvs.append(dkv.reshape(2, 2, HEAD, chip_len))
+            dkv_sum = (dkv_up, dkv_here)
             if j == n_chunks - 1:
-                dkv_up = (dkv_early + dkvs[j][:, 0].astype(F32)).astype(BF)
                 dkv_far = lax.ppermute(dkv_up, "sp", up_perm)
-            if j == n_chunks - 2:
-                dkv_early = lax.optimization_barrier(sum(d[:, 0].astype(F32) for d in dkvs))
             acts_oth.append(near(act))
             part_far = far(part)
             part_near = near(part)
@@ -761,7 +772,7 @@
             sums = combine(core, j, n_chunks, (part, part_far, part_near, part_far_near), sums)
         grad_wq, grad_wo = sums
 
-        dkv, dkvt = kv_finish(core, dkvs, dkv_far, tab_own, tab_oth)
+        dkv, dkvt = kv_finish(core, dkv_here, dkv_far, tab_own, tab_oth)
         dkv_oth = near(dkv)
         kv_part = kvgrad(core, dkvt, hidden, x_oth)
         kv_part_far = far(kv_part)

time: 553 us -> 545 us (0.986)
  other arithmetic: 11.4 us -> 4.42 us
where the time goes in v8:
time: 545 us
  Pallas kernels  255 us (47%)
  waiting for transfers between devices  215 us (39%)
  starting transfers between devices  67.6 us (12%)
    ppermute x6, waiting for transfers between devices, far(): return lax.ppermute(v, 'sp', far_perm)  185 us
    pallas_call x4, Pallas kernels, attention(): pl.pallas_call(functools.partial(attn_kernel, first), grid_spec=pltpu.Pre...  140 us
    ppermute x6, starting transfers between devices, far(): return lax.ppermute(v, 'sp', far_perm)  55 us
    pallas_call x4, Pallas kernels, combine(): pl.pallas_call(combine_kernel, grid_spec=pltpu.PrefetchScalarGridSpec(num...  33.9 us
    ppermute x1, waiting for transfers between devices, device_step(): dkv_far = lax.ppermute(dkv_up, 'sp', up_perm)  23.3 us
    pallas_call x2, Pallas kernels, qkv_proj(): pl.pallas_call(qkv_kernel, grid_spec=pltpu.PrefetchScalarGridSpec(num_sca...  21 us
    pallas_call x1, Pallas kernels, grad_hidden(): pl.pallas_call(functools.partial(hidden_kernel, n), grid_spec=pltpu.Prefe...  17 us
    pallas_call x1, Pallas kernels, dctx_proj(): pl.pallas_call(dctx_kernel, grid_spec=pltpu.PrefetchScalarGridSpec(num_sc...  14.2 us
  transfers between devices with their start and end apart: 29, of which 7 were waited for; matrix products, arithmetic and copies ran while one was open for 1% of the time, Pallas kernels for 20%

profile of v8, /device:TPU:0, one launch (start us, length us, event | category | flops | bytes accessed | tf_op | source)
XLA Modules:
  0.0 544.7 jit_solution(2990184539915572843)
XLA Ops:
  2.0 2.5 collective-permute-start.1
  5.2 1.9 multiply_cosine_fusion
  7.1 1.0 pad_maximum_fusion.tab_ref.tab_own
  8.3 10.5 %qkv_proj.2 = (bf16[1024,256]{1,0:T(8,128)(2,1)}, bf16[2048,1024]{1,0:T(8,128)(2,1)}) custom-call(s32[1]{0:T(128)} %bitcast.s_ref.core_ref, bf16[1024,2048]{1,0:T(8,128)(2,1)} %x_own.9, bf16[2048,2048]{1,0:T(8,128)(2,1)} %refs_10_.1, bf16[2048,256]{1,0:T(8,128)(2,1)} %refs_11_.1, bf16[2048,256]{1,0:T(8,128)(2,1)} %refs_12_.1, ...), custom_call_target="tpu_custom_call" | custom-call | flops 5368709120 | bytes 8388608 | tf_op jit(solution)/shard_map/qkv_proj/pallas_call | solution.py:111
  19.0 4.6 collective-permute-start.6
  25.0 10.5 %qkv_proj.3 = (bf16[1024,256]{1,0:T(8,128)(2,1)}, bf16[2048,1024]{1,0:T(8,128)(2,1)}) custom-call(s32[1]{0:T(128)} %bitcast.s_ref.core_ref, bf16[1024,2048]{1,0:T(8,128)(2,1)} %collective-permute-done.3.x_ref.x_oth, bf16[2048,2048]{1,0:T(8,128)(2,1)} %refs_10_.1, bf16[2048,256]{1,0:T(8,128)(2,1)} %refs_11_.1, ...), custom_call_target="tpu_custom_call", output_to_operand_aliasing={{1}: (6, {})} | custom-call | flops 5368709120 | bytes 8388608 | tf_op jit(solution)/shard_map/qkv_proj/pallas_call | solution.py:111
  35.5 2.1 collective-permute-start.7
  37.6 14.2 %dctx_proj.1.do_ref = bf16[2048,1024]{1,0:T(8,128)(2,1)} custom-call(s32[1]{0:T(128)} %bitcast.s_ref.core_ref, bf16[1024,2048]{1,0:T(8,128)(2,1)} %g_own.7, bf16[1024,2048]{1,0:T(8,128)(2,1)} %collective-permute-done.5.oth_ref.g_oth.before_here, bf16[2048,2048]{1,0:T(8,128)(2,1)} %refs_8_.1), custom_call_target="tpu_custom_call" | custom-call | flops 8589934592 | bytes 12582912 | tf_op jit(solution)/shard_map/dctx_proj/pallas_call | solution.py:164
  51.8 35.0 %attention.4 = (bf16[2,2048,256]{2,1,0:T(8,128)(2,1)}, bf16[512,2048]{1,0:T(8,128)(2,1)}, bf16[256,2048]{1,0:T(8,128)(2,1)}, bf16[256,2048]{1,0:T(8,128)(2,1)}) custom-call(s32[1]{0:T(128)} %bitcast.s_ref.core_ref, s32[4]{0:T(128)} %get-tuple-element.73.lo_ref, s32[4]{0:T(128)} %get-tuple-element.72.nb_ref, bf16[2048,1024]{1,0:T(8,128)(2,1)} %get-tuple-element.39.q_ref, ...), custom_call_target="tpu_custom_call" | custom-call | flops 17179869184 | bytes 12582912 | tf_op jit(solution)/shard_map/attention/pallas_call | solution.py:406
  86.8 35.0 %attention.5 = (bf16[2,2048,256]{2,1,0:T(8,128)(2,1)}, bf16[512,2048]{1,0:T(8,128)(2,1)}, bf16[256,2048]{1,0:T(8,128)(2,1)}, bf16[256,2048]{1,0:T(8,128)(2,1)}) custom-call(s32[1]{0:T(128)} %bitcast.s_ref.core_ref, s32[4]{0:T(128)} %get-tuple-element.73.lo_ref, s32[4]{0:T(128)} %get-tuple-element.72.nb_ref, bf16[2048,1024]{1,0:T(8,128)(2,1)} %get-tuple-element.39.q_ref, ...), custom_call_target="tpu_custom_call" | custom-call | flops 17179869184 | bytes 12582912 | tf_op jit(solution)/shard_map/attention/pallas_call | solution.py:406
  121.7 35.1 %attention.6 = (bf16[2,2048,256]{2,1,0:T(8,128)(2,1)}, bf16[512,2048]{1,0:T(8,128)(2,1)}, bf16[256,2048]{1,0:T(8,128)(2,1)}, bf16[256,2048]{1,0:T(8,128)(2,1)}) custom-call(s32[1]{0:T(128)} %bitcast.s_ref.core_ref, s32[4]{0:T(128)} %get-tuple-element.73.lo_ref, s32[4]{0:T(128)} %get-tuple-element.72.nb_ref, bf16[2048,1024]{1,0:T(8,128)(2,1)} %get-tuple-element.39.q_ref, ...), custom_call_target="tpu_custom_call" | custom-call | flops 17179869184 | bytes 12582912 | tf_op jit(solution)/shard_map/attention/pallas_call | solution.py:406
  156.9 35.0 %attention.7 = (bf16[2,2048,256]{2,1,0:T(8,128)(2,1)}, bf16[512,2048]{1,0:T(8,128)(2,1)}, bf16[256,2048]{1,0:T(8,128)(2,1)}, bf16[256,2048]{1,0:T(8,128)(2,1)}) custom-call(s32[1]{0:T(128)} %bitcast.s_ref.core_ref, s32[4]{0:T(128)} %get-tuple-element.73.lo_ref, s32[4]{0:T(128)} %get-tuple-element.72.nb_ref, bf16[2048,1024]{1,0:T(8,128)(2,1)} %get-tuple-element.39.q_ref, ...), custom_call_target="tpu_custom_call" | custom-call | flops 17179869184 | bytes 12582912 | tf_op jit(solution)/shard_map/attention/pallas_call | solution.py:406
  191.9 1.3 collective-permute-start.12
  193.2 48.5 %collective-permute-start.23 = (bf16[2,256,2048]{2,1,0:T(8,128)(2,1)}, bf16[2,256,2048]{2,1,0:T(8,128)(2,1)}, u32[]{:S(2)}, u32[]{:S(2)}) collective-permute-start(bf16[2,256,2048]{2,1,0:T(8,128)(2,1)} %bitcast.14), channel_id=1, source_target_pairs={{0,2},{1,3},{2,0},{3,1},{4,6},{5,7},{6,4},{7,5}} | collective-permute-start | bytes 6291464 | tf_op jit(solution)/shard_map/ppermute | solution.py:720
  241.6 23.3 %collective-permute-done.12.far_ref = bf16[256,2048]{1,0:T(8,128)(2,1)} collective-permute-done((bf16[256,2048]{1,0:T(8,128)(2,1)}, bf16[256,2048]{1,0:T(8,128)(2,1)}, u32[]{:S(2)}, u32[]{:S(2)}) %collective-permute-start.12) | collective-permute-done | bytes 1048608 | tf_op jit(solution)/shard_map/ppermute | solution.py:767
  264.9 4.6 kv_finish.1
  269.6 6.6 %kvgrad.1.a_ref = bf16[256,2048]{1,0:T(8,128)(2,1)} custom-call(s32[1]{0:T(128)} %bitcast.s_ref.core_ref, bf16[256,2048]{1,0:T(8,128)(2,1)} %get-tuple-element.66.dkvt_ref, bf16[1024,2048]{1,0:T(8,128)(2,1)} %x_own.9, bf16[1024,2048]{1,0:T(8,128)(2,1)} %collective-permute-done.3.x_ref.x_oth), custom_call_target="tpu_custom_call" | custom-call | flops 2147483648 | bytes 8388608 | tf_op jit(solution)/shard_map/kvgrad/pallas_call | solution.py:523
  276.7 2.0 collective-permute-start.20
  278.7 53.6 %collective-permute-done.26.b_ref = bf16[256,2048]{1,0:T(8,128)(2,1)S(1)} collective-permute-done((bf16[256,2048]{1,0:T(8,128)(2,1)}, bf16[256,2048]{1,0:T(8,128)(2,1)S(1)}, u32[]{:S(2)}, u32[]{:S(2)}) %collective-permute-start.26) | collective-permute-done | bytes 1048608 | tf_op jit(solution)/shard_map/ppermute | solution.py:720
  332.3 2.0 collective-permute-start.14
  334.3 43.0 %collective-permute-done.20.b_ref = bf16[2,256,2048]{2,1,0:T(8,128)(2,1)} collective-permute-done((bf16[2,256,2048]{2,1,0:T(8,128)(2,1)}, bf16[2,256,2048]{2,1,0:T(8,128)(2,1)}, u32[]{:S(2)}, u32[]{:S(2)}) %collective-permute-start.20) | collective-permute-done | bytes 2097184 | tf_op jit(solution)/shard_map/ppermute | solution.py:720
  377.8 44.4 %collective-permute-done.17.b_ref = bf16[2,256,2048]{2,1,0:T(8,128)(2,1)} collective-permute-done((bf16[2,256,2048]{2,1,0:T(8,128)(2,1)}, bf16[2,256,2048]{2,1,0:T(8,128)(2,1)}, u32[]{:S(2)}, u32[]{:S(2)}) %collective-permute-start.17) | collective-permute-done | bytes 2097184 | tf_op jit(solution)/shard_map/ppermute | solution.py:720
  422.2 43.6 %collective-permute-done.14.b_ref = bf16[2,256,2048]{2,1,0:T(8,128)(2,1)} collective-permute-done((bf16[2,256,2048]{2,1,0:T(8,128)(2,1)}, bf16[2,256,2048]{2,1,0:T(8,128)(2,1)}, u32[]{:S(2)}, u32[]{:S(2)}) %collective-permute-start.14) | collective-permute-done | bytes 2097184 | tf_op jit(solution)/shard_map/ppermute | solution.py:720
  467.9 2.3 collective-permute-done.8.refs_4_
  470.4 4.4 collective-permute-done.28.d_ref
  475.9 13.8 %attn_out.1 = bf16[1024,2048]{1,0:T(8,128)(2,1)} custom-call(s32[1]{0:T(128)} %bitcast.s_ref.core_ref, bf16[2,2048,256]{2,1,0:T(8,128)(2,1)} %get-tuple-element.42.refs_0_, bf16[2,2048,256]{2,1,0:T(8,128)(2,1)} %get-tuple-element.45.refs_1_, bf16[2,2048,256]{2,1,0:T(8,128)(2,1)} %get-tuple-element.48.refs_2_, ...), custom_call_target="tpu_custom_call" | custom-call | flops 8589934592 | bytes 16777216 | tf_op jit(solution)/shard_map/attn_out/pallas_call | solution.py:641
  489.7 17.0 %grad_hidden.1 = bf16[1024,2048]{1,0:T(8,128)(2,1)} custom-call(s32[1]{0:T(128)} %bitcast.s_ref.core_ref, bf16[2,2048,256]{2,1,0:T(8,128)(2,1)} %get-tuple-element.42.refs_0_, bf16[2,2048,256]{2,1,0:T(8,128)(2,1)} %get-tuple-element.45.refs_1_, bf16[2,2048,256]{2,1,0:T(8,128)(2,1)} %get-tuple-element.48.refs_2_, ...), custom_call_target="tpu_custom_call" | custom-call | flops 10737418240 | bytes 16777216 | tf_op jit(solution)/shard_map/grad_hidden/pallas_call | solution.py:682
  506.7 4.1 kv_combine.1
  510.8 8.5 %combine.4 = (f32[2048,2048]{1,0:T(8,128)}, f32[2048,2048]{1,0:T(8,128)}) custom-call(s32[1]{0:T(128)} %bitcast.s_ref.core_ref, bf16[2,256,2048]{2,1,0:T(8,128)(2,1)} %bitcast.16, bf16[2,256,2048]{2,1,0:T(8,128)(2,1)} %collective-permute-done.23.b_ref, bf16[2,256,2048]{2,1,0:T(8,128)(2,1)} %collective-permute-done.24.c_ref, ...), custom_call_target="tpu_custom_call" | custom-call | flops 536870912 | bytes 16777216 | tf_op jit(solution)/shard_map/combine/pallas_call | solution.py:599
  519.2 8.5 %combine.5 = (f32[2048,2048]{1,0:T(8,128)}, f32[2048,2048]{1,0:T(8,128)}) custom-call(s32[1]{0:T(128)} %bitcast.s_ref.core_ref, bf16[2,256,2048]{2,1,0:T(8,128)(2,1)} %bitcast.13, bf16[2,256,2048]{2,1,0:T(8,128)(2,1)} %collective-permute-done.20.b_ref, ...), custom_call_target="tpu_custom_call", output_to_operand_aliasing={{0}: (5, {}), {1}: (6, {})} | custom-call | flops 536870912 | bytes 16777216 | tf_op jit(solution)/shard_map/combine/pallas_call | solution.py:599
  527.7 8.5 %combine.6 = (f32[2048,2048]{1,0:T(8,128)}, f32[2048,2048]{1,0:T(8,128)}) custom-call(s32[1]{0:T(128)} %bitcast.s_ref.core_ref, bf16[2,256,2048]{2,1,0:T(8,128)(2,1)} %bitcast.10, bf16[2,256,2048]{2,1,0:T(8,128)(2,1)} %collective-permute-done.17.b_ref, ...), custom_call_target="tpu_custom_call", output_to_operand_aliasing={{0}: (5, {}), {1}: (6, {})} | custom-call | flops 536870912 | bytes 16777216 | tf_op jit(solution)/shard_map/combine/pallas_call | solution.py:599
  536.2 8.5 %combine.7 = (f32[2048,2048]{1,0:T(8,128)}, f32[2048,2048]{1,0:T(8,128)}) custom-call(s32[1]{0:T(128)} %bitcast.s_ref.core_ref, bf16[2,256,2048]{2,1,0:T(8,128)(2,1)} %bitcast.7, bf16[2,256,2048]{2,1,0:T(8,128)(2,1)} %collective-permute-done.14.b_ref, ...), custom_call_target="tpu_custom_call", output_to_operand_aliasing={{0}: (5, {}), {1}: (6, {})} | custom-call | flops 536870912 | bytes 16777216 | tf_op jit(solution)/shard_map/combine/pallas_call | solution.py:599
  (70 shorter events, 8.2 us)
Async XLA Ops:
  0.6 24.4 %collective-permute-start.3 = (bf16[1024,2048]{1,0:T(8,128)(2,1)}, bf16[1024,2048]{1,0:T(8,128)(2,1)}, u32[]{:S(2)}, u32[]{:S(2)}) collective-permute-start(bf16[1024,2048]{1,0:T(8,128)(2,1)} %x_own.9), channel_id=1, source_target_pairs={{0,1},{1,0},{2,3},{3,2},{4,5},{5,4},{6,7},{7,6}} | collective-permute-start | bytes 12582920 | tf_op jit(solution)/shard_map/ppermute | solution.py:717
  1.5 36.1 %collective-permute-start.5 = (bf16[1024,2048]{1,0:T(8,128)(2,1)}, bf16[1024,2048]{1,0:T(8,128)(2,1)}, u32[]{:S(2)}, u32[]{:S(2)}) collective-permute-start(bf16[1024,2048]{1,0:T(8,128)(2,1)} %g_own.7), channel_id=1, source_target_pairs={{0,1},{1,0},{2,3},{3,2},{4,5},{5,4},{6,7},{7,6}} | collective-permute-start | bytes 12582920 | tf_op jit(solution)/shard_map/ppermute | solution.py:717
  1.5 17.3 %collective-permute-start = (s32[1024]{0:T(1024)}, s32[1024]{0:T(1024)S(1)}, u32[]{:S(2)}, u32[]{:S(2)}) collective-permute-start(s32[1024]{0:T(1024)} %param.11), channel_id=1, source_target_pairs={{0,1},{1,0},{2,3},{3,2},{4,5},{5,4},{6,7},{7,6}} | collective-permute-start | bytes 12296 | tf_op jit(solution)/shard_map/ppermute | solution.py:717
  2.0 17.0 %collective-permute-start.1 = (s32[1024]{0:T(1024)}, s32[1024]{0:T(1024)S(1)}, u32[]{:S(2)}, u32[]{:S(2)}) collective-permute-start(s32[1024]{0:T(1024)} %param.11), channel_id=1, source_target_pairs={{0,2},{1,3},{2,0},{3,1},{4,6},{5,7},{6,4},{7,5}} | collective-permute-start | bytes 12296 | tf_op jit(solution)/shard_map/ppermute | solution.py:720
  8.1 16.9 %collective-permute-start.4 = (f32[1024,128]{1,0:T(8,128)}, f32[1024,128]{1,0:T(8,128)}, u32[]{:S(2)}, u32[]{:S(2)}) collective-permute-start(f32[1024,128]{1,0:T(8,128)} %pad_maximum_fusion.tab_ref.tab_own), channel_id=1, source_target_pairs={{0,1},{1,0},{2,3},{3,2},{4,5},{5,4},{6,7},{7,6}} | collective-permute-start | bytes 1572872 | tf_op jit(solution)/shard_map/ppermute | solution.py:717
  8.3 10.5 %copy-start.3 = (s32[1024]{0:T(1024)S(1)}, s32[1024]{0:T(1024)}, u32[]{:S(2)}) copy-start(s32[1024]{0:T(1024)} %param.11) | copy-start | bytes 12292
  18.8 4.8 collective-permute-start.2
  19.0 32.8 %collective-permute-start.6 = (bf16[1024,256]{1,0:T(8,128)(2,1)}, bf16[1024,256]{1,0:T(8,128)(2,1)}, u32[]{:S(2)}, u32[]{:S(2)}) collective-permute-start(bf16[1024,256]{1,0:T(8,128)(2,1)} %get-tuple-element.40.kvc_own), channel_id=1, source_target_pairs={{0,2},{1,3},{4,6},{5,7}} | collective-permute-start | bytes 1572872 | tf_op jit(solution)/shard_map/ppermute | solution.py:738
  35.5 16.3 %collective-permute-start.7 = (bf16[1024,256]{1,0:T(8,128)(2,1)}, bf16[1024,256]{1,0:T(8,128)(2,1)}, u32[]{:S(2)}, u32[]{:S(2)}) collective-permute-start(bf16[1024,256]{1,0:T(8,128)(2,1)} %get-tuple-element.41.kvc_oth), channel_id=1, source_target_pairs={{0,2},{1,3},{4,6},{5,7}} | collective-permute-start | bytes 1572872 | tf_op jit(solution)/shard_map/ppermute | solution.py:745
  191.9 73.1 %collective-permute-start.12 = (bf16[256,2048]{1,0:T(8,128)(2,1)}, bf16[256,2048]{1,0:T(8,128)(2,1)}, u32[]{:S(2)}, u32[]{:S(2)}) collective-permute-start(bf16[256,2048]{1,0:T(8,128)(2,1)} %get-tuple-element.53), channel_id=1, source_target_pairs={{2,0},{3,1},{6,4},{7,5}} | collective-permute-start | bytes 3145736 | tf_op jit(solution)/shard_map/ppermute | solution.py:767
  193.2 139.2 %collective-permute-start.23 = (bf16[2,256,2048]{2,1,0:T(8,128)(2,1)}, bf16[2,256,2048]{2,1,0:T(8,128)(2,1)}, u32[]{:S(2)}, u32[]{:S(2)}) collective-permute-start(bf16[2,256,2048]{2,1,0:T(8,128)(2,1)} %bitcast.14), channel_id=1, source_target_pairs={{0,2},{1,3},{2,0},{3,1},{4,6},{5,7},{6,4},{7,5}} | collective-permute-start | bytes 6291464 | tf_op jit(solution)/shard_map/ppermute | solution.py:720
  276.2 56.1 %collective-permute-start.26 = (bf16[256,2048]{1,0:T(8,128)(2,1)}, bf16[256,2048]{1,0:T(8,128)(2,1)S(1)}, u32[]{:S(2)}, u32[]{:S(2)}) collective-permute-start(bf16[256,2048]{1,0:T(8,128)(2,1)} %kvgrad.1.a_ref), channel_id=1, source_target_pairs={{0,2},{1,3},{2,0},{3,1},{4,6},{5,7},{6,4},{7,5}} | collective-permute-start | bytes 3145736 | tf_op jit(solution)/shard_map/ppermute | solution.py:720
  276.2 56.1 %collective-permute-start.27 = (bf16[256,2048]{1,0:T(8,128)(2,1)}, bf16[256,2048]{1,0:T(8,128)(2,1)S(1)}, u32[]{:S(2)}, u32[]{:S(2)}) collective-permute-start(bf16[256,2048]{1,0:T(8,128)(2,1)} %kvgrad.1.a_ref), channel_id=1, source_target_pairs={{0,1},{1,0},{2,3},{3,2},{4,5},{5,4},{6,7},{7,6}} | collective-permute-start | bytes 3145736 | tf_op jit(solution)/shard_map/ppermute | solution.py:717
  276.2 58.2 %collective-permute-start.24 = (bf16[2,256,2048]{2,1,0:T(8,128)(2,1)}, bf16[2,256,2048]{2,1,0:T(8,128)(2,1)}, u32[]{:S(2)}, u32[]{:S(2)}) collective-permute-start(bf16[2,256,2048]{2,1,0:T(8,128)(2,1)} %bitcast.15), channel_id=1, source_target_pairs={{0,1},{1,0},{2,3},{3,2},{4,5},{5,4},{6,7},{7,6}} | collective-permute-start | bytes 6291464 | tf_op jit(solution)/shard_map/ppermute | solution.py:717
  276.7 100.6 %collective-permute-start.20 = (bf16[2,256,2048]{2,1,0:T(8,128)(2,1)}, bf16[2,256,2048]{2,1,0:T(8,128)(2,1)}, u32[]{:S(2)}, u32[]{:S(2)}) collective-permute-start(bf16[2,256,2048]{2,1,0:T(8,128)(2,1)} %bitcast.11), channel_id=1, source_target_pairs={{0,2},{1,3},{2,0},{3,1},{4,6},{5,7},{6,4},{7,5}} | collective-permute-start | bytes 6291464 | tf_op jit(solution)/shard_map/ppermute | solution.py:720
  332.3 134.6 %copy-start = (bf16[256,2048]{1,0:T(8,128)(2,1)}, bf16[256,2048]{1,0:T(8,128)(2,1)S(1)}, u32[]{:S(2)}) copy-start(bf16[256,2048]{1,0:T(8,128)(2,1)S(1)} %collective-permute-done.26.b_ref) | copy-start | bytes 3145732
  332.3 45.1 %collective-permute-start.21 = (bf16[2,256,2048]{2,1,0:T(8,128)(2,1)}, bf16[2,256,2048]{2,1,0:T(8,128)(2,1)}, u32[]{:S(2)}, u32[]{:S(2)}) collective-permute-start(bf16[2,256,2048]{2,1,0:T(8,128)(2,1)} %bitcast.12), channel_id=1, source_target_pairs={{0,1},{1,0},{2,3},{3,2},{4,5},{5,4},{6,7},{7,6}} | collective-permute-start | bytes 6291464 | tf_op jit(solution)/shard_map/ppermute | solution.py:717
  332.3 142.5 %copy-start.1 = (bf16[256,2048]{1,0:T(8,128)(2,1)}, bf16[256,2048]{1,0:T(8,128)(2,1)S(1)}, u32[]{:S(2)}) copy-start(bf16[256,2048]{1,0:T(8,128)(2,1)S(1)} %collective-permute-done.27.c_ref) | copy-start | bytes 3145732
  332.3 90.0 %collective-permute-start.17 = (bf16[2,256,2048]{2,1,0:T(8,128)(2,1)}, bf16[2,256,2048]{2,1,0:T(8,128)(2,1)}, u32[]{:S(2)}, u32[]{:S(2)}) collective-permute-start(bf16[2,256,2048]{2,1,0:T(8,128)(2,1)} %bitcast.8), channel_id=1, source_target_pairs={{0,2},{1,3},{2,0},{3,1},{4,6},{5,7},{6,4},{7,5}} | collective-permute-start | bytes 6291464 | tf_op jit(solution)/shard_map/ppermute | solution.py:720
  332.3 133.5 %collective-permute-start.14 = (bf16[2,256,2048]{2,1,0:T(8,128)(2,1)}, bf16[2,256,2048]{2,1,0:T(8,128)(2,1)}, u32[]{:S(2)}, u32[]{:S(2)}) collective-permute-start(bf16[2,256,2048]{2,1,0:T(8,128)(2,1)} %bitcast.5), channel_id=1, source_target_pairs={{0,2},{1,3},{2,0},{3,1},{4,6},{5,7},{6,4},{7,5}} | collective-permute-start | bytes 6291464 | tf_op jit(solution)/shard_map/ppermute | solution.py:720
  334.3 132.5 %collective-permute-start.11 = (bf16[2,2048,256]{2,1,0:T(8,128)(2,1)}, bf16[2,2048,256]{2,1,0:T(8,128)(2,1)}, u32[]{:S(2)}, u32[]{:S(2)}) collective-permute-start(bf16[2,2048,256]{2,1,0:T(8,128)(2,1)} %get-tuple-element.51.refs_3_), channel_id=1, source_target_pairs={{0,1},{1,0},{2,3},{3,2},{4,5},{5,4},{6,7},{7,6}} | collective-permute-start | bytes 6291464 | tf_op jit(solution)/shard_map/ppermute | solution.py:717
  377.3 88.5 %collective-permute-start.13 = (bf16[2048,256]{1,0:T(8,128)(2,1)}, bf16[2048,256]{1,0:T(8,128)(2,1)S(1)}, u32[]{:S(2)}, u32[]{:S(2)}) collective-permute-start(bf16[2048,256]{1,0:T(8,128)(2,1)} %get-tuple-element.54.refs_8_), channel_id=1, source_target_pairs={{0,1},{1,0},{2,3},{3,2},{4,5},{5,4},{6,7},{7,6}} | collective-permute-start | bytes 3145736 | tf_op jit(solution)/shard_map/ppermute | solution.py:717
  377.3 90.1 %collective-permute-start.10 = (bf16[2,2048,256]{2,1,0:T(8,128)(2,1)}, bf16[2,2048,256]{2,1,0:T(8,128)(2,1)S(1)}, u32[]{:S(2)}, u32[]{:S(2)}) collective-permute-start(bf16[2,2048,256]{2,1,0:T(8,128)(2,1)} %get-tuple-element.48.refs_2_), channel_id=1, source_target_pairs={{0,1},{1,0},{2,3},{3,2},{4,5},{5,4},{6,7},{7,6}} | collective-permute-start | bytes 6291464 | tf_op jit(solution)/shard_map/ppermute | solution.py:717
  422.2 45.2 %collective-permute-start.9 = (bf16[2,2048,256]{2,1,0:T(8,128)(2,1)}, bf16[2,2048,256]{2,1,0:T(8,128)(2,1)S(1)}, u32[]{:S(2)}, u32[]{:S(2)}) collective-permute-start(bf16[2,2048,256]{2,1,0:T(8,128)(2,1)} %get-tuple-element.45.refs_1_), channel_id=1, source_target_pairs={{0,1},{1,0},{2,3},{3,2},{4,5},{5,4},{6,7},{7,6}} | collective-permute-start | bytes 6291464 | tf_op jit(solution)/shard_map/ppermute | solution.py:717
  465.8 4.4 collective-permute-start.8
  465.9 9.8 %collective-permute-start.25 = (bf16[2,256,2048]{2,1,0:T(8,128)(2,1)}, bf16[2,256,2048]{2,1,0:T(8,128)(2,1)}, u32[]{:S(2)}, u32[]{:S(2)}) collective-permute-start(bf16[2,256,2048]{2,1,0:T(8,128)(2,1)} %collective-permute-done.23.b_ref), channel_id=1, source_target_pairs={{0,1},{1,0},{2,3},{3,2},{4,5},{5,4},{6,7},{7,6}} | collective-permute-start | bytes 6291464 | tf_op jit(solution)/shard_map/ppermute | solution.py:717
  466.9 7.8 %collective-permute-start.28 = (bf16[256,2048]{1,0:T(8,128)(2,1)S(1)}, bf16[256,2048]{1,0:T(8,128)(2,1)S(1)}, u32[]{:S(2)}, u32[]{:S(2)}) collective-permute-start(bf16[256,2048]{1,0:T(8,128)(2,1)S(1)} %collective-permute-done.26.b_ref), channel_id=1, source_target_pairs={{0,1},{1,0},{2,3},{3,2},{4,5},{5,4},{6,7},{7,6}} | collective-permute-start | bytes 3145736 | tf_op jit(solution)/shard_map/ppermute | solution.py:717
  467.4 51.8 %collective-permute-start.22 = (bf16[2,256,2048]{2,1,0:T(8,128)(2,1)}, bf16[2,256,2048]{2,1,0:T(8,128)(2,1)}, u32[]{:S(2)}, u32[]{:S(2)}) collective-permute-start(bf16[2,256,2048]{2,1,0:T(8,128)(2,1)} %collective-permute-done.20.b_ref), channel_id=1, source_target_pairs={{0,1},{1,0},{2,3},{3,2},{4,5},{5,4},{6,7},{7,6}} | collective-permute-start | bytes 6291464 | tf_op jit(solution)/shard_map/ppermute | solution.py:717
  467.4 60.3 %collective-permute-start.18 = (bf16[2,256,2048]{2,1,0:T(8,128)(2,1)}, bf16[2,256,2048]{2,1,0:T(8,128)(2,1)}, u32[]{:S(2)}, u32[]{:S(2)}) collective-permute-start(bf16[2,256,2048]{2,1,0:T(8,128)(2,1)} %bitcast.9), channel_id=1, source_target_pairs={{0,1},{1,0},{2,3},{3,2},{4,5},{5,4},{6,7},{7,6}} | collective-permute-start | bytes 6291464 | tf_op jit(solution)/shard_map/ppermute | solution.py:717
  470.2 57.5 %collective-permute-start.19 = (bf16[2,256,2048]{2,1,0:T(8,128)(2,1)}, bf16[2,256,2048]{2,1,0:T(8,128)(2,1)}, u32[]{:S(2)}, u32[]{:S(2)}) collective-permute-start(bf16[2,256,2048]{2,1,0:T(8,128)(2,1)} %collective-permute-done.17.b_ref), channel_id=1, source_target_pairs={{0,1},{1,0},{2,3},{3,2},{4,5},{5,4},{6,7},{7,6}} | collective-permute-start | bytes 6291464 | tf_op jit(solution)/shard_map/ppermute | solution.py:717
  474.7 61.5 %collective-permute-start.15 = (bf16[2,256,2048]{2,1,0:T(8,128)(2,1)}, bf16[2,256,2048]{2,1,0:T(8,128)(2,1)}, u32[]{:S(2)}, u32[]{:S(2)}) collective-permute-start(bf16[2,256,2048]{2,1,0:T(8,128)(2,1)} %bitcast.6), channel_id=1, source_target_pairs={{0,1},{1,0},{2,3},{3,2},{4,5},{5,4},{6,7},{7,6}} | collective-permute-start | bytes 6291464 | tf_op jit(solution)/shard_map/ppermute | solution.py:717
  475.7 60.5 %collective-permute-start.16 = (bf16[2,256,2048]{2,1,0:T(8,128)(2,1)}, bf16[2,256,2048]{2,1,0:T(8,128)(2,1)}, u32[]{:S(2)}, u32[]{:S(2)}) collective-permute-start(bf16[2,256,2048]{2,1,0:T(8,128)(2,1)} %collective-permute-done.14.b_ref), channel_id=1, source_target_pairs={{0,1},{1,0},{2,3},{3,2},{4,5},{5,4},{6,7},{7,6}} | collective-permute-start | bytes 6291464 | tf_op jit(solution)/shard_map/ppermute | solution.py:717
  (5 other events, 24.1 us)

commit v9 on v8

--- a/solution.py
+++ b/solution.py
@@ -99,8 +99,8 @@
         q = dot_nn(x, wq_ref[:, n * step:(n + 1) * step])
         for h in range(step // HEAD):
             part = q[:, h * HEAD:(h + 1) * HEAD]
-            at = n * step + h * HEAD
-            q_ref[:, at:at + HEAD] = (part * cos_t + swap_halves(part) * sin_t).astype(BF)
+            j, at = divmod(n * step + h * HEAD, WIDE)
+            q_ref[j, :, at:at + HEAD] = (part * cos_t + swap_halves(part) * sin_t).astype(BF)
 
 
 def qkv_proj(own, core, x, w_q, w_k, w_v, tab, prev):
@@ -122,13 +122,13 @@
             ] + [pl.BlockSpec(memory_space=pl.ANY)] * len(extra),
             out_specs=[
                 pl.BlockSpec((rows, 2 * HEAD), lambda m, s: (m, 0)),
-                pl.BlockSpec((rows, cols), lambda m, s: ((s[0] if own else 1 - s[0]) * 2 + m, 0)),
+                pl.BlockSpec((cols // WIDE, rows, WIDE), lambda m, s: (0, (s[0] if own else 1 - s[0]) * 2 + m, 0)),
             ],
             scratch_shapes=[pltpu.VMEM((width, 2 * HEAD), BF)],
         ),
         out_shape=[
             jax.ShapeDtypeStruct((tokens, 2 * HEAD), BF),
-            jax.ShapeDtypeStruct((2 * tokens, cols), BF),
+            jax.ShapeDtypeStruct((cols // WIDE, 2 * tokens, WIDE), BF),
         ],
         input_output_aliases={} if prev is None else {6: 1},
         compiler_params=params(),
@@ -141,7 +141,9 @@
     def put(ref):
         step = 4 * HEAD
         for n in range(wo_ref.shape[0] // step):
-            out_ref[:, n * step:(n + 1) * step] = dot_nt(ref[...], wo_ref[n * step:(n + 1) * step, :]).astype(BF)
+            part = dot_nt(ref[...], wo_ref[n * step:(n + 1) * step, :]).astype(BF)
+            for j in range(step // WIDE):
+                out_ref[n * (step // WIDE) + j] = part[:, j * WIDE:(j + 1) * WIDE]
 
     @pl.when(pl.program_id(0) < 2)
     def _():
@@ -171,9 +173,9 @@
                 pl.BlockSpec((rows, width), lambda m, s: (jnp.maximum(m - 2, 0), 0)),
                 pl.BlockSpec((cols, width), lambda m, s: (s[0], 0)),
             ],
-            out_specs=pl.BlockSpec((rows, cols), lambda m, s: (place(m, s), 0)),
+            out_specs=pl.BlockSpec((cols // WIDE, rows, WIDE), lambda m, s: (0, place(m, s), 0)),
         ),
-        out_shape=jax.ShapeDtypeStruct((2 * tokens, cols), BF),
+        out_shape=jax.ShapeDtypeStruct((cols // WIDE, 2 * tokens, WIDE), BF),
         compiler_params=params(),
         cost_estimate=cost(4 * tokens * width * cols, tokens * width * 4 + cols * width * 2),
         name="dctx_proj",
@@ -184,13 +186,13 @@
     first, core_ref, lo_ref, nb_ref, q_ref, do_ref, kdoc_ref, tab_own, tab_oth, kvp_own, kvp_oth, kvc_own, kvc_oth,
     x_own, x_oth, g_own, g_oth, before_up, before_here, act_ref, part_ref, up_ref, here_ref,
     kv_s, s_s, dp_s, m_s, l_s, d_s, qd_s, ahead_s, ctx_s, dq_s, q_s, do_s, qt_s, dot_s, tab_s, dk_s, dv_s,
-    x_s, g_s, at_s, w_s, before_s, init_sem, row_sem, out_sem,
+    x_s, g_s, at_s, w_s, before_s, init_sem, row_sem, out_sem, part_sem,
 ):
 
     def before_copies():
         return (
-            pltpu.make_async_copy(before_up, before_s.at[pl.ds(0, 2 * HEAD), :], out_sem.at[3]),
-            pltpu.make_async_copy(before_here, before_s.at[pl.ds(2 * HEAD, 2 * HEAD), :], out_sem.at[4]),
+            pltpu.make_async_copy(before_up, before_s.at[pl.ds(0, 2 * HEAD), :], out_sem.at[2]),
+            pltpu.make_async_copy(before_here, before_s.at[pl.ds(2 * HEAD, 2 * HEAD), :], out_sem.at[3]),
         )
 
     i = pl.program_id(0)
@@ -255,7 +257,7 @@
             copy.start()
 
     def mixed(ref):
-        parts = [ref[:, h * HEAD:(h + 1) * HEAD].reshape(BQ // MIX, 1, MIX, HEAD) for h in range(PAIR)]
+        parts = [ref[0, :, h * HEAD:(h + 1) * HEAD].reshape(BQ // MIX, 1, MIX, HEAD) for h in range(PAIR)]
         return jnp.concatenate(parts, axis=1).reshape(PAIR * BQ, HEAD)
 
     def apart(v, h):
@@ -337,6 +339,35 @@
         return carry
 
     lax.fori_loop(0, n_blocks, grads, 0)
+    last = pl.num_programs(0) - 1
+
+    def out_copies():
+        return (
+            pltpu.make_async_copy(before_s.at[pl.ds(0, 2 * HEAD), :], up_ref, out_sem.at[0]),
+            pltpu.make_async_copy(before_s.at[pl.ds(2 * HEAD, 2 * HEAD), :], here_ref, out_sem.at[1]),
+        )
+
+    @pl.when(i == last)
+    def _():
+        if not first:
+            for copy in before_copies():
+                copy.wait()
+
+        def narrow_kv(r, carry):
+            rows = span(r, 16)
+            for n, acc in enumerate((dk_s, dv_s)):
+                for side in range(2):
+                    at = pl.ds(pl.multiple_of((n + 2 * side) * HEAD + r * 16, 16), 16)
+                    total = acc[rows, side * chip_len:(side + 1) * chip_len]
+                    if not first:
+                        total = total + before_s[at, :].astype(F32)
+                    before_s[at, :] = total.astype(BF)
+            return carry
+
+        lax.fori_loop(0, HEAD // 16, narrow_kv, 0)
+        for copy in out_copies():
+            copy.start()
+
     cos_t, sin_t = spread_table(tab_s[span(i, BQ), :])
     ctx_all, dq_all = ctx_s[...].astype(BF), dq_s[...].astype(BF).astype(F32)
     for h in range(PAIR):
@@ -352,50 +383,44 @@
     for copy in row_copies(x_own, g_own):
         copy.wait()
 
+    def product(c):
+        cols = span(c, step)
+        for lhs, rows_ref in ((slice(0, WIDE), x_s), (slice(WIDE, 2 * WIDE), g_s)):
+            w_s[lhs, cols] += dot_nn(at_s[lhs, :], rows_ref[:, cols])
+        return cols
+
     def products(c, carry):
+        product(c)
+        return carry
+
+    def part_copy(c):
         cols = span(c, step)
-        w_s[:WIDE, cols] += dot_nn(at_s[:WIDE, :], x_s[:, cols])
-        w_s[WIDE:, cols] += dot_nn(at_s[WIDE:, :], g_s[:, cols])
+        return pltpu.make_async_copy(x_s.at[:, cols], part_ref.at[:, cols], part_sem.at[c])
+
+    def last_products(c, carry):
+        cols = product(c)
+        x_s[:, cols] = w_s[:, cols].astype(BF)
+        part_copy(c).start()
         return carry
 
-    lax.fori_loop(0, x_s.shape[1] // step, products, 0)
-
-    @pl.when(i == pl.num_programs(0) - 1)
-    def _():
-        def narrow(r):
-            x_s[r, :] = w_s[r, :].astype(BF)
-
-        by_rows(w_s.shape[0], narrow)
-        part_copy = pltpu.make_async_copy(x_s, part_ref, out_sem.at[0])
-        part_copy.start()
-        if not first:
-            for copy in before_copies():
-                copy.wait()
-
-        def narrow_kv(r, carry):
-            rows = span(r, 16)
-            for n, acc in enumerate((dk_s, dv_s)):
-                for side in range(2):
-                    at = pl.ds(pl.multiple_of((n + 2 * side) * HEAD + r * 16, 16), 16)
-                    total = acc[rows, side * chip_len:(side + 1) * chip_len]
-                    if not first:
-                        total = total + before_s[at, :].astype(F32)
-                    g_s[at, :] = total.astype(BF)
-            return carry
-
-        lax.fori_loop(0, HEAD // 16, narrow_kv, 0)
-        up_copy = pltpu.make_async_copy(g_s.at[pl.ds(0, 2 * HEAD), :], up_ref, out_sem.at[1])
-        here_copy = pltpu.make_async_copy(g_s.at[pl.ds(2 * HEAD, 2 * HEAD), :], here_ref, out_sem.at[2])
-        up_copy.start()
-        here_copy.start()
-        part_copy.wait()
-        up_copy.wait()
-        here_copy.wait()
+    n_products = x_s.shape[1] // step
+
+    @pl.when(i < last)
+    def _():
+        lax.fori_loop(0, n_products, products, 0)
+
+    @pl.when(i == last)
+    def _():
+        lax.fori_loop(0, n_products, last_products, 0)
+        for c in range(n_products):
+            part_copy(c).wait()
+        for copy in out_copies():
+            copy.wait()
 
 
 def attention(chunk, core, lo, n_blocks, q, dctx, kdoc, tabs, kv_prev, kv_chip, xs, gs, before):
     first = before is None
-    chip_len = q.shape[0]
+    chip_len = q.shape[1]
     width = xs[0].shape[1]
     assert 2 * WIDE == BQ == 4 * HEAD and width == chip_len
     padded = 2 * chip_len + BK
@@ -409,8 +434,8 @@
             num_scalar_prefetch=3,
             grid=(chip_len // BQ,),
             in_specs=[
-                pl.BlockSpec((BQ, WIDE), lambda i, *s: (i, chunk)),
-                pl.BlockSpec((BQ, WIDE), lambda i, *s: (i, chunk)),
+                pl.BlockSpec((1, BQ, WIDE), lambda i, *s: (chunk, i, 0)),
+                pl.BlockSpec((1, BQ, WIDE), lambda i, *s: (chunk, i, 0)),
                 full((1, padded)),
             ] + [pl.BlockSpec(memory_space=pl.ANY)] * 12,
             out_specs=[
@@ -444,7 +469,8 @@
                 pltpu.VMEM((4 * HEAD, chip_len), BF),
                 pltpu.SemaphoreType.DMA((6,)),
                 pltpu.SemaphoreType.DMA((2,)),
-                pltpu.SemaphoreType.DMA((5,)),
+                pltpu.SemaphoreType.DMA((4,)),
+                pltpu.SemaphoreType.DMA((width // (4 * HEAD),)),
             ],
         ),
         out_shape=[

time: 545 us -> 541 us (level)
  no operation moved by 1% of the time
where the time goes in v9:
time: 541 us
  Pallas kernels  251 us (46%)
  waiting for transfers between devices  215 us (40%)
  starting transfers between devices  67.6 us (12%)
    ppermute x6, waiting for transfers between devices, far(): return lax.ppermute(v, 'sp', far_perm)  185 us
    pallas_call x4, Pallas kernels, attention(): pl.pallas_call(functools.partial(attn_kernel, first), grid_spec=pltpu.Pre...  136 us
    ppermute x6, starting transfers between devices, far(): return lax.ppermute(v, 'sp', far_perm)  55 us
    pallas_call x4, Pallas kernels, combine(): pl.pallas_call(combine_kernel, grid_spec=pltpu.PrefetchScalarGridSpec(num...  33.9 us
    ppermute x1, waiting for transfers between devices, device_step(): dkv_far = lax.ppermute(dkv_up, 'sp', up_perm)  23.3 us
    pallas_call x2, Pallas kernels, qkv_proj(): pl.pallas_call(qkv_kernel, grid_spec=pltpu.PrefetchScalarGridSpec(num_sca...  21 us
    pallas_call x1, Pallas kernels, grad_hidden(): pl.pallas_call(functools.partial(hidden_kernel, n), grid_spec=pltpu.Prefe...  17 us
    pallas_call x1, Pallas kernels, dctx_proj(): pl.pallas_call(dctx_kernel, grid_spec=pltpu.PrefetchScalarGridSpec(num_sc...  14.2 us
  transfers between devices with their start and end apart: 29, of which 7 were waited for; matrix products, arithmetic and copies ran while one was open for 1% of the time, Pallas kernels for 20%

profile of v9, /device:TPU:0, one launch (start us, length us, event | category | flops | bytes accessed | tf_op | source)
XLA Modules:
  0.0 540.6 jit_solution(9270450789309220419)
XLA Ops:
  2.0 2.5 collective-permute-start.1
  5.2 1.9 multiply_cosine_fusion
  7.1 1.0 pad_maximum_fusion.tab_ref.tab_own
  8.3 10.5 %qkv_proj.2 = (bf16[1024,256]{1,0:T(8,128)(2,1)}, bf16[4,2048,256]{2,1,0:T(8,128)(2,1)}) custom-call(s32[1]{0:T(128)} %bitcast.s_ref.core_ref, bf16[1024,2048]{1,0:T(8,128)(2,1)} %x_own.9, bf16[2048,2048]{1,0:T(8,128)(2,1)} %refs_10_.1, bf16[2048,256]{1,0:T(8,128)(2,1)} %refs_11_.1, bf16[2048,256]{1,0:T(8,128)(2,1)} %refs_12_.1, ...), custom_call_target="tpu_custom_call" | custom-call | flops 5368709120 | bytes 8388608 | tf_op jit(solution)/shard_map/qkv_proj/pallas_call | solution.py:111
  19.0 4.6 collective-permute-start.6
  25.0 10.5 %qkv_proj.3 = (bf16[1024,256]{1,0:T(8,128)(2,1)}, bf16[4,2048,256]{2,1,0:T(8,128)(2,1)}) custom-call(s32[1]{0:T(128)} %bitcast.s_ref.core_ref, bf16[1024,2048]{1,0:T(8,128)(2,1)} %collective-permute-done.3.x_ref.x_oth, bf16[2048,2048]{1,0:T(8,128)(2,1)} %refs_10_.1, bf16[2048,256]{1,0:T(8,128)(2,1)} %refs_11_.1, ...), custom_call_target="tpu_custom_call", output_to_operand_aliasing={{1}: (6, {})} | custom-call | flops 5368709120 | bytes 8388608 | tf_op jit(solution)/shard_map/qkv_proj/pallas_call | solution.py:111
  35.5 2.1 collective-permute-start.7
  37.6 14.2 %dctx_proj.1.do_ref = bf16[4,2048,256]{2,1,0:T(8,128)(2,1)} custom-call(s32[1]{0:T(128)} %bitcast.s_ref.core_ref, bf16[1024,2048]{1,0:T(8,128)(2,1)} %g_own.7, bf16[1024,2048]{1,0:T(8,128)(2,1)} %collective-permute-done.5.oth_ref.g_oth.before_here, bf16[2048,2048]{1,0:T(8,128)(2,1)} %refs_8_.1), custom_call_target="tpu_custom_call" | custom-call | flops 8589934592 | bytes 12582912 | tf_op jit(solution)/shard_map/dctx_proj/pallas_call | solution.py:166
  51.8 33.7 %attention.4 = (bf16[2,2048,256]{2,1,0:T(8,128)(2,1)}, bf16[512,2048]{1,0:T(8,128)(2,1)}, bf16[256,2048]{1,0:T(8,128)(2,1)}, bf16[256,2048]{1,0:T(8,128)(2,1)}) custom-call(s32[1]{0:T(128)} %bitcast.s_ref.core_ref, s32[4]{0:T(128)} %get-tuple-element.73.lo_ref, s32[4]{0:T(128)} %get-tuple-element.72.nb_ref, bf16[4,2048,256]{2,1,0:T(8,128)(2,1)} %get-tuple-element.39.q_ref, ...), custom_call_target="tpu_custom_call" | custom-call | flops 17179869184 | bytes 12582912 | tf_op jit(solution)/shard_map/attention/pallas_call | solution.py:431
  85.6 34.0 %attention.5 = (bf16[2,2048,256]{2,1,0:T(8,128)(2,1)}, bf16[512,2048]{1,0:T(8,128)(2,1)}, bf16[256,2048]{1,0:T(8,128)(2,1)}, bf16[256,2048]{1,0:T(8,128)(2,1)}) custom-call(s32[1]{0:T(128)} %bitcast.s_ref.core_ref, s32[4]{0:T(128)} %get-tuple-element.73.lo_ref, s32[4]{0:T(128)} %get-tuple-element.72.nb_ref, bf16[4,2048,256]{2,1,0:T(8,128)(2,1)} %get-tuple-element.39.q_ref, ...), custom_call_target="tpu_custom_call" | custom-call | flops 17179869184 | bytes 12582912 | tf_op jit(solution)/shard_map/attention/pallas_call | solution.py:431
  119.5 34.2 %attention.6 = (bf16[2,2048,256]{2,1,0:T(8,128)(2,1)}, bf16[512,2048]{1,0:T(8,128)(2,1)}, bf16[256,2048]{1,0:T(8,128)(2,1)}, bf16[256,2048]{1,0:T(8,128)(2,1)}) custom-call(s32[1]{0:T(128)} %bitcast.s_ref.core_ref, s32[4]{0:T(128)} %get-tuple-element.73.lo_ref, s32[4]{0:T(128)} %get-tuple-element.72.nb_ref, bf16[4,2048,256]{2,1,0:T(8,128)(2,1)} %get-tuple-element.39.q_ref, ...), custom_call_target="tpu_custom_call" | custom-call | flops 17179869184 | bytes 12582912 | tf_op jit(solution)/shard_map/attention/pallas_call | solution.py:431
  153.8 34.0 %attention.7 = (bf16[2,2048,256]{2,1,0:T(8,128)(2,1)}, bf16[512,2048]{1,0:T(8,128)(2,1)}, bf16[256,2048]{1,0:T(8,128)(2,1)}, bf16[256,2048]{1,0:T(8,128)(2,1)}) custom-call(s32[1]{0:T(128)} %bitcast.s_ref.core_ref, s32[4]{0:T(128)} %get-tuple-element.73.lo_ref, s32[4]{0:T(128)} %get-tuple-element.72.nb_ref, bf16[4,2048,256]{2,1,0:T(8,128)(2,1)} %get-tuple-element.39.q_ref, ...), custom_call_target="tpu_custom_call" | custom-call | flops 17179869184 | bytes 12582912 | tf_op jit(solution)/shard_map/attention/pallas_call | solution.py:431
  187.8 1.3 collective-permute-start.12
  189.1 48.4 %collective-permute-start.23 = (bf16[2,256,2048]{2,1,0:T(8,128)(2,1)}, bf16[2,256,2048]{2,1,0:T(8,128)(2,1)}, u32[]{:S(2)}, u32[]{:S(2)}) collective-permute-start(bf16[2,256,2048]{2,1,0:T(8,128)(2,1)} %bitcast.14), channel_id=1, source_target_pairs={{0,2},{1,3},{2,0},{3,1},{4,6},{5,7},{6,4},{7,5}} | collective-permute-start | bytes 6291464 | tf_op jit(solution)/shard_map/ppermute | solution.py:746
  237.5 23.3 %collective-permute-done.12.far_ref = bf16[256,2048]{1,0:T(8,128)(2,1)} collective-permute-done((bf16[256,2048]{1,0:T(8,128)(2,1)}, bf16[256,2048]{1,0:T(8,128)(2,1)}, u32[]{:S(2)}, u32[]{:S(2)}) %collective-permute-start.12) | collective-permute-done | bytes 1048608 | tf_op jit(solution)/shard_map/ppermute | solution.py:793
  260.8 4.6 kv_finish.1
  265.5 6.6 %kvgrad.1.a_ref = bf16[256,2048]{1,0:T(8,128)(2,1)} custom-call(s32[1]{0:T(128)} %bitcast.s_ref.core_ref, bf16[256,2048]{1,0:T(8,128)(2,1)} %get-tuple-element.66.dkvt_ref, bf16[1024,2048]{1,0:T(8,128)(2,1)} %x_own.9, bf16[1024,2048]{1,0:T(8,128)(2,1)} %collective-permute-done.3.x_ref.x_oth), custom_call_target="tpu_custom_call" | custom-call | flops 2147483648 | bytes 8388608 | tf_op jit(solution)/shard_map/kvgrad/pallas_call | solution.py:549
  272.6 2.0 collective-permute-start.20
  274.6 53.6 %collective-permute-done.26.b_ref = bf16[256,2048]{1,0:T(8,128)(2,1)S(1)} collective-permute-done((bf16[256,2048]{1,0:T(8,128)(2,1)}, bf16[256,2048]{1,0:T(8,128)(2,1)S(1)}, u32[]{:S(2)}, u32[]{:S(2)}) %collective-permute-start.26) | collective-permute-done | bytes 1048608 | tf_op jit(solution)/shard_map/ppermute | solution.py:746
  328.2 2.0 collective-permute-start.14
  330.2 43.0 %collective-permute-done.20.b_ref = bf16[2,256,2048]{2,1,0:T(8,128)(2,1)} collective-permute-done((bf16[2,256,2048]{2,1,0:T(8,128)(2,1)}, bf16[2,256,2048]{2,1,0:T(8,128)(2,1)}, u32[]{:S(2)}, u32[]{:S(2)}) %collective-permute-start.20) | collective-permute-done | bytes 2097184 | tf_op jit(solution)/shard_map/ppermute | solution.py:746
  373.7 44.4 %collective-permute-done.17.b_ref = bf16[2,256,2048]{2,1,0:T(8,128)(2,1)} collective-permute-done((bf16[2,256,2048]{2,1,0:T(8,128)(2,1)}, bf16[2,256,2048]{2,1,0:T(8,128)(2,1)}, u32[]{:S(2)}, u32[]{:S(2)}) %collective-permute-start.17) | collective-permute-done | bytes 2097184 | tf_op jit(solution)/shard_map/ppermute | solution.py:746
  418.1 43.6 %collective-permute-done.14.b_ref = bf16[2,256,2048]{2,1,0:T(8,128)(2,1)} collective-permute-done((bf16[2,256,2048]{2,1,0:T(8,128)(2,1)}, bf16[2,256,2048]{2,1,0:T(8,128)(2,1)}, u32[]{:S(2)}, u32[]{:S(2)}) %collective-permute-start.14) | collective-permute-done | bytes 2097184 | tf_op jit(solution)/shard_map/ppermute | solution.py:746
  463.8 2.3 collective-permute-done.8.refs_4_
  466.3 4.4 collective-permute-done.28.d_ref
  471.8 13.9 %attn_out.1 = bf16[1024,2048]{1,0:T(8,128)(2,1)} custom-call(s32[1]{0:T(128)} %bitcast.s_ref.core_ref, bf16[2,2048,256]{2,1,0:T(8,128)(2,1)} %get-tuple-element.42.refs_0_, bf16[2,2048,256]{2,1,0:T(8,128)(2,1)} %get-tuple-element.45.refs_1_, bf16[2,2048,256]{2,1,0:T(8,128)(2,1)} %get-tuple-element.48.refs_2_, ...), custom_call_target="tpu_custom_call" | custom-call | flops 8589934592 | bytes 16777216 | tf_op jit(solution)/shard_map/attn_out/pallas_call | solution.py:667
  485.6 17.0 %grad_hidden.1 = bf16[1024,2048]{1,0:T(8,128)(2,1)} custom-call(s32[1]{0:T(128)} %bitcast.s_ref.core_ref, bf16[2,2048,256]{2,1,0:T(8,128)(2,1)} %get-tuple-element.42.refs_0_, bf16[2,2048,256]{2,1,0:T(8,128)(2,1)} %get-tuple-element.45.refs_1_, bf16[2,2048,256]{2,1,0:T(8,128)(2,1)} %get-tuple-element.48.refs_2_, ...), custom_call_target="tpu_custom_call" | custom-call | flops 10737418240 | bytes 16777216 | tf_op jit(solution)/shard_map/grad_hidden/pallas_call | solution.py:708
  502.6 4.1 kv_combine.1
  506.7 8.5 %combine.4 = (f32[2048,2048]{1,0:T(8,128)}, f32[2048,2048]{1,0:T(8,128)}) custom-call(s32[1]{0:T(128)} %bitcast.s_ref.core_ref, bf16[2,256,2048]{2,1,0:T(8,128)(2,1)} %bitcast.16, bf16[2,256,2048]{2,1,0:T(8,128)(2,1)} %collective-permute-done.23.b_ref, bf16[2,256,2048]{2,1,0:T(8,128)(2,1)} %collective-permute-done.24.c_ref, ...), custom_call_target="tpu_custom_call" | custom-call | flops 536870912 | bytes 16777216 | tf_op jit(solution)/shard_map/combine/pallas_call | solution.py:625
  515.1 8.5 %combine.5 = (f32[2048,2048]{1,0:T(8,128)}, f32[2048,2048]{1,0:T(8,128)}) custom-call(s32[1]{0:T(128)} %bitcast.s_ref.core_ref, bf16[2,256,2048]{2,1,0:T(8,128)(2,1)} %bitcast.13, bf16[2,256,2048]{2,1,0:T(8,128)(2,1)} %collective-permute-done.20.b_ref, ...), custom_call_target="tpu_custom_call", output_to_operand_aliasing={{0}: (5, {}), {1}: (6, {})} | custom-call | flops 536870912 | bytes 16777216 | tf_op jit(solution)/shard_map/combine/pallas_call | solution.py:625
  523.6 8.5 %combine.6 = (f32[2048,2048]{1,0:T(8,128)}, f32[2048,2048]{1,0:T(8,128)}) custom-call(s32[1]{0:T(128)} %bitcast.s_ref.core_ref, bf16[2,256,2048]{2,1,0:T(8,128)(2,1)} %bitcast.10, bf16[2,256,2048]{2,1,0:T(8,128)(2,1)} %collective-permute-done.17.b_ref, ...), custom_call_target="tpu_custom_call", output_to_operand_aliasing={{0}: (5, {}), {1}: (6, {})} | custom-call | flops 536870912 | bytes 16777216 | tf_op jit(solution)/shard_map/combine/pallas_call | solution.py:625
  532.1 8.5 %combine.7 = (f32[2048,2048]{1,0:T(8,128)}, f32[2048,2048]{1,0:T(8,128)}) custom-call(s32[1]{0:T(128)} %bitcast.s_ref.core_ref, bf16[2,256,2048]{2,1,0:T(8,128)(2,1)} %bitcast.7, bf16[2,256,2048]{2,1,0:T(8,128)(2,1)} %collective-permute-done.14.b_ref, ...), custom_call_target="tpu_custom_call", output_to_operand_aliasing={{0}: (5, {}), {1}: (6, {})} | custom-call | flops 536870912 | bytes 16777216 | tf_op jit(solution)/shard_map/combine/pallas_call | solution.py:625
  (70 shorter events, 8.2 us)
Async XLA Ops:
  0.6 24.4 %collective-permute-start.3 = (bf16[1024,2048]{1,0:T(8,128)(2,1)}, bf16[1024,2048]{1,0:T(8,128)(2,1)}, u32[]{:S(2)}, u32[]{:S(2)}) collective-permute-start(bf16[1024,2048]{1,0:T(8,128)(2,1)} %x_own.9), channel_id=1, source_target_pairs={{0,1},{1,0},{2,3},{3,2},{4,5},{5,4},{6,7},{7,6}} | collective-permute-start | bytes 12582920 | tf_op jit(solution)/shard_map/ppermute | solution.py:743
  1.5 36.1 %collective-permute-start.5 = (bf16[1024,2048]{1,0:T(8,128)(2,1)}, bf16[1024,2048]{1,0:T(8,128)(2,1)}, u32[]{:S(2)}, u32[]{:S(2)}) collective-permute-start(bf16[1024,2048]{1,0:T(8,128)(2,1)} %g_own.7), channel_id=1, source_target_pairs={{0,1},{1,0},{2,3},{3,2},{4,5},{5,4},{6,7},{7,6}} | collective-permute-start | bytes 12582920 | tf_op jit(solution)/shard_map/ppermute | solution.py:743
  1.5 17.3 %collective-permute-start = (s32[1024]{0:T(1024)}, s32[1024]{0:T(1024)S(1)}, u32[]{:S(2)}, u32[]{:S(2)}) collective-permute-start(s32[1024]{0:T(1024)} %param.11), channel_id=1, source_target_pairs={{0,1},{1,0},{2,3},{3,2},{4,5},{5,4},{6,7},{7,6}} | collective-permute-start | bytes 12296 | tf_op jit(solution)/shard_map/ppermute | solution.py:743
  2.0 17.0 %collective-permute-start.1 = (s32[1024]{0:T(1024)}, s32[1024]{0:T(1024)S(1)}, u32[]{:S(2)}, u32[]{:S(2)}) collective-permute-start(s32[1024]{0:T(1024)} %param.11), channel_id=1, source_target_pairs={{0,2},{1,3},{2,0},{3,1},{4,6},{5,7},{6,4},{7,5}} | collective-permute-start | bytes 12296 | tf_op jit(solution)/shard_map/ppermute | solution.py:746
  8.1 16.9 %collective-permute-start.4 = (f32[1024,128]{1,0:T(8,128)}, f32[1024,128]{1,0:T(8,128)}, u32[]{:S(2)}, u32[]{:S(2)}) collective-permute-start(f32[1024,128]{1,0:T(8,128)} %pad_maximum_fusion.tab_ref.tab_own), channel_id=1, source_target_pairs={{0,1},{1,0},{2,3},{3,2},{4,5},{5,4},{6,7},{7,6}} | collective-permute-start | bytes 1572872 | tf_op jit(solution)/shard_map/ppermute | solution.py:743
  8.3 10.5 %copy-start.3 = (s32[1024]{0:T(1024)S(1)}, s32[1024]{0:T(1024)}, u32[]{:S(2)}) copy-start(s32[1024]{0:T(1024)} %param.11) | copy-start | bytes 12292
  18.8 4.8 collective-permute-start.2
  19.0 32.8 %collective-permute-start.6 = (bf16[1024,256]{1,0:T(8,128)(2,1)}, bf16[1024,256]{1,0:T(8,128)(2,1)}, u32[]{:S(2)}, u32[]{:S(2)}) collective-permute-start(bf16[1024,256]{1,0:T(8,128)(2,1)} %get-tuple-element.40.kvc_own), channel_id=1, source_target_pairs={{0,2},{1,3},{4,6},{5,7}} | collective-permute-start | bytes 1572872 | tf_op jit(solution)/shard_map/ppermute | solution.py:764
  35.5 16.3 %collective-permute-start.7 = (bf16[1024,256]{1,0:T(8,128)(2,1)}, bf16[1024,256]{1,0:T(8,128)(2,1)}, u32[]{:S(2)}, u32[]{:S(2)}) collective-permute-start(bf16[1024,256]{1,0:T(8,128)(2,1)} %get-tuple-element.41.kvc_oth), channel_id=1, source_target_pairs={{0,2},{1,3},{4,6},{5,7}} | collective-permute-start | bytes 1572872 | tf_op jit(solution)/shard_map/ppermute | solution.py:771
  187.8 73.1 %collective-permute-start.12 = (bf16[256,2048]{1,0:T(8,128)(2,1)}, bf16[256,2048]{1,0:T(8,128)(2,1)}, u32[]{:S(2)}, u32[]{:S(2)}) collective-permute-start(bf16[256,2048]{1,0:T(8,128)(2,1)} %get-tuple-element.53), channel_id=1, source_target_pairs={{2,0},{3,1},{6,4},{7,5}} | collective-permute-start | bytes 3145736 | tf_op jit(solution)/shard_map/ppermute | solution.py:793
  189.1 139.1 %collective-permute-start.23 = (bf16[2,256,2048]{2,1,0:T(8,128)(2,1)}, bf16[2,256,2048]{2,1,0:T(8,128)(2,1)}, u32[]{:S(2)}, u32[]{:S(2)}) collective-permute-start(bf16[2,256,2048]{2,1,0:T(8,128)(2,1)} %bitcast.14), channel_id=1, source_target_pairs={{0,2},{1,3},{2,0},{3,1},{4,6},{5,7},{6,4},{7,5}} | collective-permute-start | bytes 6291464 | tf_op jit(solution)/shard_map/ppermute | solution.py:746
  272.1 56.1 %collective-permute-start.26 = (bf16[256,2048]{1,0:T(8,128)(2,1)}, bf16[256,2048]{1,0:T(8,128)(2,1)S(1)}, u32[]{:S(2)}, u32[]{:S(2)}) collective-permute-start(bf16[256,2048]{1,0:T(8,128)(2,1)} %kvgrad.1.a_ref), channel_id=1, source_target_pairs={{0,2},{1,3},{2,0},{3,1},{4,6},{5,7},{6,4},{7,5}} | collective-permute-start | bytes 3145736 | tf_op jit(solution)/shard_map/ppermute | solution.py:746
  272.1 56.1 %collective-permute-start.27 = (bf16[256,2048]{1,0:T(8,128)(2,1)}, bf16[256,2048]{1,0:T(8,128)(2,1)S(1)}, u32[]{:S(2)}, u32[]{:S(2)}) collective-permute-start(bf16[256,2048]{1,0:T(8,128)(2,1)} %kvgrad.1.a_ref), channel_id=1, source_target_pairs={{0,1},{1,0},{2,3},{3,2},{4,5},{5,4},{6,7},{7,6}} | collective-permute-start | bytes 3145736 | tf_op jit(solution)/shard_map/ppermute | solution.py:743
  272.1 58.2 %collective-permute-start.24 = (bf16[2,256,2048]{2,1,0:T(8,128)(2,1)}, bf16[2,256,2048]{2,1,0:T(8,128)(2,1)}, u32[]{:S(2)}, u32[]{:S(2)}) collective-permute-start(bf16[2,256,2048]{2,1,0:T(8,128)(2,1)} %bitcast.15), channel_id=1, source_target_pairs={{0,1},{1,0},{2,3},{3,2},{4,5},{5,4},{6,7},{7,6}} | collective-permute-start | bytes 6291464 | tf_op jit(solution)/shard_map/ppermute | solution.py:743
  272.6 100.6 %collective-permute-start.20 = (bf16[2,256,2048]{2,1,0:T(8,128)(2,1)}, bf16[2,256,2048]{2,1,0:T(8,128)(2,1)}, u32[]{:S(2)}, u32[]{:S(2)}) collective-permute-start(bf16[2,256,2048]{2,1,0:T(8,128)(2,1)} %bitcast.11), channel_id=1, source_target_pairs={{0,2},{1,3},{2,0},{3,1},{4,6},{5,7},{6,4},{7,5}} | collective-permute-start | bytes 6291464 | tf_op jit(solution)/shard_map/ppermute | solution.py:746
  328.1 134.6 %copy-start = (bf16[256,2048]{1,0:T(8,128)(2,1)}, bf16[256,2048]{1,0:T(8,128)(2,1)S(1)}, u32[]{:S(2)}) copy-start(bf16[256,2048]{1,0:T(8,128)(2,1)S(1)} %collective-permute-done.26.b_ref) | copy-start | bytes 3145732
  328.2 45.1 %collective-permute-start.21 = (bf16[2,256,2048]{2,1,0:T(8,128)(2,1)}, bf16[2,256,2048]{2,1,0:T(8,128)(2,1)}, u32[]{:S(2)}, u32[]{:S(2)}) collective-permute-start(bf16[2,256,2048]{2,1,0:T(8,128)(2,1)} %bitcast.12), channel_id=1, source_target_pairs={{0,1},{1,0},{2,3},{3,2},{4,5},{5,4},{6,7},{7,6}} | collective-permute-start | bytes 6291464 | tf_op jit(solution)/shard_map/ppermute | solution.py:743
  328.2 142.5 %copy-start.1 = (bf16[256,2048]{1,0:T(8,128)(2,1)}, bf16[256,2048]{1,0:T(8,128)(2,1)S(1)}, u32[]{:S(2)}) copy-start(bf16[256,2048]{1,0:T(8,128)(2,1)S(1)} %collective-permute-done.27.c_ref) | copy-start | bytes 3145732
  328.2 90.0 %collective-permute-start.17 = (bf16[2,256,2048]{2,1,0:T(8,128)(2,1)}, bf16[2,256,2048]{2,1,0:T(8,128)(2,1)}, u32[]{:S(2)}, u32[]{:S(2)}) collective-permute-start(bf16[2,256,2048]{2,1,0:T(8,128)(2,1)} %bitcast.8), channel_id=1, source_target_pairs={{0,2},{1,3},{2,0},{3,1},{4,6},{5,7},{6,4},{7,5}} | collective-permute-start | bytes 6291464 | tf_op jit(solution)/shard_map/ppermute | solution.py:746
  328.2 133.5 %collective-permute-start.14 = (bf16[2,256,2048]{2,1,0:T(8,128)(2,1)}, bf16[2,256,2048]{2,1,0:T(8,128)(2,1)}, u32[]{:S(2)}, u32[]{:S(2)}) collective-permute-start(bf16[2,256,2048]{2,1,0:T(8,128)(2,1)} %bitcast.5), channel_id=1, source_target_pairs={{0,2},{1,3},{2,0},{3,1},{4,6},{5,7},{6,4},{7,5}} | collective-permute-start | bytes 6291464 | tf_op jit(solution)/shard_map/ppermute | solution.py:746
  330.2 132.5 %collective-permute-start.11 = (bf16[2,2048,256]{2,1,0:T(8,128)(2,1)}, bf16[2,2048,256]{2,1,0:T(8,128)(2,1)}, u32[]{:S(2)}, u32[]{:S(2)}) collective-permute-start(bf16[2,2048,256]{2,1,0:T(8,128)(2,1)} %get-tuple-element.51.refs_3_), channel_id=1, source_target_pairs={{0,1},{1,0},{2,3},{3,2},{4,5},{5,4},{6,7},{7,6}} | collective-permute-start | bytes 6291464 | tf_op jit(solution)/shard_map/ppermute | solution.py:743
  373.2 88.5 %collective-permute-start.13 = (bf16[2048,256]{1,0:T(8,128)(2,1)}, bf16[2048,256]{1,0:T(8,128)(2,1)S(1)}, u32[]{:S(2)}, u32[]{:S(2)}) collective-permute-start(bf16[2048,256]{1,0:T(8,128)(2,1)} %get-tuple-element.54.refs_8_), channel_id=1, source_target_pairs={{0,1},{1,0},{2,3},{3,2},{4,5},{5,4},{6,7},{7,6}} | collective-permute-start | bytes 3145736 | tf_op jit(solution)/shard_map/ppermute | solution.py:743
  373.2 90.1 %collective-permute-start.10 = (bf16[2,2048,256]{2,1,0:T(8,128)(2,1)}, bf16[2,2048,256]{2,1,0:T(8,128)(2,1)S(1)}, u32[]{:S(2)}, u32[]{:S(2)}) collective-permute-start(bf16[2,2048,256]{2,1,0:T(8,128)(2,1)} %get-tuple-element.48.refs_2_), channel_id=1, source_target_pairs={{0,1},{1,0},{2,3},{3,2},{4,5},{5,4},{6,7},{7,6}} | collective-permute-start | bytes 6291464 | tf_op jit(solution)/shard_map/ppermute | solution.py:743
  418.1 45.2 %collective-permute-start.9 = (bf16[2,2048,256]{2,1,0:T(8,128)(2,1)}, bf16[2,2048,256]{2,1,0:T(8,128)(2,1)S(1)}, u32[]{:S(2)}, u32[]{:S(2)}) collective-permute-start(bf16[2,2048,256]{2,1,0:T(8,128)(2,1)} %get-tuple-element.45.refs_1_), channel_id=1, source_target_pairs={{0,1},{1,0},{2,3},{3,2},{4,5},{5,4},{6,7},{7,6}} | collective-permute-start | bytes 6291464 | tf_op jit(solution)/shard_map/ppermute | solution.py:743
  461.7 4.4 collective-permute-start.8
  461.8 9.8 %collective-permute-start.25 = (bf16[2,256,2048]{2,1,0:T(8,128)(2,1)}, bf16[2,256,2048]{2,1,0:T(8,128)(2,1)}, u32[]{:S(2)}, u32[]{:S(2)}) collective-permute-start(bf16[2,256,2048]{2,1,0:T(8,128)(2,1)} %collective-permute-done.23.b_ref), channel_id=1, source_target_pairs={{0,1},{1,0},{2,3},{3,2},{4,5},{5,4},{6,7},{7,6}} | collective-permute-start | bytes 6291464 | tf_op jit(solution)/shard_map/ppermute | solution.py:743
  462.8 7.8 %collective-permute-start.28 = (bf16[256,2048]{1,0:T(8,128)(2,1)S(1)}, bf16[256,2048]{1,0:T(8,128)(2,1)S(1)}, u32[]{:S(2)}, u32[]{:S(2)}) collective-permute-start(bf16[256,2048]{1,0:T(8,128)(2,1)S(1)} %collective-permute-done.26.b_ref), channel_id=1, source_target_pairs={{0,1},{1,0},{2,3},{3,2},{4,5},{5,4},{6,7},{7,6}} | collective-permute-start | bytes 3145736 | tf_op jit(solution)/shard_map/ppermute | solution.py:743
  463.3 51.8 %collective-permute-start.22 = (bf16[2,256,2048]{2,1,0:T(8,128)(2,1)}, bf16[2,256,2048]{2,1,0:T(8,128)(2,1)}, u32[]{:S(2)}, u32[]{:S(2)}) collective-permute-start(bf16[2,256,2048]{2,1,0:T(8,128)(2,1)} %collective-permute-done.20.b_ref), channel_id=1, source_target_pairs={{0,1},{1,0},{2,3},{3,2},{4,5},{5,4},{6,7},{7,6}} | collective-permute-start | bytes 6291464 | tf_op jit(solution)/shard_map/ppermute | solution.py:743
  463.3 60.3 %collective-permute-start.18 = (bf16[2,256,2048]{2,1,0:T(8,128)(2,1)}, bf16[2,256,2048]{2,1,0:T(8,128)(2,1)}, u32[]{:S(2)}, u32[]{:S(2)}) collective-permute-start(bf16[2,256,2048]{2,1,0:T(8,128)(2,1)} %bitcast.9), channel_id=1, source_target_pairs={{0,1},{1,0},{2,3},{3,2},{4,5},{5,4},{6,7},{7,6}} | collective-permute-start | bytes 6291464 | tf_op jit(solution)/shard_map/ppermute | solution.py:743
  466.1 57.5 %collective-permute-start.19 = (bf16[2,256,2048]{2,1,0:T(8,128)(2,1)}, bf16[2,256,2048]{2,1,0:T(8,128)(2,1)}, u32[]{:S(2)}, u32[]{:S(2)}) collective-permute-start(bf16[2,256,2048]{2,1,0:T(8,128)(2,1)} %collective-permute-done.17.b_ref), channel_id=1, source_target_pairs={{0,1},{1,0},{2,3},{3,2},{4,5},{5,4},{6,7},{7,6}} | collective-permute-start | bytes 6291464 | tf_op jit(solution)/shard_map/ppermute | solution.py:743
  470.6 61.5 %collective-permute-start.15 = (bf16[2,256,2048]{2,1,0:T(8,128)(2,1)}, bf16[2,256,2048]{2,1,0:T(8,128)(2,1)}, u32[]{:S(2)}, u32[]{:S(2)}) collective-permute-start(bf16[2,256,2048]{2,1,0:T(8,128)(2,1)} %bitcast.6), channel_id=1, source_target_pairs={{0,1},{1,0},{2,3},{3,2},{4,5},{5,4},{6,7},{7,6}} | collective-permute-start | bytes 6291464 | tf_op jit(solution)/shard_map/ppermute | solution.py:743
  471.6 60.5 %collective-permute-start.16 = (bf16[2,256,2048]{2,1,0:T(8,128)(2,1)}, bf16[2,256,2048]{2,1,0:T(8,128)(2,1)}, u32[]{:S(2)}, u32[]{:S(2)}) collective-permute-start(bf16[2,256,2048]{2,1,0:T(8,128)(2,1)} %collective-permute-done.14.b_ref), channel_id=1, source_target_pairs={{0,1},{1,0},{2,3},{3,2},{4,5},{5,4},{6,7},{7,6}} | collective-permute-start | bytes 6291464 | tf_op jit(solution)/shard_map/ppermute | solution.py:743
  (5 other events, 24.1 us)

commit v10 on v9

--- a/solution.py
+++ b/solution.py
@@ -271,10 +271,6 @@
     qdoc = kdoc_ref[:, pl.ds(pl.multiple_of(chip_len + i * BQ, BQ), BQ)]
     qd_s[...] = jnp.broadcast_to(qdoc, (HEAD, BQ)).T
     m_s[...] = jnp.full(m_s.shape, NEG_BIG, F32)
-    l_s[...] = jnp.zeros(l_s.shape, F32)
-    d_s[...] = jnp.zeros(d_s.shape, F32)
-    ctx_s[...] = jnp.zeros(ctx_s.shape, F32)
-    dq_s[...] = jnp.zeros(dq_s.shape, F32)
     lo = lo_ref[i]
     n_blocks = nb_ref[i]
     lanes = BK // HEAD
@@ -309,6 +305,8 @@
 
     arrive(0, 4)
     lax.fori_loop(0, n_blocks, scores, 0)
+    l_s[...] = jnp.zeros(l_s.shape, F32)
+    d_s[...] = jnp.zeros(d_s.shape, F32)
     m_s[...] = jnp.broadcast_to(jnp.max(m_s[...], axis=1, keepdims=True), m_s.shape)
 
     def weights(b, carry):
@@ -322,6 +320,8 @@
 
     arrive(4, 6)
     lax.fori_loop(0, n_blocks, weights, 0)
+    ctx_s[...] = jnp.zeros(ctx_s.shape, F32)
+    dq_s[...] = jnp.zeros(dq_s.shape, F32)
     inv = 1.0 / jnp.sum(l_s[...], axis=1, keepdims=True)
     delta = jnp.sum(d_s[...], axis=1, keepdims=True) * inv
     l_s[...] = jnp.broadcast_to(inv, l_s.shape)
@@ -561,31 +561,33 @@
     )(core, dkvt, x_own, x_oth)
 
 
-def kv_combine_kernel(s_ref, a_ref, b_ref, c_ref, d_ref, gk_ref, gv_ref):
-    for place, u_ref, v_ref in ((s_ref[0], a_ref, b_ref), (1 - s_ref[0], c_ref, d_ref)):
-        total = u_ref[...].astype(F32) + v_ref[...].astype(F32)
-        where = span(place, HEAD)
-        gk_ref[:, where] = total[:HEAD, :].T
-        gv_ref[:, where] = total[HEAD:, :].T
-
-
-def kv_combine(core, parts):
+def kv_combine_kernel(s_ref, a_ref, b_ref, *rest):
+    gk_ref, gv_ref = rest[-2:]
+    total = a_ref[...].astype(F32) + b_ref[...].astype(F32)
+    gk_ref[...] = total[:HEAD, :].T
+    gv_ref[...] = total[HEAD:, :].T
+
+
+def kv_combine(own, core, parts, prev):
     rows, width = parts[0].shape
     step = 1024
     out = jax.ShapeDtypeStruct((width, rows), F32)
+    extra = [] if prev is None else list(prev)
     return pl.pallas_call(
         kv_combine_kernel,
         grid_spec=pltpu.PrefetchScalarGridSpec(
             num_scalar_prefetch=1,
             grid=(width // step,),
-            in_specs=[pl.BlockSpec((rows, step), lambda n, s: (0, n))] * 4,
-            out_specs=[pl.BlockSpec((step, rows), lambda n, s: (n, 0))] * 2,
+            in_specs=[pl.BlockSpec((rows, step), lambda n, s: (0, n))] * 2
+            + [pl.BlockSpec(memory_space=pl.ANY)] * len(extra),
+            out_specs=[pl.BlockSpec((step, HEAD), lambda n, s: (n, s[0] if own else 1 - s[0]))] * 2,
         ),
         out_shape=[out, out],
+        input_output_aliases={} if prev is None else {3: 0, 4: 1},
         compiler_params=params(),
-        cost_estimate=cost(16 * width * rows * 16, 16 * width * rows),
+        cost_estimate=cost(8 * width * rows * 16, 8 * width * rows),
         name="kv_combine",
-    )(core, *parts)
+    )(core, *parts, *extra)
 
 
 def combine_kernel(s_ref, a_ref, b_ref, c_ref, d_ref, *rest):
@@ -804,7 +806,8 @@
         kv_part_far = far(kv_part)
         kv_part_near = near(kv_part)
         kv_part_far_near = near(kv_part_far)
-        grad_wk, grad_wv = kv_combine(core, (kv_part, kv_part_far, kv_part_near, kv_part_far_near))
+        kv_sums = kv_combine(True, core, (kv_part, kv_part_far), None)
+        grad_wk, grad_wv = kv_combine(False, core, (kv_part_near, kv_part_far_near), kv_sums)
         out = attn_out(core, acts, acts_oth, w_o)
         g_hidden = grad_hidden(core, acts, acts_oth, dkv, dkv_oth, w_q, w_k, w_v)
         return out, g_hidden, grad_wq, grad_wk, grad_wv, grad_wo

time: 541 us -> 542 us (level)
  no operation moved by 1% of the time
where the time goes in v10:
time: 542 us; the launch traced here: 541 us
  Pallas kernels  252 us (46%)
  waiting for transfers between devices  216 us (40%)
  starting transfers between devices  67.5 us (12%)
    ppermute x6, waiting for transfers between devices, far(): return lax.ppermute(v, 'sp', far_perm)  185 us
    pallas_call x4, Pallas kernels, attention(): pl.pallas_call(functools.partial(attn_kernel, first), grid_spec=pltpu.Pre...  135 us
    ppermute x6, starting transfers between devices, far(): return lax.ppermute(v, 'sp', far_perm)  55.1 us
    pallas_call x4, Pallas kernels, combine(): pl.pallas_call(combine_kernel, grid_spec=pltpu.PrefetchScalarGridSpec(num...  33.9 us
    ppermute x1, waiting for transfers between devices, device_step(): dkv_far = lax.ppermute(dkv_up, 'sp', up_perm)  23.3 us
    pallas_call x2, Pallas kernels, qkv_proj(): pl.pallas_call(qkv_kernel, grid_spec=pltpu.PrefetchScalarGridSpec(num_sca...  21 us
    pallas_call x1, Pallas kernels, grad_hidden(): pl.pallas_call(functools.partial(hidden_kernel, n), grid_spec=pltpu.Prefe...  17 us
    pallas_call x1, Pallas kernels, dctx_proj(): pl.pallas_call(dctx_kernel, grid_spec=pltpu.PrefetchScalarGridSpec(num_sc...  14.2 us
  transfers between devices with their start and end apart: 29, of which 7 were waited for; matrix products, arithmetic and copies ran while one was open for 1% of the time, Pallas kernels for 20%

profile of v10, /device:TPU:0, one launch (start us, length us, event | category | flops | bytes accessed | tf_op | source)
XLA Modules:
  0.0 541.0 jit_solution(3301653951261896613)
XLA Ops:
  2.0 2.5 collective-permute-start.1
  5.2 1.9 multiply_cosine_fusion
  8.3 10.5 %qkv_proj.2 = (bf16[1024,256]{1,0:T(8,128)(2,1)}, bf16[4,2048,256]{2,1,0:T(8,128)(2,1)}) custom-call(s32[1]{0:T(128)} %bitcast.s_ref.core_ref, bf16[1024,2048]{1,0:T(8,128)(2,1)} %x_own.9, bf16[2048,2048]{1,0:T(8,128)(2,1)} %refs_10_.1, bf16[2048,256]{1,0:T(8,128)(2,1)} %refs_11_.1, bf16[2048,256]{1,0:T(8,128)(2,1)} %refs_12_.1, ...), custom_call_target="tpu_custom_call" | custom-call | flops 5368709120 | bytes 8388608 | tf_op jit(solution)/shard_map/qkv_proj/pallas_call | solution.py:111
  19.0 4.7 collective-permute-start.6
  25.1 10.5 %qkv_proj.3 = (bf16[1024,256]{1,0:T(8,128)(2,1)}, bf16[4,2048,256]{2,1,0:T(8,128)(2,1)}) custom-call(s32[1]{0:T(128)} %bitcast.s_ref.core_ref, bf16[1024,2048]{1,0:T(8,128)(2,1)} %collective-permute-done.3.x_ref.x_oth, bf16[2048,2048]{1,0:T(8,128)(2,1)} %refs_10_.1, bf16[2048,256]{1,0:T(8,128)(2,1)} %refs_11_.1, ...), custom_call_target="tpu_custom_call", output_to_operand_aliasing={{1}: (6, {})} | custom-call | flops 5368709120 | bytes 8388608 | tf_op jit(solution)/shard_map/qkv_proj/pallas_call | solution.py:111
  35.6 2.1 collective-permute-start.7
  37.7 14.2 %dctx_proj.1.do_ref = bf16[4,2048,256]{2,1,0:T(8,128)(2,1)} custom-call(s32[1]{0:T(128)} %bitcast.s_ref.core_ref, bf16[1024,2048]{1,0:T(8,128)(2,1)} %g_own.7, bf16[1024,2048]{1,0:T(8,128)(2,1)} %collective-permute-done.5.oth_ref.g_oth.before_here, bf16[2048,2048]{1,0:T(8,128)(2,1)} %refs_8_.1), custom_call_target="tpu_custom_call" | custom-call | flops 8589934592 | bytes 12582912 | tf_op jit(solution)/shard_map/dctx_proj/pallas_call | solution.py:166
  51.8 33.5 %attention.4 = (bf16[2,2048,256]{2,1,0:T(8,128)(2,1)}, bf16[512,2048]{1,0:T(8,128)(2,1)}, bf16[256,2048]{1,0:T(8,128)(2,1)}, bf16[256,2048]{1,0:T(8,128)(2,1)}) custom-call(s32[1]{0:T(128)} %bitcast.s_ref.core_ref, s32[4]{0:T(128)} %get-tuple-element.77.lo_ref, s32[4]{0:T(128)} %get-tuple-element.76.nb_ref, bf16[4,2048,256]{2,1,0:T(8,128)(2,1)} %get-tuple-element.41.q_ref, ...), custom_call_target="tpu_custom_call" | custom-call | flops 17179869184 | bytes 12582912 | tf_op jit(solution)/shard_map/attention/pallas_call | solution.py:431
  85.4 33.8 %attention.5 = (bf16[2,2048,256]{2,1,0:T(8,128)(2,1)}, bf16[512,2048]{1,0:T(8,128)(2,1)}, bf16[256,2048]{1,0:T(8,128)(2,1)}, bf16[256,2048]{1,0:T(8,128)(2,1)}) custom-call(s32[1]{0:T(128)} %bitcast.s_ref.core_ref, s32[4]{0:T(128)} %get-tuple-element.77.lo_ref, s32[4]{0:T(128)} %get-tuple-element.76.nb_ref, bf16[4,2048,256]{2,1,0:T(8,128)(2,1)} %get-tuple-element.41.q_ref, ...), custom_call_target="tpu_custom_call" | custom-call | flops 17179869184 | bytes 12582912 | tf_op jit(solution)/shard_map/attention/pallas_call | solution.py:431
  119.2 34.1 %attention.6 = (bf16[2,2048,256]{2,1,0:T(8,128)(2,1)}, bf16[512,2048]{1,0:T(8,128)(2,1)}, bf16[256,2048]{1,0:T(8,128)(2,1)}, bf16[256,2048]{1,0:T(8,128)(2,1)}) custom-call(s32[1]{0:T(128)} %bitcast.s_ref.core_ref, s32[4]{0:T(128)} %get-tuple-element.77.lo_ref, s32[4]{0:T(128)} %get-tuple-element.76.nb_ref, bf16[4,2048,256]{2,1,0:T(8,128)(2,1)} %get-tuple-element.41.q_ref, ...), custom_call_target="tpu_custom_call" | custom-call | flops 17179869184 | bytes 12582912 | tf_op jit(solution)/shard_map/attention/pallas_call | solution.py:431
  153.2 33.8 %attention.7 = (bf16[2,2048,256]{2,1,0:T(8,128)(2,1)}, bf16[512,2048]{1,0:T(8,128)(2,1)}, bf16[256,2048]{1,0:T(8,128)(2,1)}, bf16[256,2048]{1,0:T(8,128)(2,1)}) custom-call(s32[1]{0:T(128)} %bitcast.s_ref.core_ref, s32[4]{0:T(128)} %get-tuple-element.77.lo_ref, s32[4]{0:T(128)} %get-tuple-element.76.nb_ref, bf16[4,2048,256]{2,1,0:T(8,128)(2,1)} %get-tuple-element.41.q_ref, ...), custom_call_target="tpu_custom_call" | custom-call | flops 17179869184 | bytes 12582912 | tf_op jit(solution)/shard_map/attention/pallas_call | solution.py:431
  187.0 1.3 collective-permute-start.12
  188.3 48.5 %collective-permute-start.23 = (bf16[2,256,2048]{2,1,0:T(8,128)(2,1)}, bf16[2,256,2048]{2,1,0:T(8,128)(2,1)}, u32[]{:S(2)}, u32[]{:S(2)}) collective-permute-start(bf16[2,256,2048]{2,1,0:T(8,128)(2,1)} %bitcast.14), channel_id=1, source_target_pairs={{0,2},{1,3},{2,0},{3,1},{4,6},{5,7},{6,4},{7,5}} | collective-permute-start | bytes 6291464 | tf_op jit(solution)/shard_map/ppermute | solution.py:748
  236.8 23.3 %collective-permute-done.12.far_ref = bf16[256,2048]{1,0:T(8,128)(2,1)} collective-permute-done((bf16[256,2048]{1,0:T(8,128)(2,1)}, bf16[256,2048]{1,0:T(8,128)(2,1)}, u32[]{:S(2)}, u32[]{:S(2)}) %collective-permute-start.12) | collective-permute-done | bytes 1048608 | tf_op jit(solution)/shard_map/ppermute | solution.py:795
  260.2 4.6 kv_finish.1
  264.8 6.6 %kvgrad.1.a_ref = bf16[256,2048]{1,0:T(8,128)(2,1)} custom-call(s32[1]{0:T(128)} %bitcast.s_ref.core_ref, bf16[256,2048]{1,0:T(8,128)(2,1)} %get-tuple-element.68.dkvt_ref, bf16[1024,2048]{1,0:T(8,128)(2,1)} %x_own.9, bf16[1024,2048]{1,0:T(8,128)(2,1)} %collective-permute-done.3.x_ref.x_oth), custom_call_target="tpu_custom_call" | custom-call | flops 2147483648 | bytes 8388608 | tf_op jit(solution)/shard_map/kvgrad/pallas_call | solution.py:549
  271.9 2.0 collective-permute-start.20
  273.9 53.6 %collective-permute-done.27.b_ref = bf16[256,2048]{1,0:T(8,128)(2,1)S(1)} collective-permute-done((bf16[256,2048]{1,0:T(8,128)(2,1)}, bf16[256,2048]{1,0:T(8,128)(2,1)S(1)}, u32[]{:S(2)}, u32[]{:S(2)}) %collective-permute-start.27) | collective-permute-done | bytes 1048608 | tf_op jit(solution)/shard_map/ppermute | solution.py:748
  327.5 2.0 collective-permute-start.14
  329.5 43.0 %collective-permute-done.20.b_ref = bf16[2,256,2048]{2,1,0:T(8,128)(2,1)} collective-permute-done((bf16[2,256,2048]{2,1,0:T(8,128)(2,1)}, bf16[2,256,2048]{2,1,0:T(8,128)(2,1)}, u32[]{:S(2)}, u32[]{:S(2)}) %collective-permute-start.20) | collective-permute-done | bytes 2097184 | tf_op jit(solution)/shard_map/ppermute | solution.py:748
  373.0 44.4 %collective-permute-done.17.b_ref = bf16[2,256,2048]{2,1,0:T(8,128)(2,1)} collective-permute-done((bf16[2,256,2048]{2,1,0:T(8,128)(2,1)}, bf16[2,256,2048]{2,1,0:T(8,128)(2,1)}, u32[]{:S(2)}, u32[]{:S(2)}) %collective-permute-start.17) | collective-permute-done | bytes 2097184 | tf_op jit(solution)/shard_map/ppermute | solution.py:748
  417.5 43.6 %collective-permute-done.14.b_ref = bf16[2,256,2048]{2,1,0:T(8,128)(2,1)} collective-permute-done((bf16[2,256,2048]{2,1,0:T(8,128)(2,1)}, bf16[2,256,2048]{2,1,0:T(8,128)(2,1)}, u32[]{:S(2)}, u32[]{:S(2)}) %collective-permute-start.14) | collective-permute-done | bytes 2097184 | tf_op jit(solution)/shard_map/ppermute | solution.py:748
  462.2 3.3 collective-permute-done.8.refs_4_
  465.6 4.5 collective-permute-done.28.b_ref
  470.6 2.7 kv_combine.2
  473.3 13.9 %attn_out.1 = bf16[1024,2048]{1,0:T(8,128)(2,1)} custom-call(s32[1]{0:T(128)} %bitcast.s_ref.core_ref, bf16[2,2048,256]{2,1,0:T(8,128)(2,1)} %get-tuple-element.44.refs_0_, bf16[2,2048,256]{2,1,0:T(8,128)(2,1)} %get-tuple-element.47.refs_1_, bf16[2,2048,256]{2,1,0:T(8,128)(2,1)} %get-tuple-element.50.refs_2_, ...), custom_call_target="tpu_custom_call" | custom-call | flops 8589934592 | bytes 16777216 | tf_op jit(solution)/shard_map/attn_out/pallas_call | solution.py:669
  487.2 17.0 %grad_hidden.1 = bf16[1024,2048]{1,0:T(8,128)(2,1)} custom-call(s32[1]{0:T(128)} %bitcast.s_ref.core_ref, bf16[2,2048,256]{2,1,0:T(8,128)(2,1)} %get-tuple-element.44.refs_0_, bf16[2,2048,256]{2,1,0:T(8,128)(2,1)} %get-tuple-element.47.refs_1_, bf16[2,2048,256]{2,1,0:T(8,128)(2,1)} %get-tuple-element.50.refs_2_, ...), custom_call_target="tpu_custom_call" | custom-call | flops 10737418240 | bytes 16777216 | tf_op jit(solution)/shard_map/grad_hidden/pallas_call | solution.py:710
  504.2 2.8 kv_combine.3
  507.0 8.5 %combine.4 = (f32[2048,2048]{1,0:T(8,128)}, f32[2048,2048]{1,0:T(8,128)}) custom-call(s32[1]{0:T(128)} %bitcast.s_ref.core_ref, bf16[2,256,2048]{2,1,0:T(8,128)(2,1)} %bitcast.16, bf16[2,256,2048]{2,1,0:T(8,128)(2,1)} %collective-permute-done.23.b_ref, bf16[2,256,2048]{2,1,0:T(8,128)(2,1)} %collective-permute-done.24.c_ref, ...), custom_call_target="tpu_custom_call" | custom-call | flops 536870912 | bytes 16777216 | tf_op jit(solution)/shard_map/combine/pallas_call | solution.py:627
  515.5 8.5 %combine.5 = (f32[2048,2048]{1,0:T(8,128)}, f32[2048,2048]{1,0:T(8,128)}) custom-call(s32[1]{0:T(128)} %bitcast.s_ref.core_ref, bf16[2,256,2048]{2,1,0:T(8,128)(2,1)} %bitcast.13, bf16[2,256,2048]{2,1,0:T(8,128)(2,1)} %collective-permute-done.20.b_ref, ...), custom_call_target="tpu_custom_call", output_to_operand_aliasing={{0}: (5, {}), {1}: (6, {})} | custom-call | flops 536870912 | bytes 16777216 | tf_op jit(solution)/shard_map/combine/pallas_call | solution.py:627
  524.0 8.5 %combine.6 = (f32[2048,2048]{1,0:T(8,128)}, f32[2048,2048]{1,0:T(8,128)}) custom-call(s32[1]{0:T(128)} %bitcast.s_ref.core_ref, bf16[2,256,2048]{2,1,0:T(8,128)(2,1)} %bitcast.10, bf16[2,256,2048]{2,1,0:T(8,128)(2,1)} %collective-permute-done.17.b_ref, ...), custom_call_target="tpu_custom_call", output_to_operand_aliasing={{0}: (5, {}), {1}: (6, {})} | custom-call | flops 536870912 | bytes 16777216 | tf_op jit(solution)/shard_map/combine/pallas_call | solution.py:627
  532.5 8.5 %combine.7 = (f32[2048,2048]{1,0:T(8,128)}, f32[2048,2048]{1,0:T(8,128)}) custom-call(s32[1]{0:T(128)} %bitcast.s_ref.core_ref, bf16[2,256,2048]{2,1,0:T(8,128)(2,1)} %bitcast.7, bf16[2,256,2048]{2,1,0:T(8,128)(2,1)} %collective-permute-done.14.b_ref, ...), custom_call_target="tpu_custom_call", output_to_operand_aliasing={{0}: (5, {}), {1}: (6, {})} | custom-call | flops 536870912 | bytes 16777216 | tf_op jit(solution)/shard_map/combine/pallas_call | solution.py:627
  (69 shorter events, 7.7 us)
Async XLA Ops:
  0.6 24.4 %collective-permute-start.3 = (bf16[1024,2048]{1,0:T(8,128)(2,1)}, bf16[1024,2048]{1,0:T(8,128)(2,1)}, u32[]{:S(2)}, u32[]{:S(2)}) collective-permute-start(bf16[1024,2048]{1,0:T(8,128)(2,1)} %x_own.9), channel_id=1, source_target_pairs={{0,1},{1,0},{2,3},{3,2},{4,5},{5,4},{6,7},{7,6}} | collective-permute-start | bytes 12582920 | tf_op jit(solution)/shard_map/ppermute | solution.py:745
  1.5 36.2 %collective-permute-start.5 = (bf16[1024,2048]{1,0:T(8,128)(2,1)}, bf16[1024,2048]{1,0:T(8,128)(2,1)}, u32[]{:S(2)}, u32[]{:S(2)}) collective-permute-start(bf16[1024,2048]{1,0:T(8,128)(2,1)} %g_own.7), channel_id=1, source_target_pairs={{0,1},{1,0},{2,3},{3,2},{4,5},{5,4},{6,7},{7,6}} | collective-permute-start | bytes 12582920 | tf_op jit(solution)/shard_map/ppermute | solution.py:745
  1.5 17.3 %collective-permute-start = (s32[1024]{0:T(1024)}, s32[1024]{0:T(1024)S(1)}, u32[]{:S(2)}, u32[]{:S(2)}) collective-permute-start(s32[1024]{0:T(1024)} %param.11), channel_id=1, source_target_pairs={{0,1},{1,0},{2,3},{3,2},{4,5},{5,4},{6,7},{7,6}} | collective-permute-start | bytes 12296 | tf_op jit(solution)/shard_map/ppermute | solution.py:745
  2.0 17.0 %collective-permute-start.1 = (s32[1024]{0:T(1024)}, s32[1024]{0:T(1024)S(1)}, u32[]{:S(2)}, u32[]{:S(2)}) collective-permute-start(s32[1024]{0:T(1024)} %param.11), channel_id=1, source_target_pairs={{0,2},{1,3},{2,0},{3,1},{4,6},{5,7},{6,4},{7,5}} | collective-permute-start | bytes 12296 | tf_op jit(solution)/shard_map/ppermute | solution.py:748
  8.1 16.9 %collective-permute-start.4 = (f32[1024,128]{1,0:T(8,128)}, f32[1024,128]{1,0:T(8,128)}, u32[]{:S(2)}, u32[]{:S(2)}) collective-permute-start(f32[1024,128]{1,0:T(8,128)} %pad_maximum_fusion.tab_ref.tab_own), channel_id=1, source_target_pairs={{0,1},{1,0},{2,3},{3,2},{4,5},{5,4},{6,7},{7,6}} | collective-permute-start | bytes 1572872 | tf_op jit(solution)/shard_map/ppermute | solution.py:745
  8.3 10.5 %copy-start.1 = (s32[1024]{0:T(1024)S(1)}, s32[1024]{0:T(1024)}, u32[]{:S(2)}) copy-start(s32[1024]{0:T(1024)} %param.11) | copy-start | bytes 12292
  18.8 4.8 collective-permute-start.2
  19.0 32.9 %collective-permute-start.6 = (bf16[1024,256]{1,0:T(8,128)(2,1)}, bf16[1024,256]{1,0:T(8,128)(2,1)}, u32[]{:S(2)}, u32[]{:S(2)}) collective-permute-start(bf16[1024,256]{1,0:T(8,128)(2,1)} %get-tuple-element.42.kvc_own), channel_id=1, source_target_pairs={{0,2},{1,3},{4,6},{5,7}} | collective-permute-start | bytes 1572872 | tf_op jit(solution)/shard_map/ppermute | solution.py:766
  35.6 16.3 %collective-permute-start.7 = (bf16[1024,256]{1,0:T(8,128)(2,1)}, bf16[1024,256]{1,0:T(8,128)(2,1)}, u32[]{:S(2)}, u32[]{:S(2)}) collective-permute-start(bf16[1024,256]{1,0:T(8,128)(2,1)} %get-tuple-element.43.kvc_oth), channel_id=1, source_target_pairs={{0,2},{1,3},{4,6},{5,7}} | collective-permute-start | bytes 1572872 | tf_op jit(solution)/shard_map/ppermute | solution.py:773
  187.0 73.2 %collective-permute-start.12 = (bf16[256,2048]{1,0:T(8,128)(2,1)}, bf16[256,2048]{1,0:T(8,128)(2,1)}, u32[]{:S(2)}, u32[]{:S(2)}) collective-permute-start(bf16[256,2048]{1,0:T(8,128)(2,1)} %get-tuple-element.55), channel_id=1, source_target_pairs={{2,0},{3,1},{6,4},{7,5}} | collective-permute-start | bytes 3145736 | tf_op jit(solution)/shard_map/ppermute | solution.py:795
  188.3 139.2 %collective-permute-start.23 = (bf16[2,256,2048]{2,1,0:T(8,128)(2,1)}, bf16[2,256,2048]{2,1,0:T(8,128)(2,1)}, u32[]{:S(2)}, u32[]{:S(2)}) collective-permute-start(bf16[2,256,2048]{2,1,0:T(8,128)(2,1)} %bitcast.14), channel_id=1, source_target_pairs={{0,2},{1,3},{2,0},{3,1},{4,6},{5,7},{6,4},{7,5}} | collective-permute-start | bytes 6291464 | tf_op jit(solution)/shard_map/ppermute | solution.py:748
  271.4 56.1 %collective-permute-start.27 = (bf16[256,2048]{1,0:T(8,128)(2,1)}, bf16[256,2048]{1,0:T(8,128)(2,1)S(1)}, u32[]{:S(2)}, u32[]{:S(2)}) collective-permute-start(bf16[256,2048]{1,0:T(8,128)(2,1)} %kvgrad.1.a_ref), channel_id=1, source_target_pairs={{0,2},{1,3},{2,0},{3,1},{4,6},{5,7},{6,4},{7,5}} | collective-permute-start | bytes 3145736 | tf_op jit(solution)/shard_map/ppermute | solution.py:748
  271.4 56.1 %collective-permute-start.26 = (bf16[256,2048]{1,0:T(8,128)(2,1)}, bf16[256,2048]{1,0:T(8,128)(2,1)}, u32[]{:S(2)}, u32[]{:S(2)}) collective-permute-start(bf16[256,2048]{1,0:T(8,128)(2,1)} %kvgrad.1.a_ref), channel_id=1, source_target_pairs={{0,1},{1,0},{2,3},{3,2},{4,5},{5,4},{6,7},{7,6}} | collective-permute-start | bytes 3145736 | tf_op jit(solution)/shard_map/ppermute | solution.py:745
  271.4 58.2 %collective-permute-start.24 = (bf16[2,256,2048]{2,1,0:T(8,128)(2,1)}, bf16[2,256,2048]{2,1,0:T(8,128)(2,1)}, u32[]{:S(2)}, u32[]{:S(2)}) collective-permute-start(bf16[2,256,2048]{2,1,0:T(8,128)(2,1)} %bitcast.15), channel_id=1, source_target_pairs={{0,1},{1,0},{2,3},{3,2},{4,5},{5,4},{6,7},{7,6}} | collective-permute-start | bytes 6291464 | tf_op jit(solution)/shard_map/ppermute | solution.py:745
  271.9 100.6 %collective-permute-start.20 = (bf16[2,256,2048]{2,1,0:T(8,128)(2,1)}, bf16[2,256,2048]{2,1,0:T(8,128)(2,1)}, u32[]{:S(2)}, u32[]{:S(2)}) collective-permute-start(bf16[2,256,2048]{2,1,0:T(8,128)(2,1)} %bitcast.11), channel_id=1, source_target_pairs={{0,2},{1,3},{2,0},{3,1},{4,6},{5,7},{6,4},{7,5}} | collective-permute-start | bytes 6291464 | tf_op jit(solution)/shard_map/ppermute | solution.py:748
  327.5 134.1 %copy-start = (bf16[256,2048]{1,0:T(8,128)(2,1)}, bf16[256,2048]{1,0:T(8,128)(2,1)S(1)}, u32[]{:S(2)}) copy-start(bf16[256,2048]{1,0:T(8,128)(2,1)S(1)} %collective-permute-done.27.b_ref) | copy-start | bytes 3145732
  327.5 45.1 %collective-permute-start.21 = (bf16[2,256,2048]{2,1,0:T(8,128)(2,1)}, bf16[2,256,2048]{2,1,0:T(8,128)(2,1)}, u32[]{:S(2)}, u32[]{:S(2)}) collective-permute-start(bf16[2,256,2048]{2,1,0:T(8,128)(2,1)} %bitcast.12), channel_id=1, source_target_pairs={{0,1},{1,0},{2,3},{3,2},{4,5},{5,4},{6,7},{7,6}} | collective-permute-start | bytes 6291464 | tf_op jit(solution)/shard_map/ppermute | solution.py:745
  327.5 90.0 %collective-permute-start.17 = (bf16[2,256,2048]{2,1,0:T(8,128)(2,1)}, bf16[2,256,2048]{2,1,0:T(8,128)(2,1)}, u32[]{:S(2)}, u32[]{:S(2)}) collective-permute-start(bf16[2,256,2048]{2,1,0:T(8,128)(2,1)} %bitcast.8), channel_id=1, source_target_pairs={{0,2},{1,3},{2,0},{3,1},{4,6},{5,7},{6,4},{7,5}} | collective-permute-start | bytes 6291464 | tf_op jit(solution)/shard_map/ppermute | solution.py:748
  327.5 133.5 %collective-permute-start.14 = (bf16[2,256,2048]{2,1,0:T(8,128)(2,1)}, bf16[2,256,2048]{2,1,0:T(8,128)(2,1)}, u32[]{:S(2)}, u32[]{:S(2)}) collective-permute-start(bf16[2,256,2048]{2,1,0:T(8,128)(2,1)} %bitcast.5), channel_id=1, source_target_pairs={{0,2},{1,3},{2,0},{3,1},{4,6},{5,7},{6,4},{7,5}} | collective-permute-start | bytes 6291464 | tf_op jit(solution)/shard_map/ppermute | solution.py:748
  329.5 132.0 %collective-permute-start.11 = (bf16[2,2048,256]{2,1,0:T(8,128)(2,1)}, bf16[2,2048,256]{2,1,0:T(8,128)(2,1)S(1)}, u32[]{:S(2)}, u32[]{:S(2)}) collective-permute-start(bf16[2,2048,256]{2,1,0:T(8,128)(2,1)} %get-tuple-element.53.refs_3_), channel_id=1, source_target_pairs={{0,1},{1,0},{2,3},{3,2},{4,5},{5,4},{6,7},{7,6}} | collective-permute-start | bytes 6291464 | tf_op jit(solution)/shard_map/ppermute | solution.py:745
  372.5 88.5 %collective-permute-start.13 = (bf16[2048,256]{1,0:T(8,128)(2,1)}, bf16[2048,256]{1,0:T(8,128)(2,1)S(1)}, u32[]{:S(2)}, u32[]{:S(2)}) collective-permute-start(bf16[2048,256]{1,0:T(8,128)(2,1)} %get-tuple-element.56.refs_8_), channel_id=1, source_target_pairs={{0,1},{1,0},{2,3},{3,2},{4,5},{5,4},{6,7},{7,6}} | collective-permute-start | bytes 3145736 | tf_op jit(solution)/shard_map/ppermute | solution.py:745
  372.5 89.1 %collective-permute-start.10 = (bf16[2,2048,256]{2,1,0:T(8,128)(2,1)}, bf16[2,2048,256]{2,1,0:T(8,128)(2,1)S(1)}, u32[]{:S(2)}, u32[]{:S(2)}) collective-permute-start(bf16[2,2048,256]{2,1,0:T(8,128)(2,1)} %get-tuple-element.50.refs_2_), channel_id=1, source_target_pairs={{0,1},{1,0},{2,3},{3,2},{4,5},{5,4},{6,7},{7,6}} | collective-permute-start | bytes 6291464 | tf_op jit(solution)/shard_map/ppermute | solution.py:745
  417.5 44.6 %collective-permute-start.9 = (bf16[2,2048,256]{2,1,0:T(8,128)(2,1)}, bf16[2,2048,256]{2,1,0:T(8,128)(2,1)S(1)}, u32[]{:S(2)}, u32[]{:S(2)}) collective-permute-start(bf16[2,2048,256]{2,1,0:T(8,128)(2,1)} %get-tuple-element.47.refs_1_), channel_id=1, source_target_pairs={{0,1},{1,0},{2,3},{3,2},{4,5},{5,4},{6,7},{7,6}} | collective-permute-start | bytes 6291464 | tf_op jit(solution)/shard_map/ppermute | solution.py:745
  461.0 4.4 collective-permute-start.8
  461.1 9.1 %copy-start.6 = (bf16[2048,256]{1,0:T(8,128)(2,1)}, bf16[2048,256]{1,0:T(8,128)(2,1)S(1)}, u32[]{:S(2)}) copy-start(bf16[2048,256]{1,0:T(8,128)(2,1)S(1)} %collective-permute-done.13.refs_9_) | copy-start | bytes 3145732
  461.1 9.1 %collective-permute-start.25 = (bf16[2,256,2048]{2,1,0:T(8,128)(2,1)}, bf16[2,256,2048]{2,1,0:T(8,128)(2,1)}, u32[]{:S(2)}, u32[]{:S(2)}) collective-permute-start(bf16[2,256,2048]{2,1,0:T(8,128)(2,1)} %collective-permute-done.23.b_ref), channel_id=1, source_target_pairs={{0,1},{1,0},{2,3},{3,2},{4,5},{5,4},{6,7},{7,6}} | collective-permute-start | bytes 6291464 | tf_op jit(solution)/shard_map/ppermute | solution.py:745
  461.6 8.5 %collective-permute-start.28 = (bf16[256,2048]{1,0:T(8,128)(2,1)S(1)}, bf16[256,2048]{1,0:T(8,128)(2,1)}, u32[]{:S(2)}, u32[]{:S(2)}) collective-permute-start(bf16[256,2048]{1,0:T(8,128)(2,1)S(1)} %collective-permute-done.27.b_ref), channel_id=1, source_target_pairs={{0,1},{1,0},{2,3},{3,2},{4,5},{5,4},{6,7},{7,6}} | collective-permute-start | bytes 3145736 | tf_op jit(solution)/shard_map/ppermute | solution.py:745
  461.6 53.9 %collective-permute-start.22 = (bf16[2,256,2048]{2,1,0:T(8,128)(2,1)}, bf16[2,256,2048]{2,1,0:T(8,128)(2,1)}, u32[]{:S(2)}, u32[]{:S(2)}) collective-permute-start(bf16[2,256,2048]{2,1,0:T(8,128)(2,1)} %collective-permute-done.20.b_ref), channel_id=1, source_target_pairs={{0,1},{1,0},{2,3},{3,2},{4,5},{5,4},{6,7},{7,6}} | collective-permute-start | bytes 6291464 | tf_op jit(solution)/shard_map/ppermute | solution.py:745
  462.1 61.9 %collective-permute-start.18 = (bf16[2,256,2048]{2,1,0:T(8,128)(2,1)}, bf16[2,256,2048]{2,1,0:T(8,128)(2,1)}, u32[]{:S(2)}, u32[]{:S(2)}) collective-permute-start(bf16[2,256,2048]{2,1,0:T(8,128)(2,1)} %bitcast.9), channel_id=1, source_target_pairs={{0,1},{1,0},{2,3},{3,2},{4,5},{5,4},{6,7},{7,6}} | collective-permute-start | bytes 6291464 | tf_op jit(solution)/shard_map/ppermute | solution.py:745
  465.4 58.6 %collective-permute-start.19 = (bf16[2,256,2048]{2,1,0:T(8,128)(2,1)}, bf16[2,256,2048]{2,1,0:T(8,128)(2,1)}, u32[]{:S(2)}, u32[]{:S(2)}) collective-permute-start(bf16[2,256,2048]{2,1,0:T(8,128)(2,1)} %collective-permute-done.17.b_ref), channel_id=1, source_target_pairs={{0,1},{1,0},{2,3},{3,2},{4,5},{5,4},{6,7},{7,6}} | collective-permute-start | bytes 6291464 | tf_op jit(solution)/shard_map/ppermute | solution.py:745
  470.0 62.4 %collective-permute-start.15 = (bf16[2,256,2048]{2,1,0:T(8,128)(2,1)}, bf16[2,256,2048]{2,1,0:T(8,128)(2,1)}, u32[]{:S(2)}, u32[]{:S(2)}) collective-permute-start(bf16[2,256,2048]{2,1,0:T(8,128)(2,1)} %bitcast.6), channel_id=1, source_target_pairs={{0,1},{1,0},{2,3},{3,2},{4,5},{5,4},{6,7},{7,6}} | collective-permute-start | bytes 6291464 | tf_op jit(solution)/shard_map/ppermute | solution.py:745
  470.2 62.3 %collective-permute-start.16 = (bf16[2,256,2048]{2,1,0:T(8,128)(2,1)}, bf16[2,256,2048]{2,1,0:T(8,128)(2,1)}, u32[]{:S(2)}, u32[]{:S(2)}) collective-permute-start(bf16[2,256,2048]{2,1,0:T(8,128)(2,1)} %collective-permute-done.14.b_ref), channel_id=1, source_target_pairs={{0,1},{1,0},{2,3},{3,2},{4,5},{5,4},{6,7},{7,6}} | collective-permute-start | bytes 6291464 | tf_op jit(solution)/shard_map/ppermute | solution.py:745
  (4 other events, 29.9 us)
